TPU v7x, 32 devices: a whole 2x2x4 slice. The times are simulated.
32 devices in a mesh: dp: 4 (over z), ep: 8 (over y, x, core).
Axes of the slice: x: 2, y: 2, z: 4, core: 2. Of those that a mesh axis runs over, the one named last changes fastest.
Arguments:
- tok_x: bfloat16 [16384, 4096], P(('dp', 'ep'))
- tok_dy: bfloat16 [16384, 4096], P(('dp', 'ep'))
- exp_first: int32 [16384], P(('dp', 'ep'))
- exp_second: int32 [16384], P(('dp', 'ep'))
- eligible: int32 [16384, 8], P(('dp', 'ep'))
- slot_first: int32 [16384], P(('dp', 'ep'))
- slot_second: int32 [16384], P(('dp', 'ep'))
- ln_weight: bfloat16 [4096], replicated
- ln_bias: bfloat16 [4096], replicated
- router: bfloat16 [4096, 8], replicated
- w_gate: bfloat16 [8, 4096, 1376], P('ep')
- w_up: bfloat16 [8, 4096, 1376], P('ep')
- w_down: bfloat16 [8, 1376, 4096], P('ep')
Outputs:
- output 1: bfloat16 [16384, 4096], P(('dp', 'ep'))
- output 2: bfloat16 [16384, 4096], P(('dp', 'ep'))
- output 3: float32 [8, 4096, 1376], P('ep')
- output 4: float32 [8, 4096, 1376], P('ep')
- output 5: float32 [8, 1376, 4096], P('ep')
- output 6: float32 [4096, 8], replicated
- output 7: float32 [4096], replicated
- output 8: float32 [4096], replicated
All inputs are finite; a program needn't handle non-finite values.
Results may differ from a plain program's by a relative error of at most 0.00494142.
Values are sent between devices in bfloat16 or wider.
A program may use at most 1 GiB of HBM per device.

v0:
```python
import jax
import jax.numpy as jnp
from jax import lax
from jax.sharding import PartitionSpec as P

LN_EPS = 1e-5


def layer_norm(x_rows, ln_weight, ln_bias):
    x_float = x_rows.astype(jnp.float32)
    centered = x_float - jnp.mean(x_float, axis=-1, keepdims=True)
    inv_std = lax.rsqrt(jnp.mean(centered * centered, axis=-1, keepdims=True) + LN_EPS)
    x_hat = centered * inv_std
    hidden = (x_hat * ln_weight.astype(jnp.float32) + ln_bias.astype(jnp.float32)).astype(jnp.bfloat16)
    return hidden, x_hat, inv_std


def layer_norm_back(grad_h, x_hat, inv_std, ln_weight):
    scaled = grad_h * ln_weight.astype(jnp.float32)
    return inv_std * (scaled - jnp.mean(scaled, axis=-1, keepdims=True)
                      - x_hat * jnp.mean(scaled * x_hat, axis=-1, keepdims=True))


def masked_gate(logits, allowed, choice):
    expert_ids = jnp.arange(logits.shape[-1])
    prob_all = jax.nn.softmax(jnp.where(allowed, logits, -1e30), axis=-1)
    picked = (choice[:, None] == expert_ids[None, :]).astype(jnp.float32)
    return jnp.sum(prob_all * picked, axis=-1), prob_all, picked


def solution(mesh):
    n_ep = mesh.shape['ep']
    tok_spec = P(('dp', 'ep'), None)
    row_spec = P(('dp', 'ep'))
    exp_spec = P('ep', None, None)

    def local_step(tok_x, tok_dy, exp_first, exp_second, eligible, slot_first, slot_second,
                   ln_weight, ln_bias, router, w_gate, w_up, w_down):
        n_local, d_model = tok_x.shape
        n_exp = eligible.shape[1]
        local_exp = w_gate.shape[0]
        slot_cap = 3 * n_local // n_exp
        f32 = jnp.float32
        hidden, x_hat, inv_std = layer_norm(tok_x, ln_weight, ln_bias)
        logits = jnp.dot(hidden, router, preferred_element_type=f32)
        expert_ids = jnp.arange(n_exp)
        allowed = eligible > 0
        gate_one, prob_one, pick_one = masked_gate(logits, allowed, exp_first)
        gate_two, prob_two, pick_two = masked_gate(logits, allowed & (expert_ids[None, :] != exp_first[:, None]), exp_second)
        row_ids = jnp.arange(n_exp * slot_cap)
        pos_one = jnp.where(slot_first >= 0, exp_first * slot_cap + slot_first, -1)
        pos_two = jnp.where(slot_second >= 0, exp_second * slot_cap + slot_second, -1)
        sel_one = (pos_one[:, None] == row_ids[None, :]).astype(jnp.bfloat16)
        sel_two = (pos_two[:, None] == row_ids[None, :]).astype(jnp.bfloat16)
        sel_both = sel_one + sel_two
        hid_buf = jnp.einsum('tp,td->pd', sel_both, hidden, preferred_element_type=f32).astype(jnp.bfloat16)
        hid_recv = lax.all_to_all(hid_buf.reshape(n_ep, local_exp, slot_cap, d_model), 'ep', 0, 0, tiled=True)
        pre_gate = jnp.einsum('sgcd,gdf->sgcf', hid_recv, w_gate, preferred_element_type=f32)
        pre_up = jnp.einsum('sgcd,gdf->sgcf', hid_recv, w_up, preferred_element_type=f32)
        sig_gate = jax.nn.sigmoid(pre_gate)
        silu_gate = pre_gate * sig_gate
        inner_act = (silu_gate * pre_up).astype(jnp.bfloat16)
        exp_out = jnp.einsum('sgcf,gfd->sgcd', inner_act, w_down, preferred_element_type=f32).astype(jnp.bfloat16)
        out_back = lax.all_to_all(exp_out, 'ep', 0, 0, tiled=True).reshape(n_exp * slot_cap, d_model)
        out_one = jnp.dot(sel_one, out_back, preferred_element_type=f32)
        out_two = jnp.dot(sel_two, out_back, preferred_element_type=f32)
        y_mix = gate_one[:, None] * out_one + gate_two[:, None] * out_two
        out_tok = (tok_x.astype(f32) + y_mix).astype(jnp.bfloat16)
        dy_float = tok_dy.astype(f32)
        grad_one = (gate_one[:, None] * dy_float).astype(jnp.bfloat16)
        grad_two = (gate_two[:, None] * dy_float).astype(jnp.bfloat16)
        grad_buf = (jnp.einsum('tp,td->pd', sel_one, grad_one, preferred_element_type=f32)
                    + jnp.einsum('tp,td->pd', sel_two, grad_two, preferred_element_type=f32)).astype(jnp.bfloat16)
        grad_recv = lax.all_to_all(grad_buf.reshape(n_ep, local_exp, slot_cap, d_model), 'ep', 0, 0, tiled=True)
        grad_inner = jnp.einsum('sgcd,gfd->sgcf', grad_recv, w_down, preferred_element_type=f32)
        dw_down = jnp.einsum('sgcf,sgcd->gfd', inner_act, grad_recv, preferred_element_type=f32)
        grad_pre_gate = (grad_inner * pre_up * sig_gate * (1.0 + pre_gate * (1.0 - sig_gate))).astype(jnp.bfloat16)
        grad_pre_up = (grad_inner * silu_gate).astype(jnp.bfloat16)
        dw_gate = jnp.einsum('sgcd,sgcf->gdf', hid_recv, grad_pre_gate, preferred_element_type=f32)
        dw_up = jnp.einsum('sgcd,sgcf->gdf', hid_recv, grad_pre_up, preferred_element_type=f32)
        grad_hid = (jnp.einsum('sgcf,gdf->sgcd', grad_pre_gate, w_gate, preferred_element_type=f32)
                    + jnp.einsum('sgcf,gdf->sgcd', grad_pre_up, w_up, preferred_element_type=f32)).astype(jnp.bfloat16)
        hid_back = lax.all_to_all(grad_hid, 'ep', 0, 0, tiled=True).reshape(n_exp * slot_cap, d_model)
        grad_exp = jnp.dot(sel_both, hid_back, preferred_element_type=f32)
        dgate_one = jnp.sum(dy_float * out_one, axis=-1)
        dgate_two = jnp.sum(dy_float * out_two, axis=-1)
        d_logits = ((dgate_one * gate_one)[:, None] * (pick_one - prob_one)
                    + (dgate_two * gate_two)[:, None] * (pick_two - prob_two)).astype(jnp.bfloat16)
        d_router = jnp.einsum('td,te->de', hidden, d_logits, preferred_element_type=f32)
        grad_h = jnp.einsum('te,de->td', d_logits, router, preferred_element_type=f32) + grad_exp
        d_ln_weight = jnp.sum(grad_h * x_hat, axis=0)
        d_ln_bias = jnp.sum(grad_h, axis=0)
        dx_tok = (dy_float + layer_norm_back(grad_h, x_hat, inv_std, ln_weight)).astype(jnp.bfloat16)
        dw_gate = lax.psum(dw_gate, 'dp')
        dw_up = lax.psum(dw_up, 'dp')
        dw_down = lax.psum(dw_down, 'dp')
        d_router = lax.psum(d_router, ('dp', 'ep'))
        d_ln_weight = lax.psum(d_ln_weight, ('dp', 'ep'))
        d_ln_bias = lax.psum(d_ln_bias, ('dp', 'ep'))
        return out_tok, dx_tok, dw_gate, dw_up, dw_down, d_router, d_ln_weight, d_ln_bias

    return jax.shard_map(
        local_step, mesh=mesh,
        in_specs=(tok_spec, tok_spec, row_spec, row_spec, tok_spec, row_spec, row_spec,
                  P(), P(), P(), exp_spec, exp_spec, exp_spec),
        out_specs=(tok_spec, tok_spec, exp_spec, exp_spec, exp_spec, P(), P(), P()),
        check_vma=False)
```

profile of v0, /device:TPU:0, one launch (start us, length us, event | category | flops | bytes accessed | tf_op | source)
XLA Modules:
  0.0 2993.6 jit_solution(11943967398673653156)
XLA Ops:
  7.2 0.0 copy-start
  7.2 0.0 copy-start.1
  7.2 0.9 convert_element_type.85
  8.0 0.9 convert_element_type.84
  9.0 2.8 convert_reduce_fusion
  11.8 0.0 copy-start.17
  11.8 0.0 copy-start.34
  11.8 0.0 copy-start.48
  11.9 0.0 copy-start.49
  11.9 0.0 copy-start.6
  11.9 3.6 fusion.42
  15.5 2.3 fusion.37
  17.8 0.0 copy-start.4
  17.8 2.0 copy-done.4
  19.8 1.2 fusion.82
  21.0 0.0 copy-start.8
  21.1 0.0 copy-start.44
  21.2 0.5 copy-done.8
  21.7 0.0 copy-start.46
  21.8 11.9 fusion.56
  33.7 15.9 add_convert_fusion.1
  49.6 16.0 all-to-all-start.2
  65.6 12.3 convolution_convert_fusion
  77.9 127.5 %all-to-all-done.2 = bf16[8,1,192,4096]{3,2,1,0:T(8,128)(2,1)} async-done(((bf16[8,1,192,4096]{3,2,1,0:T(8,128)(2,1)}), bf16[8,1,192,4096]{3,2,1,0:T(8,128)(2,1)}, u32[]{:S(2)}, u32[]{:S(2)}) %all-to-all-start.2) | async-done | bytes 12582944 | tf_op jit(solution)/shard_map/all_to_all | solution.py:74
  205.4 5.4 all-to-all-start
  210.8 27.1 fusion.2
  238.0 111.8 %all-to-all-done = bf16[8,1,192,4096]{3,2,1,0:T(8,128)(2,1)} async-done(((bf16[8,1,192,4096]{3,2,1,0:T(8,128)(2,1)}), bf16[8,1,192,4096]{3,2,1,0:T(8,128)(2,1)}, u32[]{:S(2)}, u32[]{:S(2)}) %all-to-all-start) | async-done | bytes 12582944 | tf_op jit(solution)/shard_map/all_to_all | solution.py:57
  349.8 27.1 fusion.6
  376.9 31.9 %fusion.29 = (bf16[8,1,192,1376]{3,2,0,1:T(8,128)(2,1)}, bf16[8,192,1376]{2,1,0:T(8,128)(2,1)}, bf16[8,192,1376]{2,1,0:T(8,128)(2,1)}) fusion(f32[8,192,1376]{2,1,0:T(8,128)} %fusion.2, f32[8,192,1376]{2,1,0:T(8,128)} %fusion.6, bf16[1,4096,1376]{1,2,0:T(8,128)(2,1)} %param.23, bf16[8,1,192,4096]{3,2,1,0:T(8,128)(2,1)} %all-to-all-done), kind=kOutput, calls=%fused_computation.44 | convolution fusion | flops 17345789952 | bytes 53444608 | tf_op jit(solution)/shard_map/sgcd,gdf->sgcf/dot_general | solution.py:58
  408.8 25.1 convert_bitcast_fusion
  433.9 5.5 all-to-all-start.1
  439.4 0.0 all-reduce.5.cloned.1.call-start
  439.5 0.0 slice-start.7
  439.5 24.5 convolution_bitcast_fusion.2
  464.0 22.8 convolution_bitcast_fusion
  486.7 91.6 %all-to-all-done.1 = bf16[8,1,192,4096]{3,2,1,0:T(8,128)(2,1)} async-done(((bf16[8,1,192,4096]{3,2,1,0:T(8,128)(2,1)}), bf16[8,1,192,4096]{3,2,1,0:T(8,128)(2,1)}, u32[]{:S(2)}, u32[]{:S(2)}) %all-to-all-start.1) | async-done | bytes 12582944 | tf_op jit(solution)/shard_map/all_to_all | solution.py:64
  578.4 0.0 copy-start.47
  578.4 11.9 fusion.60
  590.3 0.0 copy-start.5
  590.3 0.0 copy-start.9
  590.4 0.0 copy-start.18
  590.4 0.0 copy-start.35
  590.4 17.1 fusion.44
  607.6 0.5 copy-done.40
  608.1 0.6 copy-done.42
  608.8 1.3 fusion.84
  610.1 0.0 all-reduce.5.cloned.1.call-update
  610.1 0.0 all-reduce.7.cloned.1.call-start
  610.2 24.6 convolution_bitcast_fusion.1
  634.7 0.0 all-reduce.7.cloned.1.call-update
  634.8 26.2 fusion.13
  660.9 28.7 fusion
  689.7 143.0 %all_to_all.20 = bf16[8,1,192,4096]{3,2,1,0:T(8,128)(2,1)S(1)} all-to-all(bf16[8,1,192,4096]{3,2,1,0:T(8,128)(2,1)} %fusion), channel_id=1, replica_groups=mesh['dp'=4,'ep'=8] {'ep'}, dimensions={0} | all-to-all | bytes 25165824 | tf_op jit(solution)/shard_map/all_to_all | solution.py:83
  832.7 0.0 copy-start.12
  832.8 0.0 copy-start.19
  832.9 6.9 fusion.65
  839.9 6.1 fusion.41
  846.1 46.3 %all-reduce = (f32[4096]{0:T(1024)}, f32[4096]{0:T(1024)}) all-reduce(f32[4096]{0:T(1024)S(1)} %get-tuple-element.8, f32[4096]{0:T(1024)S(1)} %get-tuple-element.11), channel_id=1, replica_groups=mesh['dp'=4,'ep'=8] {'dp','ep'}, use_global_device_ids=true, to_apply=%region_17.18 | all-reduce | flops 8192 | bytes 65536 | tf_op jit(solution)/shard_map/psum | solution.py:98
  892.4 9.3 fusion.48
  901.6 2039.9 %all-reduce.7.cloned.1.call-done = (f32[1,4096,1376]{1,2,0:T(8,128)}, f32[1,4096,1376]{1,2,0:T(8,128)}, f32[1,1376,4096]{2,1,0:T(8,128)}) async-done(((f32[1,4096,1376]{1,2,0:T(8,128)}, f32[1,4096,1376]{1,2,0:T(8,128)}, f32[1,1376,4096]{2,1,0:T(8,128)}), (f32[1,4096,1376]{1,2,0:T(8,128)}, f32[1,4096,1376]{1,2,0:T(8,128)}, f32[1,1376,4096]{2,1,0:T(8,128)})) %all-reduce.7.cloned.1.call-update) | async-done | bytes 67633168 | tf_op jit(solution)/shard_map/psum | solution.py:94
  2941.5 18.1 copy.29
  2959.7 18.1 copy.30
  2977.9 8.1 copy.31
  2985.9 0.7 copy.32
  (123 shorter events, 0.4 us)
Async XLA Ops:
  7.2 12.6 copy-start
  7.2 8.3 copy-start.1
  9.0 6.5 copy-start.11
  9.0 10.8 copy-start.39
  11.8 9.2 copy-start.26
  11.8 9.2 copy-start.17
  11.8 9.8 copy-start.34
  11.8 9.8 copy-start.48
  11.9 9.8 copy-start.49
  11.9 9.9 copy-start.6
  15.5 6.2 copy-start.37
  17.8 2.0 copy-start.4
  21.0 0.7 copy-start.20
  21.1 12.6 copy-start.44
  21.7 12.1 copy-start.46
  21.7 43.9 %copy-start.50 = (s32[512]{0:T(512)}, s32[512]{0:T(512)S(1)}, u32[]{:S(2)}) copy-start(s32[512]{0:T(512)S(1)} %get-tuple-element.31) | copy-start | bytes 6148
  21.7 43.9 %copy-start.53 = (s32[512]{0:T(512)}, s32[512]{0:T(512)S(1)}, u32[]{:S(2)}) copy-start(s32[512]{0:T(512)S(1)} %get-tuple-element.32) | copy-start | bytes 6148
  49.6 155.8 %all-to-all-start.2 = ((bf16[8,1,192,4096]{3,2,1,0:T(8,128)(2,1)}), bf16[8,1,192,4096]{3,2,1,0:T(8,128)(2,1)}, u32[]{:S(2)}, u32[]{:S(2)}) async-start(bf16[8,1,192,4096]{3,2,1,0:T(8,128)(2,1)} %bitcast.151), calls=%async_computation.2 | async-start | bytes 25165824 | tf_op jit(solution)/shard_map/all_to_all | solution.py:74
  205.4 144.3 %all-to-all-start = ((bf16[8,1,192,4096]{3,2,1,0:T(8,128)(2,1)}), bf16[8,1,192,4096]{3,2,1,0:T(8,128)(2,1)}, u32[]{:S(2)}, u32[]{:S(2)}) async-start(bf16[8,1,192,4096]{3,2,1,0:T(8,128)(2,1)} %bitcast.150), calls=%async_computation | async-start | bytes 25165824 | tf_op jit(solution)/shard_map/all_to_all | solution.py:57
  433.9 30.0 %slice-start.6 = ((s8[4325376]{0:T(1024)(128)(4,1)}), s8[131072]{0:T(1024)(128)(4,1)S(1)}, s32[]{:S(2)}) async-start(s8[4325376]{0:T(1024)(128)(4,1)} %bitcast.153), calls=%async_computation.12 | async-start | bytes 262144
  433.9 144.5 %all-to-all-start.1 = ((bf16[8,1,192,4096]{3,2,1,0:T(8,128)(2,1)}), bf16[8,1,192,4096]{3,2,1,0:T(8,128)(2,1)}, u32[]{:S(2)}, u32[]{:S(2)}) async-start(bf16[8,1,192,4096]{3,2,1,0:T(8,128)(2,1)} %convert_bitcast_fusion), calls=%async_computation.1 | async-start | bytes 25165824 | tf_op jit(solution)/shard_map/all_to_all | solution.py:64
  439.4 462.2 %all-reduce.5.cloned.1.call-start = ((), (), s32[]{:S(2)}) async-start(), calls=%async_computation.4 | async-start | bytes 262144 | tf_op jit(solution)/shard_map/psum | solution.py:97
  439.5 24.5 slice-start.7
  463.9 114.4 %copy-start.51 = (s32[512]{0:T(512)S(1)}, s32[512]{0:T(512)}, u32[]{:S(2)}) copy-start(s32[512]{0:T(512)} %copy-done.50) | copy-start | bytes 6148
  578.4 11.9 copy-start.2
  578.4 11.9 copy-start.7
  578.4 11.9 copy-start.45
  578.4 11.9 copy-start.47
  578.4 11.9 copy-start.54
  590.3 18.4 copy-start.5
  590.3 18.4 copy-start.9
  590.4 18.4 copy-start.15
  590.4 18.3 copy-start.18
  590.4 18.3 copy-start.21
  590.4 18.3 copy-start.24
  590.4 18.3 copy-start.29
  590.4 18.3 copy-start.32
  590.4 18.3 copy-start.35
  610.1 2331.4 %all-reduce.7.cloned.1.call-start = ((), (), s32[]{:S(2)}) async-start(), calls=%async_computation.5 | async-start | bytes 135266304 | tf_op jit(solution)/shard_map/psum | solution.py:94
  634.7 26.2 slice-start.8
  634.8 26.2 slice-start.9
  689.7 143.1 %copy-start.52 = (s32[512]{0:T(512)S(1)}, s32[512]{0:T(512)}, u32[]{:S(2)}) copy-start(s32[512]{0:T(512)} %copy-done.50) | copy-start | bytes 6148
  689.7 143.0 %copy-start.55 = (s32[512]{0:T(512)S(1)}, s32[512]{0:T(512)}, u32[]{:S(2)}) copy-start(s32[512]{0:T(512)} %copy-done.53) | copy-start | bytes 6148
  832.7 7.1 copy-start.3
  832.7 7.1 copy-start.10
  832.7 7.1 copy-start.12
  832.7 7.1 copy-start.16
  832.8 7.1 copy-start.19
  832.8 7.1 copy-start.22
  832.8 7.1 copy-start.25
  832.8 7.1 copy-start.27
  832.8 7.1 copy-start.30
  832.8 7.1 copy-start.33
  832.8 7.1 copy-start.36
  832.8 7.1 copy-start.38
  832.8 7.1 copy-start.41
  832.9 7.1 copy-start.43
  2941.5 36.3 %slice-start = ((s8[22544384]{0:T(1024)(128)(4,1)}), s8[4194304]{0:T(1024)(128)(4,1)S(1)}, s32[]{:S(2)}) async-start(s8[22544384]{0:T(1024)(128)(4,1)} %bitcast.148), calls=%async_computation.6 | async-start | bytes 8388608
  2941.5 36.3 %slice-start.1 = ((s8[22544384]{0:T(1024)(128)(4,1)}), s8[4194304]{0:T(1024)(128)(4,1)S(1)}, s32[]{:S(2)}) async-start(s8[22544384]{0:T(1024)(128)(4,1)} %bitcast.148), calls=%async_computation.7 | async-start | bytes 8388608
  2941.5 36.3 %slice-start.2 = ((s8[22544384]{0:T(1024)(128)(4,1)}), s8[4194304]{0:T(1024)(128)(4,1)S(1)}, s32[]{:S(2)}) async-start(s8[22544384]{0:T(1024)(128)(4,1)} %bitcast.148), calls=%async_computation.8 | async-start | bytes 8388608
  2959.7 18.1 slice-start.3
  2959.7 18.2 slice-start.4
  2959.7 18.2 slice-start.5
  2977.9 8.1 copy-start.13
  (7 other events, 4.3 us)
Sparse Core Ops, SparseCore 0:
  610.2 127.6 all-reduce.4
  741.4 2200.1 all-reduce.6
where the time goes:
time: 3000 us; the launch traced here: 2990 us
  waiting for transfers between devices  2370 us (79%)
  matrix products  323 us (11%)
  blocking collectives  189 us (6%)
  local copies, waits for them, and re-layouts  48.9 us (2%)
    psum x1, waiting for transfers between devices, local_step(): dw_gate = lax.psum(dw_gate, 'dp')  2040 us
    all_to_all x1, blocking collectives, local_step(): lax.all_to_all(grad_hid, 'ep', 0, 0, tiled=True)  143 us
    all_to_all x1, waiting for transfers between devices, local_step(): lax.all_to_all(grad_buf.reshape(n_ep, local_exp, slot_cap, d_model), 'ep'...  127 us
    all_to_all x1, waiting for transfers between devices, local_step(): lax.all_to_all(hid_buf.reshape(n_ep, local_exp, slot_cap, d_model), 'ep',...  112 us
    all_to_all x1, waiting for transfers between devices, local_step(): lax.all_to_all(exp_out, 'ep', 0, 0, tiled=True)  91.6 us
  transfers between devices with their start and end apart: 5, of which 4 were waited for; matrix products, arithmetic and copies ran while one was open for 6% of the time, Pallas kernels for 0%

commit v1 on v0

v1 whole, which is shorter than its diff:
```python
import jax
import jax.numpy as jnp
from jax import lax
from jax.sharding import PartitionSpec as P

LN_EPS = 1e-5
f32 = jnp.float32
bf16 = jnp.bfloat16


def layer_norm(x_rows, ln_weight, ln_bias):
    x_float = x_rows.astype(f32)
    centered = x_float - jnp.mean(x_float, axis=-1, keepdims=True)
    inv_std = lax.rsqrt(jnp.mean(centered * centered, axis=-1, keepdims=True) + LN_EPS)
    x_hat = centered * inv_std
    hidden = (x_hat * ln_weight.astype(f32) + ln_bias.astype(f32)).astype(bf16)
    return hidden, x_hat, inv_std


def layer_norm_back(grad_h, x_hat, inv_std, ln_weight):
    scaled = grad_h * ln_weight.astype(f32)
    return inv_std * (scaled - jnp.mean(scaled, axis=-1, keepdims=True)
                      - x_hat * jnp.mean(scaled * x_hat, axis=-1, keepdims=True))


def masked_gate(logits, allowed, choice):
    expert_ids = jnp.arange(logits.shape[-1])
    prob_all = jax.nn.softmax(jnp.where(allowed, logits, -1e30), axis=-1)
    picked = (choice[:, None] == expert_ids[None, :]).astype(f32)
    return jnp.sum(prob_all * picked, axis=-1), prob_all, picked


def solution(mesh):
    n_ep = mesh.shape['ep']
    n_dp = mesh.shape['dp']
    tok_spec = P(('dp', 'ep'), None)
    row_spec = P(('dp', 'ep'))
    exp_spec = P('ep', None, None)
    far = [(i, i ^ 2) for i in range(n_dp)]
    near = [(i, i ^ 1) for i in range(n_dp)]

    def local_step(tok_x, tok_dy, exp_first, exp_second, eligible, slot_first, slot_second,
                   ln_weight, ln_bias, router, w_gate, w_up, w_down):
        n_local, d_model = tok_x.shape
        n_exp = eligible.shape[1]
        slot_cap = 3 * n_local // n_exp
        n_rows = n_exp * slot_cap
        wg_t = w_gate[0].T
        wu_t = w_up[0].T
        wd = w_down[0]

        hidden, x_hat, inv_std = layer_norm(tok_x, ln_weight, ln_bias)
        logits = jnp.dot(hidden, router, preferred_element_type=f32)
        expert_ids = jnp.arange(n_exp)
        allowed = eligible > 0
        gate_one, prob_one, pick_one = masked_gate(logits, allowed, exp_first)
        gate_two, prob_two, pick_two = masked_gate(logits, allowed & (expert_ids[None, :] != exp_first[:, None]), exp_second)
        pos_one = jnp.where(slot_first >= 0, exp_first * slot_cap + slot_first, -1)
        pos_two = jnp.where(slot_second >= 0, exp_second * slot_cap + slot_second, -1)
        meta = jnp.stack([pos_one.astype(f32), pos_two.astype(f32), gate_one, gate_two])
        row_ids = jnp.arange(n_rows)

        def dispatch(h, dy, meta):
            p1 = meta[0].astype(jnp.int32)
            p2 = meta[1].astype(jnp.int32)
            m1 = p1[None, :] == row_ids[:, None]
            m2 = p2[None, :] == row_ids[:, None]
            sel = (m1 | m2).astype(bf16)
            g_row = jnp.sum(jnp.where(m1, meta[2][None, :], 0.0) + jnp.where(m2, meta[3][None, :], 0.0), axis=1)
            h_buf = jnp.dot(sel, h, preferred_element_type=f32).astype(bf16)
            q_buf = (g_row[:, None] * jnp.dot(sel, dy, preferred_element_type=f32)).astype(bf16)
            return h_buf, q_buf

        def swap(buf):
            return lax.all_to_all(buf.reshape(n_ep, slot_cap, d_model), 'ep', 0, 0, tiled=True).reshape(n_rows, d_model)

        def inner(h, q):
            pre_gate = jnp.einsum('rd,fd->rf', h, wg_t, preferred_element_type=f32)
            pre_up = jnp.einsum('rd,fd->rf', h, wu_t, preferred_element_type=f32)
            sig_gate = jax.nn.sigmoid(pre_gate)
            silu_gate = pre_gate * sig_gate
            u = (silu_gate * pre_up).astype(bf16)
            du = jnp.einsum('rd,fd->rf', q, wd, preferred_element_type=f32)
            da = (du * pre_up * sig_gate * (1.0 + pre_gate * (1.0 - sig_gate))).astype(bf16)
            db = (du * silu_gate).astype(bf16)
            return u, da, db

        def dw(u, da, db, h, q):
            def mm(a, b):
                return jnp.einsum('rf,rd->fd', a, b, preferred_element_type=f32)
            return mm(da, h), mm(db, h), mm(u, q)

        dy_f1 = lax.ppermute(tok_dy, 'dp', far)
        h_f1 = lax.ppermute(hidden, 'dp', far)
        m_f1 = lax.ppermute(meta, 'dp', far)
        dy_f2 = lax.ppermute(dy_f1, 'dp', near)
        h_f2 = lax.ppermute(h_f1, 'dp', near)
        m_f2 = lax.ppermute(m_f1, 'dp', near)

        h_buf, q_buf = dispatch(hidden, tok_dy, meta)
        h_own = swap(h_buf)
        q_own = swap(q_buf)
        h_near = lax.ppermute(h_own, 'dp', near)
        q_near = lax.ppermute(q_own, 'dp', near)
        u, da, db = inner(h_own, q_own)
        exp_out = jnp.dot(u, wd, preferred_element_type=f32).astype(bf16)
        grad_hid = (jnp.dot(da, wg_t, preferred_element_type=f32)
                    + jnp.dot(db, wu_t, preferred_element_type=f32)).astype(bf16)
        dwg, dwu, dwd = dw(u, da, db, h_own, q_own)

        h_b1, q_b1 = dispatch(h_f1, dy_f1, m_f1)
        h_b2, q_b2 = dispatch(h_f2, dy_f2, m_f2)
        out_back = swap(exp_out)
        hid_back = swap(grad_hid)
        h_r1, q_r1 = swap(h_b1), swap(q_b1)
        h_r2, q_r2 = swap(h_b2), swap(q_b2)
        for h, q in ((h_r1, q_r1), (h_r2, q_r2), (h_near, q_near)):
            a, b, c = dw(*inner(h, q), h, q)
            dwg, dwu, dwd = dwg + a, dwu + b, dwd + c

        sel_one = (pos_one[:, None] == row_ids[None, :]).astype(bf16)
        sel_two = (pos_two[:, None] == row_ids[None, :]).astype(bf16)
        out_one = jnp.dot(sel_one, out_back, preferred_element_type=f32)
        out_two = jnp.dot(sel_two, out_back, preferred_element_type=f32)
        out_tok = (tok_x.astype(f32) + gate_one[:, None] * out_one + gate_two[:, None] * out_two).astype(bf16)
        dy_float = tok_dy.astype(f32)
        dgate_one = jnp.sum(dy_float * out_one, axis=-1)
        dgate_two = jnp.sum(dy_float * out_two, axis=-1)
        d_logits = ((dgate_one * gate_one)[:, None] * (pick_one - prob_one)
                    + (dgate_two * gate_two)[:, None] * (pick_two - prob_two)).astype(bf16)
        d_router = jnp.einsum('td,te->de', hidden, d_logits, preferred_element_type=f32)
        grad_exp = jnp.dot(sel_one + sel_two, hid_back, preferred_element_type=f32)
        grad_h = jnp.einsum('te,de->td', d_logits, router, preferred_element_type=f32) + grad_exp
        d_ln_weight = jnp.sum(grad_h * x_hat, axis=0)
        d_ln_bias = jnp.sum(grad_h, axis=0)
        dx_tok = (dy_float + layer_norm_back(grad_h, x_hat, inv_std, ln_weight)).astype(bf16)
        d_router = lax.psum(d_router, ('dp', 'ep'))
        d_ln_weight = lax.psum(d_ln_weight, ('dp', 'ep'))
        d_ln_bias = lax.psum(d_ln_bias, ('dp', 'ep'))
        return (out_tok, dx_tok, dwg.T[None], dwu.T[None], dwd[None], d_router, d_ln_weight, d_ln_bias)

    return jax.shard_map(
        local_step, mesh=mesh,
        in_specs=(tok_spec, tok_spec, row_spec, row_spec, tok_spec, row_spec, row_spec,
                  P(), P(), P(), exp_spec, exp_spec, exp_spec),
        out_specs=(tok_spec, tok_spec, exp_spec, exp_spec, exp_spec, P(), P(), P()),
        check_vma=False)
```

time: 3000 us -> 1810 us (0.60)
  waiting for transfers between devices: 2370 us -> 820 us
  matrix products: 323 us -> 848 us
  blocking collectives: 189 us -> 41.6 us
  local copies, waits for them, and re-layouts: 48.9 us -> 2.4 us
    psum x1 -> x0, waiting for transfers between devices: 2040 us -> none  [local_step(): dw_gate = lax.psum(dw_gate, 'dp')]
    dot_general x13 -> x34, matrix products: 285 us -> 808 us  [the longest x12 367 us: mm(): return jnp.einsum('rf,rd->fd', a, b, preferred_element_type=f32)]
    ppermute x0 -> x8, waiting for transfers between devices: none -> 477 us  [the longest x1 264 us: local_step(): h_f1 = lax.ppermute(hidden, 'dp', far)]
    all_to_all x1 -> x0, blocking collectives: 143 us -> none  [local_step(): lax.all_to_all(grad_hid, 'ep', 0, 0, tiled=True)]
    unnamed x136 -> x147, local copies, waits for them, and re-layouts: 48.9 us -> 2.4 us
    all_to_all x3 -> x8, waiting for transfers between devices: 331 us -> 343 us  [swap(): lax.all_to_all(buf.reshape(n_ep, slot_cap, d_model), 'ep', 0, 0, tiled=True)]
  transfers between devices with their start and end apart: 5 -> 17, of which waited for: 4 -> 10; matrix products, arithmetic and copies ran while one was open for 6% -> 47% of each run, Pallas kernels for 0% -> 0%
where the time goes in v1:
time: 1810 us; the launch traced here: 1800 us
  matrix products  848 us (47%)
  waiting for transfers between devices  820 us (45%)
  starting transfers between devices  55.5 us (3%)
  blocking collectives  41.6 us (2%)
  other arithmetic  22.5 us (1%)
    dot_general x12, matrix products, mm(): return jnp.einsum('rf,rd->fd', a, b, preferred_element_type=f32)  367 us
    all_to_all x8, waiting for transfers between devices, swap(): lax.all_to_all(buf.reshape(n_ep, slot_cap, d_model), 'ep', 0, 0, tiled=True)  343 us
    ppermute x1, waiting for transfers between devices, local_step(): h_f1 = lax.ppermute(hidden, 'dp', far)  264 us
    dot_general x4, matrix products, inner(): du = jnp.einsum('rd,fd->rf', q, wd, preferred_element_type=f32)  98.5 us
    dot_general x4, matrix products, inner(): pre_gate = jnp.einsum('rd,fd->rf', h, wg_t, preferred_element_type=f32)  93.1 us
    dot_general x4, matrix products, inner(): pre_up = jnp.einsum('rd,fd->rf', h, wu_t, preferred_element_type=f32)  93 us
    ppermute x1, waiting for transfers between devices, local_step(): m_f2 = lax.ppermute(m_f1, 'dp', near)  86.7 us
    ppermute x1, waiting for transfers between devices, local_step(): m_f1 = lax.ppermute(meta, 'dp', far)  77.9 us
  transfers between devices with their start and end apart: 17, of which 10 were waited for; matrix products, arithmetic and copies ran while one was open for 47% of the time, Pallas kernels for 0%

profile of v1, /device:TPU:0, one launch (start us, length us, event | category | flops | bytes accessed | tf_op | source)
XLA Modules:
  0.0 1804.9 jit_solution(7347561165947241793)
XLA Ops:
  7.2 3.0 convert_reduce_fusion
  10.2 3.4 fusion.44
  15.8 2.3 fusion.39
  18.1 9.7 convolution_convert_fusion.3
  27.8 5.6 all-to-all-start
  33.4 4.2 collective-permute-start.1
  37.7 3.4 fusion.104
  41.8 2.9 collective-permute-start
  45.4 263.5 %collective-permute-done.1 = bf16[512,4096]{1,0:T(8,128)(2,1)} collective-permute-done((bf16[512,4096]{1,0:T(8,128)(2,1)}, bf16[512,4096]{1,0:T(8,128)(2,1)}, u32[]{:S(2)}, u32[]{:S(2)}) %collective-permute-start.1) | collective-permute-done | bytes 4194336 | tf_op jit(solution)/shard_map/ppermute | solution.py:94
  309.6 11.8 multiply_convert_fusion.2
  321.4 77.9 %collective-permute-done = f32[4,512]{1,0:T(4,128)S(1)} collective-permute-done((f32[4,512]{1,0:T(4,128)S(1)}, f32[4,512]{1,0:T(4,128)S(1)}, u32[]{:S(2)}, u32[]{:S(2)}) %collective-permute-start) | collective-permute-done | bytes 8224 | tf_op jit(solution)/shard_map/ppermute | solution.py:95
  402.2 86.7 %collective-permute-done.3 = f32[4,512]{1,0:T(4,128)S(1)} collective-permute-done((f32[4,512]{1,0:T(4,128)S(1)}, f32[4,512]{1,0:T(4,128)S(1)}, u32[]{:S(2)}, u32[]{:S(2)}) %collective-permute-start.3) | collective-permute-done | bytes 8224 | tf_op jit(solution)/shard_map/ppermute | solution.py:98
  489.6 11.8 multiply_convert_fusion.1
  501.4 5.5 all-to-all-start.2
  507.0 11.7 convolution_convert_fusion.2
  518.6 11.7 convolution_convert_fusion.1
  530.4 48.4 %collective-permute-done.5 = bf16[512,4096]{1,0:T(8,128)(2,1)} collective-permute-done((bf16[512,4096]{1,0:T(8,128)(2,1)}, bf16[512,4096]{1,0:T(8,128)(2,1)}, u32[]{:S(2)}, u32[]{:S(2)}) %collective-permute-start.5) | collective-permute-done | bytes 4194336 | tf_op jit(solution)/shard_map/ppermute | solution.py:96
  578.8 11.8 multiply_convert_fusion
  590.5 25.9 %fusion.16 = f32[1536,1376]{0,1:T(8,128)} fusion(bf16[1536,4096]{1,0:T(8,128)(2,1)} %bitcast.1, bf16[1,4096,1376]{1,2,0:T(8,128)(2,1)} %param.24), kind=kOutput, calls=%fused_computation.33 | convolution fusion | flops 17314086912 | bytes 32309248 | tf_op jit(solution)/shard_map/rd,fd->rf/dot_general | solution.py:79
  616.5 22.5 %fusion.26 = f32[1536,1376]{0,1:T(8,128)} fusion(bf16[1536,4096]{1,0:T(8,128)(2,1)} %bitcast.1, bf16[1,4096,1376]{1,2,0:T(8,128)(2,1)S(1)} %bitcast.143), kind=kOutput, calls=%fused_computation.43 | convolution fusion | flops 17314086912 | bytes 32309248 | tf_op jit(solution)/shard_map/rd,fd->rf/dot_general | solution.py:78
  638.9 7.0 all-to-all-done.2
  645.9 5.5 all-to-all-start.4
  651.5 31.9 %multiply_convert_fusion.12 = (bf16[1536,1376]{0,1:T(8,128)(2,1)}, bf16[1536,1376]{0,1:T(8,128)(2,1)}, bf16[1536,1376]{0,1:T(8,128)(2,1)}) fusion(f32[1536,1376]{0,1:T(8,128)} %fusion.26, f32[1536,1376]{0,1:T(8,128)} %fusion.16, bf16[1536,4096]{1,0:T(8,128)(2,1)} %bitcast.8, bf16[1,1376,4096]{2,1,0:T(8,128)(2,1)} %param.25), kind=kOutput, calls=%fused_computation.66 | convolution fusion | flops 17345789952 | bytes 53444608 | tf_op jit(solution)/shard_map/rd,fd->rf/dot_general | solution.py:83
  683.4 24.1 %fusion.121 = f32[4096,1376]{0,1:T(8,128)} fusion(bf16[1536,1376]{0,1:T(8,128)(2,1)} %get-tuple-element.27, bf16[1536,4096]{1,0:T(8,128)(2,1)} %bitcast.1), kind=kOutput, calls=%fused_computation.176 | convolution fusion | flops 17314086912 | bytes 39354368 | tf_op jit(solution)/shard_map/rf,rd->fd/dot_general | solution.py:90
  707.6 23.5 %fusion.24 = f32[1536,4096]{1,0:T(8,128)} fusion(bf16[1536,1376]{0,1:T(8,128)(2,1)S(1)} %copy-done.39, bf16[1,4096,1376]{1,2,0:T(8,128)(2,1)S(1)} %bitcast.145), kind=kOutput, calls=%fused_computation.41 | convolution fusion | flops 17314086912 | bytes 40665088 | tf_op jit(solution)/shard_map/dot_general | solution.py:107
  731.0 22.7 %fusion.122 = f32[4096,1376]{0,1:T(8,128)} fusion(bf16[1536,1376]{0,1:T(8,128)(2,1)S(1)} %copy-done.40, bf16[1536,4096]{1,0:T(8,128)(2,1)} %bitcast.1), kind=kOutput, calls=%fused_computation.177 | convolution fusion | flops 17314086912 | bytes 39354368 | tf_op jit(solution)/shard_map/rf,rd->fd/dot_general | solution.py:90
  753.7 28.8 %add_convert_fusion = bf16[1536,4096]{1,0:T(8,128)(2,1)} fusion(f32[1536,4096]{1,0:T(8,128)} %fusion.24, bf16[1536,1376]{0,1:T(8,128)(2,1)S(1)} %bitcast.163, bf16[1,4096,1376]{1,2,0:T(8,128)(2,1)} %param.24), kind=kOutput, calls=%fused_computation.2 | convolution fusion | flops 17326669824 | bytes 53248000 | tf_op jit(solution)/shard_map/dot_general | solution.py:108
  782.6 23.9 %fusion.120 = f32[1376,4096]{1,0:T(8,128)} fusion(bf16[1536,1376]{0,1:T(8,128)(2,1)} %get-tuple-element.28, bf16[1536,4096]{1,0:T(8,128)(2,1)} %bitcast.8), kind=kOutput, calls=%fused_computation.175 | convolution fusion | flops 17314086912 | bytes 39354368 | tf_op jit(solution)/shard_map/rf,rd->fd/dot_general | solution.py:90
  806.5 5.8 all-to-all-start.5
  812.3 25.4 %convolution_convert_fusion = bf16[1536,4096]{1,0:T(8,128)(2,1)} fusion(bf16[1536,1376]{0,1:T(8,128)(2,1)} %get-tuple-element.28, bf16[1,1376,4096]{2,1,0:T(8,128)(2,1)} %param.25), kind=kOutput, calls=%fused_computation.7 | convolution fusion | flops 17320378368 | bytes 28082176 | tf_op jit(solution)/shard_map/dot_general | solution.py:106
  837.7 22.2 %fusion.13 = f32[1536,1376]{0,1:T(8,128)} fusion(bf16[1536,4096]{1,0:T(8,128)(2,1)} %bitcast.18, bf16[1,4096,1376]{1,2,0:T(8,128)(2,1)S(1)} %bitcast.151), kind=kOutput, calls=%fused_computation.30 | convolution fusion | flops 17314086912 | bytes 32309248 | tf_op jit(solution)/shard_map/rd,fd->rf/dot_general | solution.py:79
  859.9 22.7 %fusion.22 = f32[1536,1376]{0,1:T(8,128)} fusion(bf16[1536,4096]{1,0:T(8,128)(2,1)} %bitcast.18, bf16[1,4096,1376]{1,2,0:T(8,128)(2,1)S(1)} %bitcast.147), kind=kOutput, calls=%fused_computation.39 | convolution fusion | flops 17314086912 | bytes 32309248 | tf_op jit(solution)/shard_map/rd,fd->rf/dot_general | solution.py:78
  882.6 68.7 %all-to-all-done.5 = bf16[8,192,4096]{2,1,0:T(8,128)(2,1)} async-done(((bf16[8,192,4096]{2,1,0:T(8,128)(2,1)}), bf16[8,192,4096]{2,1,0:T(8,128)(2,1)}, u32[]{:S(2)}, u32[]{:S(2)}) %all-to-all-start.5) | async-done | bytes 12582944 | tf_op jit(solution)/shard_map/all_to_all | solution.py:75
  951.2 6.0 all-to-all-start.6
  957.3 26.8 %fusion.54 = f32[1376,4096]{1,0:T(8,128)} fusion(bf16[1536,4096]{1,0:T(8,128)(2,1)} %bitcast.22, f32[1536,1376]{0,1:T(8,128)} %fusion.13, f32[1536,1376]{0,1:T(8,128)} %fusion.22), kind=kOutput, calls=%fused_computation.89 | convolution fusion | flops 17326768128 | bytes 52035584 | tf_op jit(solution)/shard_map/rf,rd->fd/dot_general | solution.py:90
  984.1 22.0 %fusion.4 = f32[1536,1376]{0,1:T(8,128)} fusion(bf16[1536,4096]{1,0:T(8,128)(2,1)} %bitcast.22, bf16[1,1376,4096]{2,1,0:T(8,128)(2,1)S(1)} %bitcast.157), kind=kOutput, calls=%fused_computation.21 | convolution fusion | flops 17314086912 | bytes 32309248 | tf_op jit(solution)/shard_map/rd,fd->rf/dot_general | solution.py:83
  1006.1 30.9 %fusion.50 = f32[4096,1376]{0,1:T(8,128)} fusion(bf16[1536,4096]{1,0:T(8,128)(2,1)} %bitcast.18, f32[1536,1376]{0,1:T(8,128)} %fusion.22, f32[1536,1376]{0,1:T(8,128)} %fusion.4, f32[1536,1376]{0,1:T(8,128)} %fusion.13), kind=kOutput, calls=%fused_computation.85 | convolution fusion | flops 17335222272 | bytes 60489728 | tf_op jit(solution)/shard_map/rf,rd->fd/dot_general | solution.py:90
  1037.0 59.3 %all-to-all-done.6 = bf16[8,192,4096]{2,1,0:T(8,128)(2,1)} async-done(((bf16[8,192,4096]{2,1,0:T(8,128)(2,1)}), bf16[8,192,4096]{2,1,0:T(8,128)(2,1)}, u32[]{:S(2)}, u32[]{:S(2)}) %all-to-all-start.6) | async-done | bytes 12582944 | tf_op jit(solution)/shard_map/all_to_all | solution.py:75
  1096.3 5.6 all-to-all-start.7
  1102.0 26.9 %fusion.52 = f32[4096,1376]{0,1:T(8,128)} fusion(bf16[1536,4096]{1,0:T(8,128)(2,1)} %bitcast.18, f32[1536,1376]{0,1:T(8,128)} %fusion.4, f32[1536,1376]{0,1:T(8,128)} %fusion.22), kind=kOutput, calls=%fused_computation.87 | convolution fusion | flops 17326768128 | bytes 52035584 | tf_op jit(solution)/shard_map/rf,rd->fd/dot_general | solution.py:90
  1128.9 22.1 %fusion.11 = f32[1536,1376]{0,1:T(8,128)} fusion(bf16[1536,4096]{1,0:T(8,128)(2,1)} %bitcast.26, bf16[1,4096,1376]{1,2,0:T(8,128)(2,1)S(1)} %bitcast.153), kind=kOutput, calls=%fused_computation.28 | convolution fusion | flops 17314086912 | bytes 32309248 | tf_op jit(solution)/shard_map/rd,fd->rf/dot_general | solution.py:79
  1151.0 22.6 %fusion.20 = f32[1536,1376]{0,1:T(8,128)} fusion(bf16[1536,4096]{1,0:T(8,128)(2,1)} %bitcast.26, bf16[1,4096,1376]{1,2,0:T(8,128)(2,1)S(1)} %bitcast.149), kind=kOutput, calls=%fused_computation.37 | convolution fusion | flops 17314086912 | bytes 32309248 | tf_op jit(solution)/shard_map/rd,fd->rf/dot_general | solution.py:78
  1173.6 67.3 %all-to-all-done.7 = bf16[8,192,4096]{2,1,0:T(8,128)(2,1)} async-done(((bf16[8,192,4096]{2,1,0:T(8,128)(2,1)}), bf16[8,192,4096]{2,1,0:T(8,128)(2,1)}, u32[]{:S(2)}, u32[]{:S(2)}) %all-to-all-start.7) | async-done | bytes 12582944 | tf_op jit(solution)/shard_map/all_to_all | solution.py:75
  1240.9 6.0 all-to-all-start.1
  1247.0 26.9 %fusion.55 = f32[1376,4096]{1,0:T(8,128)} fusion(bf16[1536,4096]{1,0:T(8,128)(2,1)} %bitcast.30, f32[1536,1376]{0,1:T(8,128)} %fusion.11, f32[1536,1376]{0,1:T(8,128)} %fusion.20), kind=kOutput, calls=%fused_computation.90 | convolution fusion | flops 17326768128 | bytes 52035584 | tf_op jit(solution)/shard_map/rf,rd->fd/dot_general | solution.py:90
  1273.9 22.1 %fusion.2 = f32[1536,1376]{0,1:T(8,128)} fusion(bf16[1536,4096]{1,0:T(8,128)(2,1)} %bitcast.30, bf16[1,1376,4096]{2,1,0:T(8,128)(2,1)S(1)} %bitcast.159), kind=kOutput, calls=%fused_computation.19 | convolution fusion | flops 17314086912 | bytes 32309248 | tf_op jit(solution)/shard_map/rd,fd->rf/dot_general | solution.py:83
  1296.0 31.0 %fusion.51 = f32[4096,1376]{0,1:T(8,128)} fusion(bf16[1536,4096]{1,0:T(8,128)(2,1)} %bitcast.26, f32[1536,1376]{0,1:T(8,128)} %fusion.20, f32[1536,1376]{0,1:T(8,128)} %fusion.2, f32[1536,1376]{0,1:T(8,128)} %fusion.11), kind=kOutput, calls=%fused_computation.86 | convolution fusion | flops 17335222272 | bytes 60489728 | tf_op jit(solution)/shard_map/rf,rd->fd/dot_general | solution.py:90
  1327.0 58.9 %all-to-all-done.1 = bf16[8,192,4096]{2,1,0:T(8,128)(2,1)} async-done(((bf16[8,192,4096]{2,1,0:T(8,128)(2,1)}), bf16[8,192,4096]{2,1,0:T(8,128)(2,1)}, u32[]{:S(2)}, u32[]{:S(2)}) %all-to-all-start.1) | async-done | bytes 12582944 | tf_op jit(solution)/shard_map/all_to_all | solution.py:75
  1385.9 5.3 all-to-all-start.3
  1391.3 26.8 %fusion.53 = f32[4096,1376]{0,1:T(8,128)} fusion(bf16[1536,4096]{1,0:T(8,128)(2,1)} %bitcast.26, f32[1536,1376]{0,1:T(8,128)} %fusion.2, f32[1536,1376]{0,1:T(8,128)} %fusion.20), kind=kOutput, calls=%fused_computation.88 | convolution fusion | flops 17326768128 | bytes 52035584 | tf_op jit(solution)/shard_map/rf,rd->fd/dot_general | solution.py:90
  1418.2 11.9 fusion.62
  1430.2 17.2 fusion.47
  1448.8 82.2 %all-to-all-done.3 = bf16[8,192,4096]{2,1,0:T(8,128)(2,1)} async-done(((bf16[8,192,4096]{2,1,0:T(8,128)(2,1)}), bf16[8,192,4096]{2,1,0:T(8,128)(2,1)}, u32[]{:S(2)}, u32[]{:S(2)}) %all-to-all-start.3) | async-done | bytes 12582944 | tf_op jit(solution)/shard_map/all_to_all | solution.py:75
  1531.0 10.4 fusion.73
  1541.5 6.1 fusion.43
  1547.6 41.6 %all-reduce = (f32[4096]{0:T(1024)}, f32[4096]{0:T(1024)}) all-reduce(f32[4096]{0:T(1024)S(1)} %get-tuple-element.8, f32[4096]{0:T(1024)S(1)} %get-tuple-element.11), channel_id=1, replica_groups=mesh['dp'=4,'ep'=8] {'dp','ep'}, use_global_device_ids=true, to_apply=%region_17.18 | all-reduce | flops 8192 | bytes 65536 | tf_op jit(solution)/shard_map/psum | solution.py:138
  1589.3 9.4 fusion.49
  1598.7 25.4 %fusion.18 = f32[1536,1376]{0,1:T(8,128)} fusion(bf16[1536,4096]{1,0:T(8,128)(2,1)} %collective-permute-done.6, bf16[1,4096,1376]{1,2,0:T(8,128)(2,1)} %param.23), kind=kOutput, calls=%fused_computation.35 | convolution fusion | flops 17314086912 | bytes 32309248 | tf_op jit(solution)/shard_map/rd,fd->rf/dot_general | solution.py:78
  1624.1 22.8 %fusion.9 = f32[1536,1376]{0,1:T(8,128)} fusion(bf16[1536,4096]{1,0:T(8,128)(2,1)} %collective-permute-done.6, bf16[1,4096,1376]{1,2,0:T(8,128)(2,1)S(1)} %bitcast.155), kind=kOutput, calls=%fused_computation.26 | convolution fusion | flops 17314086912 | bytes 32309248 | tf_op jit(solution)/shard_map/rd,fd->rf/dot_general | solution.py:79
  1647.0 22.5 %fusion = f32[1536,1376]{0,1:T(8,128)} fusion(bf16[1536,4096]{1,0:T(8,128)(2,1)} %collective-permute-done.7, bf16[1,1376,4096]{2,1,0:T(8,128)(2,1)S(1)} %bitcast.161), kind=kOutput, calls=%fused_computation.17 | convolution fusion | flops 17314086912 | bytes 32309248 | tf_op jit(solution)/shard_map/rd,fd->rf/dot_general | solution.py:83
  1669.5 42.2 %add_bitcast_fusion = f32[1,1376,4096]{2,1,0:T(8,128)} fusion(f32[1376,4096]{1,0:T(8,128)} %fusion.55, f32[1376,4096]{1,0:T(8,128)} %fusion.120, f32[1376,4096]{1,0:T(8,128)} %fusion.54, bf16[1536,4096]{1,0:T(8,128)(2,1)} %collective-permute-done.7, f32[1536,1376]{0,1:T(8,128)} %fusion.9, f32[1536,1376]{0,1:T(8,128)} %fusion.18), kind=kOutput, calls=%fused_computation.4 | convolution fusion | flops 17343676416 | bytes 119668736 | tf_op jit(solution)/shard_map/rf,rd->fd/dot_general | solution.py:90
  1711.7 42.4 %add_bitcast_fusion.2 = f32[1,4096,1376]{1,2,0:T(8,128)} fusion(f32[4096,1376]{0,1:T(8,128)} %fusion.51, f32[4096,1376]{0,1:T(8,128)} %fusion.121, f32[4096,1376]{0,1:T(8,128)} %fusion.50, bf16[1536,4096]{1,0:T(8,128)(2,1)} %collective-permute-done.6, f32[1536,1376]{0,1:T(8,128)} %fusion.18, f32[1536,1376]{0,1:T(8,128)} %fusion, f32[1536,1376]{0,1:T(8,128)} %fusion.9), kind=kOutput, calls=%fused_computation.6 | convolution fusion | flops 17352130560 | bytes 128122880 | tf_op jit(solution)/shard_map/rf,rd->fd/dot_general | solution.py:90
  1754.1 42.1 %add_bitcast_fusion.1 = f32[1,4096,1376]{1,2,0:T(8,128)} fusion(f32[4096,1376]{0,1:T(8,128)} %fusion.53, f32[4096,1376]{0,1:T(8,128)} %fusion.122, f32[4096,1376]{0,1:T(8,128)} %fusion.52, bf16[1536,4096]{1,0:T(8,128)(2,1)} %collective-permute-done.6, f32[1536,1376]{0,1:T(8,128)} %fusion, f32[1536,1376]{0,1:T(8,128)} %fusion.18), kind=kOutput, calls=%fused_computation.5 | convolution fusion | flops 17343676416 | bytes 119668736 | tf_op jit(solution)/shard_map/rf,rd->fd/dot_general | solution.py:90
  1796.3 1.6 copy.22
  (193 shorter events, 9.6 us)
Async XLA Ops:
  7.2 30.5 %copy-start = (bf16[4096,8]{0,1:T(8,128)(2,1)S(1)}, bf16[4096,8]{0,1:T(8,128)(2,1)}, u32[]{:S(2)}) copy-start(bf16[4096,8]{0,1:T(8,128)(2,1)} %param.22) | copy-start | bytes 196612
  27.8 13.3 copy-start.13
  27.8 473.6 %all-to-all-start = ((bf16[8,192,4096]{2,1,0:T(8,128)(2,1)}), bf16[8,192,4096]{2,1,0:T(8,128)(2,1)}, u32[]{:S(2)}, u32[]{:S(2)}) async-start(bf16[8,192,4096]{2,1,0:T(8,128)(2,1)} %bitcast.115), calls=%async_computation | async-start | bytes 25165824 | tf_op jit(solution)/shard_map/all_to_all | solution.py:75
  33.4 275.5 %collective-permute-start.1 = (bf16[512,4096]{1,0:T(8,128)(2,1)}, bf16[512,4096]{1,0:T(8,128)(2,1)}, u32[]{:S(2)}, u32[]{:S(2)}) collective-permute-start(bf16[512,4096]{1,0:T(8,128)(2,1)} %copy-done.4), channel_id=1, source_target_pairs={{0,16},{8,24},{16,0},{24,8},{1,17},{9,25},{17,1},{25,9},{2,18},{10... | collective-permute-start | bytes 12582920 | tf_op jit(solution)/shard_map/ppermute | solution.py:94
  37.6 363.2 %collective-permute-start.2 = (bf16[512,4096]{1,0:T(8,128)(2,1)}, bf16[512,4096]{1,0:T(8,128)(2,1)}, u32[]{:S(2)}, u32[]{:S(2)}) collective-permute-start(bf16[512,4096]{1,0:T(8,128)(2,1)} %param.14), channel_id=1, source_target_pairs={{0,16},{8,24},{16,0},{24,8},{1,17},{9,25},{17,1},{25,9},{2,18},{10... | collective-permute-start | bytes 12582920 | tf_op jit(solution)/shard_map/ppermute | solution.py:93
  41.8 357.5 %collective-permute-start = (f32[4,512]{1,0:T(4,128)S(1)}, f32[4,512]{1,0:T(4,128)S(1)}, u32[]{:S(2)}, u32[]{:S(2)}) collective-permute-start(f32[4,512]{1,0:T(4,128)S(1)} %pad_maximum_fusion), channel_id=1, source_target_pairs={{0,16},{8,24},{16,0},{24,8},{1,17},{9,25},{17,1},{25,9},{2,18},{10... | collective-permute-start | bytes 24584 | tf_op jit(solution)/shard_map/ppermute | solution.py:95
  309.0 209.7 %collective-permute-start.4 = (bf16[512,4096]{1,0:T(8,128)(2,1)}, bf16[512,4096]{1,0:T(8,128)(2,1)}, u32[]{:S(2)}, u32[]{:S(2)}) collective-permute-start(bf16[512,4096]{1,0:T(8,128)(2,1)} %collective-permute-done.1), channel_id=1, source_target_pairs={{0,8},{8,0},{16,24},{24,16},{1,9},{9,1},{17,25},{25,17},{2,10},{10... | collective-permute-start | bytes 12582920 | tf_op jit(solution)/shard_map/ppermute | solution.py:97
  399.3 89.5 %collective-permute-start.3 = (f32[4,512]{1,0:T(4,128)S(1)}, f32[4,512]{1,0:T(4,128)S(1)}, u32[]{:S(2)}, u32[]{:S(2)}) collective-permute-start(f32[4,512]{1,0:T(4,128)S(1)} %collective-permute-done), channel_id=1, source_target_pairs={{0,8},{8,0},{16,24},{24,16},{1,9},{9,1},{17,25},{25,17},{2,10},{10... | collective-permute-start | bytes 24584 | tf_op jit(solution)/shard_map/ppermute | solution.py:98
  400.8 178.0 %collective-permute-start.5 = (bf16[512,4096]{1,0:T(8,128)(2,1)}, bf16[512,4096]{1,0:T(8,128)(2,1)}, u32[]{:S(2)}, u32[]{:S(2)}) collective-permute-start(bf16[512,4096]{1,0:T(8,128)(2,1)} %collective-permute-done.2), channel_id=1, source_target_pairs={{0,8},{8,0},{16,24},{24,16},{1,9},{9,1},{17,25},{25,17},{2,10},{10... | collective-permute-start | bytes 12582920 | tf_op jit(solution)/shard_map/ppermute | solution.py:96
  501.4 144.5 %all-to-all-start.2 = ((bf16[8,192,4096]{2,1,0:T(8,128)(2,1)}), bf16[8,192,4096]{2,1,0:T(8,128)(2,1)}, u32[]{:S(2)}, u32[]{:S(2)}) async-start(bf16[8,192,4096]{2,1,0:T(8,128)(2,1)} %bitcast.118), calls=%async_computation.2 | async-start | bytes 25165824 | tf_op jit(solution)/shard_map/all_to_all | solution.py:75
  590.5 25.9 %slice-start = ((s8[11272192]{0:T(1024)(128)(4,1)}), s8[4194304]{0:T(1024)(128)(4,1)S(1)}, s32[]{:S(2)}) async-start(s8[11272192]{0:T(1024)(128)(4,1)} %bitcast.142), calls=%async_computation.9 | async-start | bytes 8388608
  590.5 25.9 %slice-start.1 = ((s8[11272192]{0:T(1024)(128)(4,1)}), s8[4194304]{0:T(1024)(128)(4,1)S(1)}, s32[]{:S(2)}) async-start(s8[11272192]{0:T(1024)(128)(4,1)} %bitcast.142), calls=%async_computation.10 | async-start | bytes 8388608
  590.5 25.9 %slice-start.2 = ((s8[11272192]{0:T(1024)(128)(4,1)}), s8[2883584]{0:T(1024)(128)(4,1)S(1)}, s32[]{:S(2)}) async-start(s8[11272192]{0:T(1024)(128)(4,1)} %bitcast.142), calls=%async_computation.11 | async-start | bytes 5767168
  590.5 1008.2 %collective-permute-start.6 = (bf16[1536,4096]{1,0:T(8,128)(2,1)}, bf16[1536,4096]{1,0:T(8,128)(2,1)}, u32[]{:S(2)}, u32[]{:S(2)}) collective-permute-start(bf16[1536,4096]{1,0:T(8,128)(2,1)} %bitcast.1), channel_id=1, source_target_pairs={{0,8},{8,0},{16,24},{24,16},{1,9},{9,1},{17,25},{25,17},{2,10},{10... | collective-permute-start | bytes 37748744 | tf_op jit(solution)/shard_map/ppermute | solution.py:103
  645.9 160.5 %all-to-all-start.4 = ((bf16[8,192,4096]{2,1,0:T(8,128)(2,1)}), bf16[8,192,4096]{2,1,0:T(8,128)(2,1)}, u32[]{:S(2)}, u32[]{:S(2)}) async-start(bf16[8,192,4096]{2,1,0:T(8,128)(2,1)} %bitcast.120), calls=%async_computation.4 | async-start | bytes 25165824 | tf_op jit(solution)/shard_map/all_to_all | solution.py:75
  651.4 995.5 %collective-permute-start.7 = (bf16[1536,4096]{1,0:T(8,128)(2,1)}, bf16[1536,4096]{1,0:T(8,128)(2,1)}, u32[]{:S(2)}, u32[]{:S(2)}) collective-permute-start(bf16[1536,4096]{1,0:T(8,128)(2,1)} %bitcast.8), channel_id=1, source_target_pairs={{0,8},{8,0},{16,24},{24,16},{1,9},{9,1},{17,25},{25,17},{2,10},{10... | collective-permute-start | bytes 37748744 | tf_op jit(solution)/shard_map/ppermute | solution.py:104
  651.5 56.0 %slice-start.3 = ((s8[11272192]{0:T(1024)(128)(4,1)}), s8[2883584]{0:T(1024)(128)(4,1)S(1)}, s32[]{:S(2)}) async-start(s8[11272192]{0:T(1024)(128)(4,1)} %bitcast.144), calls=%async_computation.12 | async-start | bytes 5767168
  651.5 56.0 %slice-start.4 = ((s8[11272192]{0:T(1024)(128)(4,1)}), s8[4194304]{0:T(1024)(128)(4,1)S(1)}, s32[]{:S(2)}) async-start(s8[11272192]{0:T(1024)(128)(4,1)} %bitcast.144), calls=%async_computation.13 | async-start | bytes 8388608
  683.4 24.1 %slice-start.5 = ((s8[11272192]{0:T(1024)(128)(4,1)}), s8[4194304]{0:T(1024)(128)(4,1)S(1)}, s32[]{:S(2)}) async-start(s8[11272192]{0:T(1024)(128)(4,1)} %bitcast.144), calls=%async_computation.14 | async-start | bytes 8388608
  683.4 24.1 %copy-start.39 = (bf16[1536,1376]{0,1:T(8,128)(2,1)S(1)}, bf16[1536,1376]{0,1:T(8,128)(2,1)}, u32[]{:S(2)}) copy-start(bf16[1536,1376]{0,1:T(8,128)(2,1)} %get-tuple-element.27) | copy-start | bytes 12681220
  707.5 23.5 %copy-start.40 = (bf16[1536,1376]{0,1:T(8,128)(2,1)S(1)}, bf16[1536,1376]{0,1:T(8,128)(2,1)}, u32[]{:S(2)}) copy-start(bf16[1536,1376]{0,1:T(8,128)(2,1)} %get-tuple-element.26) | copy-start | bytes 12681220
  707.5 46.2 %slice-start.30 = ((s8[4227072]{0:T(1024)(128)(4,1)}), s8[32768]{0:T(1024)(128)(4,1)S(1)}, s32[]{:S(2)}) async-start(s8[4227072]{0:T(1024)(128)(4,1)} %bitcast.162), calls=%async_computation.39 | async-start | bytes 65536
  731.0 22.7 %slice-start.31 = ((s8[4227072]{0:T(1024)(128)(4,1)}), s8[4194304]{0:T(1024)(128)(4,1)S(1)}, s32[]{:S(2)}) async-start(s8[4227072]{0:T(1024)(128)(4,1)} %bitcast.162), calls=%async_computation.40 | async-start | bytes 8388608
  806.5 31.2 %slice-start.12 = ((s8[11272192]{0:T(1024)(128)(4,1)}), s8[2883584]{0:T(1024)(128)(4,1)S(1)}, s32[]{:S(2)}) async-start(s8[11272192]{0:T(1024)(128)(4,1)} %bitcast.150), calls=%async_computation.21 | async-start | bytes 5767168
  806.5 144.8 %all-to-all-start.5 = ((bf16[8,192,4096]{2,1,0:T(8,128)(2,1)}), bf16[8,192,4096]{2,1,0:T(8,128)(2,1)}, u32[]{:S(2)}, u32[]{:S(2)}) async-start(bf16[8,192,4096]{2,1,0:T(8,128)(2,1)} %bitcast.117), calls=%async_computation.5 | async-start | bytes 25165824 | tf_op jit(solution)/shard_map/all_to_all | solution.py:75
  812.3 25.4 %slice-start.13 = ((s8[11272192]{0:T(1024)(128)(4,1)}), s8[4194304]{0:T(1024)(128)(4,1)S(1)}, s32[]{:S(2)}) async-start(s8[11272192]{0:T(1024)(128)(4,1)} %bitcast.150), calls=%async_computation.22 | async-start | bytes 8388608
  812.3 25.4 %slice-start.14 = ((s8[11272192]{0:T(1024)(128)(4,1)}), s8[4194304]{0:T(1024)(128)(4,1)S(1)}, s32[]{:S(2)}) async-start(s8[11272192]{0:T(1024)(128)(4,1)} %bitcast.150), calls=%async_computation.23 | async-start | bytes 8388608
  812.3 47.6 %slice-start.6 = ((s8[11272192]{0:T(1024)(128)(4,1)}), s8[4194304]{0:T(1024)(128)(4,1)S(1)}, s32[]{:S(2)}) async-start(s8[11272192]{0:T(1024)(128)(4,1)} %bitcast.146), calls=%async_computation.15 | async-start | bytes 8388608
  812.3 47.6 %slice-start.7 = ((s8[11272192]{0:T(1024)(128)(4,1)}), s8[4194304]{0:T(1024)(128)(4,1)S(1)}, s32[]{:S(2)}) async-start(s8[11272192]{0:T(1024)(128)(4,1)} %bitcast.146), calls=%async_computation.16 | async-start | bytes 8388608
  837.7 22.2 %slice-start.8 = ((s8[11272192]{0:T(1024)(128)(4,1)}), s8[2883584]{0:T(1024)(128)(4,1)S(1)}, s32[]{:S(2)}) async-start(s8[11272192]{0:T(1024)(128)(4,1)} %bitcast.146), calls=%async_computation.17 | async-start | bytes 5767168
  951.2 32.9 %slice-start.21 = ((s8[11272192]{0:T(1024)(128)(4,1)}), s8[2883584]{0:T(1024)(128)(4,1)S(1)}, s32[]{:S(2)}) async-start(s8[11272192]{0:T(1024)(128)(4,1)} %bitcast.156), calls=%async_computation.30 | async-start | bytes 5767168
  951.2 145.0 %all-to-all-start.6 = ((bf16[8,192,4096]{2,1,0:T(8,128)(2,1)}), bf16[8,192,4096]{2,1,0:T(8,128)(2,1)}, u32[]{:S(2)}, u32[]{:S(2)}) async-start(bf16[8,192,4096]{2,1,0:T(8,128)(2,1)} %bitcast.119), calls=%async_computation.6 | async-start | bytes 25165824 | tf_op jit(solution)/shard_map/all_to_all | solution.py:75
  957.3 26.8 %slice-start.22 = ((s8[11272192]{0:T(1024)(128)(4,1)}), s8[4194304]{0:T(1024)(128)(4,1)S(1)}, s32[]{:S(2)}) async-start(s8[11272192]{0:T(1024)(128)(4,1)} %bitcast.156), calls=%async_computation.31 | async-start | bytes 8388608
  957.3 26.8 %slice-start.23 = ((s8[11272192]{0:T(1024)(128)(4,1)}), s8[4194304]{0:T(1024)(128)(4,1)S(1)}, s32[]{:S(2)}) async-start(s8[11272192]{0:T(1024)(128)(4,1)} %bitcast.156), calls=%async_computation.32 | async-start | bytes 8388608
  1096.3 32.6 %slice-start.15 = ((s8[11272192]{0:T(1024)(128)(4,1)}), s8[2883584]{0:T(1024)(128)(4,1)S(1)}, s32[]{:S(2)}) async-start(s8[11272192]{0:T(1024)(128)(4,1)} %bitcast.152), calls=%async_computation.24 | async-start | bytes 5767168
  1096.3 144.6 %all-to-all-start.7 = ((bf16[8,192,4096]{2,1,0:T(8,128)(2,1)}), bf16[8,192,4096]{2,1,0:T(8,128)(2,1)}, u32[]{:S(2)}, u32[]{:S(2)}) async-start(bf16[8,192,4096]{2,1,0:T(8,128)(2,1)} %bitcast.116), calls=%async_computation.7 | async-start | bytes 25165824 | tf_op jit(solution)/shard_map/all_to_all | solution.py:75
  1101.9 26.9 %slice-start.16 = ((s8[11272192]{0:T(1024)(128)(4,1)}), s8[4194304]{0:T(1024)(128)(4,1)S(1)}, s32[]{:S(2)}) async-start(s8[11272192]{0:T(1024)(128)(4,1)} %bitcast.152), calls=%async_computation.25 | async-start | bytes 8388608
  1102.0 26.9 %slice-start.17 = ((s8[11272192]{0:T(1024)(128)(4,1)}), s8[4194304]{0:T(1024)(128)(4,1)S(1)}, s32[]{:S(2)}) async-start(s8[11272192]{0:T(1024)(128)(4,1)} %bitcast.152), calls=%async_computation.26 | async-start | bytes 8388608
  1102.0 49.0 %slice-start.9 = ((s8[11272192]{0:T(1024)(128)(4,1)}), s8[2883584]{0:T(1024)(128)(4,1)S(1)}, s32[]{:S(2)}) async-start(s8[11272192]{0:T(1024)(128)(4,1)} %bitcast.148), calls=%async_computation.18 | async-start | bytes 5767168
  1102.0 49.0 %slice-start.10 = ((s8[11272192]{0:T(1024)(128)(4,1)}), s8[4194304]{0:T(1024)(128)(4,1)S(1)}, s32[]{:S(2)}) async-start(s8[11272192]{0:T(1024)(128)(4,1)} %bitcast.148), calls=%async_computation.19 | async-start | bytes 8388608
  1128.9 22.1 %slice-start.11 = ((s8[11272192]{0:T(1024)(128)(4,1)}), s8[4194304]{0:T(1024)(128)(4,1)S(1)}, s32[]{:S(2)}) async-start(s8[11272192]{0:T(1024)(128)(4,1)} %bitcast.148), calls=%async_computation.20 | async-start | bytes 8388608
  1240.9 33.0 %slice-start.24 = ((s8[11272192]{0:T(1024)(128)(4,1)}), s8[2883584]{0:T(1024)(128)(4,1)S(1)}, s32[]{:S(2)}) async-start(s8[11272192]{0:T(1024)(128)(4,1)} %bitcast.158), calls=%async_computation.33 | async-start | bytes 5767168
  1240.9 145.0 %all-to-all-start.1 = ((bf16[8,192,4096]{2,1,0:T(8,128)(2,1)}), bf16[8,192,4096]{2,1,0:T(8,128)(2,1)}, u32[]{:S(2)}, u32[]{:S(2)}) async-start(bf16[8,192,4096]{2,1,0:T(8,128)(2,1)} %bitcast.121), calls=%async_computation.1 | async-start | bytes 25165824 | tf_op jit(solution)/shard_map/all_to_all | solution.py:75
  1246.9 27.0 %slice-start.25 = ((s8[11272192]{0:T(1024)(128)(4,1)}), s8[4194304]{0:T(1024)(128)(4,1)S(1)}, s32[]{:S(2)}) async-start(s8[11272192]{0:T(1024)(128)(4,1)} %bitcast.158), calls=%async_computation.34 | async-start | bytes 8388608
  1246.9 27.0 %slice-start.26 = ((s8[11272192]{0:T(1024)(128)(4,1)}), s8[4194304]{0:T(1024)(128)(4,1)S(1)}, s32[]{:S(2)}) async-start(s8[11272192]{0:T(1024)(128)(4,1)} %bitcast.158), calls=%async_computation.35 | async-start | bytes 8388608
  1385.9 145.1 %all-to-all-start.3 = ((bf16[8,192,4096]{2,1,0:T(8,128)(2,1)}), bf16[8,192,4096]{2,1,0:T(8,128)(2,1)}, u32[]{:S(2)}, u32[]{:S(2)}) async-start(bf16[8,192,4096]{2,1,0:T(8,128)(2,1)} %bitcast.114), calls=%async_computation.3 | async-start | bytes 25165824 | tf_op jit(solution)/shard_map/all_to_all | solution.py:75
  1391.3 26.9 %copy-start.37 = (s32[512]{0:T(512)S(1)}, s32[512]{0:T(512)}, u32[]{:S(2)}) copy-start(s32[512]{0:T(512)} %copy-done.36) | copy-start | bytes 6148
  1391.3 405.0 %all-reduce.3.cloned.1.call-start = ((), (), s32[]{:S(2)}) async-start(), calls=%async_computation.8 | async-start | bytes 262144 | tf_op jit(solution)/shard_map/psum | solution.py:137
  1418.1 12.0 copy-start.6
  1430.1 17.3 copy-start.5
  1430.2 17.3 copy-start.8
  1430.2 17.3 copy-start.12
  1430.2 17.3 copy-start.14
  1430.2 17.3 copy-start.16
  1430.2 17.3 copy-start.18
  1430.2 17.3 copy-start.22
  1430.2 17.3 copy-start.24
  1430.2 17.3 copy-start.26
  1589.3 34.8 %slice-start.18 = ((s8[11272192]{0:T(1024)(128)(4,1)}), s8[4194304]{0:T(1024)(128)(4,1)S(1)}, s32[]{:S(2)}) async-start(s8[11272192]{0:T(1024)(128)(4,1)} %bitcast.154), calls=%async_computation.27 | async-start | bytes 8388608
  1598.7 25.4 %slice-start.19 = ((s8[11272192]{0:T(1024)(128)(4,1)}), s8[4194304]{0:T(1024)(128)(4,1)S(1)}, s32[]{:S(2)}) async-start(s8[11272192]{0:T(1024)(128)(4,1)} %bitcast.154), calls=%async_computation.28 | async-start | bytes 8388608
  1598.7 25.4 %slice-start.20 = ((s8[11272192]{0:T(1024)(128)(4,1)}), s8[2883584]{0:T(1024)(128)(4,1)S(1)}, s32[]{:S(2)}) async-start(s8[11272192]{0:T(1024)(128)(4,1)} %bitcast.154), calls=%async_computation.29 | async-start | bytes 5767168
  1598.7 48.3 %slice-start.27 = ((s8[11272192]{0:T(1024)(128)(4,1)}), s8[4194304]{0:T(1024)(128)(4,1)S(1)}, s32[]{:S(2)}) async-start(s8[11272192]{0:T(1024)(128)(4,1)} %bitcast.160), calls=%async_computation.36 | async-start | bytes 8388608
  1598.7 48.3 %slice-start.28 = ((s8[11272192]{0:T(1024)(128)(4,1)}), s8[4194304]{0:T(1024)(128)(4,1)S(1)}, s32[]{:S(2)}) async-start(s8[11272192]{0:T(1024)(128)(4,1)} %bitcast.160), calls=%async_computation.37 | async-start | bytes 8388608
  1624.1 22.9 %slice-start.29 = ((s8[11272192]{0:T(1024)(128)(4,1)}), s8[2883584]{0:T(1024)(128)(4,1)S(1)}, s32[]{:S(2)}) async-start(s8[11272192]{0:T(1024)(128)(4,1)} %bitcast.160), calls=%async_computation.38 | async-start | bytes 5767168
  (26 other events, 166.8 us)
Sparse Core Ops, SparseCore 0:
  1449.0 153.1 all-reduce.2

commit v2 on v1

--- a/solution.py
+++ b/solution.py
@@ -1,7 +1,12 @@
+import functools
+
 import jax
 import jax.numpy as jnp
 from jax import lax
+from jax.experimental import pallas as pl
+from jax.experimental.pallas import tpu as pltpu
 from jax.sharding import PartitionSpec as P
+
 
 LN_EPS = 1e-5
 f32 = jnp.float32
@@ -30,13 +35,82 @@
     return jnp.sum(prob_all * picked, axis=-1), prob_all, picked
 
 
+VMEM_LIMIT = 63 * 1024 * 1024
+
+
+def grad_kernel(q_ref, wd_ref, a_ref, b_ref, u_ref, da_ref, db_ref):
+    du = lax.dot_general(wd_ref[...], q_ref[...], (((1,), (1,)), ((), ())), preferred_element_type=f32)
+    pre_gate = a_ref[...]
+    pre_up = b_ref[...]
+    sig_gate = jax.nn.sigmoid(pre_gate)
+    silu_gate = pre_gate * sig_gate
+    u_ref[...] = (silu_gate * pre_up).astype(bf16)
+    da_ref[...] = (du * pre_up * sig_gate * (1.0 + pre_gate * (1.0 - sig_gate))).astype(bf16)
+    db_ref[...] = (du * silu_gate).astype(bf16)
+
+
+def inner_grad(q, wd, a_t, b_t):
+    n_rows, d_model = q.shape
+    width = wd.shape[0]
+    w_tile, r_tile = width // 2, n_rows // 3
+    tile = pl.BlockSpec((w_tile, r_tile), lambda i, j: (i, j))
+    return pl.pallas_call(
+        grad_kernel,
+        grid=(2, 3),
+        in_specs=[pl.BlockSpec((r_tile, d_model), lambda i, j: (j, 0)),
+                  pl.BlockSpec((w_tile, d_model), lambda i, j: (i, 0)),
+                  tile, tile],
+        out_specs=[tile] * 3,
+        out_shape=[jax.ShapeDtypeStruct((width, n_rows), bf16)] * 3,
+        compiler_params=pltpu.CompilerParams(vmem_limit_bytes=VMEM_LIMIT),
+        cost_estimate=pl.CostEstimate(flops=2 * n_rows * d_model * width, bytes_accessed=4 * n_rows * d_model + 14 * width * n_rows,
+                                      transcendentals=2 * n_rows * width),
+    )(q, wd, a_t, b_t)
+
+
+def dw_kernel(first, *refs):
+    u_ref, da_ref, db_ref, h_ref, q_ref = refs[:5]
+    acc = refs[5:-3]
+    outs = refs[-3:]
+    for k, (left, right) in enumerate(((da_ref, h_ref), (db_ref, h_ref), (u_ref, q_ref))):
+        term = jnp.dot(left[...], right[...], preferred_element_type=f32)
+        outs[k][...] = term if first else acc[k][...] + term
+
+
+def add_dw(acc, u_t, da_t, db_t, h, q):
+    width, n_rows = u_t.shape
+    d_model = h.shape[1]
+    first = acc is None
+    acc = [] if first else list(acc)
+    d_tile = 512
+    whole = pl.BlockSpec((width, n_rows), lambda j: (0, 0), pipeline_mode=pl.Buffered(1))
+    rows = pl.BlockSpec((n_rows, d_tile), lambda j: (0, j))
+    tile = pl.BlockSpec((width, d_tile), lambda j: (0, j))
+    return pl.pallas_call(
+        functools.partial(dw_kernel, first),
+        grid=(d_model // d_tile,),
+        in_specs=[whole] * 3 + [rows] * 2 + [tile] * len(acc),
+        out_specs=[tile] * 3,
+        out_shape=[jax.ShapeDtypeStruct((width, d_model), f32)] * 3,
+        input_output_aliases={5 + k: k for k in range(len(acc))},
+        compiler_params=pltpu.CompilerParams(vmem_limit_bytes=VMEM_LIMIT),
+        cost_estimate=pl.CostEstimate(flops=6 * n_rows * d_model * width, bytes_accessed=4 * n_rows * d_model + 12 * width * d_model * (1 if first else 2),
+                                      transcendentals=0),
+    )(u_t, da_t, db_t, h, q, *acc)
+
+
+def after(value, *deps):
+    return lax.optimization_barrier((value,) + deps)[0]
+
+
 def solution(mesh):
     n_ep = mesh.shape['ep']
     n_dp = mesh.shape['dp']
     tok_spec = P(('dp', 'ep'), None)
     row_spec = P(('dp', 'ep'))
     exp_spec = P('ep', None, None)
-    far = [(i, i ^ 2) for i in range(n_dp)]
+    outer = [(i, i ^ 2) for i in (0, n_dp - 1)]
+    middle = [(i, i ^ 2) for i in (1, n_dp - 2)]
     near = [(i, i ^ 1) for i in range(n_dp)]
 
     def local_step(tok_x, tok_dy, exp_first, exp_second, eligible, slot_first, slot_second,
@@ -60,70 +134,73 @@
         meta = jnp.stack([pos_one.astype(f32), pos_two.astype(f32), gate_one, gate_two])
         row_ids = jnp.arange(n_rows)
 
-        def dispatch(h, dy, meta):
-            p1 = meta[0].astype(jnp.int32)
-            p2 = meta[1].astype(jnp.int32)
-            m1 = p1[None, :] == row_ids[:, None]
-            m2 = p2[None, :] == row_ids[:, None]
-            sel = (m1 | m2).astype(bf16)
+        def masks(meta):
+            return [meta[k].astype(jnp.int32)[None, :] == row_ids[:, None] for k in range(2)]
+
+        def select_h(h, meta):
+            m1, m2 = masks(meta)
+            return jnp.dot((m1 | m2).astype(bf16), h, preferred_element_type=f32).astype(bf16)
+
+        def select_q(dy, meta):
+            m1, m2 = masks(meta)
             g_row = jnp.sum(jnp.where(m1, meta[2][None, :], 0.0) + jnp.where(m2, meta[3][None, :], 0.0), axis=1)
-            h_buf = jnp.dot(sel, h, preferred_element_type=f32).astype(bf16)
-            q_buf = (g_row[:, None] * jnp.dot(sel, dy, preferred_element_type=f32)).astype(bf16)
-            return h_buf, q_buf
+            return (g_row[:, None] * jnp.dot((m1 | m2).astype(bf16), dy, preferred_element_type=f32)).astype(bf16)
 
         def swap(buf):
             return lax.all_to_all(buf.reshape(n_ep, slot_cap, d_model), 'ep', 0, 0, tiled=True).reshape(n_rows, d_model)
 
-        def inner(h, q):
-            pre_gate = jnp.einsum('rd,fd->rf', h, wg_t, preferred_element_type=f32)
-            pre_up = jnp.einsum('rd,fd->rf', h, wu_t, preferred_element_type=f32)
-            sig_gate = jax.nn.sigmoid(pre_gate)
-            silu_gate = pre_gate * sig_gate
-            u = (silu_gate * pre_up).astype(bf16)
-            du = jnp.einsum('rd,fd->rf', q, wd, preferred_element_type=f32)
-            da = (du * pre_up * sig_gate * (1.0 + pre_gate * (1.0 - sig_gate))).astype(bf16)
-            db = (du * silu_gate).astype(bf16)
-            return u, da, db
-
-        def dw(u, da, db, h, q):
-            def mm(a, b):
-                return jnp.einsum('rf,rd->fd', a, b, preferred_element_type=f32)
-            return mm(da, h), mm(db, h), mm(u, q)
-
-        dy_f1 = lax.ppermute(tok_dy, 'dp', far)
-        h_f1 = lax.ppermute(hidden, 'dp', far)
-        m_f1 = lax.ppermute(meta, 'dp', far)
-        dy_f2 = lax.ppermute(dy_f1, 'dp', near)
-        h_f2 = lax.ppermute(h_f1, 'dp', near)
+        def pre(h):
+            return (jnp.einsum('fd,rd->fr', wg_t, h, preferred_element_type=f32),
+                    jnp.einsum('fd,rd->fr', wu_t, h, preferred_element_type=f32))
+
+        own_meta = jnp.stack([pos_one.astype(f32), pos_two.astype(f32)])
+        h_buf = select_h(hidden, own_meta)
+        h_own = swap(h_buf)
+        dy_a = lax.ppermute(tok_dy, 'dp', outer)
+        m_a = lax.ppermute(meta, 'dp', outer)
+        h_a = lax.ppermute(after(hidden, meta), 'dp', outer)
+        dy_b = lax.ppermute(after(tok_dy, dy_a), 'dp', middle)
+        m_b = lax.ppermute(after(meta, m_a), 'dp', middle)
+        h_b = lax.ppermute(after(hidden, h_a), 'dp', middle)
+
+        q_buf = select_q(tok_dy, meta)
+        q_own = swap(after(q_buf, h_own))
+        h_near = lax.ppermute(h_own, 'dp', near)
+        a_t, b_t = pre(h_own)
+        u_t = (a_t * jax.nn.sigmoid(a_t) * b_t).astype(bf16)
+        exp_out = jnp.einsum('fr,fd->rd', u_t, wd, preferred_element_type=f32).astype(bf16)
+        out_back = swap(after(exp_out, q_own))
+        u_t, da_t, db_t = inner_grad(q_own, wd, a_t, b_t)
+        grad_hid = (jnp.einsum('fr,fd->rd', da_t, wg_t, preferred_element_type=f32)
+                    + jnp.einsum('fr,fd->rd', db_t, wu_t, preferred_element_type=f32)).astype(bf16)
+        acc = add_dw(None, u_t, da_t, db_t, h_own, q_own)
+
+        h_f1, dy_f1, m_f1 = h_a + h_b, dy_a + dy_b, m_a + m_b
         m_f2 = lax.ppermute(m_f1, 'dp', near)
-
-        h_buf, q_buf = dispatch(hidden, tok_dy, meta)
-        h_own = swap(h_buf)
-        q_own = swap(q_buf)
-        h_near = lax.ppermute(h_own, 'dp', near)
+        h_f2 = lax.ppermute(after(h_f1, m_f1), 'dp', near)
+        dy_f2 = lax.ppermute(after(dy_f1, h_f1), 'dp', near)
         q_near = lax.ppermute(q_own, 'dp', near)
-        u, da, db = inner(h_own, q_own)
-        exp_out = jnp.dot(u, wd, preferred_element_type=f32).astype(bf16)
-        grad_hid = (jnp.dot(da, wg_t, preferred_element_type=f32)
-                    + jnp.dot(db, wu_t, preferred_element_type=f32)).astype(bf16)
-        dwg, dwu, dwd = dw(u, da, db, h_own, q_own)
-
-        h_b1, q_b1 = dispatch(h_f1, dy_f1, m_f1)
-        h_b2, q_b2 = dispatch(h_f2, dy_f2, m_f2)
-        out_back = swap(exp_out)
-        hid_back = swap(grad_hid)
-        h_r1, q_r1 = swap(h_b1), swap(q_b1)
-        h_r2, q_r2 = swap(h_b2), swap(q_b2)
-        for h, q in ((h_r1, q_r1), (h_r2, q_r2), (h_near, q_near)):
-            a, b, c = dw(*inner(h, q), h, q)
-            dwg, dwu, dwd = dwg + a, dwu + b, dwd + c
-
+        h_b1 = select_h(h_f1, m_f1)
+        q_b1 = select_q(dy_f1, m_f1)
+        h_b2 = select_h(h_f2, m_f2)
+        q_b2 = select_q(dy_f2, m_f2)
+        h_r1 = swap(after(h_b1, out_back))
+        q_r1 = swap(after(q_b1, h_r1))
+        h_r2 = swap(after(h_b2, q_r1))
+        q_r2 = swap(after(q_b2, h_r2))
+        hid_back = swap(after(grad_hid, q_r2))
+        for h, q in ((h_r1, q_r1), (h_near, q_near), (h_r2, q_r2)):
+            a_t, b_t = pre(h)
+            u_t, da_t, db_t = inner_grad(q, wd, a_t, b_t)
+            acc = add_dw(acc, u_t, da_t, db_t, h, q)
+        dwg, dwu, dwd = acc
+
+        dy_float = tok_dy.astype(f32)
         sel_one = (pos_one[:, None] == row_ids[None, :]).astype(bf16)
         sel_two = (pos_two[:, None] == row_ids[None, :]).astype(bf16)
         out_one = jnp.dot(sel_one, out_back, preferred_element_type=f32)
         out_two = jnp.dot(sel_two, out_back, preferred_element_type=f32)
         out_tok = (tok_x.astype(f32) + gate_one[:, None] * out_one + gate_two[:, None] * out_two).astype(bf16)
-        dy_float = tok_dy.astype(f32)
         dgate_one = jnp.sum(dy_float * out_one, axis=-1)
         dgate_two = jnp.sum(dy_float * out_two, axis=-1)
         d_logits = ((dgate_one * gate_one)[:, None] * (pick_one - prob_one)

time: 1810 us -> 1720 us (0.950)
  matrix products: 848 us -> 398 us
  Pallas kernels: 0 us -> 378 us
  waiting for transfers between devices: 820 us -> 776 us
    dot_general x33 -> x17, matrix products: 797 us -> 347 us  [the longest x4 101 us: pre(): jnp.einsum('fd,rd->fr', wu_t, h, preferred_element_type=f32)]
    pallas_call x0 -> x8, Pallas kernels: none -> 378 us  [the longest x4 258 us: add_dw(): pl.pallas_call(functools.partial(dw_kernel, first), grid=(d_model // d_ti...]
    ppermute x1, waiting for transfers between devices: 0.01 us -> 177 us  [local_step(): q_near = lax.ppermute(q_own, 'dp', near)]
    all_to_all x8, waiting for transfers between devices: 343 us -> 173 us  [swap(): lax.all_to_all(buf.reshape(n_ep, slot_cap, d_model), 'ep', 0, 0, tiled=True)]
    ppermute x1, waiting for transfers between devices: 0.01 us -> 104 us  [local_step(): h_near = lax.ppermute(h_own, 'dp', near)]
    ppermute x1, waiting for transfers between devices: 86.7 us -> 0.92 us  [local_step(): m_f2 = lax.ppermute(m_f1, 'dp', near)]
    ppermute x5 -> x8, waiting for transfers between devices: 390 us -> 320 us  [the longest x1 93.8 us: local_step(): h_b = lax.ppermute(after(hidden, h_a), 'dp', middle)]
  transfers between devices with their start and end apart: 17 -> 20, of which waited for: 10 -> 10; matrix products, arithmetic and copies ran while one was open for 47% -> 24% of each run, Pallas kernels for 0% -> 22%
where the time goes in v2:
time: 1720 us; the launch traced here: 1710 us
  waiting for transfers between devices  776 us (45%)
  matrix products  398 us (23%)
  Pallas kernels  378 us (22%)
  starting transfers between devices  70.4 us (4%)
  blocking collectives  42.3 us (2%)
  other arithmetic  26.4 us (2%)
    pallas_call x4, Pallas kernels, add_dw(): pl.pallas_call(functools.partial(dw_kernel, first), grid=(d_model // d_ti...  258 us
    ppermute x1, waiting for transfers between devices, local_step(): q_near = lax.ppermute(q_own, 'dp', near)  177 us
    all_to_all x8, waiting for transfers between devices, swap(): lax.all_to_all(buf.reshape(n_ep, slot_cap, d_model), 'ep', 0, 0, tiled=True)  173 us
    pallas_call x4, Pallas kernels, inner_grad(): pl.pallas_call(grad_kernel, grid=(2, 3), in_specs=[pl.BlockSpec((r_tile,...  120 us
    ppermute x1, waiting for transfers between devices, local_step(): h_near = lax.ppermute(h_own, 'dp', near)  104 us
    dot_general x4, matrix products, pre(): jnp.einsum('fd,rd->fr', wu_t, h, preferred_element_type=f32)  101 us
    dot_general x4, matrix products, pre(): jnp.einsum('fd,rd->fr', wg_t, h, preferred_element_type=f32)  97.3 us
    ppermute x1, waiting for transfers between devices, local_step(): h_b = lax.ppermute(after(hidden, h_a), 'dp', middle)  93.8 us
  transfers between devices with their start and end apart: 20, of which 10 were waited for; matrix products, arithmetic and copies ran while one was open for 24% of the time, Pallas kernels for 22%

profile of v2, /device:TPU:0, one launch (start us, length us, event | category | flops | bytes accessed | tf_op | source)
XLA Modules:
  0.0 1709.1 jit_solution(10272284902983923678)
XLA Ops:
  7.3 3.0 convert_reduce_fusion
  10.2 3.4 fusion.55
  13.8 2.3 fusion.50
  16.2 9.6 convolution_convert_fusion.3
  25.8 5.5 all-to-all-start
  31.3 3.4 fusion.101
  35.5 8.0 collective-permute-start.5
  43.4 3.3 collective-permute-start.3
  47.4 11.8 multiply_convert_fusion.2
  59.2 111.8 %all-to-all-done = bf16[8,192,4096]{2,1,0:T(8,128)(2,1)} async-done(((bf16[8,192,4096]{2,1,0:T(8,128)(2,1)}), bf16[8,192,4096]{2,1,0:T(8,128)(2,1)}, u32[]{:S(2)}, u32[]{:S(2)}) %all-to-all-start) | async-done | bytes 12582944 | tf_op jit(solution)/shard_map/all_to_all | solution.py:150
  171.0 5.5 all-to-all-start.1
  176.5 21.2 %fusion.25.a_ref = f32[1376,1536]{1,0:T(8,128)S(1)} fusion(bf16[1536,4096]{1,0:T(8,128)(2,1)} %bitcast.1.refs_3_, bf16[1,4096,1376]{1,2,0:T(8,128)(2,1)} %param.23), kind=kOutput, calls=%fused_computation.39 | convolution fusion | flops 17314086912 | bytes 32309248 | tf_op jit(solution)/shard_map/fd,rd->fr/dot_general | solution.py:153
  197.7 28.2 %fusion.37.b_ref = f32[1376,1536]{1,0:T(8,128)} fusion(bf16[1536,4096]{1,0:T(8,128)(2,1)} %bitcast.1.refs_3_, bf16[1,4096,1376]{1,2,0:T(8,128)(2,1)} %param.24), kind=kOutput, calls=%fused_computation.43 | convolution fusion | flops 17314086912 | bytes 32309248 | tf_op jit(solution)/shard_map/fd,rd->fr/dot_general | solution.py:154
  225.9 28.1 %convolution_convert_fusion = bf16[1536,4096]{1,0:T(8,128)(2,1)} fusion(f32[1376,1536]{1,0:T(8,128)} %fusion.37.b_ref, f32[1376,1536]{1,0:T(8,128)S(1)} %fusion.25.a_ref, bf16[1,1376,4096]{2,1,0:T(8,128)(2,1)} %param.25), kind=kOutput, calls=%fused_computation.4 | convolution fusion | flops 17333059584 | bytes 40763392 | tf_op jit(solution)/shard_map/fr,fd->rd/dot_general | solution.py:171
  254.0 61.5 %all-to-all-done.1 = bf16[8,192,4096]{2,1,0:T(8,128)(2,1)} async-done(((bf16[8,192,4096]{2,1,0:T(8,128)(2,1)}), bf16[8,192,4096]{2,1,0:T(8,128)(2,1)}, u32[]{:S(2)}, u32[]{:S(2)}) %all-to-all-start.1) | async-done | bytes 12582944 | tf_op jit(solution)/shard_map/all_to_all | solution.py:150
  315.5 5.4 all-to-all-start.2
  320.9 1.3 collective-permute-start.6
  322.2 1.3 collective-permute-start.4
  323.5 93.8 %collective-permute-done.6 = bf16[512,4096]{1,0:T(8,128)(2,1)S(1)} collective-permute-done((bf16[512,4096]{1,0:T(8,128)(2,1)}, bf16[512,4096]{1,0:T(8,128)(2,1)S(1)}, u32[]{:S(2)}, u32[]{:S(2)}) %collective-permute-start.6) | collective-permute-done | bytes 4194336 | tf_op jit(solution)/shard_map/ppermute | solution.py:164
  417.3 5.7 add.89
  423.1 83.6 %collective-permute-done.4 = bf16[512,4096]{1,0:T(8,128)(2,1)S(1)} collective-permute-done((bf16[512,4096]{1,0:T(8,128)(2,1)}, bf16[512,4096]{1,0:T(8,128)(2,1)S(1)}, u32[]{:S(2)}, u32[]{:S(2)}) %collective-permute-start.4) | collective-permute-done | bytes 4194336 | tf_op jit(solution)/shard_map/ppermute | solution.py:162
  506.7 3.7 add.88
  510.4 1.6 collective-permute-start.7
  512.1 5.2 collective-permute-start
  517.2 84.5 %collective-permute-done = f32[4,512]{1,0:T(4,128)S(1)} collective-permute-done((f32[4,512]{1,0:T(4,128)S(1)}, f32[4,512]{1,0:T(4,128)S(1)}, u32[]{:S(2)}, u32[]{:S(2)}) %collective-permute-start) | collective-permute-done | bytes 8224 | tf_op jit(solution)/shard_map/ppermute | solution.py:160
  603.0 5.1 collective-permute-done.1
  609.3 1.7 collective-permute-start.8
  612.6 12.3 convolution_convert_fusion.1
  624.9 9.7 multiply_convert_fusion
  635.0 9.7 multiply_convert_fusion.1
  644.7 5.5 all-to-all-start.3
  650.2 52.9 %collective-permute-done.8 = bf16[512,4096]{1,0:T(8,128)(2,1)} collective-permute-done((bf16[512,4096]{1,0:T(8,128)(2,1)}, bf16[512,4096]{1,0:T(8,128)(2,1)}, u32[]{:S(2)}, u32[]{:S(2)}) %collective-permute-start.8) | collective-permute-done | bytes 4194336 | tf_op jit(solution)/shard_map/ppermute | solution.py:180
  703.1 11.7 convolution_convert_fusion.2
  714.8 1.6 collective-permute-start.9
  716.4 29.9 %shard_map.188 = (bf16[1376,1536]{1,0:T(8,128)(2,1)}, bf16[1376,1536]{1,0:T(8,128)(2,1)}, bf16[1376,1536]{1,0:T(8,128)(2,1)}) custom-call(bf16[1536,4096]{1,0:T(8,128)(2,1)} %bitcast.8.q_ref.refs_4_, bf16[1376,4096]{1,0:T(8,128)(2,1)} %bitcast.145, f32[1376,1536]{1,0:T(8,128)} %copy-done.55, f32[1376,1536]{1,0:T(8,128)} %fusion.37.b_ref), custom_call_target="tpu_custom_call" | custom-call | flops 17314086912 | bytes 54755328 | tf_op jit(solution)/shard_map/pallas_call | solution.py:57
  746.3 26.2 %fusion.15 = f32[1536,4096]{1,0:T(8,128)} fusion(bf16[1376,1536]{1,0:T(8,128)(2,1)} %get-tuple-element.47.refs_1_, bf16[1,4096,1376]{1,2,0:T(8,128)(2,1)} %param.23), kind=kOutput, calls=%fused_computation.29 | convolution fusion | flops 17314086912 | bytes 40665088 | tf_op jit(solution)/shard_map/fr,fd->rd/dot_general | solution.py:174
  772.5 61.3 %shard_map.192 = (f32[1376,4096]{1,0:T(8,128)}, f32[1376,4096]{1,0:T(8,128)}, f32[1376,4096]{1,0:T(8,128)}) custom-call(bf16[1376,1536]{1,0:T(8,128)(2,1)} %get-tuple-element.69.refs_0_, bf16[1376,1536]{1,0:T(8,128)(2,1)} %get-tuple-element.47.refs_1_, bf16[1376,1536]{1,0:T(8,128)(2,1)} %get-tuple-element.48.refs_2_, bf16[1536,4096]{1,0:T(8,128)(2,1)} %bitcast.1.refs_3_, ...), custom_call_target="tpu_custom_call" | custom-call | flops 51942260736 | bytes 92798976 | tf_op jit(solution)/shard_map/pallas_call | solution.py:89
  833.7 5.6 all-to-all-start.4
  839.3 29.5 %add_convert_fusion = bf16[1536,4096]{1,0:T(8,128)(2,1)} fusion(f32[1536,4096]{1,0:T(8,128)} %fusion.15, bf16[1376,1536]{1,0:T(8,128)(2,1)} %get-tuple-element.48.refs_2_, bf16[1,4096,1376]{1,2,0:T(8,128)(2,1)} %param.24), kind=kOutput, calls=%fused_computation.2 | convolution fusion | flops 17326669824 | bytes 53248000 | tf_op jit(solution)/shard_map/fr,fd->rd/dot_general | solution.py:175
  868.8 103.9 %collective-permute-done.10.refs_3_ = bf16[1536,4096]{1,0:T(8,128)(2,1)} collective-permute-done((bf16[1536,4096]{1,0:T(8,128)(2,1)}, bf16[1536,4096]{1,0:T(8,128)(2,1)}, u32[]{:S(2)}, u32[]{:S(2)}) %collective-permute-start.10) | collective-permute-done | bytes 12582944 | tf_op jit(solution)/shard_map/ppermute | solution.py:168
  972.7 25.3 %fusion.31.a_ref = f32[1376,1536]{1,0:T(8,128)} fusion(bf16[1536,4096]{1,0:T(8,128)(2,1)} %collective-permute-done.10.refs_3_, bf16[1,4096,1376]{1,2,0:T(8,128)(2,1)} %param.23), kind=kOutput, calls=%fused_computation.41 | convolution fusion | flops 17314086912 | bytes 32309248 | tf_op jit(solution)/shard_map/fd,rd->fr/dot_general | solution.py:153
  998.0 25.7 %fusion.43.b_ref = f32[1376,1536]{1,0:T(8,128)} fusion(bf16[1536,4096]{1,0:T(8,128)(2,1)} %collective-permute-done.10.refs_3_, bf16[1,4096,1376]{1,2,0:T(8,128)(2,1)} %param.24), kind=kOutput, calls=%fused_computation.45 | convolution fusion | flops 17314086912 | bytes 32309248 | tf_op jit(solution)/shard_map/fd,rd->fr/dot_general | solution.py:154
  1023.7 11.9 fusion.65
  1035.6 5.4 all-to-all-start.5
  1041.1 20.0 %fusion.58 = (f32[512]{0:T(512)S(1)}, f32[512]{0:T(512)S(1)}, bf16[512,4096]{1,0:T(8,128)(2,1)}) fusion(bf16[512,4096]{1,0:T(8,128)(2,1)} %param.14, f32[512,4096]{1,0:T(8,128)} %fusion.65, f32[512]{0:T(512)S(1)} %copy-done.37, f32[512]{0:T(512)S(1)} %copy-done.35, bf16[512,4096]{1,0:T(8,128)(2,1)} %param.13, bf16[1536,4096]{1,0:T(8,128)(2,1)} %bitcast.10, ...), kind=kOutput, calls=%fused_computation.57 | convolution fusion | flops 6466305024 | bytes 33564672 | tf_op jit(solution)/shard_map/dot_general | solution.py:201
  1062.4 1.3 fusion.105
  1063.7 177.5 %collective-permute-done.9.q_ref.refs_4_ = bf16[1536,4096]{1,0:T(8,128)(2,1)} collective-permute-done((bf16[1536,4096]{1,0:T(8,128)(2,1)}, bf16[1536,4096]{1,0:T(8,128)(2,1)}, u32[]{:S(2)}, u32[]{:S(2)}) %collective-permute-start.9) | collective-permute-done | bytes 12582944 | tf_op jit(solution)/shard_map/ppermute | solution.py:182
  1241.2 30.0 %shard_map.190 = (bf16[1376,1536]{1,0:T(8,128)(2,1)}, bf16[1376,1536]{1,0:T(8,128)(2,1)}, bf16[1376,1536]{1,0:T(8,128)(2,1)}) custom-call(bf16[1536,4096]{1,0:T(8,128)(2,1)} %collective-permute-done.9.q_ref.refs_4_, bf16[1376,4096]{1,0:T(8,128)(2,1)} %bitcast.146, f32[1376,1536]{1,0:T(8,128)} %fusion.31.a_ref, f32[1376,1536]{1,0:T(8,128)} %fusion.43.b_ref), custom_call_target="tpu_custom_call" | custom-call | flops 17314086912 | bytes 54755328 | tf_op jit(solution)/shard_map/pallas_call | solution.py:57
  1271.2 25.4 %fusion.34.a_ref = f32[1376,1536]{1,0:T(8,128)} fusion(bf16[1536,4096]{1,0:T(8,128)(2,1)} %bitcast.24.refs_3_, bf16[1,4096,1376]{1,2,0:T(8,128)(2,1)} %param.23), kind=kOutput, calls=%fused_computation.42 | convolution fusion | flops 17314086912 | bytes 32309248 | tf_op jit(solution)/shard_map/fd,rd->fr/dot_general | solution.py:153
  1296.6 25.2 %fusion.46.b_ref = f32[1376,1536]{1,0:T(8,128)} fusion(bf16[1536,4096]{1,0:T(8,128)(2,1)} %bitcast.24.refs_3_, bf16[1,4096,1376]{1,2,0:T(8,128)(2,1)} %param.24), kind=kOutput, calls=%fused_computation.46 | convolution fusion | flops 17314086912 | bytes 32309248 | tf_op jit(solution)/shard_map/fd,rd->fr/dot_general | solution.py:154
  1321.9 5.7 all-to-all-start.6
  1327.6 30.0 %shard_map.191 = (bf16[1376,1536]{1,0:T(8,128)(2,1)}, bf16[1376,1536]{1,0:T(8,128)(2,1)}, bf16[1376,1536]{1,0:T(8,128)(2,1)}) custom-call(bf16[1536,4096]{1,0:T(8,128)(2,1)} %bitcast.26.q_ref.refs_4_, bf16[1376,4096]{1,0:T(8,128)(2,1)} %bitcast.147, f32[1376,1536]{1,0:T(8,128)} %fusion.34.a_ref, f32[1376,1536]{1,0:T(8,128)} %fusion.46.b_ref), custom_call_target="tpu_custom_call" | custom-call | flops 17314086912 | bytes 54755328 | tf_op jit(solution)/shard_map/pallas_call | solution.py:57
  1357.6 65.5 %shard_map.193 = (f32[1376,4096]{1,0:T(8,128)}, f32[1376,4096]{1,0:T(8,128)}, f32[1376,4096]{1,0:T(8,128)}) custom-call(bf16[1376,1536]{1,0:T(8,128)(2,1)} %get-tuple-element.66.refs_0_, bf16[1376,1536]{1,0:T(8,128)(2,1)} %get-tuple-element.67.refs_1_, ...), custom_call_target="tpu_custom_call", output_to_operand_aliasing={{0}: (5, {}), {1}: (6, {}), {2}: (7, {})} | custom-call | flops 51942260736 | bytes 160432128 | tf_op jit(solution)/shard_map/pallas_call | solution.py:89
  1423.1 65.5 %shard_map.194 = (f32[1376,4096]{1,0:T(8,128)}, f32[1376,4096]{1,0:T(8,128)}, f32[1376,4096]{1,0:T(8,128)}) custom-call(bf16[1376,1536]{1,0:T(8,128)(2,1)} %get-tuple-element.63.refs_0_, bf16[1376,1536]{1,0:T(8,128)(2,1)} %get-tuple-element.64.refs_1_, ...), custom_call_target="tpu_custom_call", output_to_operand_aliasing={{0}: (5, {}), {1}: (6, {}), {2}: (7, {})} | custom-call | flops 51942260736 | bytes 160432128 | tf_op jit(solution)/shard_map/pallas_call | solution.py:89
  1488.6 5.8 all-to-all-start.7
  1494.5 25.4 %fusion.28.a_ref = f32[1376,1536]{1,0:T(8,128)} fusion(bf16[1536,4096]{1,0:T(8,128)(2,1)} %bitcast.28.refs_3_, bf16[1,4096,1376]{1,2,0:T(8,128)(2,1)} %param.23), kind=kOutput, calls=%fused_computation.40 | convolution fusion | flops 17314086912 | bytes 32309248 | tf_op jit(solution)/shard_map/fd,rd->fr/dot_general | solution.py:153
  1519.8 22.0 %fusion.40.b_ref = f32[1376,1536]{1,0:T(8,128)} fusion(bf16[1536,4096]{1,0:T(8,128)(2,1)} %bitcast.28.refs_3_, bf16[1,4096,1376]{1,2,0:T(8,128)(2,1)S(1)} %bitcast.144), kind=kOutput, calls=%fused_computation.44 | convolution fusion | flops 17314086912 | bytes 32309248 | tf_op jit(solution)/shard_map/fd,rd->fr/dot_general | solution.py:154
  1541.8 30.1 %shard_map.189 = (bf16[1376,1536]{1,0:T(8,128)(2,1)}, bf16[1376,1536]{1,0:T(8,128)(2,1)}, bf16[1376,1536]{1,0:T(8,128)(2,1)}) custom-call(bf16[1536,4096]{1,0:T(8,128)(2,1)} %bitcast.30.q_ref.refs_4_, bf16[1376,4096]{1,0:T(8,128)(2,1)} %bitcast.148, f32[1376,1536]{1,0:T(8,128)} %fusion.28.a_ref, f32[1376,1536]{1,0:T(8,128)} %fusion.40.b_ref), custom_call_target="tpu_custom_call" | custom-call | flops 17314086912 | bytes 54755328 | tf_op jit(solution)/shard_map/pallas_call | solution.py:57
  1572.0 65.5 %shard_map.195 = (f32[1376,4096]{1,0:T(8,128)}, f32[1376,4096]{1,0:T(8,128)}, f32[1376,4096]{1,0:T(8,128)}) custom-call(bf16[1376,1536]{1,0:T(8,128)(2,1)} %get-tuple-element.60.refs_0_, bf16[1376,1536]{1,0:T(8,128)(2,1)} %get-tuple-element.61.refs_1_, ...), custom_call_target="tpu_custom_call", output_to_operand_aliasing={{0}: (5, {}), {1}: (6, {}), {2}: (7, {})} | custom-call | flops 51942260736 | bytes 160432128 | tf_op jit(solution)/shard_map/pallas_call | solution.py:89
  1637.7 10.2 fusion.76
  1648.1 3.8 fusion.54
  1651.9 6.0 fusion.60
  1657.9 42.3 %all-reduce = (f32[4096]{0:T(1024)}, f32[4096]{0:T(1024)}) all-reduce(f32[4096]{0:T(1024)S(1)} %get-tuple-element.82, f32[4096]{0:T(1024)S(1)} %get-tuple-element.85), channel_id=1, replica_groups=mesh['dp'=4,'ep'=8] {'dp','ep'}, use_global_device_ids=true, to_apply=%region_17.18 | all-reduce | flops 8192 | bytes 65536 | tf_op jit(solution)/shard_map/psum | solution.py:215
  1700.2 1.6 copy.40
  (156 shorter events, 7.3 us)
Async XLA Ops:
  7.2 24.1 %copy-start = (bf16[4096,8]{0,1:T(8,128)(2,1)S(1)}, bf16[4096,8]{0,1:T(8,128)(2,1)}, u32[]{:S(2)}) copy-start(bf16[4096,8]{0,1:T(8,128)(2,1)} %param.22) | copy-start | bytes 196612
  7.2 6.7 copy-start.1
  7.2 6.5 copy-start.45
  7.2 6.5 copy-start.46
  7.2 6.5 copy-start.14
  7.2 6.5 copy-start.53
  7.2 6.5 copy-start.31
  7.2 6.5 copy-start.54
  10.2 5.9 copy-start.23
  16.1 9.7 copy-start.3
  25.8 145.2 %all-to-all-start = ((bf16[8,192,4096]{2,1,0:T(8,128)(2,1)}), bf16[8,192,4096]{2,1,0:T(8,128)(2,1)}, u32[]{:S(2)}, u32[]{:S(2)}) async-start(bf16[8,192,4096]{2,1,0:T(8,128)(2,1)} %bitcast.121), calls=%async_computation | async-start | bytes 25165824 | tf_op jit(solution)/shard_map/all_to_all | solution.py:150
  34.8 11.9 copy-start.34
  35.4 11.3 copy-start.36
  35.5 285.4 %collective-permute-start.5 = (bf16[512,4096]{1,0:T(8,128)(2,1)}, bf16[512,4096]{1,0:T(8,128)(2,1)}, u32[]{:S(2)}, u32[]{:S(2)}) collective-permute-start(bf16[512,4096]{1,0:T(8,128)(2,1)} %copy-done.3), channel_id=1, source_target_pairs={{0,16},{24,8},{1,17},{25,9},{2,18},{26,10},{3,19},{27,11},{4,20},{... | collective-permute-start | bytes 12582920 | tf_op jit(solution)/shard_map/ppermute | solution.py:161
  43.4 278.8 %collective-permute-start.3 = (bf16[512,4096]{1,0:T(8,128)(2,1)}, bf16[512,4096]{1,0:T(8,128)(2,1)}, u32[]{:S(2)}, u32[]{:S(2)}) collective-permute-start(bf16[512,4096]{1,0:T(8,128)(2,1)} %param.14), channel_id=1, source_target_pairs={{0,16},{24,8},{1,17},{25,9},{2,18},{26,10},{3,19},{27,11},{4,20},{... | collective-permute-start | bytes 12582920 | tf_op jit(solution)/shard_map/ppermute | solution.py:159
  171.0 144.5 %all-to-all-start.1 = ((bf16[8,192,4096]{2,1,0:T(8,128)(2,1)}), bf16[8,192,4096]{2,1,0:T(8,128)(2,1)}, u32[]{:S(2)}, u32[]{:S(2)}) async-start(bf16[8,192,4096]{2,1,0:T(8,128)(2,1)} %bitcast.122), calls=%async_computation.1 | async-start | bytes 25165824 | tf_op jit(solution)/shard_map/all_to_all | solution.py:150
  197.7 28.2 %copy-start.55 = (f32[1376,1536]{1,0:T(8,128)}, f32[1376,1536]{1,0:T(8,128)S(1)}, u32[]{:S(2)}) copy-start(f32[1376,1536]{1,0:T(8,128)S(1)} %fusion.25.a_ref) | copy-start | bytes 25362436
  315.5 329.2 %all-to-all-start.2 = ((bf16[8,192,4096]{2,1,0:T(8,128)(2,1)}), bf16[8,192,4096]{2,1,0:T(8,128)(2,1)}, u32[]{:S(2)}, u32[]{:S(2)}) async-start(bf16[8,192,4096]{2,1,0:T(8,128)(2,1)} %bitcast.117), calls=%async_computation.2 | async-start | bytes 25165824 | tf_op jit(solution)/shard_map/all_to_all | solution.py:150
  320.9 96.4 %collective-permute-start.6 = (bf16[512,4096]{1,0:T(8,128)(2,1)}, bf16[512,4096]{1,0:T(8,128)(2,1)S(1)}, u32[]{:S(2)}, u32[]{:S(2)}) collective-permute-start(bf16[512,4096]{1,0:T(8,128)(2,1)} %copy-done.3), channel_id=1, source_target_pairs={{8,24},{16,0},{9,25},{17,1},{10,26},{18,2},{11,27},{19,3},{12,28},... | collective-permute-start | bytes 12582920 | tf_op jit(solution)/shard_map/ppermute | solution.py:164
  322.2 184.5 %collective-permute-start.4 = (bf16[512,4096]{1,0:T(8,128)(2,1)}, bf16[512,4096]{1,0:T(8,128)(2,1)S(1)}, u32[]{:S(2)}, u32[]{:S(2)}) collective-permute-start(bf16[512,4096]{1,0:T(8,128)(2,1)} %param.14), channel_id=1, source_target_pairs={{8,24},{16,0},{9,25},{17,1},{10,26},{18,2},{11,27},{19,3},{12,28},... | collective-permute-start | bytes 12582920 | tf_op jit(solution)/shard_map/ppermute | solution.py:162
  510.4 124.6 %collective-permute-start.7 = (bf16[512,4096]{1,0:T(8,128)(2,1)S(1)}, bf16[512,4096]{1,0:T(8,128)(2,1)S(1)}, u32[]{:S(2)}, u32[]{:S(2)}) collective-permute-start(bf16[512,4096]{1,0:T(8,128)(2,1)S(1)} %add.88), channel_id=1, source_target_pairs={{0,8},{8,0},{16,24},{24,16},{1,9},{9,1},{17,25},{25,17},{2,10},{10... | collective-permute-start | bytes 12582920 | tf_op jit(solution)/shard_map/ppermute | solution.py:181
  512.1 89.7 %collective-permute-start = (f32[4,512]{1,0:T(4,128)S(1)}, f32[4,512]{1,0:T(4,128)S(1)}, u32[]{:S(2)}, u32[]{:S(2)}) collective-permute-start(f32[4,512]{1,0:T(4,128)S(1)} %pad_maximum_fusion), channel_id=1, source_target_pairs={{0,16},{24,8},{1,17},{25,9},{2,18},{26,10},{3,19},{27,11},{4,20},{... | collective-permute-start | bytes 24584 | tf_op jit(solution)/shard_map/ppermute | solution.py:160
  601.7 6.4 collective-permute-start.1
  608.2 3.7 collective-permute-start.2
  609.3 93.8 %collective-permute-start.8 = (bf16[512,4096]{1,0:T(8,128)(2,1)}, bf16[512,4096]{1,0:T(8,128)(2,1)}, u32[]{:S(2)}, u32[]{:S(2)}) collective-permute-start(bf16[512,4096]{1,0:T(8,128)(2,1)} %add.89), channel_id=1, source_target_pairs={{0,8},{8,0},{16,24},{24,16},{1,9},{9,1},{17,25},{25,17},{2,10},{10... | collective-permute-start | bytes 12582920 | tf_op jit(solution)/shard_map/ppermute | solution.py:180
  634.6 338.1 %collective-permute-start.10 = (bf16[1536,4096]{1,0:T(8,128)(2,1)}, bf16[1536,4096]{1,0:T(8,128)(2,1)}, u32[]{:S(2)}, u32[]{:S(2)}) collective-permute-start(bf16[1536,4096]{1,0:T(8,128)(2,1)} %bitcast.1.refs_3_), channel_id=1, source_target_pairs={{0,8},{8,0},{16,24},{24,16},{1,9},{9,1},{17,25},{25,17},{2,10},{10... | collective-permute-start | bytes 37748744 | tf_op jit(solution)/shard_map/ppermute | solution.py:168
  644.7 189.0 %all-to-all-start.3 = ((bf16[8,192,4096]{2,1,0:T(8,128)(2,1)}), bf16[8,192,4096]{2,1,0:T(8,128)(2,1)}, u32[]{:S(2)}, u32[]{:S(2)}) async-start(bf16[8,192,4096]{2,1,0:T(8,128)(2,1)} %bitcast.120), calls=%async_computation.3 | async-start | bytes 25165824 | tf_op jit(solution)/shard_map/all_to_all | solution.py:150
  714.8 526.5 %collective-permute-start.9 = (bf16[1536,4096]{1,0:T(8,128)(2,1)}, bf16[1536,4096]{1,0:T(8,128)(2,1)}, u32[]{:S(2)}, u32[]{:S(2)}) collective-permute-start(bf16[1536,4096]{1,0:T(8,128)(2,1)} %bitcast.8.q_ref.refs_4_), channel_id=1, source_target_pairs={{0,8},{8,0},{16,24},{24,16},{1,9},{9,1},{17,25},{25,17},{2,10},{10... | collective-permute-start | bytes 37748744 | tf_op jit(solution)/shard_map/ppermute | solution.py:182
  833.7 201.9 %all-to-all-start.4 = ((bf16[8,192,4096]{2,1,0:T(8,128)(2,1)}), bf16[8,192,4096]{2,1,0:T(8,128)(2,1)}, u32[]{:S(2)}, u32[]{:S(2)}) async-start(bf16[8,192,4096]{2,1,0:T(8,128)(2,1)} %bitcast.119), calls=%async_computation.4 | async-start | bytes 25165824 | tf_op jit(solution)/shard_map/all_to_all | solution.py:150
  998.0 25.7 %copy-start.51 = (s32[512]{0:T(512)S(1)}, s32[512]{0:T(512)}, u32[]{:S(2)}) copy-start(s32[512]{0:T(512)} %copy-done.50) | copy-start | bytes 6148
  1035.6 5.5 copy-start.37
  1035.6 5.5 copy-start.48
  1035.6 286.3 %all-to-all-start.5 = ((bf16[8,192,4096]{2,1,0:T(8,128)(2,1)}), bf16[8,192,4096]{2,1,0:T(8,128)(2,1)}, u32[]{:S(2)}, u32[]{:S(2)}) async-start(bf16[8,192,4096]{2,1,0:T(8,128)(2,1)} %bitcast.118), calls=%async_computation.5 | async-start | bytes 25165824 | tf_op jit(solution)/shard_map/all_to_all | solution.py:150
  1041.0 21.4 %copy-start.7 = (f32[512,8]{0,1:T(8,128)S(1)}, f32[512,8]{0,1:T(8,128)}, u32[]{:S(2)}) copy-start(f32[512,8]{0,1:T(8,128)} %copy-done.6) | copy-start | bytes 49156
  1041.0 21.4 %copy-start.12 = (pred[512,8]{0,1:T(8,128)(4,1)S(1)}, pred[512,8]{0,1:T(8,128)(4,1)}, u32[]{:S(2)}) copy-start(pred[512,8]{0,1:T(8,128)(4,1)} %copy-done.11) | copy-start | bytes 12292
  1041.0 21.3 %copy-start.15 = (s32[512]{0:T(512)S(1)}, s32[512]{0:T(512)}, u32[]{:S(2)}) copy-start(s32[512]{0:T(512)} %param.15) | copy-start | bytes 6148
  1041.0 21.3 %copy-start.18 = (f32[512]{0:T(512)S(1)}, f32[512]{0:T(512)}, u32[]{:S(2)}) copy-start(f32[512]{0:T(512)} %copy-done.17) | copy-start | bytes 6148
  1041.0 21.3 %copy-start.21 = (f32[512]{0:T(512)S(1)}, f32[512]{0:T(512)}, u32[]{:S(2)}) copy-start(f32[512]{0:T(512)} %copy-done.20) | copy-start | bytes 6148
  1041.0 21.3 %copy-start.26 = (f32[512]{0:T(512)S(1)}, f32[512]{0:T(512)}, u32[]{:S(2)}) copy-start(f32[512]{0:T(512)} %copy-done.25) | copy-start | bytes 6148
  1041.0 21.3 %copy-start.29 = (f32[512]{0:T(512)S(1)}, f32[512]{0:T(512)}, u32[]{:S(2)}) copy-start(f32[512]{0:T(512)} %copy-done.28) | copy-start | bytes 6148
  1041.0 21.3 %copy-start.32 = (s32[512]{0:T(512)S(1)}, s32[512]{0:T(512)}, u32[]{:S(2)}) copy-start(s32[512]{0:T(512)} %param.16) | copy-start | bytes 6148
  1041.1 659.2 %all-reduce.3.cloned.1.call-start = ((), (), s32[]{:S(2)}) async-start(), calls=%async_computation.8 | async-start | bytes 262144 | tf_op jit(solution)/shard_map/psum | solution.py:214
  1041.1 21.3 %copy-start.4 = (bf16[512,4096]{1,0:T(8,128)(2,1)S(1)}, bf16[512,4096]{1,0:T(8,128)(2,1)}, u32[]{:S(2)}) copy-start(bf16[512,4096]{1,0:T(8,128)(2,1)} %copy-done.3) | copy-start | bytes 12582916
  1321.9 166.8 %all-to-all-start.6 = ((bf16[8,192,4096]{2,1,0:T(8,128)(2,1)}), bf16[8,192,4096]{2,1,0:T(8,128)(2,1)}, u32[]{:S(2)}, u32[]{:S(2)}) async-start(bf16[8,192,4096]{2,1,0:T(8,128)(2,1)} %bitcast.115), calls=%async_computation.6 | async-start | bytes 25165824 | tf_op jit(solution)/shard_map/all_to_all | solution.py:150
  1488.6 31.2 %slice-start = ((s8[11272192]{0:T(1024)(128)(4,1)}), s8[2883584]{0:T(1024)(128)(4,1)S(1)}, s32[]{:S(2)}) async-start(s8[11272192]{0:T(1024)(128)(4,1)} %bitcast.143), calls=%async_computation.9 | async-start | bytes 5767168
  1488.6 148.9 %all-to-all-start.7 = ((bf16[8,192,4096]{2,1,0:T(8,128)(2,1)}), bf16[8,192,4096]{2,1,0:T(8,128)(2,1)}, u32[]{:S(2)}, u32[]{:S(2)}) async-start(bf16[8,192,4096]{2,1,0:T(8,128)(2,1)} %bitcast.116), calls=%async_computation.7 | async-start | bytes 25165824 | tf_op jit(solution)/shard_map/all_to_all | solution.py:150
  1494.4 25.4 %slice-start.1 = ((s8[11272192]{0:T(1024)(128)(4,1)}), s8[4194304]{0:T(1024)(128)(4,1)S(1)}, s32[]{:S(2)}) async-start(s8[11272192]{0:T(1024)(128)(4,1)} %bitcast.143), calls=%async_computation.10 | async-start | bytes 8388608
  1494.5 25.4 %slice-start.2 = ((s8[11272192]{0:T(1024)(128)(4,1)}), s8[4194304]{0:T(1024)(128)(4,1)S(1)}, s32[]{:S(2)}) async-start(s8[11272192]{0:T(1024)(128)(4,1)} %bitcast.143), calls=%async_computation.11 | async-start | bytes 8388608
  1572.0 65.5 %copy-start.49 = (s32[512]{0:T(512)S(1)}, s32[512]{0:T(512)}, u32[]{:S(2)}) copy-start(s32[512]{0:T(512)} %copy-done.47) | copy-start | bytes 6148
  1572.0 65.6 %copy-start.52 = (s32[512]{0:T(512)S(1)}, s32[512]{0:T(512)}, u32[]{:S(2)}) copy-start(s32[512]{0:T(512)} %copy-done.50) | copy-start | bytes 6148
  1637.5 10.4 copy-start.2
  1637.5 10.4 copy-start.8
  1637.5 10.4 copy-start.10
  1637.6 10.4 copy-start.13
  1637.6 10.4 copy-start.16
  1637.6 10.4 copy-start.19
  1637.6 10.4 copy-start.22
  1637.6 10.4 copy-start.24
  1637.6 10.4 copy-start.27
  1637.6 10.4 copy-start.30
  1637.6 10.4 copy-start.33
  1637.6 10.4 copy-start.39
  1637.7 10.4 copy-start.42
  1637.7 10.4 copy-start.44
  (15 other events, 29.3 us)
Sparse Core Ops, SparseCore 0:
  1063.9 170.3 all-reduce.2

commit v3 on v2

--- a/solution.py
+++ b/solution.py
@@ -99,6 +99,55 @@
     )(u_t, da_t, db_t, h, q, *acc)
 
 
+def sum_kernel(n_dp, n_ep, x_ref, out_ref, parts, total, send_one, recv_one, send_two, recv_two):
+    n_dev = n_dp * n_ep
+    me = lax.axis_index('dp') * n_ep + lax.axis_index('ep')
+
+    def peer(step):
+        index = lax.rem(me + step, n_dev)
+        return index, (lax.div(index, n_ep), lax.rem(index, n_ep))
+
+    scatter = []
+    for step in range(1, n_dev):
+        index, device = peer(step)
+        scatter.append(pltpu.make_async_remote_copy(
+            src_ref=x_ref.at[index], dst_ref=parts.at[step], send_sem=send_one.at[step], recv_sem=recv_one.at[step],
+            device_id=device, device_id_type=pl.DeviceIdType.MESH))
+        scatter[-1].start()
+    acc = x_ref[me]
+    for step in range(1, n_dev):
+        scatter[step - 1].wait_recv()
+        acc += parts[step]
+    total[...] = acc
+    out_ref[me] = acc
+    for copy in scatter:
+        copy.wait_send()
+    gather = []
+    for step in range(1, n_dev):
+        index, device = peer(step)
+        gather.append(pltpu.make_async_remote_copy(
+            src_ref=total, dst_ref=out_ref.at[me], send_sem=send_two.at[step], recv_sem=recv_two.at[step],
+            device_id=device, device_id_type=pl.DeviceIdType.MESH))
+        gather[-1].start()
+    for copy in gather:
+        copy.wait_recv()
+    for copy in gather:
+        copy.wait_send()
+
+
+def sum_all(x, n_dp, n_ep):
+    n_dev = n_dp * n_ep
+    vmem = pl.BlockSpec(memory_space=pltpu.VMEM)
+    dma = pltpu.SemaphoreType.DMA((n_dev,))
+    return pl.pallas_call(
+        functools.partial(sum_kernel, n_dp, n_ep),
+        out_shape=jax.ShapeDtypeStruct(x.shape, f32),
+        in_specs=[vmem], out_specs=vmem,
+        scratch_shapes=[pltpu.VMEM(x.shape, f32), pltpu.VMEM(x.shape[1:], f32), dma, dma, dma, dma],
+        compiler_params=pltpu.CompilerParams(has_side_effects=True),
+    )(x)
+
+
 def after(value, *deps):
     return lax.optimization_barrier((value,) + deps)[0]
 
@@ -156,40 +205,37 @@
         own_meta = jnp.stack([pos_one.astype(f32), pos_two.astype(f32)])
         h_buf = select_h(hidden, own_meta)
         h_own = swap(h_buf)
+        m_f1 = lax.ppermute(meta, 'dp', outer + middle)
+        h_f1 = lax.ppermute(hidden, 'dp', outer + middle)
         dy_a = lax.ppermute(tok_dy, 'dp', outer)
-        m_a = lax.ppermute(meta, 'dp', outer)
-        h_a = lax.ppermute(after(hidden, meta), 'dp', outer)
         dy_b = lax.ppermute(after(tok_dy, dy_a), 'dp', middle)
-        m_b = lax.ppermute(after(meta, m_a), 'dp', middle)
-        h_b = lax.ppermute(after(hidden, h_a), 'dp', middle)
-
         q_buf = select_q(tok_dy, meta)
         q_own = swap(after(q_buf, h_own))
-        h_near = lax.ppermute(h_own, 'dp', near)
         a_t, b_t = pre(h_own)
         u_t = (a_t * jax.nn.sigmoid(a_t) * b_t).astype(bf16)
         exp_out = jnp.einsum('fr,fd->rd', u_t, wd, preferred_element_type=f32).astype(bf16)
-        out_back = swap(after(exp_out, q_own))
         u_t, da_t, db_t = inner_grad(q_own, wd, a_t, b_t)
         grad_hid = (jnp.einsum('fr,fd->rd', da_t, wg_t, preferred_element_type=f32)
                     + jnp.einsum('fr,fd->rd', db_t, wu_t, preferred_element_type=f32)).astype(bf16)
         acc = add_dw(None, u_t, da_t, db_t, h_own, q_own)
 
-        h_f1, dy_f1, m_f1 = h_a + h_b, dy_a + dy_b, m_a + m_b
+        dy_f1 = dy_a + dy_b
         m_f2 = lax.ppermute(m_f1, 'dp', near)
-        h_f2 = lax.ppermute(after(h_f1, m_f1), 'dp', near)
-        dy_f2 = lax.ppermute(after(dy_f1, h_f1), 'dp', near)
+        h_f2 = lax.ppermute(h_f1, 'dp', near)
+        dy_f2 = lax.ppermute(dy_f1, 'dp', near)
+        h_near = lax.ppermute(h_own, 'dp', near)
         q_near = lax.ppermute(q_own, 'dp', near)
         h_b1 = select_h(h_f1, m_f1)
         q_b1 = select_q(dy_f1, m_f1)
         h_b2 = select_h(h_f2, m_f2)
         q_b2 = select_q(dy_f2, m_f2)
-        h_r1 = swap(after(h_b1, out_back))
+        h_r1 = swap(after(h_b1, q_own))
         q_r1 = swap(after(q_b1, h_r1))
         h_r2 = swap(after(h_b2, q_r1))
         q_r2 = swap(after(q_b2, h_r2))
-        hid_back = swap(after(grad_hid, q_r2))
-        for h, q in ((h_r1, q_r1), (h_near, q_near), (h_r2, q_r2)):
+        out_back = swap(after(exp_out, q_r2))
+        hid_back = swap(after(grad_hid, out_back))
+        for h, q in ((h_r1, q_r1), (h_r2, q_r2), (h_near, q_near)):
             a_t, b_t = pre(h)
             u_t, da_t, db_t = inner_grad(q, wd, a_t, b_t)
             acc = add_dw(acc, u_t, da_t, db_t, h, q)
@@ -205,15 +251,17 @@
         dgate_two = jnp.sum(dy_float * out_two, axis=-1)
         d_logits = ((dgate_one * gate_one)[:, None] * (pick_one - prob_one)
                     + (dgate_two * gate_two)[:, None] * (pick_two - prob_two)).astype(bf16)
-        d_router = jnp.einsum('td,te->de', hidden, d_logits, preferred_element_type=f32)
+        d_router = jnp.einsum('td,te->ed', hidden, d_logits, preferred_element_type=f32)
         grad_exp = jnp.dot(sel_one + sel_two, hid_back, preferred_element_type=f32)
         grad_h = jnp.einsum('te,de->td', d_logits, router, preferred_element_type=f32) + grad_exp
         d_ln_weight = jnp.sum(grad_h * x_hat, axis=0)
         d_ln_bias = jnp.sum(grad_h, axis=0)
         dx_tok = (dy_float + layer_norm_back(grad_h, x_hat, inv_std, ln_weight)).astype(bf16)
-        d_router = lax.psum(d_router, ('dp', 'ep'))
-        d_ln_weight = lax.psum(d_ln_weight, ('dp', 'ep'))
-        d_ln_bias = lax.psum(d_ln_bias, ('dp', 'ep'))
+        n_dev = n_dp * n_ep
+        parts = jnp.concatenate([d_router, d_ln_weight[None], d_ln_bias[None], jnp.zeros((6, d_model), f32)])
+        total = sum_all(parts.reshape(16, n_dev, d_model // n_dev).transpose(1, 0, 2), n_dp, n_ep)
+        total = total.transpose(1, 0, 2).reshape(16, d_model)
+        d_router, d_ln_weight, d_ln_bias = total[:n_exp].T, total[n_exp], total[n_exp + 1]
         return (out_tok, dx_tok, dwg.T[None], dwu.T[None], dwd[None], d_router, d_ln_weight, d_ln_bias)
 
     return jax.shard_map(

time: 1720 us -> 1570 us (0.913)
  waiting for transfers between devices: 776 us -> 672 us
  blocking collectives: 42.3 us -> 0 us
  Pallas kernels: 378 us -> 401 us
    ppermute x1, waiting for transfers between devices: 104 us -> 0.01 us  [local_step(): h_near = lax.ppermute(h_own, 'dp', near)]
    all_to_all x8, waiting for transfers between devices: 173 us -> 269 us  [swap(): lax.all_to_all(buf.reshape(n_ep, slot_cap, d_model), 'ep', 0, 0, tiled=True)]
    ppermute x1, waiting for transfers between devices: 0.92 us -> 85.1 us  [local_step(): m_f2 = lax.ppermute(m_f1, 'dp', near)]
    ppermute x1, waiting for transfers between devices: 83.6 us -> 0.01 us  [local_step(): dy_b = lax.ppermute(after(tok_dy, dy_a), 'dp', middle)]
    ppermute x1, waiting for transfers between devices: 177 us -> 98.7 us  [local_step(): q_near = lax.ppermute(q_own, 'dp', near)]
    psum x1 -> x0, blocking collectives: 42.3 us -> none  [local_step(): d_ln_weight = lax.psum(d_ln_weight, ('dp', 'ep'))]
    pallas_call x0 -> x1, Pallas kernels: none -> 22.4 us  [sum_all(): pl.pallas_call(functools.partial(sum_kernel, n_dp, n_ep), out_shape=jax.S...]
    ppermute x6 -> x4, waiting for transfers between devices: 236 us -> 219 us  [the longest x1 132 us: local_step(): h_f1 = lax.ppermute(hidden, 'dp', outer + middle)]
  transfers between devices with their start and end apart: 20 -> 17, of which waited for: 10 -> 8; matrix products, arithmetic and copies ran while one was open for 24% -> 24% of each run, Pallas kernels for 22% -> 24%
where the time goes in v3:
time: 1570 us; the launch traced here: 1560 us
  waiting for transfers between devices  672 us (43%)
  Pallas kernels  401 us (26%)
  matrix products  397 us (25%)
  starting transfers between devices  61.9 us (4%)
  other arithmetic  26.8 us (2%)
    all_to_all x8, waiting for transfers between devices, swap(): lax.all_to_all(buf.reshape(n_ep, slot_cap, d_model), 'ep', 0, 0, tiled=True)  269 us
    pallas_call x4, Pallas kernels, add_dw(): pl.pallas_call(functools.partial(dw_kernel, first), grid=(d_model // d_ti...  258 us
    ppermute x1, waiting for transfers between devices, local_step(): h_f1 = lax.ppermute(hidden, 'dp', outer + middle)  132 us
    pallas_call x4, Pallas kernels, inner_grad(): pl.pallas_call(grad_kernel, grid=(2, 3), in_specs=[pl.BlockSpec((r_tile,...  120 us
    dot_general x4, matrix products, pre(): jnp.einsum('fd,rd->fr', wg_t, h, preferred_element_type=f32)  99.5 us
    ppermute x1, waiting for transfers between devices, local_step(): q_near = lax.ppermute(q_own, 'dp', near)  98.7 us
    dot_general x4, matrix products, pre(): jnp.einsum('fd,rd->fr', wu_t, h, preferred_element_type=f32)  98.1 us
    ppermute x1, waiting for transfers between devices, local_step(): m_f1 = lax.ppermute(meta, 'dp', outer + middle)  86.9 us
  transfers between devices with their start and end apart: 17, of which 8 were waited for; matrix products, arithmetic and copies ran while one was open for 24% of the time, Pallas kernels for 24%

profile of v3, /device:TPU:0, one launch (start us, length us, event | category | flops | bytes accessed | tf_op | source)
XLA Modules:
  0.0 1564.8 jit_solution(9437062741994581205)
XLA Ops:
  0.7 3.0 convert_reduce_fusion
  3.7 3.4 fusion.55
  7.3 2.3 fusion.50
  9.6 9.6 convolution_convert_fusion.3
  19.3 5.5 all-to-all-start
  24.8 8.0 collective-permute-start.2
  32.8 3.4 fusion.101
  36.9 0.7 add_reduce_fusion
  37.6 11.8 multiply_convert_fusion
  49.4 115.0 %all-to-all-done = bf16[8,192,4096]{2,1,0:T(8,128)(2,1)} async-done(((bf16[8,192,4096]{2,1,0:T(8,128)(2,1)}), bf16[8,192,4096]{2,1,0:T(8,128)(2,1)}, u32[]{:S(2)}, u32[]{:S(2)}) %all-to-all-start) | async-done | bytes 12582944 | tf_op jit(solution)/shard_map/all_to_all | solution.py:199
  164.4 5.5 all-to-all-start.1
  170.0 1.3 collective-permute-start.3
  171.3 131.8 %collective-permute-done.5 = bf16[512,4096]{1,0:T(8,128)(2,1)} collective-permute-done((bf16[512,4096]{1,0:T(8,128)(2,1)}, bf16[512,4096]{1,0:T(8,128)(2,1)}, u32[]{:S(2)}, u32[]{:S(2)}) %collective-permute-start.5) | collective-permute-done | bytes 4194336 | tf_op jit(solution)/shard_map/ppermute | solution.py:209
  303.1 3.1 collective-permute-start
  306.9 86.9 %collective-permute-done = f32[4,512]{1,0:T(4,128)S(1)} collective-permute-done((f32[4,512]{1,0:T(4,128)S(1)}, f32[4,512]{1,0:T(4,128)S(1)}, u32[]{:S(2)}, u32[]{:S(2)}) %collective-permute-start) | collective-permute-done | bytes 8224 | tf_op jit(solution)/shard_map/ppermute | solution.py:208
  393.7 3.5 collective-permute-start.1
  397.2 0.7 add_reduce_fusion.1
  397.9 85.1 %collective-permute-done.1 = f32[4,512]{1,0:T(4,128)S(1)} collective-permute-done((f32[4,512]{1,0:T(4,128)S(1)}, f32[4,512]{1,0:T(4,128)S(1)}, u32[]{:S(2)}, u32[]{:S(2)}) %collective-permute-start.1) | collective-permute-done | bytes 8224 | tf_op jit(solution)/shard_map/ppermute | solution.py:223
  483.0 0.7 add_reduce_fusion.2
  483.7 11.8 convolution_convert_fusion.1
  495.5 5.7 add.69
  501.3 9.5 convolution_convert_fusion.2
  510.8 11.9 multiply_convert_fusion.1
  522.7 2.0 collective-permute-start.8
  524.7 23.4 %fusion.25.a_ref = f32[1376,1536]{1,0:T(8,128)} fusion(bf16[1536,4096]{1,0:T(8,128)(2,1)} %bitcast.1.refs_3_, bf16[1,4096,1376]{1,2,0:T(8,128)(2,1)S(1)} %bitcast.163), kind=kOutput, calls=%fused_computation.39 | convolution fusion | flops 17314086912 | bytes 32309248 | tf_op jit(solution)/shard_map/fd,rd->fr/dot_general | solution.py:202
  548.1 5.3 all-to-all-start.2
  553.5 25.3 %fusion.37.b_ref = f32[1376,1536]{1,0:T(8,128)} fusion(bf16[1536,4096]{1,0:T(8,128)(2,1)} %bitcast.1.refs_3_, bf16[1,4096,1376]{1,2,0:T(8,128)(2,1)} %param.24), kind=kOutput, calls=%fused_computation.43 | convolution fusion | flops 17314086912 | bytes 32309248 | tf_op jit(solution)/shard_map/fd,rd->fr/dot_general | solution.py:203
  578.8 28.0 %convolution_convert_fusion = bf16[1536,4096]{1,0:T(8,128)(2,1)} fusion(f32[1376,1536]{1,0:T(8,128)} %fusion.37.b_ref, f32[1376,1536]{1,0:T(8,128)S(1)} %copy-done.43, bf16[1,1376,4096]{2,1,0:T(8,128)(2,1)} %param.25), kind=kOutput, calls=%fused_computation.4 | convolution fusion | flops 17333059584 | bytes 40763392 | tf_op jit(solution)/shard_map/fr,fd->rd/dot_general | solution.py:216
  606.8 85.6 %all-to-all-done.2 = bf16[8,192,4096]{2,1,0:T(8,128)(2,1)} async-done(((bf16[8,192,4096]{2,1,0:T(8,128)(2,1)}), bf16[8,192,4096]{2,1,0:T(8,128)(2,1)}, u32[]{:S(2)}, u32[]{:S(2)}) %all-to-all-start.2) | async-done | bytes 12582944 | tf_op jit(solution)/shard_map/all_to_all | solution.py:199
  692.5 5.5 all-to-all-start.3
  698.0 11.8 multiply_convert_fusion.2
  709.8 29.9 %shard_map.188 = (bf16[1376,1536]{1,0:T(8,128)(2,1)}, bf16[1376,1536]{1,0:T(8,128)(2,1)}, bf16[1376,1536]{1,0:T(8,128)(2,1)}) custom-call(bf16[1536,4096]{1,0:T(8,128)(2,1)} %bitcast.20.q_ref.refs_4_, bf16[1376,4096]{1,0:T(8,128)(2,1)} %bitcast.166, f32[1376,1536]{1,0:T(8,128)} %fusion.25.a_ref, f32[1376,1536]{1,0:T(8,128)} %fusion.37.b_ref), custom_call_target="tpu_custom_call" | custom-call | flops 17314086912 | bytes 54755328 | tf_op jit(solution)/shard_map/pallas_call | solution.py:57
  739.7 26.2 %fusion.15 = f32[1536,4096]{1,0:T(8,128)} fusion(bf16[1376,1536]{1,0:T(8,128)(2,1)} %get-tuple-element.47.refs_1_, bf16[1,4096,1376]{1,2,0:T(8,128)(2,1)} %param.23), kind=kOutput, calls=%fused_computation.29 | convolution fusion | flops 17314086912 | bytes 40665088 | tf_op jit(solution)/shard_map/fr,fd->rd/dot_general | solution.py:218
  765.9 61.3 %shard_map.192 = (f32[1376,4096]{1,0:T(8,128)}, f32[1376,4096]{1,0:T(8,128)}, f32[1376,4096]{1,0:T(8,128)}) custom-call(bf16[1376,1536]{1,0:T(8,128)(2,1)} %get-tuple-element.59.refs_0_, bf16[1376,1536]{1,0:T(8,128)(2,1)} %get-tuple-element.47.refs_1_, bf16[1376,1536]{1,0:T(8,128)(2,1)} %get-tuple-element.48.refs_2_, bf16[1536,4096]{1,0:T(8,128)(2,1)} %bitcast.1.refs_3_, ...), custom_call_target="tpu_custom_call" | custom-call | flops 51942260736 | bytes 92798976 | tf_op jit(solution)/shard_map/pallas_call | solution.py:89
  827.1 9.8 all-to-all-done.3
  837.0 5.7 all-to-all-start.4
  842.7 29.5 %add_convert_fusion = bf16[1536,4096]{1,0:T(8,128)(2,1)} fusion(f32[1536,4096]{1,0:T(8,128)} %fusion.15, bf16[1376,1536]{1,0:T(8,128)(2,1)} %get-tuple-element.48.refs_2_, bf16[1,4096,1376]{1,2,0:T(8,128)(2,1)} %param.24), kind=kOutput, calls=%fused_computation | convolution fusion | flops 17326669824 | bytes 53248000 | tf_op jit(solution)/shard_map/fr,fd->rd/dot_general | solution.py:219
  872.2 25.3 %fusion.28.a_ref = f32[1376,1536]{1,0:T(8,128)} fusion(bf16[1536,4096]{1,0:T(8,128)(2,1)} %collective-permute-done.8.refs_3_, bf16[1,4096,1376]{1,2,0:T(8,128)(2,1)} %param.23), kind=kOutput, calls=%fused_computation.40 | convolution fusion | flops 17314086912 | bytes 32309248 | tf_op jit(solution)/shard_map/fd,rd->fr/dot_general | solution.py:202
  897.5 25.5 %fusion.40.b_ref = f32[1376,1536]{1,0:T(8,128)} fusion(bf16[1536,4096]{1,0:T(8,128)(2,1)} %collective-permute-done.8.refs_3_, bf16[1,4096,1376]{1,2,0:T(8,128)(2,1)} %param.24), kind=kOutput, calls=%fused_computation.44 | convolution fusion | flops 17314086912 | bytes 32309248 | tf_op jit(solution)/shard_map/fd,rd->fr/dot_general | solution.py:203
  922.9 58.7 %all-to-all-done.4 = bf16[8,192,4096]{2,1,0:T(8,128)(2,1)} async-done(((bf16[8,192,4096]{2,1,0:T(8,128)(2,1)}), bf16[8,192,4096]{2,1,0:T(8,128)(2,1)}, u32[]{:S(2)}, u32[]{:S(2)}) %all-to-all-start.4) | async-done | bytes 12582944 | tf_op jit(solution)/shard_map/all_to_all | solution.py:199
  981.7 5.6 all-to-all-start.5
  987.3 25.4 %fusion.34.a_ref = f32[1376,1536]{1,0:T(8,128)} fusion(bf16[1536,4096]{1,0:T(8,128)(2,1)} %bitcast.22.refs_3_, bf16[1,4096,1376]{1,2,0:T(8,128)(2,1)} %param.23), kind=kOutput, calls=%fused_computation.42 | convolution fusion | flops 17314086912 | bytes 32309248 | tf_op jit(solution)/shard_map/fd,rd->fr/dot_general | solution.py:202
  1012.7 21.9 %fusion.46.b_ref = f32[1376,1536]{1,0:T(8,128)} fusion(bf16[1536,4096]{1,0:T(8,128)(2,1)} %bitcast.22.refs_3_, bf16[1,4096,1376]{1,2,0:T(8,128)(2,1)S(1)} %bitcast.165), kind=kOutput, calls=%fused_computation.46 | convolution fusion | flops 17314086912 | bytes 32309248 | tf_op jit(solution)/shard_map/fd,rd->fr/dot_general | solution.py:203
  1034.7 98.7 %collective-permute-done.7.q_ref.refs_4_ = bf16[1536,4096]{1,0:T(8,128)(2,1)} collective-permute-done((bf16[1536,4096]{1,0:T(8,128)(2,1)}, bf16[1536,4096]{1,0:T(8,128)(2,1)}, u32[]{:S(2)}, u32[]{:S(2)}) %collective-permute-start.7) | collective-permute-done | bytes 12582944 | tf_op jit(solution)/shard_map/ppermute | solution.py:227
  1133.4 30.4 %shard_map.189 = (bf16[1376,1536]{1,0:T(8,128)(2,1)}, bf16[1376,1536]{1,0:T(8,128)(2,1)}, bf16[1376,1536]{1,0:T(8,128)(2,1)}) custom-call(bf16[1536,4096]{1,0:T(8,128)(2,1)} %collective-permute-done.7.q_ref.refs_4_, bf16[1376,4096]{1,0:T(8,128)(2,1)} %bitcast.167, f32[1376,1536]{1,0:T(8,128)} %fusion.28.a_ref, f32[1376,1536]{1,0:T(8,128)} %fusion.40.b_ref), custom_call_target="tpu_custom_call" | custom-call | flops 17314086912 | bytes 54755328 | tf_op jit(solution)/shard_map/pallas_call | solution.py:57
  1163.8 30.0 %shard_map.191 = (bf16[1376,1536]{1,0:T(8,128)(2,1)}, bf16[1376,1536]{1,0:T(8,128)(2,1)}, bf16[1376,1536]{1,0:T(8,128)(2,1)}) custom-call(bf16[1536,4096]{1,0:T(8,128)(2,1)} %bitcast.24.q_ref.refs_4_, bf16[1376,4096]{1,0:T(8,128)(2,1)} %bitcast.168, f32[1376,1536]{1,0:T(8,128)} %fusion.34.a_ref, f32[1376,1536]{1,0:T(8,128)} %fusion.46.b_ref), custom_call_target="tpu_custom_call" | custom-call | flops 17314086912 | bytes 54755328 | tf_op jit(solution)/shard_map/pallas_call | solution.py:57
  1193.8 5.3 all-to-all-start.6
  1199.2 65.5 %shard_map.193 = (f32[1376,4096]{1,0:T(8,128)}, f32[1376,4096]{1,0:T(8,128)}, f32[1376,4096]{1,0:T(8,128)}) custom-call(bf16[1376,1536]{1,0:T(8,128)(2,1)} %get-tuple-element.56.refs_0_, bf16[1376,1536]{1,0:T(8,128)(2,1)} %get-tuple-element.57.refs_1_, ...), custom_call_target="tpu_custom_call", output_to_operand_aliasing={{0}: (5, {}), {1}: (6, {}), {2}: (7, {})} | custom-call | flops 51942260736 | bytes 160432128 | tf_op jit(solution)/shard_map/pallas_call | solution.py:89
  1264.7 25.4 %fusion.31.a_ref = f32[1376,1536]{1,0:T(8,128)} fusion(bf16[1536,4096]{1,0:T(8,128)(2,1)} %bitcast.26.refs_3_, bf16[1,4096,1376]{1,2,0:T(8,128)(2,1)} %param.23), kind=kOutput, calls=%fused_computation.41 | convolution fusion | flops 17314086912 | bytes 32309248 | tf_op jit(solution)/shard_map/fd,rd->fr/dot_general | solution.py:202
  1290.1 25.4 %fusion.43.b_ref = f32[1376,1536]{1,0:T(8,128)} fusion(bf16[1536,4096]{1,0:T(8,128)(2,1)} %bitcast.26.refs_3_, bf16[1,4096,1376]{1,2,0:T(8,128)(2,1)} %param.24), kind=kOutput, calls=%fused_computation.45 | convolution fusion | flops 17314086912 | bytes 32309248 | tf_op jit(solution)/shard_map/fd,rd->fr/dot_general | solution.py:203
  1315.5 29.9 %shard_map.190 = (bf16[1376,1536]{1,0:T(8,128)(2,1)}, bf16[1376,1536]{1,0:T(8,128)(2,1)}, bf16[1376,1536]{1,0:T(8,128)(2,1)}) custom-call(bf16[1536,4096]{1,0:T(8,128)(2,1)} %bitcast.28.q_ref.refs_4_, bf16[1376,4096]{1,0:T(8,128)(2,1)} %bitcast.169, f32[1376,1536]{1,0:T(8,128)} %fusion.31.a_ref, f32[1376,1536]{1,0:T(8,128)} %fusion.43.b_ref), custom_call_target="tpu_custom_call" | custom-call | flops 17314086912 | bytes 54755328 | tf_op jit(solution)/shard_map/pallas_call | solution.py:57
  1345.4 5.5 all-to-all-start.7
  1350.9 65.5 %shard_map.194 = (f32[1376,4096]{1,0:T(8,128)}, f32[1376,4096]{1,0:T(8,128)}, f32[1376,4096]{1,0:T(8,128)}) custom-call(bf16[1376,1536]{1,0:T(8,128)(2,1)} %get-tuple-element.53.refs_0_, bf16[1376,1536]{1,0:T(8,128)(2,1)} %get-tuple-element.54.refs_1_, ...), custom_call_target="tpu_custom_call", output_to_operand_aliasing={{0}: (5, {}), {1}: (6, {}), {2}: (7, {})} | custom-call | flops 51942260736 | bytes 160432128 | tf_op jit(solution)/shard_map/pallas_call | solution.py:89
  1416.5 65.5 %shard_map.195 = (f32[1376,4096]{1,0:T(8,128)}, f32[1376,4096]{1,0:T(8,128)}, f32[1376,4096]{1,0:T(8,128)}) custom-call(bf16[1376,1536]{1,0:T(8,128)(2,1)} %get-tuple-element.50.refs_0_, bf16[1376,1536]{1,0:T(8,128)(2,1)} %get-tuple-element.51.refs_1_, ...), custom_call_target="tpu_custom_call", output_to_operand_aliasing={{0}: (5, {}), {1}: (6, {}), {2}: (7, {})} | custom-call | flops 51942260736 | bytes 160432128 | tf_op jit(solution)/shard_map/pallas_call | solution.py:89
  1482.0 12.2 fusion.63
  1494.4 17.2 %fusion.58 = (f32[512]{0:T(512)S(1)}, f32[512]{0:T(512)S(1)}, bf16[512,4096]{1,0:T(8,128)(2,1)}) fusion(bf16[512,4096]{1,0:T(8,128)(2,1)S(1)} %copy-done.6, f32[512,4096]{1,0:T(8,128)} %fusion.63, f32[512]{0:T(512)S(1)} %copy-done.30, f32[512]{0:T(512)S(1)} %copy-done.28, bf16[512,4096]{1,0:T(8,128)(2,1)S(1)} %copy-done.2, bf16[1536,4096]{1,0:T(8,128)(2,1)} %bitcast.30, ...), kind=kOutput, calls=%fused_computation.57 | convolution fusion | flops 6466305024 | bytes 33564672 | tf_op jit(solution)/shard_map/dot_general | solution.py:247
  1511.6 0.7 convolution_bitcast_fusion
  1512.3 10.0 fusion.76
  1522.3 6.3 fusion.54
  1528.7 0.8 maximum_bitcast_fusion.x_ref
  1529.5 22.4 %shard_map.196 = f32[32,16,128]{2,1,0:T(8,128)} custom-call(f32[32,16,128]{2,1,0:T(8,128)} %maximum_bitcast_fusion.x_ref), custom_call_target="tpu_custom_call" | custom-call | tf_op jit(solution)/shard_map/pallas_call | solution.py:142
  1551.8 1.6 slice_bitcast_fusion
  1553.4 1.6 fusion.107
  1555.0 9.3 fusion.60
  (134 shorter events, 1.7 us)
Async XLA Ops:
  0.6 32.1 %copy-start = (bf16[4096,8]{0,1:T(8,128)(2,1)S(1)}, bf16[4096,8]{0,1:T(8,128)(2,1)}, u32[]{:S(2)}) copy-start(bf16[4096,8]{0,1:T(8,128)(2,1)} %param.22) | copy-start | bytes 196612
  0.6 6.7 copy-start.1
  0.7 6.5 copy-start.34
  0.7 6.5 copy-start.35
  0.7 6.5 copy-start.13
  0.7 6.5 copy-start.40
  0.7 6.5 copy-start.25
  0.7 6.5 copy-start.41
  3.7 5.9 copy-start.19
  7.1 2.5 copy-start.31
  7.2 2.4 copy-start.9
  7.3 2.4 copy-start.36
  7.3 2.4 copy-start.38
  9.6 9.7 copy-start.4
  19.3 13.5 copy-start.33
  19.3 145.2 %all-to-all-start = ((bf16[8,192,4096]{2,1,0:T(8,128)(2,1)}), bf16[8,192,4096]{2,1,0:T(8,128)(2,1)}, u32[]{:S(2)}, u32[]{:S(2)}) async-start(bf16[8,192,4096]{2,1,0:T(8,128)(2,1)} %bitcast.135), calls=%async_computation | async-start | bytes 25165824 | tf_op jit(solution)/shard_map/all_to_all | solution.py:199
  24.8 145.2 %collective-permute-start.2 = (bf16[512,4096]{1,0:T(8,128)(2,1)}, bf16[512,4096]{1,0:T(8,128)(2,1)}, u32[]{:S(2)}, u32[]{:S(2)}) collective-permute-start(bf16[512,4096]{1,0:T(8,128)(2,1)} %param.14), channel_id=1, source_target_pairs={{0,16},{24,8},{1,17},{25,9},{2,18},{26,10},{3,19},{27,11},{4,20},{... | collective-permute-start | bytes 12582920 | tf_op jit(solution)/shard_map/ppermute | solution.py:210
  32.8 270.3 %collective-permute-start.5 = (bf16[512,4096]{1,0:T(8,128)(2,1)}, bf16[512,4096]{1,0:T(8,128)(2,1)}, u32[]{:S(2)}, u32[]{:S(2)}) collective-permute-start(bf16[512,4096]{1,0:T(8,128)(2,1)} %copy-done.4), channel_id=1, source_target_pairs={{0,16},{24,8},{8,24},{16,0},{1,17},{25,9},{9,25},{17,1},{2,18},{26... | collective-permute-start | bytes 12582920 | tf_op jit(solution)/shard_map/ppermute | solution.py:209
  36.2 0.6 copy-start.7
  36.2 0.6 copy-start.11
  36.2 0.7 copy-start.15
  36.3 266.8 %copy-start.27 = (f32[512]{0:T(512)}, f32[512]{0:T(512)S(1)}, u32[]{:S(2)}) copy-start(f32[512]{0:T(512)S(1)} %get-tuple-element.78) | copy-start | bytes 6148
  36.9 266.2 %copy-start.29 = (f32[512]{0:T(512)}, f32[512]{0:T(512)S(1)}, u32[]{:S(2)}) copy-start(f32[512]{0:T(512)S(1)} %select_reduce_fusion) | copy-start | bytes 6148
  164.4 383.7 %all-to-all-start.1 = ((bf16[8,192,4096]{2,1,0:T(8,128)(2,1)}), bf16[8,192,4096]{2,1,0:T(8,128)(2,1)}, u32[]{:S(2)}, u32[]{:S(2)}) async-start(bf16[8,192,4096]{2,1,0:T(8,128)(2,1)} %bitcast.130), calls=%async_computation.1 | async-start | bytes 25165824 | tf_op jit(solution)/shard_map/all_to_all | solution.py:199
  170.0 325.5 %collective-permute-start.3 = (bf16[512,4096]{1,0:T(8,128)(2,1)}, bf16[512,4096]{1,0:T(8,128)(2,1)S(1)}, u32[]{:S(2)}, u32[]{:S(2)}) collective-permute-start(bf16[512,4096]{1,0:T(8,128)(2,1)} %param.14), channel_id=1, source_target_pairs={{8,24},{16,0},{9,25},{17,1},{10,26},{18,2},{11,27},{19,3},{12,28},... | collective-permute-start | bytes 12582920 | tf_op jit(solution)/shard_map/ppermute | solution.py:211
  303.1 198.1 %collective-permute-start.6 = (bf16[512,4096]{1,0:T(8,128)(2,1)}, bf16[512,4096]{1,0:T(8,128)(2,1)S(1)}, u32[]{:S(2)}, u32[]{:S(2)}) collective-permute-start(bf16[512,4096]{1,0:T(8,128)(2,1)} %collective-permute-done.5), channel_id=1, source_target_pairs={{0,8},{8,0},{16,24},{24,16},{1,9},{9,1},{17,25},{25,17},{2,10},{10... | collective-permute-start | bytes 12582920 | tf_op jit(solution)/shard_map/ppermute | solution.py:224
  303.1 90.6 %collective-permute-start = (f32[4,512]{1,0:T(4,128)S(1)}, f32[4,512]{1,0:T(4,128)S(1)}, u32[]{:S(2)}, u32[]{:S(2)}) collective-permute-start(f32[4,512]{1,0:T(4,128)S(1)} %pad_maximum_fusion), channel_id=1, source_target_pairs={{0,16},{24,8},{8,24},{16,0},{1,17},{25,9},{9,25},{17,1},{2,18},{26... | collective-permute-start | bytes 24584 | tf_op jit(solution)/shard_map/ppermute | solution.py:208
  393.7 89.3 %collective-permute-start.1 = (f32[4,512]{1,0:T(4,128)S(1)}, f32[4,512]{1,0:T(4,128)S(1)}, u32[]{:S(2)}, u32[]{:S(2)}) collective-permute-start(f32[4,512]{1,0:T(4,128)S(1)} %collective-permute-done), channel_id=1, source_target_pairs={{0,8},{8,0},{16,24},{24,16},{1,9},{9,1},{17,25},{25,17},{2,10},{10... | collective-permute-start | bytes 24584 | tf_op jit(solution)/shard_map/ppermute | solution.py:223
  501.2 196.7 %collective-permute-start.4 = (bf16[512,4096]{1,0:T(8,128)(2,1)}, bf16[512,4096]{1,0:T(8,128)(2,1)}, u32[]{:S(2)}, u32[]{:S(2)}) collective-permute-start(bf16[512,4096]{1,0:T(8,128)(2,1)} %add.69), channel_id=1, source_target_pairs={{0,8},{8,0},{16,24},{24,16},{1,9},{9,1},{17,25},{25,17},{2,10},{10... | collective-permute-start | bytes 12582920 | tf_op jit(solution)/shard_map/ppermute | solution.py:225
  501.2 23.5 %slice-start = ((s8[11272192]{0:T(1024)(128)(4,1)}), s8[4194304]{0:T(1024)(128)(4,1)S(1)}, s32[]{:S(2)}) async-start(s8[11272192]{0:T(1024)(128)(4,1)} %bitcast.162), calls=%async_computation.8 | async-start | bytes 8388608
  501.2 23.5 %slice-start.1 = ((s8[11272192]{0:T(1024)(128)(4,1)}), s8[4194304]{0:T(1024)(128)(4,1)S(1)}, s32[]{:S(2)}) async-start(s8[11272192]{0:T(1024)(128)(4,1)} %bitcast.162), calls=%async_computation.9 | async-start | bytes 8388608
  510.8 13.9 slice-start.2
  522.7 349.5 %collective-permute-start.8 = (bf16[1536,4096]{1,0:T(8,128)(2,1)}, bf16[1536,4096]{1,0:T(8,128)(2,1)}, u32[]{:S(2)}, u32[]{:S(2)}) collective-permute-start(bf16[1536,4096]{1,0:T(8,128)(2,1)} %bitcast.1.refs_3_), channel_id=1, source_target_pairs={{0,8},{8,0},{16,24},{24,16},{1,9},{9,1},{17,25},{25,17},{2,10},{10... | collective-permute-start | bytes 37748744 | tf_op jit(solution)/shard_map/ppermute | solution.py:226
  548.1 144.3 %all-to-all-start.2 = ((bf16[8,192,4096]{2,1,0:T(8,128)(2,1)}), bf16[8,192,4096]{2,1,0:T(8,128)(2,1)}, u32[]{:S(2)}, u32[]{:S(2)}) async-start(bf16[8,192,4096]{2,1,0:T(8,128)(2,1)} %bitcast.134), calls=%async_computation.2 | async-start | bytes 25165824 | tf_op jit(solution)/shard_map/all_to_all | solution.py:199
  553.5 25.3 %copy-start.43 = (f32[1376,1536]{1,0:T(8,128)S(1)}, f32[1376,1536]{1,0:T(8,128)}, u32[]{:S(2)}) copy-start(f32[1376,1536]{1,0:T(8,128)} %fusion.25.a_ref) | copy-start | bytes 25362436
  692.5 144.5 %all-to-all-start.3 = ((bf16[8,192,4096]{2,1,0:T(8,128)(2,1)}), bf16[8,192,4096]{2,1,0:T(8,128)(2,1)}, u32[]{:S(2)}, u32[]{:S(2)}) async-start(bf16[8,192,4096]{2,1,0:T(8,128)(2,1)} %bitcast.133), calls=%async_computation.3 | async-start | bytes 25165824 | tf_op jit(solution)/shard_map/all_to_all | solution.py:199
  709.7 423.6 %collective-permute-start.7 = (bf16[1536,4096]{1,0:T(8,128)(2,1)}, bf16[1536,4096]{1,0:T(8,128)(2,1)}, u32[]{:S(2)}, u32[]{:S(2)}) collective-permute-start(bf16[1536,4096]{1,0:T(8,128)(2,1)} %bitcast.20.q_ref.refs_4_), channel_id=1, source_target_pairs={{0,8},{8,0},{16,24},{24,16},{1,9},{9,1},{17,25},{25,17},{2,10},{10... | collective-permute-start | bytes 37748744 | tf_op jit(solution)/shard_map/ppermute | solution.py:227
  837.0 144.7 %all-to-all-start.4 = ((bf16[8,192,4096]{2,1,0:T(8,128)(2,1)}), bf16[8,192,4096]{2,1,0:T(8,128)(2,1)}, u32[]{:S(2)}, u32[]{:S(2)}) async-start(bf16[8,192,4096]{2,1,0:T(8,128)(2,1)} %bitcast.131), calls=%async_computation.4 | async-start | bytes 25165824 | tf_op jit(solution)/shard_map/all_to_all | solution.py:199
  981.7 31.1 %slice-start.3 = ((s8[11272192]{0:T(1024)(128)(4,1)}), s8[2883584]{0:T(1024)(128)(4,1)S(1)}, s32[]{:S(2)}) async-start(s8[11272192]{0:T(1024)(128)(4,1)} %bitcast.164), calls=%async_computation.11 | async-start | bytes 5767168
  981.7 212.1 %all-to-all-start.5 = ((bf16[8,192,4096]{2,1,0:T(8,128)(2,1)}), bf16[8,192,4096]{2,1,0:T(8,128)(2,1)}, u32[]{:S(2)}, u32[]{:S(2)}) async-start(bf16[8,192,4096]{2,1,0:T(8,128)(2,1)} %bitcast.132), calls=%async_computation.5 | async-start | bytes 25165824 | tf_op jit(solution)/shard_map/all_to_all | solution.py:199
  987.3 25.4 %slice-start.4 = ((s8[11272192]{0:T(1024)(128)(4,1)}), s8[4194304]{0:T(1024)(128)(4,1)S(1)}, s32[]{:S(2)}) async-start(s8[11272192]{0:T(1024)(128)(4,1)} %bitcast.164), calls=%async_computation.12 | async-start | bytes 8388608
  987.3 25.4 %slice-start.5 = ((s8[11272192]{0:T(1024)(128)(4,1)}), s8[4194304]{0:T(1024)(128)(4,1)S(1)}, s32[]{:S(2)}) async-start(s8[11272192]{0:T(1024)(128)(4,1)} %bitcast.164), calls=%async_computation.13 | async-start | bytes 8388608
  1193.8 151.6 %all-to-all-start.6 = ((bf16[8,192,4096]{2,1,0:T(8,128)(2,1)}), bf16[8,192,4096]{2,1,0:T(8,128)(2,1)}, u32[]{:S(2)}, u32[]{:S(2)}) async-start(bf16[8,192,4096]{2,1,0:T(8,128)(2,1)} %bitcast.129), calls=%async_computation.6 | async-start | bytes 25165824 | tf_op jit(solution)/shard_map/all_to_all | solution.py:199
  1345.4 166.9 %all-to-all-start.7 = ((bf16[8,192,4096]{2,1,0:T(8,128)(2,1)}), bf16[8,192,4096]{2,1,0:T(8,128)(2,1)}, u32[]{:S(2)}, u32[]{:S(2)}) async-start(bf16[8,192,4096]{2,1,0:T(8,128)(2,1)} %bitcast.128), calls=%async_computation.7 | async-start | bytes 25165824 | tf_op jit(solution)/shard_map/all_to_all | solution.py:199
  1416.5 65.5 %copy-start.39 = (s32[512]{0:T(512)S(1)}, s32[512]{0:T(512)}, u32[]{:S(2)}) copy-start(s32[512]{0:T(512)} %copy-done.38) | copy-start | bytes 6148
  1482.0 12.2 copy-start.2
  1482.0 12.2 copy-start.6
  1482.0 12.2 copy-start.28
  1482.0 12.2 copy-start.30
  1482.0 12.2 copy-start.37
  1494.3 17.3 %copy-start.5 = (bf16[512,4096]{1,0:T(8,128)(2,1)S(1)}, bf16[512,4096]{1,0:T(8,128)(2,1)}, u32[]{:S(2)}) copy-start(bf16[512,4096]{1,0:T(8,128)(2,1)} %copy-done.4) | copy-start | bytes 12582916
  1494.3 17.3 %copy-start.8 = (f32[512,8]{0,1:T(8,128)S(1)}, f32[512,8]{0,1:T(8,128)}, u32[]{:S(2)}) copy-start(f32[512,8]{0,1:T(8,128)} %copy-done.7) | copy-start | bytes 49156
  1494.3 17.3 %copy-start.12 = (pred[512,8]{0,1:T(8,128)(4,1)S(1)}, pred[512,8]{0,1:T(8,128)(4,1)}, u32[]{:S(2)}) copy-start(pred[512,8]{0,1:T(8,128)(4,1)} %copy-done.11) | copy-start | bytes 12292
  1494.3 17.3 %copy-start.14 = (s32[512]{0:T(512)S(1)}, s32[512]{0:T(512)}, u32[]{:S(2)}) copy-start(s32[512]{0:T(512)} %param.15) | copy-start | bytes 6148
  1494.3 17.3 %copy-start.16 = (f32[512]{0:T(512)S(1)}, f32[512]{0:T(512)}, u32[]{:S(2)}) copy-start(f32[512]{0:T(512)} %copy-done.15) | copy-start | bytes 6148
  1494.3 17.3 %copy-start.18 = (f32[512]{0:T(512)S(1)}, f32[512]{0:T(512)}, u32[]{:S(2)}) copy-start(f32[512]{0:T(512)} %copy-done.17) | copy-start | bytes 6148
  1494.3 17.3 %copy-start.22 = (f32[512]{0:T(512)S(1)}, f32[512]{0:T(512)}, u32[]{:S(2)}) copy-start(f32[512]{0:T(512)} %copy-done.21) | copy-start | bytes 6148
  1494.3 17.3 %copy-start.24 = (f32[512]{0:T(512)S(1)}, f32[512]{0:T(512)}, u32[]{:S(2)}) copy-start(f32[512]{0:T(512)} %copy-done.23) | copy-start | bytes 6148
  1494.3 17.3 %copy-start.26 = (s32[512]{0:T(512)S(1)}, s32[512]{0:T(512)}, u32[]{:S(2)}) copy-start(s32[512]{0:T(512)} %param.16) | copy-start | bytes 6148
  1512.3 10.0 copy-start.3
  1512.3 10.0 copy-start.10
  1512.3 10.0 copy-start.20
  1512.3 10.0 copy-start.32
  1522.3 6.4 copy-start.42
  (3 other events, 1.8 us)

commit v4 on v3

--- a/solution.py
+++ b/solution.py
@@ -207,10 +207,9 @@
         h_own = swap(h_buf)
         m_f1 = lax.ppermute(meta, 'dp', outer + middle)
         h_f1 = lax.ppermute(hidden, 'dp', outer + middle)
-        dy_a = lax.ppermute(tok_dy, 'dp', outer)
-        dy_b = lax.ppermute(after(tok_dy, dy_a), 'dp', middle)
+        dy_f1 = lax.ppermute(after(tok_dy, h_f1), 'dp', outer + middle)
         q_buf = select_q(tok_dy, meta)
-        q_own = swap(after(q_buf, h_own))
+        q_own = swap(q_buf)
         a_t, b_t = pre(h_own)
         u_t = (a_t * jax.nn.sigmoid(a_t) * b_t).astype(bf16)
         exp_out = jnp.einsum('fr,fd->rd', u_t, wd, preferred_element_type=f32).astype(bf16)
@@ -219,7 +218,6 @@
                     + jnp.einsum('fr,fd->rd', db_t, wu_t, preferred_element_type=f32)).astype(bf16)
         acc = add_dw(None, u_t, da_t, db_t, h_own, q_own)
 
-        dy_f1 = dy_a + dy_b
         m_f2 = lax.ppermute(m_f1, 'dp', near)
         h_f2 = lax.ppermute(h_f1, 'dp', near)
         dy_f2 = lax.ppermute(dy_f1, 'dp', near)
@@ -229,12 +227,12 @@
         q_b1 = select_q(dy_f1, m_f1)
         h_b2 = select_h(h_f2, m_f2)
         q_b2 = select_q(dy_f2, m_f2)
-        h_r1 = swap(after(h_b1, q_own))
-        q_r1 = swap(after(q_b1, h_r1))
-        h_r2 = swap(after(h_b2, q_r1))
-        q_r2 = swap(after(q_b2, h_r2))
-        out_back = swap(after(exp_out, q_r2))
-        hid_back = swap(after(grad_hid, out_back))
+        h_r1 = swap(h_b1)
+        q_r1 = swap(q_b1)
+        h_r2 = swap(h_b2)
+        q_r2 = swap(q_b2)
+        out_back = swap(exp_out)
+        hid_back = swap(grad_hid)
         for h, q in ((h_r1, q_r1), (h_r2, q_r2), (h_near, q_near)):
             a_t, b_t = pre(h)
             u_t, da_t, db_t = inner_grad(q, wd, a_t, b_t)
@@ -258,10 +256,13 @@
         d_ln_bias = jnp.sum(grad_h, axis=0)
         dx_tok = (dy_float + layer_norm_back(grad_h, x_hat, inv_std, ln_weight)).astype(bf16)
         n_dev = n_dp * n_ep
-        parts = jnp.concatenate([d_router, d_ln_weight[None], d_ln_bias[None], jnp.zeros((6, d_model), f32)])
-        total = sum_all(parts.reshape(16, n_dev, d_model // n_dev).transpose(1, 0, 2), n_dp, n_ep)
-        total = total.transpose(1, 0, 2).reshape(16, d_model)
-        d_router, d_ln_weight, d_ln_bias = total[:n_exp].T, total[n_exp], total[n_exp + 1]
+
+        def all_sum(rows):
+            parts = rows.reshape(rows.shape[0], n_dev, d_model // n_dev).transpose(1, 0, 2)
+            return sum_all(parts, n_dp, n_ep).transpose(1, 0, 2).reshape(rows.shape)
+
+        d_router = all_sum(d_router).T
+        d_ln_weight, d_ln_bias = all_sum(jnp.stack([d_ln_weight, d_ln_bias]))
         return (out_tok, dx_tok, dwg.T[None], dwu.T[None], dwd[None], d_router, d_ln_weight, d_ln_bias)
 
     return jax.shard_map(

time: 1570 us -> 1610 us (1.025)
  Pallas kernels: 401 us -> 486 us
  waiting for transfers between devices: 672 us -> 632 us
    ppermute x1, waiting for transfers between devices: 132 us -> 0.01 us  [local_step(): h_f1 = lax.ppermute(hidden, 'dp', outer + middle)]
    ppermute x1, waiting for transfers between devices: 98.7 us -> 0.01 us  [local_step(): q_near = lax.ppermute(q_own, 'dp', near)]
    ppermute x1, waiting for transfers between devices: 86.9 us -> 181 us  [local_step(): m_f1 = lax.ppermute(meta, 'dp', outer + middle)]
    ppermute x1, waiting for transfers between devices: 85.1 us -> 179 us  [local_step(): m_f2 = lax.ppermute(m_f1, 'dp', near)]
    pallas_call x1 -> x2, Pallas kernels: 22.4 us -> 108 us  [sum_all(): pl.pallas_call(functools.partial(sum_kernel, n_dp, n_ep), out_shape=jax.S...]
  transfers between devices with their start and end apart: 17 -> 16, of which waited for: 8 -> 6; matrix products, arithmetic and copies ran while one was open for 24% -> 25% of each run, Pallas kernels for 24% -> 24%
where the time goes in v4:
time: 1610 us; the launch traced here: 1600 us
  waiting for transfers between devices  632 us (39%)
  Pallas kernels  486 us (30%)
  matrix products  398 us (25%)
  starting transfers between devices  54.5 us (3%)
  other arithmetic  21.7 us (1%)
    all_to_all x8, waiting for transfers between devices, swap(): lax.all_to_all(buf.reshape(n_ep, slot_cap, d_model), 'ep', 0, 0, tiled=True)  271 us
    pallas_call x4, Pallas kernels, add_dw(): pl.pallas_call(functools.partial(dw_kernel, first), grid=(d_model // d_ti...  258 us
    ppermute x1, waiting for transfers between devices, local_step(): m_f1 = lax.ppermute(meta, 'dp', outer + middle)  181 us
    ppermute x1, waiting for transfers between devices, local_step(): m_f2 = lax.ppermute(m_f1, 'dp', near)  179 us
    pallas_call x4, Pallas kernels, inner_grad(): pl.pallas_call(grad_kernel, grid=(2, 3), in_specs=[pl.BlockSpec((r_tile,...  120 us
    pallas_call x2, Pallas kernels, sum_all(): pl.pallas_call(functools.partial(sum_kernel, n_dp, n_ep), out_shape=jax.S...  108 us
    dot_general x4, matrix products, pre(): jnp.einsum('fd,rd->fr', wg_t, h, preferred_element_type=f32)  102 us
    dot_general x4, matrix products, pre(): jnp.einsum('fd,rd->fr', wu_t, h, preferred_element_type=f32)  98.6 us
  transfers between devices with their start and end apart: 16, of which 6 were waited for; matrix products, arithmetic and copies ran while one was open for 25% of the time, Pallas kernels for 24%

profile of v4, /device:TPU:0, one launch (start us, length us, event | category | flops | bytes accessed | tf_op | source)
XLA Modules:
  0.0 1602.1 jit_solution(14436029158773134204)
XLA Ops:
  0.7 3.0 convert_reduce_fusion
  3.7 3.6 fusion.55
  7.4 0.5 copy-done.33
  7.9 2.2 fusion.50
  10.2 2.0 copy-done.4
  12.2 1.2 fusion.101
  14.1 0.5 copy-done.40
  14.7 0.7 add_reduce_fusion.2
  15.4 9.8 multiply_convert_fusion.2
  25.1 5.4 all-to-all-start.2
  30.5 11.8 convolution_convert_fusion.3
  42.2 128.0 %all-to-all-done.2 = bf16[8,192,4096]{2,1,0:T(8,128)(2,1)} async-done(((bf16[8,192,4096]{2,1,0:T(8,128)(2,1)}), bf16[8,192,4096]{2,1,0:T(8,128)(2,1)}, u32[]{:S(2)}, u32[]{:S(2)}) %all-to-all-start.2) | async-done | bytes 12582944 | tf_op jit(solution)/shard_map/all_to_all | solution.py:199
  170.3 5.8 all-to-all-start
  176.1 3.3 collective-permute-start.4
  179.5 181.4 %collective-permute-done.2 = f32[4,512]{1,0:T(4,128)S(1)} collective-permute-done((f32[4,512]{1,0:T(4,128)S(1)}, f32[4,512]{1,0:T(4,128)S(1)}, u32[]{:S(2)}, u32[]{:S(2)}) %collective-permute-start.2) | collective-permute-done | bytes 8224 | tf_op jit(solution)/shard_map/ppermute | solution.py:208
  360.9 2.0 copy-done.48
  362.9 9.6 convolution_convert_fusion.1
  372.6 5.3 all-to-all-start.7
  378.0 4.1 collective-permute-start.7
  382.1 0.7 add_reduce_fusion
  382.8 179.3 %collective-permute-done.3 = f32[4,512]{1,0:T(4,128)S(1)} collective-permute-done((f32[4,512]{1,0:T(4,128)S(1)}, f32[4,512]{1,0:T(4,128)S(1)}, u32[]{:S(2)}, u32[]{:S(2)}) %collective-permute-start.3) | collective-permute-done | bytes 8224 | tf_op jit(solution)/shard_map/ppermute | solution.py:221
  562.2 1.3 add_reduce_fusion.1
  563.5 11.8 multiply_convert_fusion
  575.3 5.5 all-to-all-start.6
  580.9 11.7 convolution_convert_fusion.2
  592.6 2.0 collective-permute-start
  594.7 25.3 %fusion.25.a_ref = f32[1376,1536]{1,0:T(8,128)} fusion(bf16[1536,4096]{1,0:T(8,128)(2,1)} %bitcast.1.refs_3_, bf16[1,4096,1376]{1,2,0:T(8,128)(2,1)} %param.23), kind=kOutput, calls=%fused_computation.39 | convolution fusion | flops 17314086912 | bytes 32309248 | tf_op jit(solution)/shard_map/fd,rd->fr/dot_general | solution.py:202
  620.0 22.8 %fusion.37.b_ref = f32[1376,1536]{1,0:T(8,128)} fusion(bf16[1536,4096]{1,0:T(8,128)(2,1)} %bitcast.1.refs_3_, bf16[1,4096,1376]{1,2,0:T(8,128)(2,1)S(1)} %bitcast.166), kind=kOutput, calls=%fused_computation.43 | convolution fusion | flops 17314086912 | bytes 32309248 | tf_op jit(solution)/shard_map/fd,rd->fr/dot_general | solution.py:203
  642.8 30.0 %shard_map.188 = (bf16[1376,1536]{1,0:T(8,128)(2,1)}, bf16[1376,1536]{1,0:T(8,128)(2,1)}, bf16[1376,1536]{1,0:T(8,128)(2,1)}) custom-call(bf16[1536,4096]{1,0:T(8,128)(2,1)} %bitcast.10.q_ref.refs_4_, bf16[1376,4096]{1,0:T(8,128)(2,1)} %bitcast.167, f32[1376,1536]{1,0:T(8,128)} %fusion.25.a_ref, f32[1376,1536]{1,0:T(8,128)} %fusion.37.b_ref), custom_call_target="tpu_custom_call" | custom-call | flops 17314086912 | bytes 54755328 | tf_op jit(solution)/shard_map/pallas_call | solution.py:57
  672.8 47.0 %all-to-all-done.6 = bf16[8,192,4096]{2,1,0:T(8,128)(2,1)} async-done(((bf16[8,192,4096]{2,1,0:T(8,128)(2,1)}), bf16[8,192,4096]{2,1,0:T(8,128)(2,1)}, u32[]{:S(2)}, u32[]{:S(2)}) %all-to-all-start.6) | async-done | bytes 12582944 | tf_op jit(solution)/shard_map/all_to_all | solution.py:199
  719.9 5.7 all-to-all-start.5
  725.6 61.3 %shard_map.192 = (f32[1376,4096]{1,0:T(8,128)}, f32[1376,4096]{1,0:T(8,128)}, f32[1376,4096]{1,0:T(8,128)}) custom-call(bf16[1376,1536]{1,0:T(8,128)(2,1)} %get-tuple-element.45.refs_0_, bf16[1376,1536]{1,0:T(8,128)(2,1)} %get-tuple-element.33.refs_1_, bf16[1376,1536]{1,0:T(8,128)(2,1)} %get-tuple-element.34.refs_2_, bf16[1536,4096]{1,0:T(8,128)(2,1)} %bitcast.1.refs_3_, ...), custom_call_target="tpu_custom_call" | custom-call | flops 51942260736 | bytes 92798976 | tf_op jit(solution)/shard_map/pallas_call | solution.py:89
  786.9 28.7 %convolution_convert_fusion = bf16[1536,4096]{1,0:T(8,128)(2,1)} fusion(f32[1376,1536]{1,0:T(8,128)} %fusion.37.b_ref, f32[1376,1536]{1,0:T(8,128)} %fusion.25.a_ref, bf16[1,1376,4096]{2,1,0:T(8,128)(2,1)} %param.25), kind=kOutput, calls=%fused_computation.4 | convolution fusion | flops 17333059584 | bytes 40763392 | tf_op jit(solution)/shard_map/fr,fd->rd/dot_general | solution.py:215
  815.6 49.0 %all-to-all-done.5 = bf16[8,192,4096]{2,1,0:T(8,128)(2,1)} async-done(((bf16[8,192,4096]{2,1,0:T(8,128)(2,1)}), bf16[8,192,4096]{2,1,0:T(8,128)(2,1)}, u32[]{:S(2)}, u32[]{:S(2)}) %all-to-all-start.5) | async-done | bytes 12582944 | tf_op jit(solution)/shard_map/all_to_all | solution.py:199
  864.6 5.6 all-to-all-start.1
  870.2 26.3 %fusion.15 = f32[1536,4096]{1,0:T(8,128)} fusion(bf16[1376,1536]{1,0:T(8,128)(2,1)} %get-tuple-element.33.refs_1_, bf16[1,4096,1376]{1,2,0:T(8,128)(2,1)} %param.23), kind=kOutput, calls=%fused_computation.29 | convolution fusion | flops 17314086912 | bytes 40665088 | tf_op jit(solution)/shard_map/fr,fd->rd/dot_general | solution.py:217
  896.6 28.5 %add_convert_fusion = bf16[1536,4096]{1,0:T(8,128)(2,1)} fusion(f32[1536,4096]{1,0:T(8,128)} %fusion.15, bf16[1376,1536]{1,0:T(8,128)(2,1)S(1)} %bitcast.175, bf16[1,4096,1376]{1,2,0:T(8,128)(2,1)} %param.24), kind=kOutput, calls=%fused_computation.2 | convolution fusion | flops 17326669824 | bytes 53248000 | tf_op jit(solution)/shard_map/fr,fd->rd/dot_general | solution.py:218
  925.1 12.0 multiply_convert_fusion.1
  937.1 25.2 %fusion.34.a_ref = f32[1376,1536]{1,0:T(8,128)} fusion(bf16[1536,4096]{1,0:T(8,128)(2,1)} %bitcast.36.refs_3_, bf16[1,4096,1376]{1,2,0:T(8,128)(2,1)} %param.23), kind=kOutput, calls=%fused_computation.42 | convolution fusion | flops 17314086912 | bytes 32309248 | tf_op jit(solution)/shard_map/fd,rd->fr/dot_general | solution.py:202
  962.3 46.9 %all-to-all-done.1 = bf16[8,192,4096]{2,1,0:T(8,128)(2,1)} async-done(((bf16[8,192,4096]{2,1,0:T(8,128)(2,1)}), bf16[8,192,4096]{2,1,0:T(8,128)(2,1)}, u32[]{:S(2)}, u32[]{:S(2)}) %all-to-all-start.1) | async-done | bytes 12582944 | tf_op jit(solution)/shard_map/all_to_all | solution.py:199
  1009.2 5.7 all-to-all-start.3
  1015.0 25.4 %fusion.46.b_ref = f32[1376,1536]{1,0:T(8,128)} fusion(bf16[1536,4096]{1,0:T(8,128)(2,1)} %bitcast.36.refs_3_, bf16[1,4096,1376]{1,2,0:T(8,128)(2,1)} %param.24), kind=kOutput, calls=%fused_computation.46 | convolution fusion | flops 17314086912 | bytes 32309248 | tf_op jit(solution)/shard_map/fd,rd->fr/dot_general | solution.py:203
  1040.3 30.0 %shard_map.191 = (bf16[1376,1536]{1,0:T(8,128)(2,1)}, bf16[1376,1536]{1,0:T(8,128)(2,1)}, bf16[1376,1536]{1,0:T(8,128)(2,1)}) custom-call(bf16[1536,4096]{1,0:T(8,128)(2,1)} %bitcast.34.q_ref.refs_4_, bf16[1376,4096]{1,0:T(8,128)(2,1)} %bitcast.168, f32[1376,1536]{1,0:T(8,128)} %fusion.34.a_ref, f32[1376,1536]{1,0:T(8,128)} %fusion.46.b_ref), custom_call_target="tpu_custom_call" | custom-call | flops 17314086912 | bytes 54755328 | tf_op jit(solution)/shard_map/pallas_call | solution.py:57
  1070.3 25.5 %fusion.31.a_ref = f32[1376,1536]{1,0:T(8,128)} fusion(bf16[1536,4096]{1,0:T(8,128)(2,1)} %bitcast.26.refs_3_, bf16[1,4096,1376]{1,2,0:T(8,128)(2,1)} %param.23), kind=kOutput, calls=%fused_computation.41 | convolution fusion | flops 17314086912 | bytes 32309248 | tf_op jit(solution)/shard_map/fd,rd->fr/dot_general | solution.py:202
  1095.8 65.5 %shard_map.193 = (f32[1376,4096]{1,0:T(8,128)}, f32[1376,4096]{1,0:T(8,128)}, f32[1376,4096]{1,0:T(8,128)}) custom-call(bf16[1376,1536]{1,0:T(8,128)(2,1)} %get-tuple-element.42.refs_0_, bf16[1376,1536]{1,0:T(8,128)(2,1)} %get-tuple-element.43.refs_1_, ...), custom_call_target="tpu_custom_call", output_to_operand_aliasing={{0}: (5, {}), {1}: (6, {}), {2}: (7, {})} | custom-call | flops 51942260736 | bytes 160432128 | tf_op jit(solution)/shard_map/pallas_call | solution.py:89
  1161.4 5.6 all-to-all-start.4
  1167.0 25.2 %fusion.43.b_ref = f32[1376,1536]{1,0:T(8,128)} fusion(bf16[1536,4096]{1,0:T(8,128)(2,1)} %bitcast.26.refs_3_, bf16[1,4096,1376]{1,2,0:T(8,128)(2,1)} %param.24), kind=kOutput, calls=%fused_computation.45 | convolution fusion | flops 17314086912 | bytes 32309248 | tf_op jit(solution)/shard_map/fd,rd->fr/dot_general | solution.py:203
  1192.2 11.9 fusion.65
  1204.3 17.7 %fusion.58 = (f32[512]{0:T(512)S(1)}, f32[512]{0:T(512)S(1)}, bf16[512,4096]{1,0:T(8,128)(2,1)}) fusion(bf16[512,4096]{1,0:T(8,128)(2,1)S(1)} %copy-done.7, f32[512,4096]{1,0:T(8,128)} %fusion.65, f32[512]{0:T(512)S(1)} %copy-done.32, f32[512]{0:T(512)S(1)} %copy-done.30, bf16[512,4096]{1,0:T(8,128)(2,1)S(1)} %copy-done.2, bf16[1536,4096]{1,0:T(8,128)(2,1)} %bitcast.8, ...), kind=kOutput, calls=%fused_computation.57 | convolution fusion | flops 6466305024 | bytes 33564672 | tf_op jit(solution)/shard_map/dot_general | solution.py:245
  1222.0 1.3 convolution_bitcast_fusion.x_ref
  1223.3 90.7 %shard_map.196 = f32[32,8,128]{2,1,0:T(8,128)} custom-call(f32[32,8,128]{2,1,0:T(8,128)} %convolution_bitcast_fusion.x_ref), custom_call_target="tpu_custom_call" | custom-call | tf_op jit(solution)/shard_map/pallas_call | solution.py:142
  1314.1 10.0 fusion.76
  1324.2 6.1 fusion.54
  1330.2 0.6 maximum_bitcast_fusion.x_ref
  1330.9 17.3 %shard_map.197 = f32[32,2,128]{2,1,0:T(2,128)} custom-call(f32[32,2,128]{2,1,0:T(2,128)} %maximum_bitcast_fusion.x_ref), custom_call_target="tpu_custom_call" | custom-call | tf_op jit(solution)/shard_map/pallas_call | solution.py:142
  1348.2 1.5 fusion.107
  1349.7 9.4 fusion.60
  1359.1 29.9 %shard_map.190 = (bf16[1376,1536]{1,0:T(8,128)(2,1)}, bf16[1376,1536]{1,0:T(8,128)(2,1)}, bf16[1376,1536]{1,0:T(8,128)(2,1)}) custom-call(bf16[1536,4096]{1,0:T(8,128)(2,1)} %bitcast.24.q_ref.refs_4_, bf16[1376,4096]{1,0:T(8,128)(2,1)} %bitcast.169, f32[1376,1536]{1,0:T(8,128)} %fusion.31.a_ref, f32[1376,1536]{1,0:T(8,128)} %fusion.43.b_ref), custom_call_target="tpu_custom_call" | custom-call | flops 17314086912 | bytes 54755328 | tf_op jit(solution)/shard_map/pallas_call | solution.py:57
  1389.0 65.5 %shard_map.194 = (f32[1376,4096]{1,0:T(8,128)}, f32[1376,4096]{1,0:T(8,128)}, f32[1376,4096]{1,0:T(8,128)}) custom-call(bf16[1376,1536]{1,0:T(8,128)(2,1)} %get-tuple-element.39.refs_0_, bf16[1376,1536]{1,0:T(8,128)(2,1)} %get-tuple-element.40.refs_1_, ...), custom_call_target="tpu_custom_call", output_to_operand_aliasing={{0}: (5, {}), {1}: (6, {}), {2}: (7, {})} | custom-call | flops 51942260736 | bytes 160432128 | tf_op jit(solution)/shard_map/pallas_call | solution.py:89
  1454.5 25.5 %fusion.28.a_ref = f32[1376,1536]{1,0:T(8,128)} fusion(bf16[1536,4096]{1,0:T(8,128)(2,1)} %collective-permute-done.1.refs_3_, bf16[1,4096,1376]{1,2,0:T(8,128)(2,1)} %param.23), kind=kOutput, calls=%fused_computation.40 | convolution fusion | flops 17314086912 | bytes 32309248 | tf_op jit(solution)/shard_map/fd,rd->fr/dot_general | solution.py:202
  1480.0 25.2 %fusion.40.b_ref = f32[1376,1536]{1,0:T(8,128)} fusion(bf16[1536,4096]{1,0:T(8,128)(2,1)} %collective-permute-done.1.refs_3_, bf16[1,4096,1376]{1,2,0:T(8,128)(2,1)} %param.24), kind=kOutput, calls=%fused_computation.44 | convolution fusion | flops 17314086912 | bytes 32309248 | tf_op jit(solution)/shard_map/fd,rd->fr/dot_general | solution.py:203
  1505.2 30.2 %shard_map.189 = (bf16[1376,1536]{1,0:T(8,128)(2,1)}, bf16[1376,1536]{1,0:T(8,128)(2,1)}, bf16[1376,1536]{1,0:T(8,128)(2,1)}) custom-call(bf16[1536,4096]{1,0:T(8,128)(2,1)} %collective-permute-done.q_ref.refs_4_, bf16[1376,4096]{1,0:T(8,128)(2,1)} %bitcast.170, f32[1376,1536]{1,0:T(8,128)} %fusion.28.a_ref, f32[1376,1536]{1,0:T(8,128)} %fusion.40.b_ref), custom_call_target="tpu_custom_call" | custom-call | flops 17314086912 | bytes 54755328 | tf_op jit(solution)/shard_map/pallas_call | solution.py:57
  1535.4 65.5 %shard_map.195 = (f32[1376,4096]{1,0:T(8,128)}, f32[1376,4096]{1,0:T(8,128)}, f32[1376,4096]{1,0:T(8,128)}) custom-call(bf16[1376,1536]{1,0:T(8,128)(2,1)} %get-tuple-element.35.refs_0_, bf16[1376,1536]{1,0:T(8,128)(2,1)} %get-tuple-element.36.refs_1_, ...), custom_call_target="tpu_custom_call", output_to_operand_aliasing={{0}: (5, {}), {1}: (6, {}), {2}: (7, {})} | custom-call | flops 51942260736 | bytes 160432128 | tf_op jit(solution)/shard_map/pallas_call | solution.py:89
  1601.0 0.7 copy.40
  (140 shorter events, 1.2 us)
Async XLA Ops:
  0.6 11.5 copy-start
  0.6 7.3 copy-start.1
  0.7 6.6 copy-start.36
  0.7 6.7 copy-start.37
  0.7 6.7 copy-start.15
  0.7 6.7 copy-start.42
  0.7 11.5 copy-start.35
  3.7 3.7 copy-start.21
  3.7 10.3 copy-start.27
  3.7 10.3 copy-start.43
  3.7 11.6 copy-start.6
  7.3 6.7 copy-start.11
  7.9 6.2 copy-start.38
  10.1 2.0 copy-start.4
  13.4 0.7 copy-start.17
  13.5 165.9 %copy-start.29 = (f32[512]{0:T(512)}, f32[512]{0:T(512)S(1)}, u32[]{:S(2)}) copy-start(f32[512]{0:T(512)S(1)} %get-tuple-element.64) | copy-start | bytes 6148
  14.0 165.4 %copy-start.31 = (f32[512]{0:T(512)}, f32[512]{0:T(512)S(1)}, u32[]{:S(2)}) copy-start(f32[512]{0:T(512)S(1)} %select_reduce_fusion) | copy-start | bytes 6148
  25.1 145.1 %all-to-all-start.2 = ((bf16[8,192,4096]{2,1,0:T(8,128)(2,1)}), bf16[8,192,4096]{2,1,0:T(8,128)(2,1)}, u32[]{:S(2)}, u32[]{:S(2)}) async-start(bf16[8,192,4096]{2,1,0:T(8,128)(2,1)} %bitcast.138), calls=%async_computation.2 | async-start | bytes 25165824 | tf_op jit(solution)/shard_map/all_to_all | solution.py:199
  170.3 202.3 %all-to-all-start = ((bf16[8,192,4096]{2,1,0:T(8,128)(2,1)}), bf16[8,192,4096]{2,1,0:T(8,128)(2,1)}, u32[]{:S(2)}, u32[]{:S(2)}) async-start(bf16[8,192,4096]{2,1,0:T(8,128)(2,1)} %bitcast.134), calls=%async_computation | async-start | bytes 25165824 | tf_op jit(solution)/shard_map/all_to_all | solution.py:199
  176.1 184.9 %collective-permute-start.4 = (bf16[512,4096]{1,0:T(8,128)(2,1)}, bf16[512,4096]{1,0:T(8,128)(2,1)S(1)}, u32[]{:S(2)}, u32[]{:S(2)}) collective-permute-start(bf16[512,4096]{1,0:T(8,128)(2,1)} %copy-done.4), channel_id=1, source_target_pairs={{0,16},{24,8},{8,24},{16,0},{1,17},{25,9},{9,25},{17,1},{2,18},{26... | collective-permute-start | bytes 12582920 | tf_op jit(solution)/shard_map/ppermute | solution.py:209
  179.4 181.5 %collective-permute-start.2 = (f32[4,512]{1,0:T(4,128)S(1)}, f32[4,512]{1,0:T(4,128)S(1)}, u32[]{:S(2)}, u32[]{:S(2)}) collective-permute-start(f32[4,512]{1,0:T(4,128)S(1)} %pad_maximum_fusion), channel_id=1, source_target_pairs={{0,16},{24,8},{8,24},{16,0},{1,17},{25,9},{9,25},{17,1},{2,18},{26... | collective-permute-start | bytes 24584 | tf_op jit(solution)/shard_map/ppermute | solution.py:208
  360.9 2.0 copy-start.48
  372.6 202.7 %all-to-all-start.7 = ((bf16[8,192,4096]{2,1,0:T(8,128)(2,1)}), bf16[8,192,4096]{2,1,0:T(8,128)(2,1)}, u32[]{:S(2)}, u32[]{:S(2)}) async-start(bf16[8,192,4096]{2,1,0:T(8,128)(2,1)} %bitcast.132), calls=%async_computation.7 | async-start | bytes 25165824 | tf_op jit(solution)/shard_map/all_to_all | solution.py:199
  377.9 185.6 %collective-permute-start.5 = (bf16[512,4096]{1,0:T(8,128)(2,1)}, bf16[512,4096]{1,0:T(8,128)(2,1)}, u32[]{:S(2)}, u32[]{:S(2)}) collective-permute-start(bf16[512,4096]{1,0:T(8,128)(2,1)} %param.14), channel_id=1, source_target_pairs={{0,16},{24,8},{8,24},{16,0},{1,17},{25,9},{9,25},{17,1},{2,18},{26... | collective-permute-start | bytes 12582920 | tf_op jit(solution)/shard_map/ppermute | solution.py:210
  378.0 202.9 %collective-permute-start.7 = (bf16[512,4096]{1,0:T(8,128)(2,1)}, bf16[512,4096]{1,0:T(8,128)(2,1)}, u32[]{:S(2)}, u32[]{:S(2)}) collective-permute-start(bf16[512,4096]{1,0:T(8,128)(2,1)} %copy-done.48), channel_id=1, source_target_pairs={{0,8},{8,0},{16,24},{24,16},{1,9},{9,1},{17,25},{25,17},{2,10},{10... | collective-permute-start | bytes 12582920 | tf_op jit(solution)/shard_map/ppermute | solution.py:222
  382.1 180.1 %collective-permute-start.3 = (f32[4,512]{1,0:T(4,128)S(1)}, f32[4,512]{1,0:T(4,128)S(1)}, u32[]{:S(2)}, u32[]{:S(2)}) collective-permute-start(f32[4,512]{1,0:T(4,128)S(1)} %collective-permute-done.2), channel_id=1, source_target_pairs={{0,8},{8,0},{16,24},{24,16},{1,9},{9,1},{17,25},{25,17},{2,10},{10... | collective-permute-start | bytes 24584 | tf_op jit(solution)/shard_map/ppermute | solution.py:221
  562.2 18.7 %copy-start.44 = (s32[1,512]{1,0:T(1,128)}, s32[1,512]{1,0:T(1,128)S(1)}, u32[]{:S(2)}) copy-start(s32[1,512]{1,0:T(1,128)S(1)} %get-tuple-element.81) | copy-start | bytes 6148
  562.2 18.7 %copy-start.46 = (s32[1,512]{1,0:T(1,128)}, s32[1,512]{1,0:T(1,128)S(1)}, u32[]{:S(2)}) copy-start(s32[1,512]{1,0:T(1,128)S(1)} %get-tuple-element.83) | copy-start | bytes 6148
  563.5 361.6 %collective-permute-start.6 = (bf16[512,4096]{1,0:T(8,128)(2,1)}, bf16[512,4096]{1,0:T(8,128)(2,1)}, u32[]{:S(2)}, u32[]{:S(2)}) collective-permute-start(bf16[512,4096]{1,0:T(8,128)(2,1)} %collective-permute-done.5), channel_id=1, source_target_pairs={{0,8},{8,0},{16,24},{24,16},{1,9},{9,1},{17,25},{25,17},{2,10},{10... | collective-permute-start | bytes 12582920 | tf_op jit(solution)/shard_map/ppermute | solution.py:223
  575.3 144.5 %all-to-all-start.6 = ((bf16[8,192,4096]{2,1,0:T(8,128)(2,1)}), bf16[8,192,4096]{2,1,0:T(8,128)(2,1)}, u32[]{:S(2)}, u32[]{:S(2)}) async-start(bf16[8,192,4096]{2,1,0:T(8,128)(2,1)} %bitcast.136), calls=%async_computation.6 | async-start | bytes 25165824 | tf_op jit(solution)/shard_map/all_to_all | solution.py:199
  592.6 912.7 %collective-permute-start = (bf16[1536,4096]{1,0:T(8,128)(2,1)}, bf16[1536,4096]{1,0:T(8,128)(2,1)}, u32[]{:S(2)}, u32[]{:S(2)}) collective-permute-start(bf16[1536,4096]{1,0:T(8,128)(2,1)} %bitcast.10.q_ref.refs_4_), channel_id=1, source_target_pairs={{0,8},{8,0},{16,24},{24,16},{1,9},{9,1},{17,25},{25,17},{2,10},{10... | collective-permute-start | bytes 37748744 | tf_op jit(solution)/shard_map/ppermute | solution.py:225
  594.6 25.4 %slice-start = ((s8[11272192]{0:T(1024)(128)(4,1)}), s8[4194304]{0:T(1024)(128)(4,1)S(1)}, s32[]{:S(2)}) async-start(s8[11272192]{0:T(1024)(128)(4,1)} %bitcast.165), calls=%async_computation.8 | async-start | bytes 8388608
  594.6 25.4 %slice-start.1 = ((s8[11272192]{0:T(1024)(128)(4,1)}), s8[4194304]{0:T(1024)(128)(4,1)S(1)}, s32[]{:S(2)}) async-start(s8[11272192]{0:T(1024)(128)(4,1)} %bitcast.165), calls=%async_computation.9 | async-start | bytes 8388608
  594.6 25.4 %slice-start.2 = ((s8[11272192]{0:T(1024)(128)(4,1)}), s8[2883584]{0:T(1024)(128)(4,1)S(1)}, s32[]{:S(2)}) async-start(s8[11272192]{0:T(1024)(128)(4,1)} %bitcast.165), calls=%async_computation.10 | async-start | bytes 5767168
  594.6 859.9 %collective-permute-start.1 = (bf16[1536,4096]{1,0:T(8,128)(2,1)}, bf16[1536,4096]{1,0:T(8,128)(2,1)}, u32[]{:S(2)}, u32[]{:S(2)}) collective-permute-start(bf16[1536,4096]{1,0:T(8,128)(2,1)} %bitcast.1.refs_3_), channel_id=1, source_target_pairs={{0,8},{8,0},{16,24},{24,16},{1,9},{9,1},{17,25},{25,17},{2,10},{10... | collective-permute-start | bytes 37748744 | tf_op jit(solution)/shard_map/ppermute | solution.py:224
  719.9 144.7 %all-to-all-start.5 = ((bf16[8,192,4096]{2,1,0:T(8,128)(2,1)}), bf16[8,192,4096]{2,1,0:T(8,128)(2,1)}, u32[]{:S(2)}, u32[]{:S(2)}) async-start(bf16[8,192,4096]{2,1,0:T(8,128)(2,1)} %bitcast.135), calls=%async_computation.5 | async-start | bytes 25165824 | tf_op jit(solution)/shard_map/all_to_all | solution.py:199
  864.6 31.9 %slice-start.3 = ((s8[4227072]{0:T(1024)(128)(4,1)}), s8[32768]{0:T(1024)(128)(4,1)S(1)}, s32[]{:S(2)}) async-start(s8[4227072]{0:T(1024)(128)(4,1)} %bitcast.174), calls=%async_computation.11 | async-start | bytes 65536
  864.6 144.6 %all-to-all-start.1 = ((bf16[8,192,4096]{2,1,0:T(8,128)(2,1)}), bf16[8,192,4096]{2,1,0:T(8,128)(2,1)}, u32[]{:S(2)}, u32[]{:S(2)}) async-start(bf16[8,192,4096]{2,1,0:T(8,128)(2,1)} %bitcast.137), calls=%async_computation.1 | async-start | bytes 25165824 | tf_op jit(solution)/shard_map/all_to_all | solution.py:199
  870.2 26.3 %slice-start.4 = ((s8[4227072]{0:T(1024)(128)(4,1)}), s8[4194304]{0:T(1024)(128)(4,1)S(1)}, s32[]{:S(2)}) async-start(s8[4227072]{0:T(1024)(128)(4,1)} %bitcast.174), calls=%async_computation.12 | async-start | bytes 8388608
  896.5 28.5 %copy-start.45 = (s32[1,512]{1,0:T(1,128)S(1)}, s32[1,512]{1,0:T(1,128)}, u32[]{:S(2)}) copy-start(s32[1,512]{1,0:T(1,128)} %copy-done.44) | copy-start | bytes 6148
  896.5 28.5 %copy-start.47 = (s32[1,512]{1,0:T(1,128)S(1)}, s32[1,512]{1,0:T(1,128)}, u32[]{:S(2)}) copy-start(s32[1,512]{1,0:T(1,128)} %copy-done.46) | copy-start | bytes 6148
  896.6 28.5 %copy-start.49 = (f32[1536]{0:T(1024)S(1)}, f32[1536]{0:T(1024)}, u32[]{:S(2)}) copy-start(f32[1536]{0:T(1024)} %add_reduce_fusion.1) | copy-start | bytes 18436
  1009.2 152.1 %all-to-all-start.3 = ((bf16[8,192,4096]{2,1,0:T(8,128)(2,1)}), bf16[8,192,4096]{2,1,0:T(8,128)(2,1)}, u32[]{:S(2)}, u32[]{:S(2)}) async-start(bf16[8,192,4096]{2,1,0:T(8,128)(2,1)} %bitcast.133), calls=%async_computation.3 | async-start | bytes 25165824 | tf_op jit(solution)/shard_map/all_to_all | solution.py:199
  1161.4 197.7 %all-to-all-start.4 = ((bf16[8,192,4096]{2,1,0:T(8,128)(2,1)}), bf16[8,192,4096]{2,1,0:T(8,128)(2,1)}, u32[]{:S(2)}, u32[]{:S(2)}) async-start(bf16[8,192,4096]{2,1,0:T(8,128)(2,1)} %bitcast.131), calls=%async_computation.4 | async-start | bytes 25165824 | tf_op jit(solution)/shard_map/all_to_all | solution.py:199
  1167.0 25.2 %copy-start.41 = (s32[512]{0:T(512)S(1)}, s32[512]{0:T(512)}, u32[]{:S(2)}) copy-start(s32[512]{0:T(512)} %copy-done.40) | copy-start | bytes 6148
  1192.2 11.9 copy-start.2
  1192.2 11.9 copy-start.7
  1192.2 11.9 copy-start.30
  1192.2 11.9 copy-start.32
  1192.2 11.9 copy-start.39
  1204.2 17.8 %copy-start.5 = (bf16[512,4096]{1,0:T(8,128)(2,1)S(1)}, bf16[512,4096]{1,0:T(8,128)(2,1)}, u32[]{:S(2)}) copy-start(bf16[512,4096]{1,0:T(8,128)(2,1)} %copy-done.4) | copy-start | bytes 12582916
  1204.2 17.8 %copy-start.10 = (f32[512,8]{0,1:T(8,128)S(1)}, f32[512,8]{0,1:T(8,128)}, u32[]{:S(2)}) copy-start(f32[512,8]{0,1:T(8,128)} %copy-done.9) | copy-start | bytes 49156
  1204.2 17.8 %copy-start.14 = (pred[512,8]{0,1:T(8,128)(4,1)S(1)}, pred[512,8]{0,1:T(8,128)(4,1)}, u32[]{:S(2)}) copy-start(pred[512,8]{0,1:T(8,128)(4,1)} %copy-done.13) | copy-start | bytes 12292
  1204.2 17.8 %copy-start.16 = (s32[512]{0:T(512)S(1)}, s32[512]{0:T(512)}, u32[]{:S(2)}) copy-start(s32[512]{0:T(512)} %param.15) | copy-start | bytes 6148
  1204.2 17.8 %copy-start.18 = (f32[512]{0:T(512)S(1)}, f32[512]{0:T(512)}, u32[]{:S(2)}) copy-start(f32[512]{0:T(512)} %copy-done.17) | copy-start | bytes 6148
  1204.2 17.8 %copy-start.20 = (f32[512]{0:T(512)S(1)}, f32[512]{0:T(512)}, u32[]{:S(2)}) copy-start(f32[512]{0:T(512)} %copy-done.19) | copy-start | bytes 6148
  1204.2 17.8 %copy-start.24 = (f32[512]{0:T(512)S(1)}, f32[512]{0:T(512)}, u32[]{:S(2)}) copy-start(f32[512]{0:T(512)} %copy-done.23) | copy-start | bytes 6148
  1204.2 17.8 %copy-start.26 = (f32[512]{0:T(512)S(1)}, f32[512]{0:T(512)}, u32[]{:S(2)}) copy-start(f32[512]{0:T(512)} %copy-done.25) | copy-start | bytes 6148
  1204.2 17.8 %copy-start.28 = (s32[512]{0:T(512)S(1)}, s32[512]{0:T(512)}, u32[]{:S(2)}) copy-start(s32[512]{0:T(512)} %param.16) | copy-start | bytes 6148
  1314.1 10.0 copy-start.3
  1314.1 10.0 copy-start.12
  1314.1 10.0 copy-start.22
  1314.1 10.0 copy-start.34
  1535.4 65.5 %copy-start.8 = (f32[32,8,128]{2,1,0:T(8,128)S(1)}, f32[32,8,128]{2,1,0:T(8,128)}, u32[]{:S(2)}) copy-start(f32[32,8,128]{2,1,0:T(8,128)} %shard_map.196) | copy-start | bytes 393220
  (7 other events, 4.4 us)

commit v5 on v4

--- a/solution.py
+++ b/solution.py
@@ -52,13 +52,13 @@
 def inner_grad(q, wd, a_t, b_t):
     n_rows, d_model = q.shape
     width = wd.shape[0]
-    w_tile, r_tile = width // 2, n_rows // 3
-    tile = pl.BlockSpec((w_tile, r_tile), lambda i, j: (i, j))
+    r_tile = n_rows // 6
+    tile = pl.BlockSpec((width, r_tile), lambda j: (0, j))
     return pl.pallas_call(
         grad_kernel,
-        grid=(2, 3),
-        in_specs=[pl.BlockSpec((r_tile, d_model), lambda i, j: (j, 0)),
-                  pl.BlockSpec((w_tile, d_model), lambda i, j: (i, 0)),
+        grid=(n_rows // r_tile,),
+        in_specs=[pl.BlockSpec((r_tile, d_model), lambda j: (j, 0)),
+                  pl.BlockSpec((width, d_model), lambda j: (0, 0), pipeline_mode=pl.Buffered(1)),
                   tile, tile],
         out_specs=[tile] * 3,
         out_shape=[jax.ShapeDtypeStruct((width, n_rows), bf16)] * 3,
@@ -213,6 +213,14 @@
         a_t, b_t = pre(h_own)
         u_t = (a_t * jax.nn.sigmoid(a_t) * b_t).astype(bf16)
         exp_out = jnp.einsum('fr,fd->rd', u_t, wd, preferred_element_type=f32).astype(bf16)
+        ep_id = lax.axis_index('ep')
+        by_dest = exp_out.reshape(n_ep, slot_cap, d_model)
+        pieces = []
+        for k in range(n_ep):
+            piece = lax.dynamic_index_in_dim(by_dest, ep_id ^ k, 0, keepdims=False)
+            if k:
+                piece = lax.ppermute(piece, 'ep', [(i, i ^ k) for i in range(n_ep)])
+            pieces.append(piece)
         u_t, da_t, db_t = inner_grad(q_own, wd, a_t, b_t)
         grad_hid = (jnp.einsum('fr,fd->rd', da_t, wg_t, preferred_element_type=f32)
                     + jnp.einsum('fr,fd->rd', db_t, wu_t, preferred_element_type=f32)).astype(bf16)
@@ -231,7 +239,6 @@
         q_r1 = swap(q_b1)
         h_r2 = swap(h_b2)
         q_r2 = swap(q_b2)
-        out_back = swap(exp_out)
         hid_back = swap(grad_hid)
         for h, q in ((h_r1, q_r1), (h_r2, q_r2), (h_near, q_near)):
             a_t, b_t = pre(h)
@@ -242,8 +249,11 @@
         dy_float = tok_dy.astype(f32)
         sel_one = (pos_one[:, None] == row_ids[None, :]).astype(bf16)
         sel_two = (pos_two[:, None] == row_ids[None, :]).astype(bf16)
-        out_one = jnp.dot(sel_one, out_back, preferred_element_type=f32)
-        out_two = jnp.dot(sel_two, out_back, preferred_element_type=f32)
+        back_one = jnp.where(slot_first >= 0, (exp_first ^ ep_id) * slot_cap + slot_first, -1)
+        back_two = jnp.where(slot_second >= 0, (exp_second ^ ep_id) * slot_cap + slot_second, -1)
+        out_back = jnp.concatenate(pieces)
+        out_one = jnp.dot((back_one[:, None] == row_ids[None, :]).astype(bf16), out_back, preferred_element_type=f32)
+        out_two = jnp.dot((back_two[:, None] == row_ids[None, :]).astype(bf16), out_back, preferred_element_type=f32)
         out_tok = (tok_x.astype(f32) + gate_one[:, None] * out_one + gate_two[:, None] * out_two).astype(bf16)
         dgate_one = jnp.sum(dy_float * out_one, axis=-1)
         dgate_two = jnp.sum(dy_float * out_two, axis=-1)
@@ -256,13 +266,10 @@
         d_ln_bias = jnp.sum(grad_h, axis=0)
         dx_tok = (dy_float + layer_norm_back(grad_h, x_hat, inv_std, ln_weight)).astype(bf16)
         n_dev = n_dp * n_ep
-
-        def all_sum(rows):
-            parts = rows.reshape(rows.shape[0], n_dev, d_model // n_dev).transpose(1, 0, 2)
-            return sum_all(parts, n_dp, n_ep).transpose(1, 0, 2).reshape(rows.shape)
-
-        d_router = all_sum(d_router).T
-        d_ln_weight, d_ln_bias = all_sum(jnp.stack([d_ln_weight, d_ln_bias]))
+        parts = jnp.concatenate([d_router, d_ln_weight[None], d_ln_bias[None], jnp.zeros((6, d_model), f32)])
+        total = sum_all(parts.reshape(16, n_dev, d_model // n_dev).transpose(1, 0, 2), n_dp, n_ep)
+        total = total.transpose(1, 0, 2).reshape(16, d_model)
+        d_router, d_ln_weight, d_ln_bias = total[:n_exp].T, total[n_exp], total[n_exp + 1]
         return (out_tok, dx_tok, dwg.T[None], dwu.T[None], dwd[None], d_router, d_ln_weight, d_ln_bias)
 
     return jax.shard_map(

time: 1610 us -> 1630 us (1.012)
  Pallas kernels: 486 us -> 460 us
  local copies, waits for them, and re-layouts: 7.85 us -> 31.7 us
  waiting for transfers between devices: 632 us -> 650 us
    ppermute x0 -> x7, waiting for transfers between devices: none -> 211 us  [local_step(): piece = lax.ppermute(piece, 'ep', [(i, i ^ k) for i in range(n_ep)])]
    ppermute x1, waiting for transfers between devices: 179 us -> 1.22 us  [local_step(): m_f2 = lax.ppermute(m_f1, 'dp', near)]
    all_to_all x8 -> x7, waiting for transfers between devices: 271 us -> 218 us  [swap(): lax.all_to_all(buf.reshape(n_ep, slot_cap, d_model), 'ep', 0, 0, tiled=True)]
    ppermute x1, waiting for transfers between devices: 0.01 us -> 40.1 us  [local_step(): h_f1 = lax.ppermute(hidden, 'dp', outer + middle)]
    pallas_call x2 -> x1, Pallas kernels: 108 us -> 83.5 us  [sum_all(): pl.pallas_call(functools.partial(sum_kernel, n_dp, n_ep), out_shape=jax.S...]
    all_to_all x8 -> x7, starting transfers between devices: 44.8 us -> 39.4 us  [swap(): lax.all_to_all(buf.reshape(n_ep, slot_cap, d_model), 'ep', 0, 0, tiled=True)]
  transfers between devices with their start and end apart: 16 -> 22, of which waited for: 6 -> 9; matrix products, arithmetic and copies ran while one was open for 25% -> 26% of each run, Pallas kernels for 24% -> 22%
where the time goes in v5:
time: 1630 us; the launch traced here: 1620 us
  waiting for transfers between devices  650 us (40%)
  Pallas kernels  460 us (28%)
  matrix products  394 us (24%)
  starting transfers between devices  60.7 us (4%)
  local copies, waits for them, and re-layouts  31.7 us (2%)
  other arithmetic  22.9 us (1%)
    pallas_call x4, Pallas kernels, add_dw(): pl.pallas_call(functools.partial(dw_kernel, first), grid=(d_model // d_ti...  258 us
    all_to_all x7, waiting for transfers between devices, swap(): lax.all_to_all(buf.reshape(n_ep, slot_cap, d_model), 'ep', 0, 0, tiled=True)  218 us
    ppermute x7, waiting for transfers between devices, local_step(): piece = lax.ppermute(piece, 'ep', [(i, i ^ k) for i in range(n_ep)])  211 us
    ppermute x1, waiting for transfers between devices, local_step(): m_f1 = lax.ppermute(meta, 'dp', outer + middle)  179 us
    pallas_call x4, Pallas kernels, inner_grad(): pl.pallas_call(grad_kernel, grid=(n_rows // r_tile,), in_specs=[pl.BlockS...  118 us
    dot_general x4, matrix products, pre(): jnp.einsum('fd,rd->fr', wg_t, h, preferred_element_type=f32)  99 us
    dot_general x4, matrix products, pre(): jnp.einsum('fd,rd->fr', wu_t, h, preferred_element_type=f32)  94.4 us
    pallas_call x1, Pallas kernels, sum_all(): pl.pallas_call(functools.partial(sum_kernel, n_dp, n_ep), out_shape=jax.S...  83.5 us
  transfers between devices with their start and end apart: 22, of which 9 were waited for; matrix products, arithmetic and copies ran while one was open for 26% of the time, Pallas kernels for 22%

profile of v5, /device:TPU:0, one launch (start us, length us, event | category | flops | bytes accessed | tf_op | source)
XLA Modules:
  0.0 1621.0 jit_solution(7392741051527771261)
XLA Ops:
  2.8 2.8 convert_reduce_fusion
  5.6 3.4 fusion.55
  9.7 2.2 fusion.50
  11.9 9.6 convolution_convert_fusion.3
  21.6 5.5 all-to-all-start
  27.1 4.1 collective-permute-start.11
  31.2 3.4 fusion.101
  36.1 11.8 multiply_convert_fusion.2
  47.9 118.9 %all-to-all-done = bf16[8,192,4096]{2,1,0:T(8,128)(2,1)} async-done(((bf16[8,192,4096]{2,1,0:T(8,128)(2,1)}), bf16[8,192,4096]{2,1,0:T(8,128)(2,1)}, u32[]{:S(2)}, u32[]{:S(2)}) %all-to-all-start) | async-done | bytes 12582944 | tf_op jit(solution)/shard_map/all_to_all | solution.py:199
  166.8 5.5 all-to-all-start.1
  172.3 40.1 %collective-permute-done.11 = bf16[512,4096]{1,0:T(8,128)(2,1)} collective-permute-done((bf16[512,4096]{1,0:T(8,128)(2,1)}, bf16[512,4096]{1,0:T(8,128)(2,1)}, u32[]{:S(2)}, u32[]{:S(2)}) %collective-permute-start.11) | collective-permute-done | bytes 4194336 | tf_op jit(solution)/shard_map/ppermute | solution.py:209
  212.4 4.1 collective-permute-start.14
  217.3 178.7 %collective-permute-done.9 = f32[4,512]{1,0:T(4,128)S(1)} collective-permute-done((f32[4,512]{1,0:T(4,128)S(1)}, f32[4,512]{1,0:T(4,128)S(1)}, u32[]{:S(2)}, u32[]{:S(2)}) %collective-permute-start.9) | collective-permute-done | bytes 8224 | tf_op jit(solution)/shard_map/ppermute | solution.py:208
  395.9 1.7 collective-permute-start.10
  400.9 11.7 convolution_convert_fusion.1
  412.7 1.7 collective-permute-start.13
  414.4 11.9 convolution_convert_fusion.2
  426.3 11.9 multiply_convert_fusion
  438.2 22.7 %fusion.25.a_ref = f32[1376,1536]{1,0:T(8,128)} fusion(bf16[1536,4096]{1,0:T(8,128)(2,1)} %bitcast.1.refs_3_, bf16[1,4096,1376]{1,2,0:T(8,128)(2,1)S(1)} %bitcast.179), kind=kOutput, calls=%fused_computation.39 | convolution fusion | flops 17314086912 | bytes 32309248 | tf_op jit(solution)/shard_map/fd,rd->fr/dot_general | solution.py:202
  460.9 5.6 all-to-all-start.6
  466.5 25.3 %fusion.37.b_ref = f32[1376,1536]{1,0:T(8,128)} fusion(bf16[1536,4096]{1,0:T(8,128)(2,1)} %bitcast.1.refs_3_, bf16[1,4096,1376]{1,2,0:T(8,128)(2,1)} %param.24), kind=kOutput, calls=%fused_computation.43 | convolution fusion | flops 17314086912 | bytes 32309248 | tf_op jit(solution)/shard_map/fd,rd->fr/dot_general | solution.py:203
  491.9 25.9 %convolution_convert_fusion = bf16[1536,4096]{1,0:T(8,128)(2,1)} fusion(f32[1376,1536]{1,0:T(8,128)} %fusion.37.b_ref, f32[1376,1536]{1,0:T(8,128)} %fusion.25.a_ref, bf16[1,1376,4096]{2,1,0:T(8,128)(2,1)S(1)} %bitcast.189), kind=kOutput, calls=%fused_computation.4 | convolution fusion | flops 17333059584 | bytes 40763392 | tf_op jit(solution)/shard_map/fr,fd->rd/dot_general | solution.py:215
  517.8 87.7 %all-to-all-done.6 = bf16[8,192,4096]{2,1,0:T(8,128)(2,1)} async-done(((bf16[8,192,4096]{2,1,0:T(8,128)(2,1)}), bf16[8,192,4096]{2,1,0:T(8,128)(2,1)}, u32[]{:S(2)}, u32[]{:S(2)}) %all-to-all-start.6) | async-done | bytes 12582944 | tf_op jit(solution)/shard_map/all_to_all | solution.py:199
  605.5 5.5 all-to-all-start.5
  611.0 8.5 dynamic-slice_bitcast_fusion
  620.0 1.6 collective-permute-start.1
  621.9 29.4 %shard_map.188 = (bf16[1376,1536]{1,0:T(8,128)(2,1)}, bf16[1376,1536]{1,0:T(8,128)(2,1)}, bf16[1376,1536]{1,0:T(8,128)(2,1)}) custom-call(bf16[1536,4096]{1,0:T(8,128)(2,1)} %bitcast.17.q_ref.refs_4_, bf16[1376,4096]{1,0:T(8,128)(2,1)} %bitcast.184, f32[1376,1536]{1,0:T(8,128)} %fusion.25.a_ref, f32[1376,1536]{1,0:T(8,128)} %fusion.37.b_ref), custom_call_target="tpu_custom_call" | custom-call | flops 17314086912 | bytes 54755328 | tf_op jit(solution)/shard_map/pallas_call | solution.py:57
  651.4 26.1 %fusion.15 = f32[1536,4096]{1,0:T(8,128)} fusion(bf16[1376,1536]{1,0:T(8,128)(2,1)} %get-tuple-element.33.refs_1_, bf16[1,4096,1376]{1,2,0:T(8,128)(2,1)} %param.23), kind=kOutput, calls=%fused_computation.29 | convolution fusion | flops 17314086912 | bytes 40665088 | tf_op jit(solution)/shard_map/fr,fd->rd/dot_general | solution.py:225
  677.4 61.3 %shard_map.192 = (f32[1376,4096]{1,0:T(8,128)}, f32[1376,4096]{1,0:T(8,128)}, f32[1376,4096]{1,0:T(8,128)}) custom-call(bf16[1376,1536]{1,0:T(8,128)(2,1)} %get-tuple-element.45.refs_0_, bf16[1376,1536]{1,0:T(8,128)(2,1)} %get-tuple-element.33.refs_1_, bf16[1376,1536]{1,0:T(8,128)(2,1)} %get-tuple-element.34.refs_2_, bf16[1536,4096]{1,0:T(8,128)(2,1)} %bitcast.1.refs_3_, ...), custom_call_target="tpu_custom_call" | custom-call | flops 51942260736 | bytes 92798976 | tf_op jit(solution)/shard_map/pallas_call | solution.py:89
  738.7 11.8 all-to-all-done.5
  750.5 5.5 all-to-all-start.4
  756.1 29.5 %add_convert_fusion = bf16[1536,4096]{1,0:T(8,128)(2,1)} fusion(f32[1536,4096]{1,0:T(8,128)} %fusion.15, bf16[1376,1536]{1,0:T(8,128)(2,1)} %get-tuple-element.34.refs_2_, bf16[1,4096,1376]{1,2,0:T(8,128)(2,1)} %param.24), kind=kOutput, calls=%fused_computation.2 | convolution fusion | flops 17326669824 | bytes 53248000 | tf_op jit(solution)/shard_map/fr,fd->rd/dot_general | solution.py:226
  785.6 2.7 bitcast_dynamic-update-slice_fusion
  788.4 2.0 collective-permute-start.3
  790.4 11.8 multiply_convert_fusion.1
  802.2 2.8 constant_dynamic-update-slice_fusion.6
  805.0 2.5 collective-permute-start.5
  807.5 2.8 constant_dynamic-update-slice_fusion.5
  810.2 5.7 collective-permute-done.2
  815.9 2.3 collective-permute-start.6
  818.3 2.7 constant_dynamic-update-slice_fusion.4
  821.0 73.6 %collective-permute-done.3 = bf16[192,4096]{1,0:T(8,128)(2,1)S(1)} collective-permute-done((bf16[192,4096]{1,0:T(8,128)(2,1)S(1)}, bf16[192,4096]{1,0:T(8,128)(2,1)S(1)}, u32[]{:S(2)}, u32[]{:S(2)}) %collective-permute-start.3) | collective-permute-done | bytes 1572896 | tf_op jit(solution)/shard_map/ppermute | solution.py:222
  896.3 131.9 %collective-permute-done.4 = bf16[192,4096]{1,0:T(8,128)(2,1)S(1)} collective-permute-done((bf16[192,4096]{1,0:T(8,128)(2,1)S(1)}, bf16[192,4096]{1,0:T(8,128)(2,1)S(1)}, u32[]{:S(2)}, u32[]{:S(2)}) %collective-permute-start.4) | collective-permute-done | bytes 1572896 | tf_op jit(solution)/shard_map/ppermute | solution.py:222
  1032.1 12.3 fusion.66
  1044.6 17.1 %fusion.58 = (f32[512]{0:T(512)S(1)}, f32[512]{0:T(512)S(1)}, bf16[512,4096]{1,0:T(8,128)(2,1)}) fusion(bf16[512,4096]{1,0:T(8,128)(2,1)S(1)} %copy-done.6, f32[512,4096]{1,0:T(8,128)} %fusion.66, f32[512]{0:T(512)S(1)} %copy-done.43, f32[512]{0:T(512)S(1)} %copy-done.41, bf16[512,4096]{1,0:T(8,128)(2,1)S(1)} %copy-done.2, ...), kind=kOutput, calls=%fused_computation.57 | convolution fusion | flops 6466305024 | bytes 33564672 | tf_op jit(solution)/shard_map/dot_general | solution.py:255
  1064.3 5.8 all-to-all-start.2
  1070.1 25.5 %fusion.34.a_ref = f32[1376,1536]{1,0:T(8,128)} fusion(bf16[1536,4096]{1,0:T(8,128)(2,1)} %bitcast.43.refs_3_, bf16[1,4096,1376]{1,2,0:T(8,128)(2,1)} %param.23), kind=kOutput, calls=%fused_computation.42 | convolution fusion | flops 17314086912 | bytes 32309248 | tf_op jit(solution)/shard_map/fd,rd->fr/dot_general | solution.py:202
  1095.6 22.0 %fusion.46.b_ref = f32[1376,1536]{1,0:T(8,128)} fusion(bf16[1536,4096]{1,0:T(8,128)(2,1)} %bitcast.43.refs_3_, bf16[1,4096,1376]{1,2,0:T(8,128)(2,1)S(1)} %bitcast.181), kind=kOutput, calls=%fused_computation.46 | convolution fusion | flops 17314086912 | bytes 32309248 | tf_op jit(solution)/shard_map/fd,rd->fr/dot_general | solution.py:203
  1117.6 29.6 %shard_map.191 = (bf16[1376,1536]{1,0:T(8,128)(2,1)}, bf16[1376,1536]{1,0:T(8,128)(2,1)}, bf16[1376,1536]{1,0:T(8,128)(2,1)}) custom-call(bf16[1536,4096]{1,0:T(8,128)(2,1)} %bitcast.41.q_ref.refs_4_, bf16[1376,4096]{1,0:T(8,128)(2,1)} %bitcast.185, f32[1376,1536]{1,0:T(8,128)} %fusion.34.a_ref, f32[1376,1536]{1,0:T(8,128)} %fusion.46.b_ref), custom_call_target="tpu_custom_call" | custom-call | flops 17314086912 | bytes 54755328 | tf_op jit(solution)/shard_map/pallas_call | solution.py:57
  1147.2 65.5 %shard_map.193 = (f32[1376,4096]{1,0:T(8,128)}, f32[1376,4096]{1,0:T(8,128)}, f32[1376,4096]{1,0:T(8,128)}) custom-call(bf16[1376,1536]{1,0:T(8,128)(2,1)} %get-tuple-element.42.refs_0_, bf16[1376,1536]{1,0:T(8,128)(2,1)} %get-tuple-element.43.refs_1_, ...), custom_call_target="tpu_custom_call", output_to_operand_aliasing={{0}: (5, {}), {1}: (6, {}), {2}: (7, {})} | custom-call | flops 51942260736 | bytes 160432128 | tf_op jit(solution)/shard_map/pallas_call | solution.py:89
  1212.8 6.0 all-to-all-start.3
  1218.8 25.4 %fusion.31.a_ref = f32[1376,1536]{1,0:T(8,128)} fusion(bf16[1536,4096]{1,0:T(8,128)(2,1)} %bitcast.33.refs_3_, bf16[1,4096,1376]{1,2,0:T(8,128)(2,1)} %param.23), kind=kOutput, calls=%fused_computation.41 | convolution fusion | flops 17314086912 | bytes 32309248 | tf_op jit(solution)/shard_map/fd,rd->fr/dot_general | solution.py:202
  1244.3 21.9 %fusion.43.b_ref = f32[1376,1536]{1,0:T(8,128)} fusion(bf16[1536,4096]{1,0:T(8,128)(2,1)} %bitcast.33.refs_3_, bf16[1,4096,1376]{1,2,0:T(8,128)(2,1)S(1)} %bitcast.183), kind=kOutput, calls=%fused_computation.45 | convolution fusion | flops 17314086912 | bytes 32309248 | tf_op jit(solution)/shard_map/fd,rd->fr/dot_general | solution.py:203
  1266.3 10.1 fusion.76
  1276.6 6.1 fusion.54
  1283.5 83.5 %shard_map.196 = f32[32,16,128]{2,1,0:T(8,128)} custom-call(f32[32,16,128]{2,1,0:T(8,128)} %maximum_bitcast_fusion.x_ref), custom_call_target="tpu_custom_call" | custom-call | tf_op jit(solution)/shard_map/pallas_call | solution.py:142
  1367.0 1.6 fusion.107
  1370.1 9.3 fusion.60
  1379.4 29.6 %shard_map.190 = (bf16[1376,1536]{1,0:T(8,128)(2,1)}, bf16[1376,1536]{1,0:T(8,128)(2,1)}, bf16[1376,1536]{1,0:T(8,128)(2,1)}) custom-call(bf16[1536,4096]{1,0:T(8,128)(2,1)} %bitcast.31.q_ref.refs_4_, bf16[1376,4096]{1,0:T(8,128)(2,1)} %bitcast.186, f32[1376,1536]{1,0:T(8,128)} %fusion.31.a_ref, f32[1376,1536]{1,0:T(8,128)} %fusion.43.b_ref), custom_call_target="tpu_custom_call" | custom-call | flops 17314086912 | bytes 54755328 | tf_op jit(solution)/shard_map/pallas_call | solution.py:57
  1409.0 65.5 %shard_map.194 = (f32[1376,4096]{1,0:T(8,128)}, f32[1376,4096]{1,0:T(8,128)}, f32[1376,4096]{1,0:T(8,128)}) custom-call(bf16[1376,1536]{1,0:T(8,128)(2,1)} %get-tuple-element.39.refs_0_, bf16[1376,1536]{1,0:T(8,128)(2,1)} %get-tuple-element.40.refs_1_, ...), custom_call_target="tpu_custom_call", output_to_operand_aliasing={{0}: (5, {}), {1}: (6, {}), {2}: (7, {})} | custom-call | flops 51942260736 | bytes 160432128 | tf_op jit(solution)/shard_map/pallas_call | solution.py:89
  1474.5 25.5 %fusion.28.a_ref = f32[1376,1536]{1,0:T(8,128)} fusion(bf16[1536,4096]{1,0:T(8,128)(2,1)} %collective-permute-done.8.refs_3_, bf16[1,4096,1376]{1,2,0:T(8,128)(2,1)} %param.23), kind=kOutput, calls=%fused_computation.40 | convolution fusion | flops 17314086912 | bytes 32309248 | tf_op jit(solution)/shard_map/fd,rd->fr/dot_general | solution.py:202
  1500.0 25.2 %fusion.40.b_ref = f32[1376,1536]{1,0:T(8,128)} fusion(bf16[1536,4096]{1,0:T(8,128)(2,1)} %collective-permute-done.8.refs_3_, bf16[1,4096,1376]{1,2,0:T(8,128)(2,1)} %param.24), kind=kOutput, calls=%fused_computation.44 | convolution fusion | flops 17314086912 | bytes 32309248 | tf_op jit(solution)/shard_map/fd,rd->fr/dot_general | solution.py:203
  1525.3 29.8 %shard_map.189 = (bf16[1376,1536]{1,0:T(8,128)(2,1)}, bf16[1376,1536]{1,0:T(8,128)(2,1)}, bf16[1376,1536]{1,0:T(8,128)(2,1)}) custom-call(bf16[1536,4096]{1,0:T(8,128)(2,1)} %collective-permute-done.7.q_ref.refs_4_, bf16[1376,4096]{1,0:T(8,128)(2,1)} %bitcast.187, f32[1376,1536]{1,0:T(8,128)} %fusion.28.a_ref, f32[1376,1536]{1,0:T(8,128)} %fusion.40.b_ref), custom_call_target="tpu_custom_call" | custom-call | flops 17314086912 | bytes 54755328 | tf_op jit(solution)/shard_map/pallas_call | solution.py:57
  1555.1 65.5 %shard_map.195 = (f32[1376,4096]{1,0:T(8,128)}, f32[1376,4096]{1,0:T(8,128)}, f32[1376,4096]{1,0:T(8,128)}) custom-call(bf16[1376,1536]{1,0:T(8,128)(2,1)} %get-tuple-element.35.refs_0_, bf16[1376,1536]{1,0:T(8,128)(2,1)} %get-tuple-element.36.refs_1_, ...), custom_call_target="tpu_custom_call", output_to_operand_aliasing={{0}: (5, {}), {1}: (6, {}), {2}: (7, {})} | custom-call | flops 51942260736 | bytes 160432128 | tf_op jit(solution)/shard_map/pallas_call | solution.py:89
  (208 shorter events, 19.5 us)
Async XLA Ops:
  0.6 30.6 %copy-start = (bf16[4096,8]{0,1:T(8,128)(2,1)S(1)}, bf16[4096,8]{0,1:T(8,128)(2,1)}, u32[]{:S(2)}) copy-start(bf16[4096,8]{0,1:T(8,128)(2,1)} %param.22) | copy-start | bytes 196612
  21.6 13.1 copy-start.20
  21.6 13.7 copy-start.37
  21.6 145.2 %all-to-all-start = ((bf16[8,192,4096]{2,1,0:T(8,128)(2,1)}), bf16[8,192,4096]{2,1,0:T(8,128)(2,1)}, u32[]{:S(2)}, u32[]{:S(2)}) async-start(bf16[8,192,4096]{2,1,0:T(8,128)(2,1)} %bitcast.151), calls=%async_computation | async-start | bytes 25165824 | tf_op jit(solution)/shard_map/all_to_all | solution.py:199
  27.1 185.4 %collective-permute-start.11 = (bf16[512,4096]{1,0:T(8,128)(2,1)}, bf16[512,4096]{1,0:T(8,128)(2,1)}, u32[]{:S(2)}, u32[]{:S(2)}) collective-permute-start(bf16[512,4096]{1,0:T(8,128)(2,1)} %copy-done.4), channel_id=1, source_target_pairs={{0,16},{24,8},{8,24},{16,0},{1,17},{25,9},{9,25},{17,1},{2,18},{26... | collective-permute-start | bytes 12582920 | tf_op jit(solution)/shard_map/ppermute | solution.py:209
  34.8 181.8 %copy-start.40 = (f32[512]{0:T(512)}, f32[512]{0:T(512)S(1)}, u32[]{:S(2)}) copy-start(f32[512]{0:T(512)S(1)} %get-tuple-element.64) | copy-start | bytes 6148
  35.3 181.2 %copy-start.42 = (f32[512]{0:T(512)}, f32[512]{0:T(512)S(1)}, u32[]{:S(2)}) copy-start(f32[512]{0:T(512)S(1)} %select_reduce_fusion) | copy-start | bytes 6148
  166.8 294.1 %all-to-all-start.1 = ((bf16[8,192,4096]{2,1,0:T(8,128)(2,1)}), bf16[8,192,4096]{2,1,0:T(8,128)(2,1)}, u32[]{:S(2)}, u32[]{:S(2)}) async-start(bf16[8,192,4096]{2,1,0:T(8,128)(2,1)} %bitcast.145), calls=%async_computation.1 | async-start | bytes 25165824 | tf_op jit(solution)/shard_map/all_to_all | solution.py:199
  212.4 200.2 %collective-permute-start.12 = (bf16[512,4096]{1,0:T(8,128)(2,1)}, bf16[512,4096]{1,0:T(8,128)(2,1)}, u32[]{:S(2)}, u32[]{:S(2)}) collective-permute-start(bf16[512,4096]{1,0:T(8,128)(2,1)} %param.14), channel_id=1, source_target_pairs={{0,16},{24,8},{8,24},{16,0},{1,17},{25,9},{9,25},{17,1},{2,18},{26... | collective-permute-start | bytes 12582920 | tf_op jit(solution)/shard_map/ppermute | solution.py:210
  212.4 201.9 %collective-permute-start.14 = (bf16[512,4096]{1,0:T(8,128)(2,1)}, bf16[512,4096]{1,0:T(8,128)(2,1)}, u32[]{:S(2)}, u32[]{:S(2)}) collective-permute-start(bf16[512,4096]{1,0:T(8,128)(2,1)} %collective-permute-done.11), channel_id=1, source_target_pairs={{0,8},{8,0},{16,24},{24,16},{1,9},{9,1},{17,25},{25,17},{2,10},{10... | collective-permute-start | bytes 12582920 | tf_op jit(solution)/shard_map/ppermute | solution.py:230
  216.6 179.4 %collective-permute-start.9 = (f32[4,512]{1,0:T(4,128)S(1)}, f32[4,512]{1,0:T(4,128)S(1)}, u32[]{:S(2)}, u32[]{:S(2)}) collective-permute-start(f32[4,512]{1,0:T(4,128)S(1)} %pad_maximum_fusion), channel_id=1, source_target_pairs={{0,16},{24,8},{8,24},{16,0},{1,17},{25,9},{9,25},{17,1},{2,18},{26... | collective-permute-start | bytes 24584 | tf_op jit(solution)/shard_map/ppermute | solution.py:208
  395.9 3.7 collective-permute-start.10
  399.6 14.8 copy-start.59
  399.6 14.8 copy-start.61
  412.7 375.7 %collective-permute-start.13 = (bf16[512,4096]{1,0:T(8,128)(2,1)}, bf16[512,4096]{1,0:T(8,128)(2,1)}, u32[]{:S(2)}, u32[]{:S(2)}) collective-permute-start(bf16[512,4096]{1,0:T(8,128)(2,1)} %collective-permute-done.12), channel_id=1, source_target_pairs={{0,8},{8,0},{16,24},{24,16},{1,9},{9,1},{17,25},{25,17},{2,10},{10... | collective-permute-start | bytes 12582920 | tf_op jit(solution)/shard_map/ppermute | solution.py:231
  414.4 23.8 %slice-start = ((s8[11272192]{0:T(1024)(128)(4,1)}), s8[4194304]{0:T(1024)(128)(4,1)S(1)}, s32[]{:S(2)}) async-start(s8[11272192]{0:T(1024)(128)(4,1)} %bitcast.178), calls=%async_computation.7 | async-start | bytes 8388608
  414.4 23.8 %slice-start.1 = ((s8[11272192]{0:T(1024)(128)(4,1)}), s8[4194304]{0:T(1024)(128)(4,1)S(1)}, s32[]{:S(2)}) async-start(s8[11272192]{0:T(1024)(128)(4,1)} %bitcast.178), calls=%async_computation.8 | async-start | bytes 8388608
  460.9 30.9 %slice-start.9 = ((s8[11272192]{0:T(1024)(128)(4,1)}), s8[2883584]{0:T(1024)(128)(4,1)S(1)}, s32[]{:S(2)}) async-start(s8[11272192]{0:T(1024)(128)(4,1)} %bitcast.188), calls=%async_computation.16 | async-start | bytes 5767168
  460.9 144.6 %all-to-all-start.6 = ((bf16[8,192,4096]{2,1,0:T(8,128)(2,1)}), bf16[8,192,4096]{2,1,0:T(8,128)(2,1)}, u32[]{:S(2)}, u32[]{:S(2)}) async-start(bf16[8,192,4096]{2,1,0:T(8,128)(2,1)} %bitcast.150), calls=%async_computation.6 | async-start | bytes 25165824 | tf_op jit(solution)/shard_map/all_to_all | solution.py:199
  466.5 25.3 %slice-start.10 = ((s8[11272192]{0:T(1024)(128)(4,1)}), s8[4194304]{0:T(1024)(128)(4,1)S(1)}, s32[]{:S(2)}) async-start(s8[11272192]{0:T(1024)(128)(4,1)} %bitcast.188), calls=%async_computation.17 | async-start | bytes 8388608
  466.5 25.3 %slice-start.11 = ((s8[11272192]{0:T(1024)(128)(4,1)}), s8[4194304]{0:T(1024)(128)(4,1)S(1)}, s32[]{:S(2)}) async-start(s8[11272192]{0:T(1024)(128)(4,1)} %bitcast.188), calls=%async_computation.18 | async-start | bytes 8388608
  605.5 145.0 %all-to-all-start.5 = ((bf16[8,192,4096]{2,1,0:T(8,128)(2,1)}), bf16[8,192,4096]{2,1,0:T(8,128)(2,1)}, u32[]{:S(2)}, u32[]{:S(2)}) async-start(bf16[8,192,4096]{2,1,0:T(8,128)(2,1)} %bitcast.147), calls=%async_computation.5 | async-start | bytes 25165824 | tf_op jit(solution)/shard_map/all_to_all | solution.py:199
  619.5 182.7 %collective-permute-start = (bf16[192,4096]{1,0:T(8,128)(2,1)}, bf16[192,4096]{1,0:T(8,128)(2,1)}, u32[]{:S(2)}, u32[]{:S(2)}) collective-permute-start(bf16[192,4096]{1,0:T(8,128)(2,1)} %get-tuple-element.81), channel_id=1, source_target_pairs={{0,1},{1,0},{2,3},{3,2},{4,5},{5,4},{6,7},{7,6},{8,9},{9,8},{10,11... | collective-permute-start | bytes 4718600 | tf_op jit(solution)/shard_map/ppermute | solution.py:222
  620.0 185.0 %collective-permute-start.1 = (bf16[192,4096]{1,0:T(8,128)(2,1)}, bf16[192,4096]{1,0:T(8,128)(2,1)}, u32[]{:S(2)}, u32[]{:S(2)}) collective-permute-start(bf16[192,4096]{1,0:T(8,128)(2,1)} %get-tuple-element.80), channel_id=1, source_target_pairs={{0,2},{1,3},{2,0},{3,1},{4,6},{5,7},{6,4},{7,5},{8,10},{9,11},{10,... | collective-permute-start | bytes 4718600 | tf_op jit(solution)/shard_map/ppermute | solution.py:222
  621.6 194.3 %collective-permute-start.2 = (bf16[192,4096]{1,0:T(8,128)(2,1)}, bf16[192,4096]{1,0:T(8,128)(2,1)}, u32[]{:S(2)}, u32[]{:S(2)}) collective-permute-start(bf16[192,4096]{1,0:T(8,128)(2,1)} %get-tuple-element.79), channel_id=1, source_target_pairs={{0,3},{1,2},{2,1},{3,0},{4,7},{5,6},{6,5},{7,4},{8,11},{9,10},{10,... | collective-permute-start | bytes 4718600 | tf_op jit(solution)/shard_map/ppermute | solution.py:222
  621.6 903.7 %collective-permute-start.7 = (bf16[1536,4096]{1,0:T(8,128)(2,1)}, bf16[1536,4096]{1,0:T(8,128)(2,1)}, u32[]{:S(2)}, u32[]{:S(2)}) collective-permute-start(bf16[1536,4096]{1,0:T(8,128)(2,1)} %bitcast.17.q_ref.refs_4_), channel_id=1, source_target_pairs={{0,8},{8,0},{16,24},{24,16},{1,9},{9,1},{17,25},{25,17},{2,10},{10... | collective-permute-start | bytes 37748744 | tf_op jit(solution)/shard_map/ppermute | solution.py:233
  750.5 313.7 %all-to-all-start.4 = ((bf16[8,192,4096]{2,1,0:T(8,128)(2,1)}), bf16[8,192,4096]{2,1,0:T(8,128)(2,1)}, u32[]{:S(2)}, u32[]{:S(2)}) async-start(bf16[8,192,4096]{2,1,0:T(8,128)(2,1)} %bitcast.143), calls=%async_computation.4 | async-start | bytes 25165824 | tf_op jit(solution)/shard_map/all_to_all | solution.py:199
  756.1 32.3 %copy-start.10 = (bf16[192,4096]{1,0:T(8,128)(2,1)S(1)}, bf16[192,4096]{1,0:T(8,128)(2,1)}, u32[]{:S(2)}) copy-start(bf16[192,4096]{1,0:T(8,128)(2,1)} %get-tuple-element.78) | copy-start | bytes 4718596
  756.1 34.3 %copy-start.60 = (s32[1,512]{1,0:T(1,128)S(1)}, s32[1,512]{1,0:T(1,128)}, u32[]{:S(2)}) copy-start(s32[1,512]{1,0:T(1,128)} %copy-done.59) | copy-start | bytes 6148
  756.1 34.3 %copy-start.62 = (s32[1,512]{1,0:T(1,128)S(1)}, s32[1,512]{1,0:T(1,128)}, u32[]{:S(2)}) copy-start(s32[1,512]{1,0:T(1,128)} %copy-done.61) | copy-start | bytes 6148
  756.1 34.3 %copy-start.64 = (f32[1536]{0:T(1024)S(1)}, f32[1536]{0:T(1024)}, u32[]{:S(2)}) copy-start(f32[1536]{0:T(1024)} %add_reduce_fusion.1) | copy-start | bytes 18436
  788.3 13.9 copy-start.9
  788.3 16.7 %copy-start.8 = (bf16[192,4096]{1,0:T(8,128)(2,1)S(1)}, bf16[192,4096]{1,0:T(8,128)(2,1)}, u32[]{:S(2)}) copy-start(bf16[192,4096]{1,0:T(8,128)(2,1)} %get-tuple-element.76) | copy-start | bytes 4718596
  788.3 27.6 %copy-start.7 = (bf16[192,4096]{1,0:T(8,128)(2,1)S(1)}, bf16[192,4096]{1,0:T(8,128)(2,1)}, u32[]{:S(2)}) copy-start(bf16[192,4096]{1,0:T(8,128)(2,1)} %get-tuple-element.75) | copy-start | bytes 4718596
  788.4 106.2 %collective-permute-start.3 = (bf16[192,4096]{1,0:T(8,128)(2,1)S(1)}, bf16[192,4096]{1,0:T(8,128)(2,1)S(1)}, u32[]{:S(2)}, u32[]{:S(2)}) collective-permute-start(bf16[192,4096]{1,0:T(8,128)(2,1)S(1)} %copy-done.10), channel_id=1, source_target_pairs={{0,4},{1,5},{2,6},{3,7},{4,0},{5,1},{6,2},{7,3},{8,12},{9,13},{10,... | collective-permute-start | bytes 4718600 | tf_op jit(solution)/shard_map/ppermute | solution.py:222
  802.2 226.0 %collective-permute-start.4 = (bf16[192,4096]{1,0:T(8,128)(2,1)S(1)}, bf16[192,4096]{1,0:T(8,128)(2,1)S(1)}, u32[]{:S(2)}, u32[]{:S(2)}) collective-permute-start(bf16[192,4096]{1,0:T(8,128)(2,1)S(1)} %copy-done.9), channel_id=1, source_target_pairs={{0,5},{1,4},{2,7},{3,6},{4,1},{5,0},{6,3},{7,2},{8,13},{9,12},{10,... | collective-permute-start | bytes 4718600 | tf_op jit(solution)/shard_map/ppermute | solution.py:222
  805.0 224.5 %collective-permute-start.5 = (bf16[192,4096]{1,0:T(8,128)(2,1)S(1)}, bf16[192,4096]{1,0:T(8,128)(2,1)S(1)}, u32[]{:S(2)}, u32[]{:S(2)}) collective-permute-start(bf16[192,4096]{1,0:T(8,128)(2,1)S(1)} %copy-done.8), channel_id=1, source_target_pairs={{0,6},{1,7},{2,4},{3,5},{4,2},{5,3},{6,0},{7,1},{8,14},{9,15},{10,... | collective-permute-start | bytes 4718600 | tf_op jit(solution)/shard_map/ppermute | solution.py:222
  810.2 221.9 %copy-start.58 = (s32[512]{0:T(512)S(1)}, s32[512]{0:T(512)}, u32[]{:S(2)}) copy-start(s32[512]{0:T(512)} %get-tuple-element.96) | copy-start | bytes 6148
  815.9 214.9 %collective-permute-start.6 = (bf16[192,4096]{1,0:T(8,128)(2,1)S(1)}, bf16[192,4096]{1,0:T(8,128)(2,1)S(1)}, u32[]{:S(2)}, u32[]{:S(2)}) collective-permute-start(bf16[192,4096]{1,0:T(8,128)(2,1)S(1)} %copy-done.7), channel_id=1, source_target_pairs={{0,7},{1,6},{2,5},{3,4},{4,3},{5,2},{6,1},{7,0},{8,15},{9,14},{10,... | collective-permute-start | bytes 4718600 | tf_op jit(solution)/shard_map/ppermute | solution.py:222
  894.6 579.9 %collective-permute-start.8 = (bf16[1536,4096]{1,0:T(8,128)(2,1)}, bf16[1536,4096]{1,0:T(8,128)(2,1)}, u32[]{:S(2)}, u32[]{:S(2)}) collective-permute-start(bf16[1536,4096]{1,0:T(8,128)(2,1)} %bitcast.1.refs_3_), channel_id=1, source_target_pairs={{0,8},{8,0},{16,24},{24,16},{1,9},{9,1},{17,25},{25,17},{2,10},{10... | collective-permute-start | bytes 37748744 | tf_op jit(solution)/shard_map/ppermute | solution.py:232
  1032.1 12.3 copy-start.2
  1032.1 12.3 copy-start.6
  1032.1 12.3 copy-start.41
  1032.1 12.3 copy-start.43
  1032.1 12.3 copy-start.57
  1044.5 18.4 %copy-start.5 = (bf16[512,4096]{1,0:T(8,128)(2,1)S(1)}, bf16[512,4096]{1,0:T(8,128)(2,1)}, u32[]{:S(2)}) copy-start(bf16[512,4096]{1,0:T(8,128)(2,1)} %copy-done.4) | copy-start | bytes 12582916
  1044.5 18.4 %copy-start.13 = (f32[512,8]{0,1:T(8,128)S(1)}, f32[512,8]{0,1:T(8,128)}, u32[]{:S(2)}) copy-start(f32[512,8]{0,1:T(8,128)} %copy-done.12) | copy-start | bytes 49156
  1044.5 18.4 %copy-start.18 = (pred[512,8]{0,1:T(8,128)(4,1)S(1)}, pred[512,8]{0,1:T(8,128)(4,1)}, u32[]{:S(2)}) copy-start(pred[512,8]{0,1:T(8,128)(4,1)} %copy-done.17) | copy-start | bytes 12292
  1044.5 18.4 %copy-start.21 = (s32[512]{0:T(512)S(1)}, s32[512]{0:T(512)}, u32[]{:S(2)}) copy-start(s32[512]{0:T(512)} %param.15) | copy-start | bytes 6148
  1044.5 18.4 %copy-start.24 = (f32[512]{0:T(512)S(1)}, f32[512]{0:T(512)}, u32[]{:S(2)}) copy-start(f32[512]{0:T(512)} %copy-done.23) | copy-start | bytes 6148
  1044.5 18.4 %copy-start.27 = (f32[512]{0:T(512)S(1)}, f32[512]{0:T(512)}, u32[]{:S(2)}) copy-start(f32[512]{0:T(512)} %copy-done.26) | copy-start | bytes 6148
  1044.5 18.4 %copy-start.32 = (f32[512]{0:T(512)S(1)}, f32[512]{0:T(512)}, u32[]{:S(2)}) copy-start(f32[512]{0:T(512)} %copy-done.31) | copy-start | bytes 6148
  1044.6 18.4 %copy-start.35 = (f32[512]{0:T(512)S(1)}, f32[512]{0:T(512)}, u32[]{:S(2)}) copy-start(f32[512]{0:T(512)} %copy-done.34) | copy-start | bytes 6148
  1044.6 18.4 %copy-start.38 = (s32[512]{0:T(512)S(1)}, s32[512]{0:T(512)}, u32[]{:S(2)}) copy-start(s32[512]{0:T(512)} %param.16) | copy-start | bytes 6148
  1064.3 31.3 %slice-start.3 = ((s8[11272192]{0:T(1024)(128)(4,1)}), s8[2883584]{0:T(1024)(128)(4,1)S(1)}, s32[]{:S(2)}) async-start(s8[11272192]{0:T(1024)(128)(4,1)} %bitcast.180), calls=%async_computation.10 | async-start | bytes 5767168
  1064.3 148.5 %all-to-all-start.2 = ((bf16[8,192,4096]{2,1,0:T(8,128)(2,1)}), bf16[8,192,4096]{2,1,0:T(8,128)(2,1)}, u32[]{:S(2)}, u32[]{:S(2)}) async-start(bf16[8,192,4096]{2,1,0:T(8,128)(2,1)} %bitcast.146), calls=%async_computation.2 | async-start | bytes 25165824 | tf_op jit(solution)/shard_map/all_to_all | solution.py:199
  1070.1 25.5 %slice-start.4 = ((s8[11272192]{0:T(1024)(128)(4,1)}), s8[4194304]{0:T(1024)(128)(4,1)S(1)}, s32[]{:S(2)}) async-start(s8[11272192]{0:T(1024)(128)(4,1)} %bitcast.180), calls=%async_computation.11 | async-start | bytes 8388608
  1070.1 25.5 %slice-start.5 = ((s8[11272192]{0:T(1024)(128)(4,1)}), s8[4194304]{0:T(1024)(128)(4,1)S(1)}, s32[]{:S(2)}) async-start(s8[11272192]{0:T(1024)(128)(4,1)} %bitcast.180), calls=%async_computation.12 | async-start | bytes 8388608
  1212.8 31.5 %slice-start.6 = ((s8[11272192]{0:T(1024)(128)(4,1)}), s8[2883584]{0:T(1024)(128)(4,1)S(1)}, s32[]{:S(2)}) async-start(s8[11272192]{0:T(1024)(128)(4,1)} %bitcast.182), calls=%async_computation.13 | async-start | bytes 5767168
  1212.8 166.6 %all-to-all-start.3 = ((bf16[8,192,4096]{2,1,0:T(8,128)(2,1)}), bf16[8,192,4096]{2,1,0:T(8,128)(2,1)}, u32[]{:S(2)}, u32[]{:S(2)}) async-start(bf16[8,192,4096]{2,1,0:T(8,128)(2,1)} %bitcast.144), calls=%async_computation.3 | async-start | bytes 25165824 | tf_op jit(solution)/shard_map/all_to_all | solution.py:199
  1218.8 25.4 %slice-start.7 = ((s8[11272192]{0:T(1024)(128)(4,1)}), s8[4194304]{0:T(1024)(128)(4,1)S(1)}, s32[]{:S(2)}) async-start(s8[11272192]{0:T(1024)(128)(4,1)} %bitcast.182), calls=%async_computation.14 | async-start | bytes 8388608
  1218.8 25.4 %slice-start.8 = ((s8[11272192]{0:T(1024)(128)(4,1)}), s8[4194304]{0:T(1024)(128)(4,1)S(1)}, s32[]{:S(2)}) async-start(s8[11272192]{0:T(1024)(128)(4,1)} %bitcast.182), calls=%async_computation.15 | async-start | bytes 8388608
  1244.2 21.9 %copy-start.54 = (s32[512]{0:T(512)S(1)}, s32[512]{0:T(512)}, u32[]{:S(2)}) copy-start(s32[512]{0:T(512)} %copy-done.53) | copy-start | bytes 6148
  1244.2 21.9 %copy-start.56 = (s32[512]{0:T(512)S(1)}, s32[512]{0:T(512)}, u32[]{:S(2)}) copy-start(s32[512]{0:T(512)} %copy-done.55) | copy-start | bytes 6148
  (35 other events, 224.0 us)

commit v6 on v4

--- a/solution.py
+++ b/solution.py
@@ -13,13 +13,55 @@
 bf16 = jnp.bfloat16
 
 
-def layer_norm(x_rows, ln_weight, ln_bias):
-    x_float = x_rows.astype(f32)
-    centered = x_float - jnp.mean(x_float, axis=-1, keepdims=True)
-    inv_std = lax.rsqrt(jnp.mean(centered * centered, axis=-1, keepdims=True) + LN_EPS)
-    x_hat = centered * inv_std
-    hidden = (x_hat * ln_weight.astype(f32) + ln_bias.astype(f32)).astype(bf16)
-    return hidden, x_hat, inv_std
+def row_mean(value):
+    return jnp.mean(value, axis=-1, keepdims=True)
+
+
+def enter_kernel(x_ref, w_ref, b_ref, pos_ref, hid_ref, buf_ref, mean_ref, inv_ref, h_all, select):
+    step = pl.program_id(0)
+    n_tok, _ = x_ref.shape
+    chunk = n_tok // 8
+
+    @pl.when(step == 0)
+    def _():
+        def normalize(i, carry):
+            rows = pl.ds(pl.multiple_of(i * chunk, chunk), chunk)
+            x_float = x_ref[rows, :].astype(f32)
+            mean = row_mean(x_float)
+            centered = x_float - mean
+            inv_std = lax.rsqrt(row_mean(centered * centered) + LN_EPS)
+            h_all[rows, :] = (centered * inv_std * w_ref[...].astype(f32) + b_ref[...].astype(f32)).astype(bf16)
+            mean_ref[rows, :] = mean
+            inv_ref[rows, :] = inv_std
+            return carry
+
+        lax.fori_loop(0, n_tok // chunk, normalize, 0)
+        row_ids = lax.broadcasted_iota(jnp.int32, select.shape, 0)
+        hit = (row_ids == pos_ref[0:1, :]) | (row_ids == pos_ref[1:2, :])
+        select[...] = jnp.where(hit, 1.0, 0.0).astype(bf16)
+
+    n_cols = hid_ref.shape[1]
+    columns = pl.ds(pl.multiple_of(step * n_cols, n_cols), n_cols)
+    part = h_all[:, columns]
+    hid_ref[...] = part
+    buf_ref[...] = jnp.dot(select[...], part, preferred_element_type=f32).astype(bf16)
+
+
+def enter(x_rows, weight, bias, pos, n_rows):
+    n_tok, d_model = x_rows.shape
+    n_cols = d_model // 8
+    whole = lambda shape: pl.BlockSpec(shape, lambda j: (0, 0))
+    stat = jax.ShapeDtypeStruct((n_tok, 1), f32)
+    return pl.pallas_call(
+        enter_kernel, grid=(8,),
+        in_specs=[whole((n_tok, d_model)), whole((1, d_model)), whole((1, d_model)), whole(pos.shape)],
+        out_specs=[pl.BlockSpec((n_tok, n_cols), lambda j: (0, j)), pl.BlockSpec((n_rows, n_cols), lambda j: (0, j)),
+                   whole((n_tok, 1)), whole((n_tok, 1))],
+        out_shape=[jax.ShapeDtypeStruct((n_tok, d_model), bf16), jax.ShapeDtypeStruct((n_rows, d_model), bf16), stat, stat],
+        scratch_shapes=[pltpu.VMEM((n_tok, d_model), bf16), pltpu.VMEM((n_rows, n_tok), bf16)],
+        compiler_params=pltpu.CompilerParams(vmem_limit_bytes=48 * 1024 * 1024),
+        cost_estimate=pl.CostEstimate(flops=2 * n_rows * n_tok * d_model, bytes_accessed=4 * (n_tok + n_rows) * d_model, transcendentals=n_tok),
+    )(x_rows, weight[None], bias[None], pos)
 
 
 def layer_norm_back(grad_h, x_hat, inv_std, ln_weight):
@@ -52,13 +94,13 @@
 def inner_grad(q, wd, a_t, b_t):
     n_rows, d_model = q.shape
     width = wd.shape[0]
-    w_tile, r_tile = width // 2, n_rows // 3
-    tile = pl.BlockSpec((w_tile, r_tile), lambda i, j: (i, j))
+    r_tile = n_rows // 6
+    tile = pl.BlockSpec((width, r_tile), lambda j: (0, j))
     return pl.pallas_call(
         grad_kernel,
-        grid=(2, 3),
-        in_specs=[pl.BlockSpec((r_tile, d_model), lambda i, j: (j, 0)),
-                  pl.BlockSpec((w_tile, d_model), lambda i, j: (i, 0)),
+        grid=(n_rows // r_tile,),
+        in_specs=[pl.BlockSpec((r_tile, d_model), lambda j: (j, 0)),
+                  pl.BlockSpec((width, d_model), lambda j: (0, 0), pipeline_mode=pl.Buffered(1)),
                   tile, tile],
         out_specs=[tile] * 3,
         out_shape=[jax.ShapeDtypeStruct((width, n_rows), bf16)] * 3,
@@ -99,52 +141,54 @@
     )(u_t, da_t, db_t, h, q, *acc)
 
 
-def sum_kernel(n_dp, n_ep, x_ref, out_ref, parts, total, send_one, recv_one, send_two, recv_two):
-    n_dev = n_dp * n_ep
-    me = lax.axis_index('dp') * n_ep + lax.axis_index('ep')
-
-    def peer(step):
-        index = lax.rem(me + step, n_dev)
-        return index, (lax.div(index, n_ep), lax.rem(index, n_ep))
-
-    scatter = []
-    for step in range(1, n_dev):
-        index, device = peer(step)
-        scatter.append(pltpu.make_async_remote_copy(
-            src_ref=x_ref.at[index], dst_ref=parts.at[step], send_sem=send_one.at[step], recv_sem=recv_one.at[step],
-            device_id=device, device_id_type=pl.DeviceIdType.MESH))
-        scatter[-1].start()
-    acc = x_ref[me]
-    for step in range(1, n_dev):
-        scatter[step - 1].wait_recv()
-        acc += parts[step]
-    total[...] = acc
-    out_ref[me] = acc
-    for copy in scatter:
+def sum_kernel(n_dp, n_ep, x_ref, out_ref, from_ep, from_dp, send_one, recv_one, send_two, recv_two, send_three, recv_three):
+    dp, ep = lax.axis_index('dp'), lax.axis_index('ep')
+    barrier = pltpu.get_barrier_semaphore()
+    peers = [(dp, ep ^ k) for k in range(1, n_ep)] + [(dp ^ k, ep) for k in range(1, n_dp)]
+    for device in peers:
+        pl.semaphore_signal(barrier, inc=1, device_id=device, device_id_type=pl.DeviceIdType.MESH)
+    pl.semaphore_wait(barrier, len(peers))
+
+    def send(src, dst, device, send_sem, recv_sem):
+        copy = pltpu.make_async_remote_copy(src_ref=src, dst_ref=dst, send_sem=send_sem, recv_sem=recv_sem,
+                                            device_id=device, device_id_type=pl.DeviceIdType.MESH)
+        copy.start()
+        return copy
+
+    copies = [send(x_ref.at[ep ^ k], from_ep.at[k], (dp, ep ^ k), send_one.at[k], recv_one.at[k]) for k in range(1, n_ep)]
+    acc = x_ref[ep]
+    for k in range(1, n_ep):
+        copies[k - 1].wait_recv()
+        acc += from_ep[k]
+    from_dp[dp] = acc
+    for copy in copies:
         copy.wait_send()
-    gather = []
-    for step in range(1, n_dev):
-        index, device = peer(step)
-        gather.append(pltpu.make_async_remote_copy(
-            src_ref=total, dst_ref=out_ref.at[me], send_sem=send_two.at[step], recv_sem=recv_two.at[step],
-            device_id=device, device_id_type=pl.DeviceIdType.MESH))
-        gather[-1].start()
-    for copy in gather:
+    copies = [send(from_dp.at[dp], from_dp.at[dp], (dp ^ k, ep), send_two.at[k], recv_two.at[k]) for k in range(1, n_dp)]
+    for copy in copies:
         copy.wait_recv()
-    for copy in gather:
+    acc = from_dp[0]
+    for k in range(1, n_dp):
+        acc += from_dp[k]
+    out_ref[ep] = acc
+    for copy in copies:
         copy.wait_send()
+    copies = [send(out_ref.at[ep], out_ref.at[ep], (dp, ep ^ k), send_three.at[k], recv_three.at[k]) for k in range(1, n_ep)]
+    for copy in copies:
+        copy.wait_recv()
+    for copy in copies:
+        copy.wait_send()
 
 
 def sum_all(x, n_dp, n_ep):
-    n_dev = n_dp * n_ep
     vmem = pl.BlockSpec(memory_space=pltpu.VMEM)
-    dma = pltpu.SemaphoreType.DMA((n_dev,))
+    dma_ep, dma_dp = pltpu.SemaphoreType.DMA((n_ep,)), pltpu.SemaphoreType.DMA((n_dp,))
     return pl.pallas_call(
         functools.partial(sum_kernel, n_dp, n_ep),
         out_shape=jax.ShapeDtypeStruct(x.shape, f32),
         in_specs=[vmem], out_specs=vmem,
-        scratch_shapes=[pltpu.VMEM(x.shape, f32), pltpu.VMEM(x.shape[1:], f32), dma, dma, dma, dma],
-        compiler_params=pltpu.CompilerParams(has_side_effects=True),
+        scratch_shapes=[pltpu.VMEM(x.shape, f32), pltpu.VMEM((n_dp,) + x.shape[1:], f32),
+                        dma_ep, dma_ep, dma_dp, dma_dp, dma_ep, dma_ep],
+        compiler_params=pltpu.CompilerParams(collective_id=0, has_side_effects=True),
     )(x)
 
 
@@ -172,14 +216,14 @@
         wu_t = w_up[0].T
         wd = w_down[0]
 
-        hidden, x_hat, inv_std = layer_norm(tok_x, ln_weight, ln_bias)
+        pos_one = jnp.where(slot_first >= 0, exp_first * slot_cap + slot_first, -1)
+        pos_two = jnp.where(slot_second >= 0, exp_second * slot_cap + slot_second, -1)
+        hidden, h_buf, mean, inv_std = enter(tok_x, ln_weight, ln_bias, jnp.stack([pos_one, pos_two]), n_rows)
         logits = jnp.dot(hidden, router, preferred_element_type=f32)
         expert_ids = jnp.arange(n_exp)
         allowed = eligible > 0
         gate_one, prob_one, pick_one = masked_gate(logits, allowed, exp_first)
         gate_two, prob_two, pick_two = masked_gate(logits, allowed & (expert_ids[None, :] != exp_first[:, None]), exp_second)
-        pos_one = jnp.where(slot_first >= 0, exp_first * slot_cap + slot_first, -1)
-        pos_two = jnp.where(slot_second >= 0, exp_second * slot_cap + slot_second, -1)
         meta = jnp.stack([pos_one.astype(f32), pos_two.astype(f32), gate_one, gate_two])
         row_ids = jnp.arange(n_rows)
 
@@ -202,8 +246,6 @@
             return (jnp.einsum('fd,rd->fr', wg_t, h, preferred_element_type=f32),
                     jnp.einsum('fd,rd->fr', wu_t, h, preferred_element_type=f32))
 
-        own_meta = jnp.stack([pos_one.astype(f32), pos_two.astype(f32)])
-        h_buf = select_h(hidden, own_meta)
         h_own = swap(h_buf)
         m_f1 = lax.ppermute(meta, 'dp', outer + middle)
         h_f1 = lax.ppermute(hidden, 'dp', outer + middle)
@@ -252,17 +294,13 @@
         d_router = jnp.einsum('td,te->ed', hidden, d_logits, preferred_element_type=f32)
         grad_exp = jnp.dot(sel_one + sel_two, hid_back, preferred_element_type=f32)
         grad_h = jnp.einsum('te,de->td', d_logits, router, preferred_element_type=f32) + grad_exp
+        x_hat = (tok_x.astype(f32) - mean) * inv_std
         d_ln_weight = jnp.sum(grad_h * x_hat, axis=0)
         d_ln_bias = jnp.sum(grad_h, axis=0)
         dx_tok = (dy_float + layer_norm_back(grad_h, x_hat, inv_std, ln_weight)).astype(bf16)
-        n_dev = n_dp * n_ep
-
-        def all_sum(rows):
-            parts = rows.reshape(rows.shape[0], n_dev, d_model // n_dev).transpose(1, 0, 2)
-            return sum_all(parts, n_dp, n_ep).transpose(1, 0, 2).reshape(rows.shape)
-
-        d_router = all_sum(d_router).T
-        d_ln_weight, d_ln_bias = all_sum(jnp.stack([d_ln_weight, d_ln_bias]))
+        small = jnp.concatenate([d_router, d_ln_weight[None], d_ln_bias[None], jnp.zeros((6, d_model), f32)])
+        total = sum_all(small.reshape(16, n_ep, d_model // n_ep).transpose(1, 0, 2), n_dp, n_ep).transpose(1, 0, 2).reshape(16, d_model)
+        d_router, d_ln_weight, d_ln_bias = total[:n_exp].T, total[n_exp], total[n_exp + 1]
         return (out_tok, dx_tok, dwg.T[None], dwu.T[None], dwd[None], d_router, d_ln_weight, d_ln_bias)
 
     return jax.shard_map(

time: 1610 us -> 1580 us (0.981)
    pallas_call x2 -> x1, Pallas kernels: 108 us -> 80.2 us  [sum_all(): pl.pallas_call(functools.partial(sum_kernel, n_dp, n_ep), out_shape=jax.S...]
    pallas_call x4 -> x5, Pallas kernels: 120 us -> 135 us  [the longest x4 118 us: inner_grad(): pl.pallas_call(grad_kernel, grid=(n_rows // r_tile,), in_specs=[pl.BlockS...]
    dot_general x3 -> x2, matrix products: 33.1 us -> 21.3 us  [select_h(): jnp.dot((m1 | m2).astype(bf16), h, preferred_element_type=f32).astype(bf16)]
  transfers between devices with their start and end apart: 16 -> 16, of which waited for: 6 -> 6; matrix products, arithmetic and copies ran while one was open for 25% -> 26% of each run, Pallas kernels for 24% -> 23%
where the time goes in v6:
time: 1580 us; the launch traced here: 1570 us
  waiting for transfers between devices  625 us (40%)
  Pallas kernels  473 us (30%)
  matrix products  390 us (25%)
  starting transfers between devices  54.4 us (3%)
  other arithmetic  16.8 us (1%)
    all_to_all x8, waiting for transfers between devices, swap(): lax.all_to_all(buf.reshape(n_ep, slot_cap, d_model), 'ep', 0, 0, tiled=True)  266 us
    pallas_call x4, Pallas kernels, add_dw(): pl.pallas_call(functools.partial(dw_kernel, first), grid=(d_model // d_ti...  258 us
    ppermute x1, waiting for transfers between devices, local_step(): m_f1 = lax.ppermute(meta, 'dp', outer + middle)  181 us
    ppermute x1, waiting for transfers between devices, local_step(): m_f2 = lax.ppermute(m_f1, 'dp', near)  177 us
    pallas_call x4, Pallas kernels, inner_grad(): pl.pallas_call(grad_kernel, grid=(n_rows // r_tile,), in_specs=[pl.BlockS...  118 us
    dot_general x4, matrix products, pre(): jnp.einsum('fd,rd->fr', wg_t, h, preferred_element_type=f32)  102 us
    dot_general x4, matrix products, pre(): jnp.einsum('fd,rd->fr', wu_t, h, preferred_element_type=f32)  98.6 us
    pallas_call x1, Pallas kernels, sum_all(): pl.pallas_call(functools.partial(sum_kernel, n_dp, n_ep), out_shape=jax.S...  80.2 us
  transfers between devices with their start and end apart: 16, of which 6 were waited for; matrix products, arithmetic and copies ran while one was open for 26% of the time, Pallas kernels for 23%

profile of v6, /device:TPU:0, one launch (start us, length us, event | category | flops | bytes accessed | tf_op | source)
XLA Modules:
  0.0 1569.8 jit_solution(8016994508213394625)
XLA Ops:
  0.6 0.7 broadcast_in_dim.124.w_ref
  1.4 0.7 broadcast_in_dim.125.b_ref
  2.1 0.7 fusion.98
  2.8 0.7 fusion.99
  3.5 16.6 %shard_map.188 = (bf16[512,4096]{1,0:T(8,128)(2,1)S(1)}, bf16[1536,4096]{1,0:T(8,128)(2,1)}, f32[512,1]{1,0:T(8,128)S(1)}, f32[512,1]{1,0:T(8,128)S(1)}) custom-call(bf16[512,4096]{1,0:T(8,128)(2,1)} %x_ref.1, bf16[1,4096]{1,0:T(2,128)(2,1)S(1)} %broadcast_in_dim.124.w_ref, bf16[1,4096]{1,0:T(2,128)(2,1)S(1)} %broadcast_in_dim.125.b_ref, ...), custom_call_target="tpu_custom_call" | custom-call | flops 6442450944 | bytes 33554432 | tf_op jit(solution)/shard_map/pallas_call | solution.py:55
  20.1 2.0 copy-done.1
  22.1 5.5 all-to-all-start
  27.6 3.4 fusion.93
  31.8 0.7 add_reduce_fusion.2
  32.5 11.8 multiply_convert_fusion.2
  44.3 123.1 %all-to-all-done = bf16[8,192,4096]{2,1,0:T(8,128)(2,1)} async-done(((bf16[8,192,4096]{2,1,0:T(8,128)(2,1)}), bf16[8,192,4096]{2,1,0:T(8,128)(2,1)}, u32[]{:S(2)}, u32[]{:S(2)}) %all-to-all-start) | async-done | bytes 12582944 | tf_op jit(solution)/shard_map/all_to_all | solution.py:243
  167.3 5.3 all-to-all-start.2
  172.7 3.4 collective-permute-start.4
  176.2 181.4 %collective-permute-done.2 = f32[4,512]{1,0:T(4,128)S(1)} collective-permute-done((f32[4,512]{1,0:T(4,128)S(1)}, f32[4,512]{1,0:T(4,128)S(1)}, u32[]{:S(2)}, u32[]{:S(2)}) %collective-permute-start.2) | collective-permute-done | bytes 8224 | tf_op jit(solution)/shard_map/ppermute | solution.py:250
  357.6 2.0 copy-done.39
  359.6 9.6 convolution_convert_fusion.1
  369.2 5.9 all-to-all-start.7
  375.3 4.1 collective-permute-start.7
  380.0 0.7 reduce
  380.7 0.7 reduce.1
  381.4 0.7 pad.3.clone
  382.1 0.7 add_reduce_fusion
  382.8 176.8 %collective-permute-done.3 = f32[4,512]{1,0:T(4,128)S(1)} collective-permute-done((f32[4,512]{1,0:T(4,128)S(1)}, f32[4,512]{1,0:T(4,128)S(1)}, u32[]{:S(2)}, u32[]{:S(2)}) %collective-permute-start.3) | collective-permute-done | bytes 8224 | tf_op jit(solution)/shard_map/ppermute | solution.py:263
  559.6 1.3 add_reduce_fusion.1
  560.9 11.8 multiply_convert_fusion
  572.7 5.4 all-to-all-start.6
  578.1 11.7 convolution_convert_fusion.2
  589.8 2.0 collective-permute-start
  591.9 25.5 %fusion.19.a_ref = f32[1376,1536]{1,0:T(8,128)} fusion(bf16[1536,4096]{1,0:T(8,128)(2,1)} %bitcast.3.refs_3_, bf16[1,4096,1376]{1,2,0:T(8,128)(2,1)} %param.23), kind=kOutput, calls=%fused_computation.31 | convolution fusion | flops 17314086912 | bytes 32309248 | tf_op jit(solution)/shard_map/fd,rd->fr/dot_general | solution.py:246
  617.4 22.8 %fusion.31.b_ref = f32[1376,1536]{1,0:T(8,128)} fusion(bf16[1536,4096]{1,0:T(8,128)(2,1)} %bitcast.3.refs_3_, bf16[1,4096,1376]{1,2,0:T(8,128)(2,1)S(1)} %bitcast.166), kind=kOutput, calls=%fused_computation.35 | convolution fusion | flops 17314086912 | bytes 32309248 | tf_op jit(solution)/shard_map/fd,rd->fr/dot_general | solution.py:247
  640.2 29.4 %shard_map.189 = (bf16[1376,1536]{1,0:T(8,128)(2,1)}, bf16[1376,1536]{1,0:T(8,128)(2,1)}, bf16[1376,1536]{1,0:T(8,128)(2,1)}) custom-call(bf16[1536,4096]{1,0:T(8,128)(2,1)} %bitcast.12.q_ref.refs_4_, bf16[1376,4096]{1,0:T(8,128)(2,1)} %bitcast.167, f32[1376,1536]{1,0:T(8,128)} %fusion.19.a_ref, f32[1376,1536]{1,0:T(8,128)} %fusion.31.b_ref), custom_call_target="tpu_custom_call" | custom-call | flops 17314086912 | bytes 54755328 | tf_op jit(solution)/shard_map/pallas_call | solution.py:99
  669.6 47.5 %all-to-all-done.6 = bf16[8,192,4096]{2,1,0:T(8,128)(2,1)} async-done(((bf16[8,192,4096]{2,1,0:T(8,128)(2,1)}), bf16[8,192,4096]{2,1,0:T(8,128)(2,1)}, u32[]{:S(2)}, u32[]{:S(2)}) %all-to-all-start.6) | async-done | bytes 12582944 | tf_op jit(solution)/shard_map/all_to_all | solution.py:243
  717.0 5.5 all-to-all-start.5
  722.6 61.3 %shard_map.193 = (f32[1376,4096]{1,0:T(8,128)}, f32[1376,4096]{1,0:T(8,128)}, f32[1376,4096]{1,0:T(8,128)}) custom-call(bf16[1376,1536]{1,0:T(8,128)(2,1)} %get-tuple-element.53.refs_0_, bf16[1376,1536]{1,0:T(8,128)(2,1)} %get-tuple-element.40.refs_1_, bf16[1376,1536]{1,0:T(8,128)(2,1)} %get-tuple-element.41.refs_2_, bf16[1536,4096]{1,0:T(8,128)(2,1)} %bitcast.3.refs_3_, ...), custom_call_target="tpu_custom_call" | custom-call | flops 51942260736 | bytes 92798976 | tf_op jit(solution)/shard_map/pallas_call | solution.py:131
  783.9 28.7 %convolution_convert_fusion = bf16[1536,4096]{1,0:T(8,128)(2,1)} fusion(f32[1376,1536]{1,0:T(8,128)} %fusion.31.b_ref, f32[1376,1536]{1,0:T(8,128)} %fusion.19.a_ref, bf16[1,1376,4096]{2,1,0:T(8,128)(2,1)} %param.25), kind=kOutput, calls=%fused_computation.4 | convolution fusion | flops 17333059584 | bytes 40763392 | tf_op jit(solution)/shard_map/fr,fd->rd/dot_general | solution.py:257
  812.6 49.0 %all-to-all-done.5 = bf16[8,192,4096]{2,1,0:T(8,128)(2,1)} async-done(((bf16[8,192,4096]{2,1,0:T(8,128)(2,1)}), bf16[8,192,4096]{2,1,0:T(8,128)(2,1)}, u32[]{:S(2)}, u32[]{:S(2)}) %all-to-all-start.5) | async-done | bytes 12582944 | tf_op jit(solution)/shard_map/all_to_all | solution.py:243
  861.6 5.9 all-to-all-start.1
  867.5 26.4 %fusion.15 = f32[1536,4096]{1,0:T(8,128)} fusion(bf16[1376,1536]{1,0:T(8,128)(2,1)} %get-tuple-element.40.refs_1_, bf16[1,4096,1376]{1,2,0:T(8,128)(2,1)} %param.23), kind=kOutput, calls=%fused_computation.25 | convolution fusion | flops 17314086912 | bytes 40665088 | tf_op jit(solution)/shard_map/fr,fd->rd/dot_general | solution.py:259
  893.9 28.5 %add_convert_fusion = bf16[1536,4096]{1,0:T(8,128)(2,1)} fusion(f32[1536,4096]{1,0:T(8,128)} %fusion.15, bf16[1376,1536]{1,0:T(8,128)(2,1)S(1)} %bitcast.175, bf16[1,4096,1376]{1,2,0:T(8,128)(2,1)} %param.24), kind=kOutput, calls=%fused_computation.2 | convolution fusion | flops 17326669824 | bytes 53248000 | tf_op jit(solution)/shard_map/fr,fd->rd/dot_general | solution.py:260
  922.5 11.9 multiply_convert_fusion.1
  934.4 25.2 %fusion.28.a_ref = f32[1376,1536]{1,0:T(8,128)} fusion(bf16[1536,4096]{1,0:T(8,128)(2,1)} %bitcast.38.refs_3_, bf16[1,4096,1376]{1,2,0:T(8,128)(2,1)} %param.23), kind=kOutput, calls=%fused_computation.34 | convolution fusion | flops 17314086912 | bytes 32309248 | tf_op jit(solution)/shard_map/fd,rd->fr/dot_general | solution.py:246
  959.6 46.9 %all-to-all-done.1 = bf16[8,192,4096]{2,1,0:T(8,128)(2,1)} async-done(((bf16[8,192,4096]{2,1,0:T(8,128)(2,1)}), bf16[8,192,4096]{2,1,0:T(8,128)(2,1)}, u32[]{:S(2)}, u32[]{:S(2)}) %all-to-all-start.1) | async-done | bytes 12582944 | tf_op jit(solution)/shard_map/all_to_all | solution.py:243
  1006.4 5.5 all-to-all-start.3
  1012.0 25.3 %fusion.40.b_ref = f32[1376,1536]{1,0:T(8,128)} fusion(bf16[1536,4096]{1,0:T(8,128)(2,1)} %bitcast.38.refs_3_, bf16[1,4096,1376]{1,2,0:T(8,128)(2,1)} %param.24), kind=kOutput, calls=%fused_computation.38 | convolution fusion | flops 17314086912 | bytes 32309248 | tf_op jit(solution)/shard_map/fd,rd->fr/dot_general | solution.py:247
  1037.2 29.5 %shard_map.192 = (bf16[1376,1536]{1,0:T(8,128)(2,1)}, bf16[1376,1536]{1,0:T(8,128)(2,1)}, bf16[1376,1536]{1,0:T(8,128)(2,1)}) custom-call(bf16[1536,4096]{1,0:T(8,128)(2,1)} %bitcast.36.q_ref.refs_4_, bf16[1376,4096]{1,0:T(8,128)(2,1)} %bitcast.168, f32[1376,1536]{1,0:T(8,128)} %fusion.28.a_ref, f32[1376,1536]{1,0:T(8,128)} %fusion.40.b_ref), custom_call_target="tpu_custom_call" | custom-call | flops 17314086912 | bytes 54755328 | tf_op jit(solution)/shard_map/pallas_call | solution.py:99
  1066.7 25.6 %fusion.25.a_ref = f32[1376,1536]{1,0:T(8,128)} fusion(bf16[1536,4096]{1,0:T(8,128)(2,1)} %bitcast.28.refs_3_, bf16[1,4096,1376]{1,2,0:T(8,128)(2,1)} %param.23), kind=kOutput, calls=%fused_computation.33 | convolution fusion | flops 17314086912 | bytes 32309248 | tf_op jit(solution)/shard_map/fd,rd->fr/dot_general | solution.py:246
  1092.4 65.5 %shard_map.194 = (f32[1376,4096]{1,0:T(8,128)}, f32[1376,4096]{1,0:T(8,128)}, f32[1376,4096]{1,0:T(8,128)}) custom-call(bf16[1376,1536]{1,0:T(8,128)(2,1)} %get-tuple-element.50.refs_0_, bf16[1376,1536]{1,0:T(8,128)(2,1)} %get-tuple-element.51.refs_1_, ...), custom_call_target="tpu_custom_call", output_to_operand_aliasing={{0}: (5, {}), {1}: (6, {}), {2}: (7, {})} | custom-call | flops 51942260736 | bytes 160432128 | tf_op jit(solution)/shard_map/pallas_call | solution.py:131
  1157.9 5.5 all-to-all-start.4
  1163.4 25.2 %fusion.37.b_ref = f32[1376,1536]{1,0:T(8,128)} fusion(bf16[1536,4096]{1,0:T(8,128)(2,1)} %bitcast.28.refs_3_, bf16[1,4096,1376]{1,2,0:T(8,128)(2,1)} %param.24), kind=kOutput, calls=%fused_computation.37 | convolution fusion | flops 17314086912 | bytes 32309248 | tf_op jit(solution)/shard_map/fd,rd->fr/dot_general | solution.py:247
  1188.7 11.9 fusion.61
  1200.7 17.4 %fusion.53 = (f32[512]{0:T(512)S(1)}, f32[512]{0:T(512)S(1)}, bf16[512,4096]{1,0:T(8,128)(2,1)}) fusion(bf16[512,4096]{1,0:T(8,128)(2,1)S(1)} %copy-done.3, f32[512,4096]{1,0:T(8,128)} %fusion.61, f32[512]{0:T(512)S(1)} %copy-done.30, f32[512]{0:T(512)S(1)} %copy-done.24, bf16[512,4096]{1,0:T(8,128)(2,1)S(1)} %copy-done.4, bf16[1536,4096]{1,0:T(8,128)(2,1)} %bitcast.10, ...), kind=kOutput, calls=%fused_computation.50 | convolution fusion | flops 6466305024 | bytes 33564672 | tf_op jit(solution)/shard_map/dot_general | solution.py:287
  1218.9 9.8 fusion.70
  1228.8 6.0 fusion.52
  1234.8 0.8 maximum_bitcast_fusion.x_ref
  1235.6 80.2 %shard_map.197 = f32[8,16,512]{2,1,0:T(8,128)} custom-call(f32[8,16,512]{2,1,0:T(8,128)} %maximum_bitcast_fusion.x_ref), custom_call_target="tpu_custom_call" | custom-call | tf_op jit(solution)/shard_map/pallas_call | solution.py:185
  1315.8 1.6 slice.62
  1317.4 1.6 fusion.100
  1319.0 9.7 fusion.55
  1328.7 29.4 %shard_map.191 = (bf16[1376,1536]{1,0:T(8,128)(2,1)}, bf16[1376,1536]{1,0:T(8,128)(2,1)}, bf16[1376,1536]{1,0:T(8,128)(2,1)}) custom-call(bf16[1536,4096]{1,0:T(8,128)(2,1)} %bitcast.26.q_ref.refs_4_, bf16[1376,4096]{1,0:T(8,128)(2,1)} %bitcast.169, f32[1376,1536]{1,0:T(8,128)} %fusion.25.a_ref, f32[1376,1536]{1,0:T(8,128)} %fusion.37.b_ref), custom_call_target="tpu_custom_call" | custom-call | flops 17314086912 | bytes 54755328 | tf_op jit(solution)/shard_map/pallas_call | solution.py:99
  1358.0 65.5 %shard_map.195 = (f32[1376,4096]{1,0:T(8,128)}, f32[1376,4096]{1,0:T(8,128)}, f32[1376,4096]{1,0:T(8,128)}) custom-call(bf16[1376,1536]{1,0:T(8,128)(2,1)} %get-tuple-element.47.refs_0_, bf16[1376,1536]{1,0:T(8,128)(2,1)} %get-tuple-element.48.refs_1_, ...), custom_call_target="tpu_custom_call", output_to_operand_aliasing={{0}: (5, {}), {1}: (6, {}), {2}: (7, {})} | custom-call | flops 51942260736 | bytes 160432128 | tf_op jit(solution)/shard_map/pallas_call | solution.py:131
  1423.6 25.5 %fusion.22.a_ref = f32[1376,1536]{1,0:T(8,128)} fusion(bf16[1536,4096]{1,0:T(8,128)(2,1)} %collective-permute-done.1.refs_3_, bf16[1,4096,1376]{1,2,0:T(8,128)(2,1)} %param.23), kind=kOutput, calls=%fused_computation.32 | convolution fusion | flops 17314086912 | bytes 32309248 | tf_op jit(solution)/shard_map/fd,rd->fr/dot_general | solution.py:246
  1449.1 25.3 %fusion.34.b_ref = f32[1376,1536]{1,0:T(8,128)} fusion(bf16[1536,4096]{1,0:T(8,128)(2,1)} %collective-permute-done.1.refs_3_, bf16[1,4096,1376]{1,2,0:T(8,128)(2,1)} %param.24), kind=kOutput, calls=%fused_computation.36 | convolution fusion | flops 17314086912 | bytes 32309248 | tf_op jit(solution)/shard_map/fd,rd->fr/dot_general | solution.py:247
  1474.3 29.7 %shard_map.190 = (bf16[1376,1536]{1,0:T(8,128)(2,1)}, bf16[1376,1536]{1,0:T(8,128)(2,1)}, bf16[1376,1536]{1,0:T(8,128)(2,1)}) custom-call(bf16[1536,4096]{1,0:T(8,128)(2,1)} %collective-permute-done.q_ref.refs_4_, bf16[1376,4096]{1,0:T(8,128)(2,1)} %bitcast.170, f32[1376,1536]{1,0:T(8,128)} %fusion.22.a_ref, f32[1376,1536]{1,0:T(8,128)} %fusion.34.b_ref), custom_call_target="tpu_custom_call" | custom-call | flops 17314086912 | bytes 54755328 | tf_op jit(solution)/shard_map/pallas_call | solution.py:99
  1504.1 65.5 %shard_map.196 = (f32[1376,4096]{1,0:T(8,128)}, f32[1376,4096]{1,0:T(8,128)}, f32[1376,4096]{1,0:T(8,128)}) custom-call(bf16[1376,1536]{1,0:T(8,128)(2,1)} %get-tuple-element.43.refs_0_, bf16[1376,1536]{1,0:T(8,128)(2,1)} %get-tuple-element.44.refs_1_, ...), custom_call_target="tpu_custom_call", output_to_operand_aliasing={{0}: (5, {}), {1}: (6, {}), {2}: (7, {})} | custom-call | flops 51942260736 | bytes 160432128 | tf_op jit(solution)/shard_map/pallas_call | solution.py:131
  (122 shorter events, 2.4 us)
Async XLA Ops:
  0.6 27.0 %copy-start = (bf16[4096,8]{0,1:T(8,128)(2,1)S(1)}, bf16[4096,8]{0,1:T(8,128)(2,1)}, u32[]{:S(2)}) copy-start(bf16[4096,8]{0,1:T(8,128)(2,1)} %param.22) | copy-start | bytes 196612
  2.8 28.9 %copy-start.25 = (s32[512]{0:T(512)}, s32[512]{0:T(512)S(1)}, u32[]{:S(2)}) copy-start(s32[512]{0:T(512)S(1)} %get-tuple-element.77) | copy-start | bytes 6148
  3.5 28.2 %copy-start.27 = (s32[512]{0:T(512)}, s32[512]{0:T(512)S(1)}, u32[]{:S(2)}) copy-start(s32[512]{0:T(512)S(1)} %get-tuple-element.79) | copy-start | bytes 6148
  20.1 2.0 copy-start.1
  22.1 5.5 copy-start.31
  22.1 9.0 copy-start.10
  22.1 9.5 copy-start.21
  22.1 145.2 %all-to-all-start = ((bf16[8,192,4096]{2,1,0:T(8,128)(2,1)}), bf16[8,192,4096]{2,1,0:T(8,128)(2,1)}, u32[]{:S(2)}, u32[]{:S(2)}) async-start(bf16[8,192,4096]{2,1,0:T(8,128)(2,1)} %bitcast.131), calls=%async_computation | async-start | bytes 25165824 | tf_op jit(solution)/shard_map/all_to_all | solution.py:243
  31.0 0.6 copy-start.5
  31.0 0.7 copy-start.7
  31.1 0.7 copy-start.12
  31.1 0.6 copy-start.14
  31.1 0.6 copy-start.17
  31.2 0.6 copy-start.19
  31.2 144.9 %copy-start.23 = (f32[512]{0:T(512)}, f32[512]{0:T(512)S(1)}, u32[]{:S(2)}) copy-start(f32[512]{0:T(512)S(1)} %get-tuple-element.72) | copy-start | bytes 6148
  31.7 144.4 %copy-start.29 = (f32[512]{0:T(512)}, f32[512]{0:T(512)S(1)}, u32[]{:S(2)}) copy-start(f32[512]{0:T(512)S(1)} %select_reduce_fusion) | copy-start | bytes 6148
  167.3 201.9 %all-to-all-start.2 = ((bf16[8,192,4096]{2,1,0:T(8,128)(2,1)}), bf16[8,192,4096]{2,1,0:T(8,128)(2,1)}, u32[]{:S(2)}, u32[]{:S(2)}) async-start(bf16[8,192,4096]{2,1,0:T(8,128)(2,1)} %bitcast.130), calls=%async_computation.2 | async-start | bytes 25165824 | tf_op jit(solution)/shard_map/all_to_all | solution.py:243
  172.7 184.9 %collective-permute-start.4 = (bf16[512,4096]{1,0:T(8,128)(2,1)}, bf16[512,4096]{1,0:T(8,128)(2,1)S(1)}, u32[]{:S(2)}, u32[]{:S(2)}) collective-permute-start(bf16[512,4096]{1,0:T(8,128)(2,1)} %copy-done.1), channel_id=1, source_target_pairs={{0,16},{24,8},{8,24},{16,0},{1,17},{25,9},{9,25},{17,1},{2,18},{26... | collective-permute-start | bytes 12582920 | tf_op jit(solution)/shard_map/ppermute | solution.py:251
  176.1 181.5 %collective-permute-start.2 = (f32[4,512]{1,0:T(4,128)S(1)}, f32[4,512]{1,0:T(4,128)S(1)}, u32[]{:S(2)}, u32[]{:S(2)}) collective-permute-start(f32[4,512]{1,0:T(4,128)S(1)} %pad_maximum_fusion), channel_id=1, source_target_pairs={{0,16},{24,8},{8,24},{16,0},{1,17},{25,9},{9,25},{17,1},{2,18},{26... | collective-permute-start | bytes 24584 | tf_op jit(solution)/shard_map/ppermute | solution.py:250
  357.6 2.0 copy-start.39
  369.2 10.1 copy-start.16
  369.2 203.4 %all-to-all-start.7 = ((bf16[8,192,4096]{2,1,0:T(8,128)(2,1)}), bf16[8,192,4096]{2,1,0:T(8,128)(2,1)}, u32[]{:S(2)}, u32[]{:S(2)}) async-start(bf16[8,192,4096]{2,1,0:T(8,128)(2,1)} %bitcast.128), calls=%async_computation.7 | async-start | bytes 25165824 | tf_op jit(solution)/shard_map/all_to_all | solution.py:243
  375.2 185.7 %collective-permute-start.5 = (bf16[512,4096]{1,0:T(8,128)(2,1)}, bf16[512,4096]{1,0:T(8,128)(2,1)}, u32[]{:S(2)}, u32[]{:S(2)}) collective-permute-start(bf16[512,4096]{1,0:T(8,128)(2,1)} %param.14), channel_id=1, source_target_pairs={{0,16},{24,8},{8,24},{16,0},{1,17},{25,9},{9,25},{17,1},{2,18},{26... | collective-permute-start | bytes 12582920 | tf_op jit(solution)/shard_map/ppermute | solution.py:252
  375.3 202.8 %collective-permute-start.7 = (bf16[512,4096]{1,0:T(8,128)(2,1)}, bf16[512,4096]{1,0:T(8,128)(2,1)}, u32[]{:S(2)}, u32[]{:S(2)}) collective-permute-start(bf16[512,4096]{1,0:T(8,128)(2,1)} %copy-done.39), channel_id=1, source_target_pairs={{0,8},{8,0},{16,24},{24,16},{1,9},{9,1},{17,25},{25,17},{2,10},{10... | collective-permute-start | bytes 12582920 | tf_op jit(solution)/shard_map/ppermute | solution.py:264
  382.1 177.5 %collective-permute-start.3 = (f32[4,512]{1,0:T(4,128)S(1)}, f32[4,512]{1,0:T(4,128)S(1)}, u32[]{:S(2)}, u32[]{:S(2)}) collective-permute-start(f32[4,512]{1,0:T(4,128)S(1)} %collective-permute-done.2), channel_id=1, source_target_pairs={{0,8},{8,0},{16,24},{24,16},{1,9},{9,1},{17,25},{25,17},{2,10},{10... | collective-permute-start | bytes 24584 | tf_op jit(solution)/shard_map/ppermute | solution.py:263
  559.5 18.5 %copy-start.34 = (s32[1,512]{1,0:T(1,128)}, s32[1,512]{1,0:T(1,128)S(1)}, u32[]{:S(2)}) copy-start(s32[1,512]{1,0:T(1,128)S(1)} %get-tuple-element.89) | copy-start | bytes 6148
  559.5 18.5 %copy-start.36 = (s32[1,512]{1,0:T(1,128)}, s32[1,512]{1,0:T(1,128)S(1)}, u32[]{:S(2)}) copy-start(s32[1,512]{1,0:T(1,128)S(1)} %get-tuple-element.91) | copy-start | bytes 6148
  560.9 361.6 %collective-permute-start.6 = (bf16[512,4096]{1,0:T(8,128)(2,1)}, bf16[512,4096]{1,0:T(8,128)(2,1)}, u32[]{:S(2)}, u32[]{:S(2)}) collective-permute-start(bf16[512,4096]{1,0:T(8,128)(2,1)} %collective-permute-done.5), channel_id=1, source_target_pairs={{0,8},{8,0},{16,24},{24,16},{1,9},{9,1},{17,25},{25,17},{2,10},{10... | collective-permute-start | bytes 12582920 | tf_op jit(solution)/shard_map/ppermute | solution.py:265
  572.7 144.4 %all-to-all-start.6 = ((bf16[8,192,4096]{2,1,0:T(8,128)(2,1)}), bf16[8,192,4096]{2,1,0:T(8,128)(2,1)}, u32[]{:S(2)}, u32[]{:S(2)}) async-start(bf16[8,192,4096]{2,1,0:T(8,128)(2,1)} %bitcast.133), calls=%async_computation.6 | async-start | bytes 25165824 | tf_op jit(solution)/shard_map/all_to_all | solution.py:243
  589.8 884.6 %collective-permute-start = (bf16[1536,4096]{1,0:T(8,128)(2,1)}, bf16[1536,4096]{1,0:T(8,128)(2,1)}, u32[]{:S(2)}, u32[]{:S(2)}) collective-permute-start(bf16[1536,4096]{1,0:T(8,128)(2,1)} %bitcast.12.q_ref.refs_4_), channel_id=1, source_target_pairs={{0,8},{8,0},{16,24},{24,16},{1,9},{9,1},{17,25},{25,17},{2,10},{10... | collective-permute-start | bytes 37748744 | tf_op jit(solution)/shard_map/ppermute | solution.py:267
  591.8 25.5 %slice-start = ((s8[11272192]{0:T(1024)(128)(4,1)}), s8[4194304]{0:T(1024)(128)(4,1)S(1)}, s32[]{:S(2)}) async-start(s8[11272192]{0:T(1024)(128)(4,1)} %bitcast.165), calls=%async_computation.8 | async-start | bytes 8388608
  591.8 25.5 %slice-start.1 = ((s8[11272192]{0:T(1024)(128)(4,1)}), s8[4194304]{0:T(1024)(128)(4,1)S(1)}, s32[]{:S(2)}) async-start(s8[11272192]{0:T(1024)(128)(4,1)} %bitcast.165), calls=%async_computation.9 | async-start | bytes 8388608
  591.8 25.5 %slice-start.2 = ((s8[11272192]{0:T(1024)(128)(4,1)}), s8[2883584]{0:T(1024)(128)(4,1)S(1)}, s32[]{:S(2)}) async-start(s8[11272192]{0:T(1024)(128)(4,1)} %bitcast.165), calls=%async_computation.10 | async-start | bytes 5767168
  591.8 831.8 %collective-permute-start.1 = (bf16[1536,4096]{1,0:T(8,128)(2,1)}, bf16[1536,4096]{1,0:T(8,128)(2,1)}, u32[]{:S(2)}, u32[]{:S(2)}) collective-permute-start(bf16[1536,4096]{1,0:T(8,128)(2,1)} %bitcast.3.refs_3_), channel_id=1, source_target_pairs={{0,8},{8,0},{16,24},{24,16},{1,9},{9,1},{17,25},{25,17},{2,10},{10... | collective-permute-start | bytes 37748744 | tf_op jit(solution)/shard_map/ppermute | solution.py:266
  717.0 144.5 %all-to-all-start.5 = ((bf16[8,192,4096]{2,1,0:T(8,128)(2,1)}), bf16[8,192,4096]{2,1,0:T(8,128)(2,1)}, u32[]{:S(2)}, u32[]{:S(2)}) async-start(bf16[8,192,4096]{2,1,0:T(8,128)(2,1)} %bitcast.132), calls=%async_computation.5 | async-start | bytes 25165824 | tf_op jit(solution)/shard_map/all_to_all | solution.py:243
  861.6 32.3 %slice-start.3 = ((s8[4227072]{0:T(1024)(128)(4,1)}), s8[32768]{0:T(1024)(128)(4,1)S(1)}, s32[]{:S(2)}) async-start(s8[4227072]{0:T(1024)(128)(4,1)} %bitcast.174), calls=%async_computation.11 | async-start | bytes 65536
  861.6 144.9 %all-to-all-start.1 = ((bf16[8,192,4096]{2,1,0:T(8,128)(2,1)}), bf16[8,192,4096]{2,1,0:T(8,128)(2,1)}, u32[]{:S(2)}, u32[]{:S(2)}) async-start(bf16[8,192,4096]{2,1,0:T(8,128)(2,1)} %bitcast.134), calls=%async_computation.1 | async-start | bytes 25165824 | tf_op jit(solution)/shard_map/all_to_all | solution.py:243
  867.5 26.5 %slice-start.4 = ((s8[4227072]{0:T(1024)(128)(4,1)}), s8[4194304]{0:T(1024)(128)(4,1)S(1)}, s32[]{:S(2)}) async-start(s8[4227072]{0:T(1024)(128)(4,1)} %bitcast.174), calls=%async_computation.12 | async-start | bytes 8388608
  893.9 28.5 %copy-start.35 = (s32[1,512]{1,0:T(1,128)S(1)}, s32[1,512]{1,0:T(1,128)}, u32[]{:S(2)}) copy-start(s32[1,512]{1,0:T(1,128)} %copy-done.34) | copy-start | bytes 6148
  893.9 28.5 %copy-start.37 = (s32[1,512]{1,0:T(1,128)S(1)}, s32[1,512]{1,0:T(1,128)}, u32[]{:S(2)}) copy-start(s32[1,512]{1,0:T(1,128)} %copy-done.36) | copy-start | bytes 6148
  893.9 28.5 %copy-start.40 = (f32[1536]{0:T(1024)S(1)}, f32[1536]{0:T(1024)}, u32[]{:S(2)}) copy-start(f32[1536]{0:T(1024)} %add_reduce_fusion.1) | copy-start | bytes 18436
  1006.4 151.5 %all-to-all-start.3 = ((bf16[8,192,4096]{2,1,0:T(8,128)(2,1)}), bf16[8,192,4096]{2,1,0:T(8,128)(2,1)}, u32[]{:S(2)}, u32[]{:S(2)}) async-start(bf16[8,192,4096]{2,1,0:T(8,128)(2,1)} %bitcast.129), calls=%async_computation.3 | async-start | bytes 25165824 | tf_op jit(solution)/shard_map/all_to_all | solution.py:243
  1157.9 170.8 %all-to-all-start.4 = ((bf16[8,192,4096]{2,1,0:T(8,128)(2,1)}), bf16[8,192,4096]{2,1,0:T(8,128)(2,1)}, u32[]{:S(2)}, u32[]{:S(2)}) async-start(bf16[8,192,4096]{2,1,0:T(8,128)(2,1)} %bitcast.127), calls=%async_computation.4 | async-start | bytes 25165824 | tf_op jit(solution)/shard_map/all_to_all | solution.py:243
  1163.4 25.2 %copy-start.28 = (s32[512]{0:T(512)S(1)}, s32[512]{0:T(512)}, u32[]{:S(2)}) copy-start(s32[512]{0:T(512)} %copy-done.27) | copy-start | bytes 6148
  1188.7 11.9 copy-start.3
  1188.7 11.9 copy-start.4
  1188.7 11.9 copy-start.24
  1188.7 11.9 copy-start.26
  1188.7 11.9 copy-start.30
  1200.6 17.5 %copy-start.2 = (bf16[512,4096]{1,0:T(8,128)(2,1)S(1)}, bf16[512,4096]{1,0:T(8,128)(2,1)}, u32[]{:S(2)}) copy-start(bf16[512,4096]{1,0:T(8,128)(2,1)} %copy-done.1) | copy-start | bytes 12582916
  1200.7 17.5 %copy-start.6 = (f32[512,8]{0,1:T(8,128)S(1)}, f32[512,8]{0,1:T(8,128)}, u32[]{:S(2)}) copy-start(f32[512,8]{0,1:T(8,128)} %copy-done.5) | copy-start | bytes 49156
  1200.7 17.5 %copy-start.8 = (pred[512,8]{0,1:T(8,128)(4,1)S(1)}, pred[512,8]{0,1:T(8,128)(4,1)}, u32[]{:S(2)}) copy-start(pred[512,8]{0,1:T(8,128)(4,1)} %copy-done.7) | copy-start | bytes 12292
  1200.7 17.5 %copy-start.11 = (s32[512]{0:T(512)S(1)}, s32[512]{0:T(512)}, u32[]{:S(2)}) copy-start(s32[512]{0:T(512)} %param.15) | copy-start | bytes 6148
  1200.7 17.5 %copy-start.13 = (f32[512]{0:T(512)S(1)}, f32[512]{0:T(512)}, u32[]{:S(2)}) copy-start(f32[512]{0:T(512)} %copy-done.12) | copy-start | bytes 6148
  1200.7 17.5 %copy-start.15 = (f32[512]{0:T(512)S(1)}, f32[512]{0:T(512)}, u32[]{:S(2)}) copy-start(f32[512]{0:T(512)} %copy-done.14) | copy-start | bytes 6148
  1200.7 17.5 %copy-start.18 = (f32[512]{0:T(512)S(1)}, f32[512]{0:T(512)}, u32[]{:S(2)}) copy-start(f32[512]{0:T(512)} %copy-done.17) | copy-start | bytes 6148
  1200.7 17.5 %copy-start.20 = (f32[512]{0:T(512)S(1)}, f32[512]{0:T(512)}, u32[]{:S(2)}) copy-start(f32[512]{0:T(512)} %copy-done.19) | copy-start | bytes 6148
  1200.7 17.5 %copy-start.22 = (s32[512]{0:T(512)S(1)}, s32[512]{0:T(512)}, u32[]{:S(2)}) copy-start(s32[512]{0:T(512)} %param.16) | copy-start | bytes 6148
  1218.9 9.8 copy-start.9
  1218.9 9.9 copy-start.32
  1218.9 9.9 copy-start.33
  1228.8 6.0 copy-start.38

commit v7 on v6

--- a/solution.py
+++ b/solution.py
@@ -13,55 +13,13 @@
 bf16 = jnp.bfloat16
 
 
-def row_mean(value):
-    return jnp.mean(value, axis=-1, keepdims=True)
-
-
-def enter_kernel(x_ref, w_ref, b_ref, pos_ref, hid_ref, buf_ref, mean_ref, inv_ref, h_all, select):
-    step = pl.program_id(0)
-    n_tok, _ = x_ref.shape
-    chunk = n_tok // 8
-
-    @pl.when(step == 0)
-    def _():
-        def normalize(i, carry):
-            rows = pl.ds(pl.multiple_of(i * chunk, chunk), chunk)
-            x_float = x_ref[rows, :].astype(f32)
-            mean = row_mean(x_float)
-            centered = x_float - mean
-            inv_std = lax.rsqrt(row_mean(centered * centered) + LN_EPS)
-            h_all[rows, :] = (centered * inv_std * w_ref[...].astype(f32) + b_ref[...].astype(f32)).astype(bf16)
-            mean_ref[rows, :] = mean
-            inv_ref[rows, :] = inv_std
-            return carry
-
-        lax.fori_loop(0, n_tok // chunk, normalize, 0)
-        row_ids = lax.broadcasted_iota(jnp.int32, select.shape, 0)
-        hit = (row_ids == pos_ref[0:1, :]) | (row_ids == pos_ref[1:2, :])
-        select[...] = jnp.where(hit, 1.0, 0.0).astype(bf16)
-
-    n_cols = hid_ref.shape[1]
-    columns = pl.ds(pl.multiple_of(step * n_cols, n_cols), n_cols)
-    part = h_all[:, columns]
-    hid_ref[...] = part
-    buf_ref[...] = jnp.dot(select[...], part, preferred_element_type=f32).astype(bf16)
-
-
-def enter(x_rows, weight, bias, pos, n_rows):
-    n_tok, d_model = x_rows.shape
-    n_cols = d_model // 8
-    whole = lambda shape: pl.BlockSpec(shape, lambda j: (0, 0))
-    stat = jax.ShapeDtypeStruct((n_tok, 1), f32)
-    return pl.pallas_call(
-        enter_kernel, grid=(8,),
-        in_specs=[whole((n_tok, d_model)), whole((1, d_model)), whole((1, d_model)), whole(pos.shape)],
-        out_specs=[pl.BlockSpec((n_tok, n_cols), lambda j: (0, j)), pl.BlockSpec((n_rows, n_cols), lambda j: (0, j)),
-                   whole((n_tok, 1)), whole((n_tok, 1))],
-        out_shape=[jax.ShapeDtypeStruct((n_tok, d_model), bf16), jax.ShapeDtypeStruct((n_rows, d_model), bf16), stat, stat],
-        scratch_shapes=[pltpu.VMEM((n_tok, d_model), bf16), pltpu.VMEM((n_rows, n_tok), bf16)],
-        compiler_params=pltpu.CompilerParams(vmem_limit_bytes=48 * 1024 * 1024),
-        cost_estimate=pl.CostEstimate(flops=2 * n_rows * n_tok * d_model, bytes_accessed=4 * (n_tok + n_rows) * d_model, transcendentals=n_tok),
-    )(x_rows, weight[None], bias[None], pos)
+def layer_norm(x_rows, ln_weight, ln_bias):
+    x_float = x_rows.astype(f32)
+    centered = x_float - jnp.mean(x_float, axis=-1, keepdims=True)
+    inv_std = lax.rsqrt(jnp.mean(centered * centered, axis=-1, keepdims=True) + LN_EPS)
+    x_hat = centered * inv_std
+    hidden = (x_hat * ln_weight.astype(f32) + ln_bias.astype(f32)).astype(bf16)
+    return hidden, x_hat, inv_std
 
 
 def layer_norm_back(grad_h, x_hat, inv_std, ln_weight):
@@ -216,14 +174,14 @@
         wu_t = w_up[0].T
         wd = w_down[0]
 
-        pos_one = jnp.where(slot_first >= 0, exp_first * slot_cap + slot_first, -1)
-        pos_two = jnp.where(slot_second >= 0, exp_second * slot_cap + slot_second, -1)
-        hidden, h_buf, mean, inv_std = enter(tok_x, ln_weight, ln_bias, jnp.stack([pos_one, pos_two]), n_rows)
+        hidden, x_hat, inv_std = layer_norm(tok_x, ln_weight, ln_bias)
         logits = jnp.dot(hidden, router, preferred_element_type=f32)
         expert_ids = jnp.arange(n_exp)
         allowed = eligible > 0
         gate_one, prob_one, pick_one = masked_gate(logits, allowed, exp_first)
         gate_two, prob_two, pick_two = masked_gate(logits, allowed & (expert_ids[None, :] != exp_first[:, None]), exp_second)
+        pos_one = jnp.where(slot_first >= 0, exp_first * slot_cap + slot_first, -1)
+        pos_two = jnp.where(slot_second >= 0, exp_second * slot_cap + slot_second, -1)
         meta = jnp.stack([pos_one.astype(f32), pos_two.astype(f32), gate_one, gate_two])
         row_ids = jnp.arange(n_rows)
 
@@ -246,6 +204,8 @@
             return (jnp.einsum('fd,rd->fr', wg_t, h, preferred_element_type=f32),
                     jnp.einsum('fd,rd->fr', wu_t, h, preferred_element_type=f32))
 
+        own_meta = jnp.stack([pos_one.astype(f32), pos_two.astype(f32)])
+        h_buf = select_h(hidden, own_meta)
         h_own = swap(h_buf)
         m_f1 = lax.ppermute(meta, 'dp', outer + middle)
         h_f1 = lax.ppermute(hidden, 'dp', outer + middle)
@@ -255,6 +215,14 @@
         a_t, b_t = pre(h_own)
         u_t = (a_t * jax.nn.sigmoid(a_t) * b_t).astype(bf16)
         exp_out = jnp.einsum('fr,fd->rd', u_t, wd, preferred_element_type=f32).astype(bf16)
+        ep_id = lax.axis_index('ep')
+        by_dest = exp_out.reshape(n_ep, slot_cap, d_model)
+        pieces = []
+        for k in range(n_ep):
+            piece = lax.dynamic_index_in_dim(by_dest, ep_id ^ k, 0, keepdims=False)
+            if k:
+                piece = lax.ppermute(piece, 'ep', [(i, i ^ k) for i in range(n_ep)])
+            pieces.append(piece)
         u_t, da_t, db_t = inner_grad(q_own, wd, a_t, b_t)
         grad_hid = (jnp.einsum('fr,fd->rd', da_t, wg_t, preferred_element_type=f32)
                     + jnp.einsum('fr,fd->rd', db_t, wu_t, preferred_element_type=f32)).astype(bf16)
@@ -273,7 +241,6 @@
         q_r1 = swap(q_b1)
         h_r2 = swap(h_b2)
         q_r2 = swap(q_b2)
-        out_back = swap(exp_out)
         hid_back = swap(grad_hid)
         for h, q in ((h_r1, q_r1), (h_r2, q_r2), (h_near, q_near)):
             a_t, b_t = pre(h)
@@ -284,8 +251,11 @@
         dy_float = tok_dy.astype(f32)
         sel_one = (pos_one[:, None] == row_ids[None, :]).astype(bf16)
         sel_two = (pos_two[:, None] == row_ids[None, :]).astype(bf16)
-        out_one = jnp.dot(sel_one, out_back, preferred_element_type=f32)
-        out_two = jnp.dot(sel_two, out_back, preferred_element_type=f32)
+        back_one = jnp.where(slot_first >= 0, (after(exp_first, a_t) ^ ep_id) * slot_cap + slot_first, -1)
+        back_two = jnp.where(slot_second >= 0, (after(exp_second, a_t) ^ ep_id) * slot_cap + slot_second, -1)
+        out_back = jnp.concatenate(pieces)
+        out_one = jnp.dot((back_one[:, None] == row_ids[None, :]).astype(bf16), out_back, preferred_element_type=f32)
+        out_two = jnp.dot((back_two[:, None] == row_ids[None, :]).astype(bf16), out_back, preferred_element_type=f32)
         out_tok = (tok_x.astype(f32) + gate_one[:, None] * out_one + gate_two[:, None] * out_two).astype(bf16)
         dgate_one = jnp.sum(dy_float * out_one, axis=-1)
         dgate_two = jnp.sum(dy_float * out_two, axis=-1)
@@ -294,7 +264,6 @@
         d_router = jnp.einsum('td,te->ed', hidden, d_logits, preferred_element_type=f32)
         grad_exp = jnp.dot(sel_one + sel_two, hid_back, preferred_element_type=f32)
         grad_h = jnp.einsum('te,de->td', d_logits, router, preferred_element_type=f32) + grad_exp
-        x_hat = (tok_x.astype(f32) - mean) * inv_std
         d_ln_weight = jnp.sum(grad_h * x_hat, axis=0)
         d_ln_bias = jnp.sum(grad_h, axis=0)
         dx_tok = (dy_float + layer_norm_back(grad_h, x_hat, inv_std, ln_weight)).astype(bf16)

time: 1580 us -> 1730 us (1.095)
  waiting for transfers between devices: 625 us -> 821 us
  Pallas kernels: 473 us -> 394 us
  local copies, waits for them, and re-layouts: 9.97 us -> 29.8 us
    ppermute x0 -> x7, waiting for transfers between devices: none -> 186 us  [local_step(): piece = lax.ppermute(piece, 'ep', [(i, i ^ k) for i in range(n_ep)])]
    ppermute x1, waiting for transfers between devices: 0.01 us -> 181 us  [local_step(): h_f1 = lax.ppermute(hidden, 'dp', outer + middle)]
    ppermute x1, waiting for transfers between devices: 177 us -> 1.34 us  [local_step(): m_f2 = lax.ppermute(m_f1, 'dp', near)]
    pallas_call x1, Pallas kernels: 80.2 us -> 17.3 us  [sum_all(): pl.pallas_call(functools.partial(sum_kernel, n_dp, n_ep), out_shape=jax.S...]
    all_to_all x8 -> x7, waiting for transfers between devices: 266 us -> 274 us  [swap(): lax.all_to_all(buf.reshape(n_ep, slot_cap, d_model), 'ep', 0, 0, tiled=True)]
    all_to_all x8 -> x7, starting transfers between devices: 44.6 us -> 38.6 us  [swap(): lax.all_to_all(buf.reshape(n_ep, slot_cap, d_model), 'ep', 0, 0, tiled=True)]
  transfers between devices with their start and end apart: 16 -> 22, of which waited for: 6 -> 10; matrix products, arithmetic and copies ran while one was open for 26% -> 25% of each run, Pallas kernels for 23% -> 17%
where the time goes in v7:
time: 1730 us
  waiting for transfers between devices  821 us (47%)
  matrix products  399 us (23%)
  Pallas kernels  394 us (23%)
  starting transfers between devices  58.2 us (3%)
  local copies, waits for them, and re-layouts  29.8 us (2%)
  other arithmetic  21.8 us (1%)
    all_to_all x7, waiting for transfers between devices, swap(): lax.all_to_all(buf.reshape(n_ep, slot_cap, d_model), 'ep', 0, 0, tiled=True)  274 us
    pallas_call x4, Pallas kernels, add_dw(): pl.pallas_call(functools.partial(dw_kernel, first), grid=(d_model // d_ti...  258 us
    ppermute x7, waiting for transfers between devices, local_step(): piece = lax.ppermute(piece, 'ep', [(i, i ^ k) for i in range(n_ep)])  186 us
    ppermute x1, waiting for transfers between devices, local_step(): h_f1 = lax.ppermute(hidden, 'dp', outer + middle)  181 us
    ppermute x1, waiting for transfers between devices, local_step(): m_f1 = lax.ppermute(meta, 'dp', outer + middle)  179 us
    pallas_call x4, Pallas kernels, inner_grad(): pl.pallas_call(grad_kernel, grid=(n_rows // r_tile,), in_specs=[pl.BlockS...  118 us
    dot_general x4, matrix products, pre(): jnp.einsum('fd,rd->fr', wg_t, h, preferred_element_type=f32)  97 us
    dot_general x4, matrix products, pre(): jnp.einsum('fd,rd->fr', wu_t, h, preferred_element_type=f32)  95 us
  transfers between devices with their start and end apart: 22, of which 10 were waited for; matrix products, arithmetic and copies ran while one was open for 25% of the time, Pallas kernels for 17%

profile of v7, /device:TPU:0, one launch (start us, length us, event | category | flops | bytes accessed | tf_op | source)
XLA Modules:
  0.0 1725.1 jit_solution(13924863811868286542)
XLA Ops:
  0.7 3.0 convert_reduce_fusion
  3.7 3.4 fusion.55
  7.9 2.3 fusion.50
  10.2 9.6 convolution_convert_fusion.3
  19.8 5.5 all-to-all-start
  25.3 3.4 fusion.101
  30.1 11.8 multiply_convert_fusion.2
  41.9 123.1 %all-to-all-done = bf16[8,192,4096]{2,1,0:T(8,128)(2,1)} async-done(((bf16[8,192,4096]{2,1,0:T(8,128)(2,1)}), bf16[8,192,4096]{2,1,0:T(8,128)(2,1)}, u32[]{:S(2)}, u32[]{:S(2)}) %all-to-all-start) | async-done | bytes 12582944 | tf_op jit(solution)/shard_map/all_to_all | solution.py:201
  165.0 5.5 all-to-all-start.1
  170.5 3.4 collective-permute-start.11
  173.9 181.4 %collective-permute-done.11 = bf16[512,4096]{1,0:T(8,128)(2,1)} collective-permute-done((bf16[512,4096]{1,0:T(8,128)(2,1)}, bf16[512,4096]{1,0:T(8,128)(2,1)}, u32[]{:S(2)}, u32[]{:S(2)}) %collective-permute-start.11) | collective-permute-done | bytes 4194336 | tf_op jit(solution)/shard_map/ppermute | solution.py:211
  355.3 4.1 collective-permute-start.14
  360.2 178.8 %collective-permute-done.9 = f32[4,512]{1,0:T(4,128)S(1)} collective-permute-done((f32[4,512]{1,0:T(4,128)S(1)}, f32[4,512]{1,0:T(4,128)S(1)}, u32[]{:S(2)}, u32[]{:S(2)}) %collective-permute-start.9) | collective-permute-done | bytes 8224 | tf_op jit(solution)/shard_map/ppermute | solution.py:210
  542.6 11.8 convolution_convert_fusion.1
  554.4 5.3 all-to-all-start.6
  561.0 1.6 collective-permute-start.13
  562.7 11.8 convolution_convert_fusion.2
  574.5 11.9 multiply_convert_fusion
  586.9 23.3 %fusion.28.a_ref = f32[1376,1536]{1,0:T(8,128)} fusion(bf16[1536,4096]{1,0:T(8,128)(2,1)} %bitcast.1.refs_3_, bf16[1,4096,1376]{1,2,0:T(8,128)(2,1)S(1)} %bitcast.179), kind=kOutput, calls=%fused_computation.40 | convolution fusion | flops 17314086912 | bytes 32309248 | tf_op jit(solution)/shard_map/fd,rd->fr/dot_general | solution.py:204
  610.2 22.4 %fusion.37.b_ref = f32[1376,1536]{1,0:T(8,128)} fusion(bf16[1536,4096]{1,0:T(8,128)(2,1)} %bitcast.1.refs_3_, bf16[1,4096,1376]{1,2,0:T(8,128)(2,1)S(1)} %bitcast.183), kind=kOutput, calls=%fused_computation.43 | convolution fusion | flops 17314086912 | bytes 32309248 | tf_op jit(solution)/shard_map/fd,rd->fr/dot_general | solution.py:205
  632.6 66.1 %all-to-all-done.6 = bf16[8,192,4096]{2,1,0:T(8,128)(2,1)} async-done(((bf16[8,192,4096]{2,1,0:T(8,128)(2,1)}), bf16[8,192,4096]{2,1,0:T(8,128)(2,1)}, u32[]{:S(2)}, u32[]{:S(2)}) %all-to-all-start.6) | async-done | bytes 12582944 | tf_op jit(solution)/shard_map/all_to_all | solution.py:201
  698.7 5.5 all-to-all-start.5
  704.2 28.7 %convolution_convert_fusion = bf16[1536,4096]{1,0:T(8,128)(2,1)} fusion(f32[1376,1536]{1,0:T(8,128)} %fusion.37.b_ref, f32[1376,1536]{1,0:T(8,128)} %fusion.28.a_ref, bf16[1,1376,4096]{2,1,0:T(8,128)(2,1)} %param.25), kind=kOutput, calls=%fused_computation.4 | convolution fusion | flops 17333059584 | bytes 40763392 | tf_op jit(solution)/shard_map/fr,fd->rd/dot_general | solution.py:217
  732.9 8.5 dynamic-slice_bitcast_fusion
  741.8 1.6 collective-permute-start.2
  743.5 29.5 %shard_map.188 = (bf16[1376,1536]{1,0:T(8,128)(2,1)}, bf16[1376,1536]{1,0:T(8,128)(2,1)}, bf16[1376,1536]{1,0:T(8,128)(2,1)}) custom-call(bf16[1536,4096]{1,0:T(8,128)(2,1)} %bitcast.18.q_ref.refs_4_, bf16[1376,4096]{1,0:T(8,128)(2,1)} %bitcast.186, f32[1376,1536]{1,0:T(8,128)} %fusion.28.a_ref, f32[1376,1536]{1,0:T(8,128)} %fusion.37.b_ref), custom_call_target="tpu_custom_call" | custom-call | flops 17314086912 | bytes 54755328 | tf_op jit(solution)/shard_map/pallas_call | solution.py:57
  772.9 61.3 %shard_map.192 = (f32[1376,4096]{1,0:T(8,128)}, f32[1376,4096]{1,0:T(8,128)}, f32[1376,4096]{1,0:T(8,128)}) custom-call(bf16[1376,1536]{1,0:T(8,128)(2,1)} %get-tuple-element.49.refs_0_, bf16[1376,1536]{1,0:T(8,128)(2,1)} %get-tuple-element.37.refs_1_, bf16[1376,1536]{1,0:T(8,128)(2,1)} %get-tuple-element.38.refs_2_, bf16[1536,4096]{1,0:T(8,128)(2,1)} %bitcast.1.refs_3_, ...), custom_call_target="tpu_custom_call" | custom-call | flops 51942260736 | bytes 92798976 | tf_op jit(solution)/shard_map/pallas_call | solution.py:89
  834.2 9.6 all-to-all-done.5
  843.8 5.8 all-to-all-start.4
  849.6 26.1 %fusion.13 = f32[1536,4096]{1,0:T(8,128)} fusion(bf16[1376,1536]{1,0:T(8,128)(2,1)} %get-tuple-element.37.refs_1_, bf16[1,4096,1376]{1,2,0:T(8,128)(2,1)} %param.23), kind=kOutput, calls=%fused_computation.27 | convolution fusion | flops 17314086912 | bytes 40665088 | tf_op jit(solution)/shard_map/fr,fd->rd/dot_general | solution.py:227
  875.7 29.5 %add_convert_fusion = bf16[1536,4096]{1,0:T(8,128)(2,1)} fusion(f32[1536,4096]{1,0:T(8,128)} %fusion.13, bf16[1376,1536]{1,0:T(8,128)(2,1)} %get-tuple-element.38.refs_2_, bf16[1,4096,1376]{1,2,0:T(8,128)(2,1)} %param.24), kind=kOutput, calls=%fused_computation.2 | convolution fusion | flops 17326669824 | bytes 53248000 | tf_op jit(solution)/shard_map/fr,fd->rd/dot_general | solution.py:228
  905.2 2.8 bitcast_dynamic-update-slice_fusion
  908.0 2.0 collective-permute-start.4
  910.1 12.0 multiply_convert_fusion.1
  922.0 2.7 constant_dynamic-update-slice_fusion.6
  924.8 2.4 collective-permute-start.6
  927.1 2.8 constant_dynamic-update-slice_fusion.5
  930.2 2.7 constant_dynamic-update-slice_fusion.4
  932.9 55.2 %collective-permute-done.4 = bf16[192,4096]{1,0:T(8,128)(2,1)S(1)} collective-permute-done((bf16[192,4096]{1,0:T(8,128)(2,1)S(1)}, bf16[192,4096]{1,0:T(8,128)(2,1)S(1)}, u32[]{:S(2)}, u32[]{:S(2)}) %collective-permute-start.4) | collective-permute-done | bytes 1572896 | tf_op jit(solution)/shard_map/ppermute | solution.py:224
  988.1 1.6 collective-permute-start.8
  991.0 130.7 %collective-permute-done.5 = bf16[192,4096]{1,0:T(8,128)(2,1)S(1)} collective-permute-done((bf16[192,4096]{1,0:T(8,128)(2,1)S(1)}, bf16[192,4096]{1,0:T(8,128)(2,1)S(1)}, u32[]{:S(2)}, u32[]{:S(2)}) %collective-permute-start.5) | collective-permute-done | bytes 1572896 | tf_op jit(solution)/shard_map/ppermute | solution.py:224
  1125.6 5.6 all-to-all-start.2
  1131.3 25.4 %fusion.34.a_ref = f32[1376,1536]{1,0:T(8,128)} fusion(bf16[1536,4096]{1,0:T(8,128)(2,1)} %bitcast.43.refs_3_, bf16[1,4096,1376]{1,2,0:T(8,128)(2,1)} %param.23), kind=kOutput, calls=%fused_computation.42 | convolution fusion | flops 17314086912 | bytes 32309248 | tf_op jit(solution)/shard_map/fd,rd->fr/dot_general | solution.py:204
  1156.7 22.1 %fusion.46.b_ref = f32[1376,1536]{1,0:T(8,128)} fusion(bf16[1536,4096]{1,0:T(8,128)(2,1)} %bitcast.43.refs_3_, bf16[1,4096,1376]{1,2,0:T(8,128)(2,1)S(1)} %bitcast.185), kind=kOutput, calls=%fused_computation.46 | convolution fusion | flops 17314086912 | bytes 32309248 | tf_op jit(solution)/shard_map/fd,rd->fr/dot_general | solution.py:205
  1178.8 23.1 %fusion.31.a_ref = f32[1376,1536]{1,0:T(8,128)} fusion(bf16[1536,4096]{1,0:T(8,128)(2,1)} %bitcast.33.refs_3_, bf16[1,4096,1376]{1,2,0:T(8,128)(2,1)S(1)} %bitcast.181), kind=kOutput, calls=%fused_computation.41 | convolution fusion | flops 17314086912 | bytes 32309248 | tf_op jit(solution)/shard_map/fd,rd->fr/dot_general | solution.py:204
  1201.8 68.4 %all-to-all-done.2 = bf16[8,192,4096]{2,1,0:T(8,128)(2,1)} async-done(((bf16[8,192,4096]{2,1,0:T(8,128)(2,1)}), bf16[8,192,4096]{2,1,0:T(8,128)(2,1)}, u32[]{:S(2)}, u32[]{:S(2)}) %all-to-all-start.2) | async-done | bytes 12582944 | tf_op jit(solution)/shard_map/all_to_all | solution.py:201
  1270.2 5.3 all-to-all-start.3
  1275.6 29.5 %shard_map.191 = (bf16[1376,1536]{1,0:T(8,128)(2,1)}, bf16[1376,1536]{1,0:T(8,128)(2,1)}, bf16[1376,1536]{1,0:T(8,128)(2,1)}) custom-call(bf16[1536,4096]{1,0:T(8,128)(2,1)} %bitcast.41.q_ref.refs_4_, bf16[1376,4096]{1,0:T(8,128)(2,1)} %bitcast.187, f32[1376,1536]{1,0:T(8,128)} %fusion.34.a_ref, f32[1376,1536]{1,0:T(8,128)} %fusion.46.b_ref), custom_call_target="tpu_custom_call" | custom-call | flops 17314086912 | bytes 54755328 | tf_op jit(solution)/shard_map/pallas_call | solution.py:57
  1305.0 25.2 %fusion.43.b_ref = f32[1376,1536]{1,0:T(8,128)} fusion(bf16[1536,4096]{1,0:T(8,128)(2,1)} %bitcast.33.refs_3_, bf16[1,4096,1376]{1,2,0:T(8,128)(2,1)} %param.24), kind=kOutput, calls=%fused_computation.45 | convolution fusion | flops 17314086912 | bytes 32309248 | tf_op jit(solution)/shard_map/fd,rd->fr/dot_general | solution.py:205
  1330.2 65.7 %shard_map.193 = (f32[1376,4096]{1,0:T(8,128)}, f32[1376,4096]{1,0:T(8,128)}, f32[1376,4096]{1,0:T(8,128)}) custom-call(bf16[1376,1536]{1,0:T(8,128)(2,1)} %get-tuple-element.46.refs_0_, bf16[1376,1536]{1,0:T(8,128)(2,1)} %get-tuple-element.47.refs_1_, ...), custom_call_target="tpu_custom_call", output_to_operand_aliasing={{0}: (5, {}), {1}: (6, {}), {2}: (7, {})} | custom-call | flops 51942260736 | bytes 160432128 | tf_op jit(solution)/shard_map/pallas_call | solution.py:89
  1395.9 11.8 fusion.76
  1407.7 6.8 all-to-all-done.3
  1414.5 29.5 %shard_map.190 = (bf16[1376,1536]{1,0:T(8,128)(2,1)}, bf16[1376,1536]{1,0:T(8,128)(2,1)}, bf16[1376,1536]{1,0:T(8,128)(2,1)}) custom-call(bf16[1536,4096]{1,0:T(8,128)(2,1)} %bitcast.31.q_ref.refs_4_, bf16[1376,4096]{1,0:T(8,128)(2,1)} %bitcast.188, f32[1376,1536]{1,0:T(8,128)} %fusion.31.a_ref, f32[1376,1536]{1,0:T(8,128)} %fusion.43.b_ref), custom_call_target="tpu_custom_call" | custom-call | flops 17314086912 | bytes 54755328 | tf_op jit(solution)/shard_map/pallas_call | solution.py:57
  1444.0 65.8 %shard_map.194 = (f32[1376,4096]{1,0:T(8,128)}, f32[1376,4096]{1,0:T(8,128)}, f32[1376,4096]{1,0:T(8,128)}) custom-call(bf16[1376,1536]{1,0:T(8,128)(2,1)} %get-tuple-element.43.refs_0_, bf16[1376,1536]{1,0:T(8,128)(2,1)} %get-tuple-element.44.refs_1_, ...), custom_call_target="tpu_custom_call", output_to_operand_aliasing={{0}: (5, {}), {1}: (6, {}), {2}: (7, {})} | custom-call | flops 51942260736 | bytes 160432128 | tf_op jit(solution)/shard_map/pallas_call | solution.py:89
  1509.8 25.3 %fusion.25.a_ref = f32[1376,1536]{1,0:T(8,128)} fusion(bf16[1536,4096]{1,0:T(8,128)(2,1)} %collective-permute-done.refs_3_, bf16[1,4096,1376]{1,2,0:T(8,128)(2,1)} %param.23), kind=kOutput, calls=%fused_computation.39 | convolution fusion | flops 17314086912 | bytes 32309248 | tf_op jit(solution)/shard_map/fd,rd->fr/dot_general | solution.py:204
  1535.2 12.3 fusion.66
  1547.6 17.2 fusion.58
  1565.5 8.2 fusion.54
  1574.5 17.3 %shard_map.196 = f32[8,16,512]{2,1,0:T(8,128)} custom-call(f32[8,16,512]{2,1,0:T(8,128)} %maximum_bitcast_fusion.x_ref), custom_call_target="tpu_custom_call" | custom-call | tf_op jit(solution)/shard_map/pallas_call | solution.py:143
  1593.4 1.6 fusion.108
  1595.0 9.4 fusion.60
  1604.4 25.3 %fusion.40.b_ref = f32[1376,1536]{1,0:T(8,128)} fusion(bf16[1536,4096]{1,0:T(8,128)(2,1)} %collective-permute-done.refs_3_, bf16[1,4096,1376]{1,2,0:T(8,128)(2,1)} %param.24), kind=kOutput, calls=%fused_computation.44 | convolution fusion | flops 17314086912 | bytes 32309248 | tf_op jit(solution)/shard_map/fd,rd->fr/dot_general | solution.py:205
  1629.7 29.4 %shard_map.189 = (bf16[1376,1536]{1,0:T(8,128)(2,1)}, bf16[1376,1536]{1,0:T(8,128)(2,1)}, bf16[1376,1536]{1,0:T(8,128)(2,1)}) custom-call(bf16[1536,4096]{1,0:T(8,128)(2,1)} %collective-permute-done.8.q_ref.refs_4_, bf16[1376,4096]{1,0:T(8,128)(2,1)} %bitcast.189, f32[1376,1536]{1,0:T(8,128)} %fusion.25.a_ref, f32[1376,1536]{1,0:T(8,128)} %fusion.40.b_ref), custom_call_target="tpu_custom_call" | custom-call | flops 17314086912 | bytes 54755328 | tf_op jit(solution)/shard_map/pallas_call | solution.py:57
  1659.2 65.7 %shard_map.195 = (f32[1376,4096]{1,0:T(8,128)}, f32[1376,4096]{1,0:T(8,128)}, f32[1376,4096]{1,0:T(8,128)}) custom-call(bf16[1376,1536]{1,0:T(8,128)(2,1)} %get-tuple-element.39.refs_0_, bf16[1376,1536]{1,0:T(8,128)(2,1)} %get-tuple-element.40.refs_1_, ...), custom_call_target="tpu_custom_call", output_to_operand_aliasing={{0}: (5, {}), {1}: (6, {}), {2}: (7, {})} | custom-call | flops 51942260736 | bytes 160432128 | tf_op jit(solution)/shard_map/pallas_call | solution.py:89
  (186 shorter events, 17.4 us)
Async XLA Ops:
  0.6 24.7 %copy-start = (bf16[4096,8]{0,1:T(8,128)(2,1)S(1)}, bf16[4096,8]{0,1:T(8,128)(2,1)}, u32[]{:S(2)}) copy-start(bf16[4096,8]{0,1:T(8,128)(2,1)} %param.22) | copy-start | bytes 196612
  19.8 145.2 %all-to-all-start = ((bf16[8,192,4096]{2,1,0:T(8,128)(2,1)}), bf16[8,192,4096]{2,1,0:T(8,128)(2,1)}, u32[]{:S(2)}, u32[]{:S(2)}) async-start(bf16[8,192,4096]{2,1,0:T(8,128)(2,1)} %bitcast.149), calls=%async_computation | async-start | bytes 25165824 | tf_op jit(solution)/shard_map/all_to_all | solution.py:201
  28.8 330.6 %copy-start.30 = (f32[512]{0:T(512)}, f32[512]{0:T(512)S(1)}, u32[]{:S(2)}) copy-start(f32[512]{0:T(512)S(1)} %get-tuple-element.68) | copy-start | bytes 6148
  29.4 330.0 %copy-start.32 = (f32[512]{0:T(512)}, f32[512]{0:T(512)S(1)}, u32[]{:S(2)}) copy-start(f32[512]{0:T(512)S(1)} %select_reduce_fusion) | copy-start | bytes 6148
  165.0 389.4 %all-to-all-start.1 = ((bf16[8,192,4096]{2,1,0:T(8,128)(2,1)}), bf16[8,192,4096]{2,1,0:T(8,128)(2,1)}, u32[]{:S(2)}, u32[]{:S(2)}) async-start(bf16[8,192,4096]{2,1,0:T(8,128)(2,1)} %bitcast.142), calls=%async_computation.1 | async-start | bytes 25165824 | tf_op jit(solution)/shard_map/all_to_all | solution.py:201
  170.5 184.8 %collective-permute-start.11 = (bf16[512,4096]{1,0:T(8,128)(2,1)}, bf16[512,4096]{1,0:T(8,128)(2,1)}, u32[]{:S(2)}, u32[]{:S(2)}) collective-permute-start(bf16[512,4096]{1,0:T(8,128)(2,1)} %copy-done.3), channel_id=1, source_target_pairs={{0,16},{24,8},{8,24},{16,0},{1,17},{25,9},{9,25},{17,1},{2,18},{26... | collective-permute-start | bytes 12582920 | tf_op jit(solution)/shard_map/ppermute | solution.py:211
  355.3 205.7 %collective-permute-start.12 = (bf16[512,4096]{1,0:T(8,128)(2,1)}, bf16[512,4096]{1,0:T(8,128)(2,1)}, u32[]{:S(2)}, u32[]{:S(2)}) collective-permute-start(bf16[512,4096]{1,0:T(8,128)(2,1)} %param.14), channel_id=1, source_target_pairs={{0,16},{24,8},{8,24},{16,0},{1,17},{25,9},{9,25},{17,1},{2,18},{26... | collective-permute-start | bytes 12582920 | tf_op jit(solution)/shard_map/ppermute | solution.py:212
  355.3 207.3 %collective-permute-start.14 = (bf16[512,4096]{1,0:T(8,128)(2,1)}, bf16[512,4096]{1,0:T(8,128)(2,1)}, u32[]{:S(2)}, u32[]{:S(2)}) collective-permute-start(bf16[512,4096]{1,0:T(8,128)(2,1)} %collective-permute-done.11), channel_id=1, source_target_pairs={{0,8},{8,0},{16,24},{24,16},{1,9},{9,1},{17,25},{25,17},{2,10},{10... | collective-permute-start | bytes 12582920 | tf_op jit(solution)/shard_map/ppermute | solution.py:232
  359.4 179.5 %collective-permute-start.9 = (f32[4,512]{1,0:T(4,128)S(1)}, f32[4,512]{1,0:T(4,128)S(1)}, u32[]{:S(2)}, u32[]{:S(2)}) collective-permute-start(f32[4,512]{1,0:T(4,128)S(1)} %pad_maximum_fusion), channel_id=1, source_target_pairs={{0,16},{24,8},{8,24},{16,0},{1,17},{25,9},{9,25},{17,1},{2,18},{26... | collective-permute-start | bytes 24584 | tf_op jit(solution)/shard_map/ppermute | solution.py:210
  538.9 3.7 collective-permute-start.10
  542.6 20.0 %copy-start.47 = (s32[1,512]{1,0:T(1,128)}, s32[1,512]{1,0:T(1,128)S(1)}, u32[]{:S(2)}) copy-start(s32[1,512]{1,0:T(1,128)S(1)} %get-tuple-element.92) | copy-start | bytes 6148
  542.6 20.0 %copy-start.49 = (s32[1,512]{1,0:T(1,128)}, s32[1,512]{1,0:T(1,128)S(1)}, u32[]{:S(2)}) copy-start(s32[1,512]{1,0:T(1,128)S(1)} %get-tuple-element.94) | copy-start | bytes 6148
  554.4 144.3 %all-to-all-start.6 = ((bf16[8,192,4096]{2,1,0:T(8,128)(2,1)}), bf16[8,192,4096]{2,1,0:T(8,128)(2,1)}, u32[]{:S(2)}, u32[]{:S(2)}) async-start(bf16[8,192,4096]{2,1,0:T(8,128)(2,1)} %bitcast.148), calls=%async_computation.6 | async-start | bytes 25165824 | tf_op jit(solution)/shard_map/all_to_all | solution.py:201
  561.0 346.9 %collective-permute-start.13 = (bf16[512,4096]{1,0:T(8,128)(2,1)}, bf16[512,4096]{1,0:T(8,128)(2,1)}, u32[]{:S(2)}, u32[]{:S(2)}) collective-permute-start(bf16[512,4096]{1,0:T(8,128)(2,1)} %collective-permute-done.12), channel_id=1, source_target_pairs={{0,8},{8,0},{16,24},{24,16},{1,9},{9,1},{17,25},{25,17},{2,10},{10... | collective-permute-start | bytes 12582920 | tf_op jit(solution)/shard_map/ppermute | solution.py:233
  562.6 24.2 %slice-start = ((s8[11272192]{0:T(1024)(128)(4,1)}), s8[4194304]{0:T(1024)(128)(4,1)S(1)}, s32[]{:S(2)}) async-start(s8[11272192]{0:T(1024)(128)(4,1)} %bitcast.178), calls=%async_computation.7 | async-start | bytes 8388608
  562.7 24.2 %slice-start.1 = ((s8[11272192]{0:T(1024)(128)(4,1)}), s8[4194304]{0:T(1024)(128)(4,1)S(1)}, s32[]{:S(2)}) async-start(s8[11272192]{0:T(1024)(128)(4,1)} %bitcast.178), calls=%async_computation.8 | async-start | bytes 8388608
  574.5 12.4 slice-start.2
  586.4 23.7 %slice-start.6 = ((s8[11272192]{0:T(1024)(128)(4,1)}), s8[4194304]{0:T(1024)(128)(4,1)S(1)}, s32[]{:S(2)}) async-start(s8[11272192]{0:T(1024)(128)(4,1)} %bitcast.182), calls=%async_computation.13 | async-start | bytes 8388608
  586.5 23.7 %slice-start.7 = ((s8[11272192]{0:T(1024)(128)(4,1)}), s8[4194304]{0:T(1024)(128)(4,1)S(1)}, s32[]{:S(2)}) async-start(s8[11272192]{0:T(1024)(128)(4,1)} %bitcast.182), calls=%async_computation.14 | async-start | bytes 8388608
  586.5 23.7 %slice-start.8 = ((s8[11272192]{0:T(1024)(128)(4,1)}), s8[2883584]{0:T(1024)(128)(4,1)S(1)}, s32[]{:S(2)}) async-start(s8[11272192]{0:T(1024)(128)(4,1)} %bitcast.182), calls=%async_computation.15 | async-start | bytes 5767168
  586.5 923.3 %collective-permute-start = (bf16[1536,4096]{1,0:T(8,128)(2,1)}, bf16[1536,4096]{1,0:T(8,128)(2,1)}, u32[]{:S(2)}, u32[]{:S(2)}) collective-permute-start(bf16[1536,4096]{1,0:T(8,128)(2,1)} %bitcast.1.refs_3_), channel_id=1, source_target_pairs={{0,8},{8,0},{16,24},{24,16},{1,9},{9,1},{17,25},{25,17},{2,10},{10... | collective-permute-start | bytes 37748744 | tf_op jit(solution)/shard_map/ppermute | solution.py:234
  698.7 145.1 %all-to-all-start.5 = ((bf16[8,192,4096]{2,1,0:T(8,128)(2,1)}), bf16[8,192,4096]{2,1,0:T(8,128)(2,1)}, u32[]{:S(2)}, u32[]{:S(2)}) async-start(bf16[8,192,4096]{2,1,0:T(8,128)(2,1)} %bitcast.145), calls=%async_computation.5 | async-start | bytes 25165824 | tf_op jit(solution)/shard_map/all_to_all | solution.py:201
  741.4 180.6 %collective-permute-start.1 = (bf16[192,4096]{1,0:T(8,128)(2,1)}, bf16[192,4096]{1,0:T(8,128)(2,1)}, u32[]{:S(2)}, u32[]{:S(2)}) collective-permute-start(bf16[192,4096]{1,0:T(8,128)(2,1)} %get-tuple-element.85), channel_id=1, source_target_pairs={{0,1},{1,0},{2,3},{3,2},{4,5},{5,4},{6,7},{7,6},{8,9},{9,8},{10,11... | collective-permute-start | bytes 4718600 | tf_op jit(solution)/shard_map/ppermute | solution.py:224
  741.8 182.9 %collective-permute-start.2 = (bf16[192,4096]{1,0:T(8,128)(2,1)}, bf16[192,4096]{1,0:T(8,128)(2,1)}, u32[]{:S(2)}, u32[]{:S(2)}) collective-permute-start(bf16[192,4096]{1,0:T(8,128)(2,1)} %get-tuple-element.84), channel_id=1, source_target_pairs={{0,2},{1,3},{2,0},{3,1},{4,6},{5,7},{6,4},{7,5},{8,10},{9,11},{10,... | collective-permute-start | bytes 4718600 | tf_op jit(solution)/shard_map/ppermute | solution.py:224
  743.5 186.4 %collective-permute-start.3 = (bf16[192,4096]{1,0:T(8,128)(2,1)}, bf16[192,4096]{1,0:T(8,128)(2,1)}, u32[]{:S(2)}, u32[]{:S(2)}) collective-permute-start(bf16[192,4096]{1,0:T(8,128)(2,1)} %get-tuple-element.83), channel_id=1, source_target_pairs={{0,3},{1,2},{2,1},{3,0},{4,7},{5,6},{6,5},{7,4},{8,11},{9,10},{10,... | collective-permute-start | bytes 4718600 | tf_op jit(solution)/shard_map/ppermute | solution.py:224
  843.8 281.8 %all-to-all-start.4 = ((bf16[8,192,4096]{2,1,0:T(8,128)(2,1)}), bf16[8,192,4096]{2,1,0:T(8,128)(2,1)}, u32[]{:S(2)}, u32[]{:S(2)}) async-start(bf16[8,192,4096]{2,1,0:T(8,128)(2,1)} %bitcast.141), calls=%async_computation.4 | async-start | bytes 25165824 | tf_op jit(solution)/shard_map/all_to_all | solution.py:201
  875.7 32.3 %copy-start.9 = (bf16[192,4096]{1,0:T(8,128)(2,1)S(1)}, bf16[192,4096]{1,0:T(8,128)(2,1)}, u32[]{:S(2)}) copy-start(bf16[192,4096]{1,0:T(8,128)(2,1)} %get-tuple-element.82) | copy-start | bytes 4718596
  875.7 34.4 %copy-start.48 = (s32[1,512]{1,0:T(1,128)S(1)}, s32[1,512]{1,0:T(1,128)}, u32[]{:S(2)}) copy-start(s32[1,512]{1,0:T(1,128)} %copy-done.47) | copy-start | bytes 6148
  875.7 34.4 %copy-start.50 = (s32[1,512]{1,0:T(1,128)S(1)}, s32[1,512]{1,0:T(1,128)}, u32[]{:S(2)}) copy-start(s32[1,512]{1,0:T(1,128)} %copy-done.49) | copy-start | bytes 6148
  875.7 34.4 %copy-start.52 = (f32[1536]{0:T(1024)S(1)}, f32[1536]{0:T(1024)}, u32[]{:S(2)}) copy-start(f32[1536]{0:T(1024)} %add_reduce_fusion.1) | copy-start | bytes 18436
  908.0 14.0 copy-start.8
  908.0 16.8 copy-start.7
  908.0 21.9 %copy-start.6 = (bf16[192,4096]{1,0:T(8,128)(2,1)S(1)}, bf16[192,4096]{1,0:T(8,128)(2,1)}, u32[]{:S(2)}) copy-start(bf16[192,4096]{1,0:T(8,128)(2,1)} %get-tuple-element.79) | copy-start | bytes 4718596
  908.0 80.1 %collective-permute-start.4 = (bf16[192,4096]{1,0:T(8,128)(2,1)S(1)}, bf16[192,4096]{1,0:T(8,128)(2,1)S(1)}, u32[]{:S(2)}, u32[]{:S(2)}) collective-permute-start(bf16[192,4096]{1,0:T(8,128)(2,1)S(1)} %copy-done.9), channel_id=1, source_target_pairs={{0,4},{1,5},{2,6},{3,7},{4,0},{5,1},{6,2},{7,3},{8,12},{9,13},{10,... | collective-permute-start | bytes 4718600 | tf_op jit(solution)/shard_map/ppermute | solution.py:224
  922.0 199.7 %collective-permute-start.5 = (bf16[192,4096]{1,0:T(8,128)(2,1)S(1)}, bf16[192,4096]{1,0:T(8,128)(2,1)S(1)}, u32[]{:S(2)}, u32[]{:S(2)}) collective-permute-start(bf16[192,4096]{1,0:T(8,128)(2,1)S(1)} %copy-done.8), channel_id=1, source_target_pairs={{0,5},{1,4},{2,7},{3,6},{4,1},{5,0},{6,3},{7,2},{8,13},{9,12},{10,... | collective-permute-start | bytes 4718600 | tf_op jit(solution)/shard_map/ppermute | solution.py:224
  924.8 198.2 %collective-permute-start.6 = (bf16[192,4096]{1,0:T(8,128)(2,1)S(1)}, bf16[192,4096]{1,0:T(8,128)(2,1)S(1)}, u32[]{:S(2)}, u32[]{:S(2)}) collective-permute-start(bf16[192,4096]{1,0:T(8,128)(2,1)S(1)} %copy-done.7), channel_id=1, source_target_pairs={{0,6},{1,7},{2,4},{3,5},{4,2},{5,3},{6,0},{7,1},{8,14},{9,15},{10,... | collective-permute-start | bytes 4718600 | tf_op jit(solution)/shard_map/ppermute | solution.py:224
  929.9 194.4 %collective-permute-start.7 = (bf16[192,4096]{1,0:T(8,128)(2,1)S(1)}, bf16[192,4096]{1,0:T(8,128)(2,1)S(1)}, u32[]{:S(2)}, u32[]{:S(2)}) collective-permute-start(bf16[192,4096]{1,0:T(8,128)(2,1)S(1)} %copy-done.6), channel_id=1, source_target_pairs={{0,7},{1,6},{2,5},{3,4},{4,3},{5,2},{6,1},{7,0},{8,15},{9,14},{10,... | collective-permute-start | bytes 4718600 | tf_op jit(solution)/shard_map/ppermute | solution.py:224
  988.1 641.7 %collective-permute-start.8 = (bf16[1536,4096]{1,0:T(8,128)(2,1)}, bf16[1536,4096]{1,0:T(8,128)(2,1)}, u32[]{:S(2)}, u32[]{:S(2)}) collective-permute-start(bf16[1536,4096]{1,0:T(8,128)(2,1)} %bitcast.18.q_ref.refs_4_), channel_id=1, source_target_pairs={{0,8},{8,0},{16,24},{24,16},{1,9},{9,1},{17,25},{25,17},{2,10},{10... | collective-permute-start | bytes 37748744 | tf_op jit(solution)/shard_map/ppermute | solution.py:235
  1125.6 31.0 %slice-start.9 = ((s8[11272192]{0:T(1024)(128)(4,1)}), s8[2883584]{0:T(1024)(128)(4,1)S(1)}, s32[]{:S(2)}) async-start(s8[11272192]{0:T(1024)(128)(4,1)} %bitcast.184), calls=%async_computation.16 | async-start | bytes 5767168
  1125.6 144.6 %all-to-all-start.2 = ((bf16[8,192,4096]{2,1,0:T(8,128)(2,1)}), bf16[8,192,4096]{2,1,0:T(8,128)(2,1)}, u32[]{:S(2)}, u32[]{:S(2)}) async-start(bf16[8,192,4096]{2,1,0:T(8,128)(2,1)} %bitcast.144), calls=%async_computation.2 | async-start | bytes 25165824 | tf_op jit(solution)/shard_map/all_to_all | solution.py:201
  1131.2 25.4 %slice-start.10 = ((s8[11272192]{0:T(1024)(128)(4,1)}), s8[4194304]{0:T(1024)(128)(4,1)S(1)}, s32[]{:S(2)}) async-start(s8[11272192]{0:T(1024)(128)(4,1)} %bitcast.184), calls=%async_computation.17 | async-start | bytes 8388608
  1131.2 25.4 %slice-start.11 = ((s8[11272192]{0:T(1024)(128)(4,1)}), s8[4194304]{0:T(1024)(128)(4,1)S(1)}, s32[]{:S(2)}) async-start(s8[11272192]{0:T(1024)(128)(4,1)} %bitcast.184), calls=%async_computation.18 | async-start | bytes 8388608
  1131.2 47.5 %slice-start.3 = ((s8[11272192]{0:T(1024)(128)(4,1)}), s8[4194304]{0:T(1024)(128)(4,1)S(1)}, s32[]{:S(2)}) async-start(s8[11272192]{0:T(1024)(128)(4,1)} %bitcast.180), calls=%async_computation.10 | async-start | bytes 8388608
  1131.3 47.5 %slice-start.4 = ((s8[11272192]{0:T(1024)(128)(4,1)}), s8[4194304]{0:T(1024)(128)(4,1)S(1)}, s32[]{:S(2)}) async-start(s8[11272192]{0:T(1024)(128)(4,1)} %bitcast.180), calls=%async_computation.11 | async-start | bytes 8388608
  1156.7 22.1 %slice-start.5 = ((s8[11272192]{0:T(1024)(128)(4,1)}), s8[2883584]{0:T(1024)(128)(4,1)S(1)}, s32[]{:S(2)}) async-start(s8[11272192]{0:T(1024)(128)(4,1)} %bitcast.180), calls=%async_computation.12 | async-start | bytes 5767168
  1270.2 144.3 %all-to-all-start.3 = ((bf16[8,192,4096]{2,1,0:T(8,128)(2,1)}), bf16[8,192,4096]{2,1,0:T(8,128)(2,1)}, u32[]{:S(2)}, u32[]{:S(2)}) async-start(bf16[8,192,4096]{2,1,0:T(8,128)(2,1)} %bitcast.143), calls=%async_computation.3 | async-start | bytes 25165824 | tf_op jit(solution)/shard_map/all_to_all | solution.py:201
  1330.2 65.7 %copy-start.44 = (s32[512]{0:T(512)S(1)}, s32[512]{0:T(512)}, u32[]{:S(2)}) copy-start(s32[512]{0:T(512)} %copy-done.43) | copy-start | bytes 6148
  1330.2 65.7 %copy-start.46 = (s32[512]{0:T(512)S(1)}, s32[512]{0:T(512)}, u32[]{:S(2)}) copy-start(s32[512]{0:T(512)} %copy-done.45) | copy-start | bytes 6148
  1509.8 25.3 %copy-start.23 = (s32[512]{0:T(512)S(1)}, s32[512]{0:T(512)}, u32[]{:S(2)}) copy-start(s32[512]{0:T(512)} %param.16) | copy-start | bytes 6148
  1509.8 25.3 %copy-start.40 = (s32[512]{0:T(512)S(1)}, s32[512]{0:T(512)}, u32[]{:S(2)}) copy-start(s32[512]{0:T(512)} %param.19) | copy-start | bytes 6148
  1509.8 25.3 %copy-start.17 = (s32[512]{0:T(512)S(1)}, s32[512]{0:T(512)}, u32[]{:S(2)}) copy-start(s32[512]{0:T(512)} %param.15) | copy-start | bytes 6148
  1509.8 25.3 %copy-start.42 = (s32[512]{0:T(512)S(1)}, s32[512]{0:T(512)}, u32[]{:S(2)}) copy-start(s32[512]{0:T(512)} %param.18) | copy-start | bytes 6148
  1535.1 12.4 copy-start.2
  1535.1 12.4 copy-start.5
  1547.5 17.3 %copy-start.4 = (bf16[512,4096]{1,0:T(8,128)(2,1)S(1)}, bf16[512,4096]{1,0:T(8,128)(2,1)}, u32[]{:S(2)}) copy-start(bf16[512,4096]{1,0:T(8,128)(2,1)} %copy-done.3) | copy-start | bytes 12582916
  1547.5 17.3 %copy-start.11 = (f32[512,8]{0,1:T(8,128)S(1)}, f32[512,8]{0,1:T(8,128)}, u32[]{:S(2)}) copy-start(f32[512,8]{0,1:T(8,128)} %copy-done.10) | copy-start | bytes 49156
  1547.6 17.3 %copy-start.15 = (pred[512,8]{0,1:T(8,128)(4,1)S(1)}, pred[512,8]{0,1:T(8,128)(4,1)}, u32[]{:S(2)}) copy-start(pred[512,8]{0,1:T(8,128)(4,1)} %copy-done.14) | copy-start | bytes 12292
  1547.6 17.3 %copy-start.19 = (f32[512]{0:T(512)S(1)}, f32[512]{0:T(512)}, u32[]{:S(2)}) copy-start(f32[512]{0:T(512)} %copy-done.18) | copy-start | bytes 6148
  1547.6 17.3 %copy-start.21 = (f32[512]{0:T(512)S(1)}, f32[512]{0:T(512)}, u32[]{:S(2)}) copy-start(f32[512]{0:T(512)} %copy-done.20) | copy-start | bytes 6148
  1547.6 17.3 %copy-start.27 = (f32[512]{0:T(512)S(1)}, f32[512]{0:T(512)}, u32[]{:S(2)}) copy-start(f32[512]{0:T(512)} %copy-done.26) | copy-start | bytes 6148
  1547.6 17.3 %copy-start.29 = (f32[512]{0:T(512)S(1)}, f32[512]{0:T(512)}, u32[]{:S(2)}) copy-start(f32[512]{0:T(512)} %copy-done.28) | copy-start | bytes 6148
  1547.6 17.9 %copy-start.13 = (f32[4096]{0:T(1024)S(1)}, f32[4096]{0:T(1024)}, u32[]{:S(2)}) copy-start(f32[4096]{0:T(1024)} %copy-done.12) | copy-start | bytes 49156
  1547.6 17.9 %copy-start.25 = (f32[512]{0:T(512)S(1)}, f32[512]{0:T(512)}, u32[]{:S(2)}) copy-start(f32[512]{0:T(512)} %copy-done.24) | copy-start | bytes 6148
  1547.6 17.9 %copy-start.35 = (f32[512]{0:T(512)S(1)}, f32[512]{0:T(512)}, u32[]{:S(2)}) copy-start(f32[512]{0:T(512)} %copy-done.34) | copy-start | bytes 6148
  (23 other events, 104.7 us)

commit v8 on v7

--- a/solution.py
+++ b/solution.py
@@ -211,11 +211,18 @@
         h_f1 = lax.ppermute(hidden, 'dp', outer + middle)
         dy_f1 = lax.ppermute(after(tok_dy, h_f1), 'dp', outer + middle)
         q_buf = select_q(tok_dy, meta)
-        q_own = swap(q_buf)
+        ep_id = lax.axis_index('ep')
+        by_dest = q_buf.reshape(n_ep, slot_cap, d_model)
+        q_own = jnp.zeros_like(by_dest)
+        for k in range(n_ep):
+            piece = lax.dynamic_index_in_dim(by_dest, ep_id ^ k, 0, keepdims=False)
+            if k:
+                piece = lax.ppermute(piece, 'ep', [(i, i ^ k) for i in range(n_ep)])
+            q_own = lax.dynamic_update_index_in_dim(q_own, piece, ep_id ^ k, 0)
+        q_own = q_own.reshape(n_rows, d_model)
         a_t, b_t = pre(h_own)
         u_t = (a_t * jax.nn.sigmoid(a_t) * b_t).astype(bf16)
         exp_out = jnp.einsum('fr,fd->rd', u_t, wd, preferred_element_type=f32).astype(bf16)
-        ep_id = lax.axis_index('ep')
         by_dest = exp_out.reshape(n_ep, slot_cap, d_model)
         pieces = []
         for k in range(n_ep):

time: 1730 us -> 1620 us (0.936)
  waiting for transfers between devices: 821 us -> 539 us
  starting transfers between devices: 58.2 us -> 162 us
  Pallas kernels: 394 us -> 441 us
  local copies, waits for them, and re-layouts: 29.8 us -> 51.5 us
    all_to_all x7 -> x6, waiting for transfers between devices: 274 us -> 85 us  [swap(): lax.all_to_all(buf.reshape(n_ep, slot_cap, d_model), 'ep', 0, 0, tiled=True)]
    ppermute x1, waiting for transfers between devices: 179 us -> 0.01 us  [local_step(): m_f1 = lax.ppermute(meta, 'dp', outer + middle)]
    ppermute x1, waiting for transfers between devices: 181 us -> 6.34 us  [local_step(): h_f1 = lax.ppermute(hidden, 'dp', outer + middle)]
    ppermute x1, starting transfers between devices: 4.1 us -> 107 us  [local_step(): h_f2 = lax.ppermute(h_f1, 'dp', near)]
    ppermute x1, waiting for transfers between devices: 1.34 us -> 85.5 us  [local_step(): m_f2 = lax.ppermute(m_f1, 'dp', near)]
    ppermute x1, waiting for transfers between devices: 0.01 us -> 57.9 us  [local_step(): dy_f2 = lax.ppermute(dy_f1, 'dp', near)]
    ppermute x1, waiting for transfers between devices: 0.01 us -> 54.7 us  [local_step(): dy_f1 = lax.ppermute(after(tok_dy, h_f1), 'dp', outer + middle)]
    pallas_call x1, Pallas kernels: 17.3 us -> 64.1 us  [sum_all(): pl.pallas_call(functools.partial(sum_kernel, n_dp, n_ep), out_shape=jax.S...]
  transfers between devices with their start and end apart: 22 -> 28, of which waited for: 10 -> 12; matrix products, arithmetic and copies ran while one was open for 25% -> 28% of each run, Pallas kernels for 17% -> 21%
where the time goes in v8:
time: 1620 us
  waiting for transfers between devices  539 us (33%)
  Pallas kernels  441 us (27%)
  matrix products  400 us (25%)
  starting transfers between devices  162 us (10%)
  local copies, waits for them, and re-layouts  51.5 us (3%)
  other arithmetic  21.8 us (1%)
    pallas_call x4, Pallas kernels, add_dw(): pl.pallas_call(functools.partial(dw_kernel, first), grid=(d_model // d_ti...  259 us
    ppermute x14, waiting for transfers between devices, local_step(): piece = lax.ppermute(piece, 'ep', [(i, i ^ k) for i in range(n_ep)])  227 us
    pallas_call x4, Pallas kernels, inner_grad(): pl.pallas_call(grad_kernel, grid=(n_rows // r_tile,), in_specs=[pl.BlockS...  118 us
    ppermute x1, starting transfers between devices, local_step(): h_f2 = lax.ppermute(h_f1, 'dp', near)  107 us
    dot_general x4, matrix products, pre(): jnp.einsum('fd,rd->fr', wg_t, h, preferred_element_type=f32)  96.9 us
    dot_general x4, matrix products, pre(): jnp.einsum('fd,rd->fr', wu_t, h, preferred_element_type=f32)  95.1 us
    ppermute x1, waiting for transfers between devices, local_step(): m_f2 = lax.ppermute(m_f1, 'dp', near)  85.5 us
    all_to_all x6, waiting for transfers between devices, swap(): lax.all_to_all(buf.reshape(n_ep, slot_cap, d_model), 'ep', 0, 0, tiled=True)  85 us
  transfers between devices with their start and end apart: 28, of which 12 were waited for; matrix products, arithmetic and copies ran while one was open for 28% of the time, Pallas kernels for 21%

profile of v8, /device:TPU:0, one launch (start us, length us, event | category | flops | bytes accessed | tf_op | source)
XLA Modules:
  0.0 1616.5 jit_solution(6584899080205928140)
XLA Ops:
  0.7 3.0 convert_reduce_fusion
  3.7 3.4 fusion.55
  7.9 2.3 fusion.50
  10.2 9.6 convolution_convert_fusion.3
  19.8 5.6 all-to-all-start
  25.5 3.4 fusion.101
  30.3 11.8 multiply_convert_fusion.2
  42.1 6.1 broadcast_in_dim.160
  48.3 6.6 dynamic-slice_bitcast_fusion
  55.4 4.1 collective-permute-start.16
  64.4 85.5 %collective-permute-done.17 = f32[4,512]{1,0:T(4,128)S(1)} collective-permute-done((f32[4,512]{1,0:T(4,128)S(1)}, f32[4,512]{1,0:T(4,128)S(1)}, u32[]{:S(2)}, u32[]{:S(2)}) %collective-permute-start.17) | collective-permute-done | bytes 8224 | tf_op jit(solution)/shard_map/ppermute | solution.py:238
  154.6 44.1 %collective-permute-done.9 = bf16[192,4096]{1,0:T(8,128)(2,1)S(1)} collective-permute-done((bf16[192,4096]{1,0:T(8,128)(2,1)S(1)}, bf16[192,4096]{1,0:T(8,128)(2,1)S(1)}, u32[]{:S(2)}, u32[]{:S(2)}) %collective-permute-start.9) | collective-permute-done | bytes 1572896 | tf_op jit(solution)/shard_map/ppermute | solution.py:220
  201.5 29.2 %collective-permute-done.10 = bf16[192,4096]{1,0:T(8,128)(2,1)S(1)} collective-permute-done((bf16[192,4096]{1,0:T(8,128)(2,1)S(1)}, bf16[192,4096]{1,0:T(8,128)(2,1)S(1)}, u32[]{:S(2)}, u32[]{:S(2)}) %collective-permute-start.10) | collective-permute-done | bytes 1572896 | tf_op jit(solution)/shard_map/ppermute | solution.py:220
  230.7 3.0 collective-permute-start.14
  236.3 6.3 collective-permute-done.18
  242.7 106.9 %collective-permute-start.21 = (bf16[512,4096]{1,0:T(8,128)(2,1)}, bf16[512,4096]{1,0:T(8,128)(2,1)}, u32[]{:S(2)}, u32[]{:S(2)}) collective-permute-start(bf16[512,4096]{1,0:T(8,128)(2,1)} %collective-permute-done.18), channel_id=1, source_target_pairs={{0,8},{8,0},{16,24},{24,16},{1,9},{9,1},{17,25},{25,17},{2,10},{10... | collective-permute-start | bytes 12582920 | tf_op jit(solution)/shard_map/ppermute | solution.py:239
  352.1 11.9 convolution_convert_fusion.1
  364.1 5.4 all-to-all-start.5
  370.7 54.7 %collective-permute-done.19 = bf16[512,4096]{1,0:T(8,128)(2,1)} collective-permute-done((bf16[512,4096]{1,0:T(8,128)(2,1)}, bf16[512,4096]{1,0:T(8,128)(2,1)}, u32[]{:S(2)}, u32[]{:S(2)}) %collective-permute-start.19) | collective-permute-done | bytes 4194336 | tf_op jit(solution)/shard_map/ppermute | solution.py:212
  425.4 22.8 %collective-permute-done.21 = bf16[512,4096]{1,0:T(8,128)(2,1)} collective-permute-done((bf16[512,4096]{1,0:T(8,128)(2,1)}, bf16[512,4096]{1,0:T(8,128)(2,1)}, u32[]{:S(2)}, u32[]{:S(2)}) %collective-permute-start.21) | collective-permute-done | bytes 4194336 | tf_op jit(solution)/shard_map/ppermute | solution.py:239
  448.2 11.9 convolution_convert_fusion.2
  460.1 11.9 multiply_convert_fusion
  472.0 23.2 %fusion.28.a_ref = f32[1376,1536]{1,0:T(8,128)} fusion(bf16[1536,4096]{1,0:T(8,128)(2,1)} %bitcast.1.refs_3_, bf16[1,4096,1376]{1,2,0:T(8,128)(2,1)S(1)} %bitcast.210), kind=kOutput, calls=%fused_computation.40 | convolution fusion | flops 17314086912 | bytes 32309248 | tf_op jit(solution)/shard_map/fd,rd->fr/dot_general | solution.py:204
  495.2 22.5 %fusion.37.b_ref = f32[1376,1536]{1,0:T(8,128)} fusion(bf16[1536,4096]{1,0:T(8,128)(2,1)} %bitcast.1.refs_3_, bf16[1,4096,1376]{1,2,0:T(8,128)(2,1)S(1)} %bitcast.214), kind=kOutput, calls=%fused_computation.43 | convolution fusion | flops 17314086912 | bytes 32309248 | tf_op jit(solution)/shard_map/fd,rd->fr/dot_general | solution.py:205
  517.6 5.5 all-to-all-start.4
  523.2 28.7 %convolution_convert_fusion = bf16[1536,4096]{1,0:T(8,128)(2,1)} fusion(f32[1376,1536]{1,0:T(8,128)} %fusion.37.b_ref, f32[1376,1536]{1,0:T(8,128)} %fusion.28.a_ref, bf16[1,1376,4096]{2,1,0:T(8,128)(2,1)} %param.25), kind=kOutput, calls=%fused_computation.4 | convolution fusion | flops 17333059584 | bytes 40763392 | tf_op jit(solution)/shard_map/fr,fd->rd/dot_general | solution.py:225
  551.9 8.5 dynamic-slice_bitcast_fusion.7
  562.5 29.4 %shard_map.188 = (bf16[1376,1536]{1,0:T(8,128)(2,1)}, bf16[1376,1536]{1,0:T(8,128)(2,1)}, bf16[1376,1536]{1,0:T(8,128)(2,1)}) custom-call(bf16[1536,4096]{1,0:T(8,128)(2,1)} %bitcast.178, bf16[1376,4096]{1,0:T(8,128)(2,1)} %bitcast.217, f32[1376,1536]{1,0:T(8,128)} %fusion.28.a_ref, f32[1376,1536]{1,0:T(8,128)} %fusion.37.b_ref), custom_call_target="tpu_custom_call" | custom-call | flops 17314086912 | bytes 54755328 | tf_op jit(solution)/shard_map/pallas_call | solution.py:57
  591.9 61.4 %shard_map.192 = (f32[1376,4096]{1,0:T(8,128)}, f32[1376,4096]{1,0:T(8,128)}, f32[1376,4096]{1,0:T(8,128)}) custom-call(bf16[1376,1536]{1,0:T(8,128)(2,1)} %get-tuple-element.49.refs_0_, bf16[1376,1536]{1,0:T(8,128)(2,1)} %get-tuple-element.37.refs_1_, bf16[1376,1536]{1,0:T(8,128)(2,1)} %get-tuple-element.38.refs_2_, bf16[1536,4096]{1,0:T(8,128)(2,1)} %bitcast.1.refs_3_, ...), custom_call_target="tpu_custom_call" | custom-call | flops 51942260736 | bytes 92798976 | tf_op jit(solution)/shard_map/pallas_call | solution.py:89
  653.3 9.9 all-to-all-done.4
  663.2 5.7 all-to-all-start.3
  668.9 26.1 %fusion.13 = f32[1536,4096]{1,0:T(8,128)} fusion(bf16[1376,1536]{1,0:T(8,128)(2,1)} %get-tuple-element.37.refs_1_, bf16[1,4096,1376]{1,2,0:T(8,128)(2,1)} %param.23), kind=kOutput, calls=%fused_computation.27 | convolution fusion | flops 17314086912 | bytes 40665088 | tf_op jit(solution)/shard_map/fr,fd->rd/dot_general | solution.py:234
  695.1 29.6 %add_convert_fusion = bf16[1536,4096]{1,0:T(8,128)(2,1)} fusion(f32[1536,4096]{1,0:T(8,128)} %fusion.13, bf16[1376,1536]{1,0:T(8,128)(2,1)} %get-tuple-element.38.refs_2_, bf16[1,4096,1376]{1,2,0:T(8,128)(2,1)} %param.24), kind=kOutput, calls=%fused_computation.2 | convolution fusion | flops 17326669824 | bytes 53248000 | tf_op jit(solution)/shard_map/fr,fd->rd/dot_general | solution.py:235
  724.7 2.7 bitcast_dynamic-update-slice_fusion.7
  727.4 57.9 %collective-permute-done.20 = bf16[512,4096]{1,0:T(8,128)(2,1)} collective-permute-done((bf16[512,4096]{1,0:T(8,128)(2,1)}, bf16[512,4096]{1,0:T(8,128)(2,1)}, u32[]{:S(2)}, u32[]{:S(2)}) %collective-permute-start.20) | collective-permute-done | bytes 4194336 | tf_op jit(solution)/shard_map/ppermute | solution.py:240
  785.3 2.4 collective-permute-start.4
  787.7 12.0 multiply_convert_fusion.1
  799.7 2.7 constant_dynamic-update-slice_fusion.6
  804.1 2.7 constant_dynamic-update-slice_fusion.5
  807.7 2.7 constant_dynamic-update-slice_fusion.4
  810.4 21.3 %collective-permute-done.4 = bf16[192,4096]{1,0:T(8,128)(2,1)S(1)} collective-permute-done((bf16[192,4096]{1,0:T(8,128)(2,1)S(1)}, bf16[192,4096]{1,0:T(8,128)(2,1)S(1)}, u32[]{:S(2)}, u32[]{:S(2)}) %collective-permute-start.4) | collective-permute-done | bytes 1572896 | tf_op jit(solution)/shard_map/ppermute | solution.py:231
  833.0 132.3 %collective-permute-done.5 = bf16[192,4096]{1,0:T(8,128)(2,1)S(1)} collective-permute-done((bf16[192,4096]{1,0:T(8,128)(2,1)S(1)}, bf16[192,4096]{1,0:T(8,128)(2,1)S(1)}, u32[]{:S(2)}, u32[]{:S(2)}) %collective-permute-start.5) | collective-permute-done | bytes 1572896 | tf_op jit(solution)/shard_map/ppermute | solution.py:231
  969.3 5.6 all-to-all-start.1
  975.0 25.4 %fusion.34.a_ref = f32[1376,1536]{1,0:T(8,128)} fusion(bf16[1536,4096]{1,0:T(8,128)(2,1)} %bitcast.57.refs_3_, bf16[1,4096,1376]{1,2,0:T(8,128)(2,1)} %param.23), kind=kOutput, calls=%fused_computation.42 | convolution fusion | flops 17314086912 | bytes 32309248 | tf_op jit(solution)/shard_map/fd,rd->fr/dot_general | solution.py:204
  1000.4 22.1 %fusion.46.b_ref = f32[1376,1536]{1,0:T(8,128)} fusion(bf16[1536,4096]{1,0:T(8,128)(2,1)} %bitcast.57.refs_3_, bf16[1,4096,1376]{1,2,0:T(8,128)(2,1)S(1)} %bitcast.216), kind=kOutput, calls=%fused_computation.46 | convolution fusion | flops 17314086912 | bytes 32309248 | tf_op jit(solution)/shard_map/fd,rd->fr/dot_general | solution.py:205
  1022.5 23.1 %fusion.31.a_ref = f32[1376,1536]{1,0:T(8,128)} fusion(bf16[1536,4096]{1,0:T(8,128)(2,1)} %bitcast.47.refs_3_, bf16[1,4096,1376]{1,2,0:T(8,128)(2,1)S(1)} %bitcast.212), kind=kOutput, calls=%fused_computation.41 | convolution fusion | flops 17314086912 | bytes 32309248 | tf_op jit(solution)/shard_map/fd,rd->fr/dot_general | solution.py:204
  1045.6 68.3 %all-to-all-done.1 = bf16[8,192,4096]{2,1,0:T(8,128)(2,1)} async-done(((bf16[8,192,4096]{2,1,0:T(8,128)(2,1)}), bf16[8,192,4096]{2,1,0:T(8,128)(2,1)}, u32[]{:S(2)}, u32[]{:S(2)}) %all-to-all-start.1) | async-done | bytes 12582944 | tf_op jit(solution)/shard_map/all_to_all | solution.py:201
  1113.9 5.3 all-to-all-start.2
  1119.3 29.5 %shard_map.191 = (bf16[1376,1536]{1,0:T(8,128)(2,1)}, bf16[1376,1536]{1,0:T(8,128)(2,1)}, bf16[1376,1536]{1,0:T(8,128)(2,1)}) custom-call(bf16[1536,4096]{1,0:T(8,128)(2,1)} %bitcast.55.q_ref.refs_4_, bf16[1376,4096]{1,0:T(8,128)(2,1)} %bitcast.218, f32[1376,1536]{1,0:T(8,128)} %fusion.34.a_ref, f32[1376,1536]{1,0:T(8,128)} %fusion.46.b_ref), custom_call_target="tpu_custom_call" | custom-call | flops 17314086912 | bytes 54755328 | tf_op jit(solution)/shard_map/pallas_call | solution.py:57
  1148.7 25.3 %fusion.43.b_ref = f32[1376,1536]{1,0:T(8,128)} fusion(bf16[1536,4096]{1,0:T(8,128)(2,1)} %bitcast.47.refs_3_, bf16[1,4096,1376]{1,2,0:T(8,128)(2,1)} %param.24), kind=kOutput, calls=%fused_computation.45 | convolution fusion | flops 17314086912 | bytes 32309248 | tf_op jit(solution)/shard_map/fd,rd->fr/dot_general | solution.py:205
  1174.0 65.7 %shard_map.193 = (f32[1376,4096]{1,0:T(8,128)}, f32[1376,4096]{1,0:T(8,128)}, f32[1376,4096]{1,0:T(8,128)}) custom-call(bf16[1376,1536]{1,0:T(8,128)(2,1)} %get-tuple-element.46.refs_0_, bf16[1376,1536]{1,0:T(8,128)(2,1)} %get-tuple-element.47.refs_1_, ...), custom_call_target="tpu_custom_call", output_to_operand_aliasing={{0}: (5, {}), {1}: (6, {}), {2}: (7, {})} | custom-call | flops 51942260736 | bytes 160432128 | tf_op jit(solution)/shard_map/pallas_call | solution.py:89
  1239.7 11.7 fusion.76
  1251.5 6.8 all-to-all-done.2
  1258.2 29.5 %shard_map.190 = (bf16[1376,1536]{1,0:T(8,128)(2,1)}, bf16[1376,1536]{1,0:T(8,128)(2,1)}, bf16[1376,1536]{1,0:T(8,128)(2,1)}) custom-call(bf16[1536,4096]{1,0:T(8,128)(2,1)} %bitcast.45.q_ref.refs_4_, bf16[1376,4096]{1,0:T(8,128)(2,1)} %bitcast.219, f32[1376,1536]{1,0:T(8,128)} %fusion.31.a_ref, f32[1376,1536]{1,0:T(8,128)} %fusion.43.b_ref), custom_call_target="tpu_custom_call" | custom-call | flops 17314086912 | bytes 54755328 | tf_op jit(solution)/shard_map/pallas_call | solution.py:57
  1287.8 65.8 %shard_map.194 = (f32[1376,4096]{1,0:T(8,128)}, f32[1376,4096]{1,0:T(8,128)}, f32[1376,4096]{1,0:T(8,128)}) custom-call(bf16[1376,1536]{1,0:T(8,128)(2,1)} %get-tuple-element.43.refs_0_, bf16[1376,1536]{1,0:T(8,128)(2,1)} %get-tuple-element.44.refs_1_, ...), custom_call_target="tpu_custom_call", output_to_operand_aliasing={{0}: (5, {}), {1}: (6, {}), {2}: (7, {})} | custom-call | flops 51942260736 | bytes 160432128 | tf_op jit(solution)/shard_map/pallas_call | solution.py:89
  1353.6 25.3 %fusion.25.a_ref = f32[1376,1536]{1,0:T(8,128)} fusion(bf16[1536,4096]{1,0:T(8,128)(2,1)} %collective-permute-done.refs_3_, bf16[1,4096,1376]{1,2,0:T(8,128)(2,1)} %param.23), kind=kOutput, calls=%fused_computation.39 | convolution fusion | flops 17314086912 | bytes 32309248 | tf_op jit(solution)/shard_map/fd,rd->fr/dot_general | solution.py:204
  1379.0 12.3 fusion.66
  1391.4 17.9 %fusion.58 = (f32[512]{0:T(512)S(1)}, f32[512]{0:T(512)S(1)}, bf16[512,4096]{1,0:T(8,128)(2,1)}) fusion(bf16[512,4096]{1,0:T(8,128)(2,1)} %param.14, f32[512,4096]{1,0:T(8,128)} %fusion.66, f32[512]{0:T(512)S(1)} %copy-done.33, f32[512]{0:T(512)S(1)} %copy-done.31, bf16[512,4096]{1,0:T(8,128)(2,1)S(1)} %copy-done.2, ...), kind=kOutput, calls=%fused_computation.57 | convolution fusion | flops 6466305024 | bytes 33564672 | tf_op jit(solution)/shard_map/dot_general | solution.py:264
  1410.1 8.2 fusion.54
  1419.1 64.1 %shard_map.196 = f32[8,16,512]{2,1,0:T(8,128)} custom-call(f32[8,16,512]{2,1,0:T(8,128)} %maximum_bitcast_fusion.x_ref), custom_call_target="tpu_custom_call" | custom-call | tf_op jit(solution)/shard_map/pallas_call | solution.py:143
  1486.3 9.4 fusion.60
  1495.8 25.2 %fusion.40.b_ref = f32[1376,1536]{1,0:T(8,128)} fusion(bf16[1536,4096]{1,0:T(8,128)(2,1)} %collective-permute-done.refs_3_, bf16[1,4096,1376]{1,2,0:T(8,128)(2,1)} %param.24), kind=kOutput, calls=%fused_computation.44 | convolution fusion | flops 17314086912 | bytes 32309248 | tf_op jit(solution)/shard_map/fd,rd->fr/dot_general | solution.py:205
  1521.0 29.5 %shard_map.189 = (bf16[1376,1536]{1,0:T(8,128)(2,1)}, bf16[1376,1536]{1,0:T(8,128)(2,1)}, bf16[1376,1536]{1,0:T(8,128)(2,1)}) custom-call(bf16[1536,4096]{1,0:T(8,128)(2,1)} %collective-permute-done.15.q_ref.refs_4_, bf16[1376,4096]{1,0:T(8,128)(2,1)} %bitcast.220, f32[1376,1536]{1,0:T(8,128)} %fusion.25.a_ref, f32[1376,1536]{1,0:T(8,128)} %fusion.40.b_ref), custom_call_target="tpu_custom_call" | custom-call | flops 17314086912 | bytes 54755328 | tf_op jit(solution)/shard_map/pallas_call | solution.py:57
  1550.5 65.7 %shard_map.195 = (f32[1376,4096]{1,0:T(8,128)}, f32[1376,4096]{1,0:T(8,128)}, f32[1376,4096]{1,0:T(8,128)}) custom-call(bf16[1376,1536]{1,0:T(8,128)(2,1)} %get-tuple-element.39.refs_0_, bf16[1376,1536]{1,0:T(8,128)(2,1)} %get-tuple-element.40.refs_1_, ...), custom_call_target="tpu_custom_call", output_to_operand_aliasing={{0}: (5, {}), {1}: (6, {}), {2}: (7, {})} | custom-call | flops 51942260736 | bytes 160432128 | tf_op jit(solution)/shard_map/pallas_call | solution.py:89
  (207 shorter events, 36.1 us)
Async XLA Ops:
  0.6 24.8 %copy-start = (bf16[4096,8]{0,1:T(8,128)(2,1)S(1)}, bf16[4096,8]{0,1:T(8,128)(2,1)}, u32[]{:S(2)}) copy-start(bf16[4096,8]{0,1:T(8,128)(2,1)} %param.22) | copy-start | bytes 196612
  19.8 344.2 %all-to-all-start = ((bf16[8,192,4096]{2,1,0:T(8,128)(2,1)}), bf16[8,192,4096]{2,1,0:T(8,128)(2,1)}, u32[]{:S(2)}, u32[]{:S(2)}) async-start(bf16[8,192,4096]{2,1,0:T(8,128)(2,1)} %bitcast.169), calls=%async_computation | async-start | bytes 25165824 | tf_op jit(solution)/shard_map/all_to_all | solution.py:201
  29.0 26.4 %copy-start.30 = (f32[512]{0:T(512)}, f32[512]{0:T(512)S(1)}, u32[]{:S(2)}) copy-start(f32[512]{0:T(512)S(1)} %get-tuple-element.68) | copy-start | bytes 6148
  29.6 25.9 %copy-start.32 = (f32[512]{0:T(512)}, f32[512]{0:T(512)S(1)}, u32[]{:S(2)}) copy-start(f32[512]{0:T(512)S(1)} %select_reduce_fusion) | copy-start | bytes 6148
  54.9 98.4 %collective-permute-start.8 = (bf16[192,4096]{1,0:T(8,128)(2,1)S(1)}, bf16[192,4096]{1,0:T(8,128)(2,1)S(1)}, u32[]{:S(2)}, u32[]{:S(2)}) collective-permute-start(bf16[192,4096]{1,0:T(8,128)(2,1)S(1)} %get-tuple-element.85), channel_id=1, source_target_pairs={{0,1},{1,0},{2,3},{3,2},{4,5},{5,4},{6,7},{7,6},{8,9},{9,8},{10,11... | collective-permute-start | bytes 4718600 | tf_op jit(solution)/shard_map/ppermute | solution.py:220
  55.4 6.5 collective-permute-start.16
  59.5 183.1 %collective-permute-start.18 = (bf16[512,4096]{1,0:T(8,128)(2,1)S(1)}, bf16[512,4096]{1,0:T(8,128)(2,1)}, u32[]{:S(2)}, u32[]{:S(2)}) collective-permute-start(bf16[512,4096]{1,0:T(8,128)(2,1)S(1)} %copy-done.4), channel_id=1, source_target_pairs={{0,16},{24,8},{8,24},{16,0},{1,17},{25,9},{9,25},{17,1},{2,18},{26... | collective-permute-start | bytes 12582920 | tf_op jit(solution)/shard_map/ppermute | solution.py:211
  59.6 139.1 %collective-permute-start.9 = (bf16[192,4096]{1,0:T(8,128)(2,1)S(1)}, bf16[192,4096]{1,0:T(8,128)(2,1)S(1)}, u32[]{:S(2)}, u32[]{:S(2)}) collective-permute-start(bf16[192,4096]{1,0:T(8,128)(2,1)S(1)} %get-tuple-element.84), channel_id=1, source_target_pairs={{0,2},{1,3},{2,0},{3,1},{4,6},{5,7},{6,4},{7,5},{8,10},{9,11},{10,... | collective-permute-start | bytes 4718600 | tf_op jit(solution)/shard_map/ppermute | solution.py:220
  61.2 169.5 %collective-permute-start.10 = (bf16[192,4096]{1,0:T(8,128)(2,1)S(1)}, bf16[192,4096]{1,0:T(8,128)(2,1)S(1)}, u32[]{:S(2)}, u32[]{:S(2)}) collective-permute-start(bf16[192,4096]{1,0:T(8,128)(2,1)S(1)} %get-tuple-element.83), channel_id=1, source_target_pairs={{0,3},{1,2},{2,1},{3,0},{4,7},{5,6},{6,5},{7,4},{8,11},{9,10},{10,... | collective-permute-start | bytes 4718600 | tf_op jit(solution)/shard_map/ppermute | solution.py:220
  61.9 88.1 %collective-permute-start.17 = (f32[4,512]{1,0:T(4,128)S(1)}, f32[4,512]{1,0:T(4,128)S(1)}, u32[]{:S(2)}, u32[]{:S(2)}) collective-permute-start(f32[4,512]{1,0:T(4,128)S(1)} %collective-permute-done.16), channel_id=1, source_target_pairs={{0,8},{8,0},{16,24},{24,16},{1,9},{9,1},{17,25},{25,17},{2,10},{10... | collective-permute-start | bytes 24584 | tf_op jit(solution)/shard_map/ppermute | solution.py:238
  150.0 85.0 %collective-permute-start.11 = (bf16[192,4096]{1,0:T(8,128)(2,1)S(1)}, bf16[192,4096]{1,0:T(8,128)(2,1)S(1)}, u32[]{:S(2)}, u32[]{:S(2)}) collective-permute-start(bf16[192,4096]{1,0:T(8,128)(2,1)S(1)} %get-tuple-element.82), channel_id=1, source_target_pairs={{0,4},{1,5},{2,6},{3,7},{4,0},{5,1},{6,2},{7,3},{8,12},{9,13},{10,... | collective-permute-start | bytes 4718600 | tf_op jit(solution)/shard_map/ppermute | solution.py:220
  152.0 296.2 %copy-start.47 = (s32[1,512]{1,0:T(1,128)}, s32[1,512]{1,0:T(1,128)S(1)}, u32[]{:S(2)}) copy-start(s32[1,512]{1,0:T(1,128)S(1)} %get-tuple-element.100) | copy-start | bytes 6148
  152.0 296.2 %copy-start.49 = (s32[1,512]{1,0:T(1,128)}, s32[1,512]{1,0:T(1,128)S(1)}, u32[]{:S(2)}) copy-start(s32[1,512]{1,0:T(1,128)S(1)} %get-tuple-element.102) | copy-start | bytes 6148
  153.3 196.3 %collective-permute-start.12 = (bf16[192,4096]{1,0:T(8,128)(2,1)S(1)}, bf16[192,4096]{1,0:T(8,128)(2,1)S(1)}, u32[]{:S(2)}, u32[]{:S(2)}) collective-permute-start(bf16[192,4096]{1,0:T(8,128)(2,1)S(1)} %get-tuple-element.81), channel_id=1, source_target_pairs={{0,5},{1,4},{2,7},{3,6},{4,1},{5,0},{6,3},{7,2},{8,13},{9,12},{10,... | collective-permute-start | bytes 4718600 | tf_op jit(solution)/shard_map/ppermute | solution.py:220
  198.7 152.2 %collective-permute-start.13 = (bf16[192,4096]{1,0:T(8,128)(2,1)S(1)}, bf16[192,4096]{1,0:T(8,128)(2,1)S(1)}, u32[]{:S(2)}, u32[]{:S(2)}) collective-permute-start(bf16[192,4096]{1,0:T(8,128)(2,1)S(1)} %get-tuple-element.80), channel_id=1, source_target_pairs={{0,6},{1,7},{2,4},{3,5},{4,2},{5,3},{6,0},{7,1},{8,14},{9,15},{10,... | collective-permute-start | bytes 4718600 | tf_op jit(solution)/shard_map/ppermute | solution.py:220
  230.7 138.7 %collective-permute-start.14 = (bf16[192,4096]{1,0:T(8,128)(2,1)S(1)}, bf16[192,4096]{1,0:T(8,128)(2,1)S(1)}, u32[]{:S(2)}, u32[]{:S(2)}) collective-permute-start(bf16[192,4096]{1,0:T(8,128)(2,1)S(1)} %get-tuple-element.79), channel_id=1, source_target_pairs={{0,7},{1,6},{2,5},{3,4},{4,3},{5,2},{6,1},{7,0},{8,15},{9,14},{10,... | collective-permute-start | bytes 4718600 | tf_op jit(solution)/shard_map/ppermute | solution.py:220
  242.7 182.7 %collective-permute-start.19 = (bf16[512,4096]{1,0:T(8,128)(2,1)}, bf16[512,4096]{1,0:T(8,128)(2,1)}, u32[]{:S(2)}, u32[]{:S(2)}) collective-permute-start(bf16[512,4096]{1,0:T(8,128)(2,1)} %param.14), channel_id=1, source_target_pairs={{0,16},{24,8},{8,24},{16,0},{1,17},{25,9},{9,25},{17,1},{2,18},{26... | collective-permute-start | bytes 12582920 | tf_op jit(solution)/shard_map/ppermute | solution.py:212
  242.7 205.5 %collective-permute-start.21 = (bf16[512,4096]{1,0:T(8,128)(2,1)}, bf16[512,4096]{1,0:T(8,128)(2,1)}, u32[]{:S(2)}, u32[]{:S(2)}) collective-permute-start(bf16[512,4096]{1,0:T(8,128)(2,1)} %collective-permute-done.18), channel_id=1, source_target_pairs={{0,8},{8,0},{16,24},{24,16},{1,9},{9,1},{17,25},{25,17},{2,10},{10... | collective-permute-start | bytes 12582920 | tf_op jit(solution)/shard_map/ppermute | solution.py:239
  364.1 153.6 %all-to-all-start.5 = ((bf16[8,192,4096]{2,1,0:T(8,128)(2,1)}), bf16[8,192,4096]{2,1,0:T(8,128)(2,1)}, u32[]{:S(2)}, u32[]{:S(2)}) async-start(bf16[8,192,4096]{2,1,0:T(8,128)(2,1)} %bitcast.176), calls=%async_computation.5 | async-start | bytes 25165824 | tf_op jit(solution)/shard_map/all_to_all | solution.py:201
  370.7 1150.3 %collective-permute-start.15 = (bf16[1536,4096]{1,0:T(8,128)(2,1)}, bf16[1536,4096]{1,0:T(8,128)(2,1)}, u32[]{:S(2)}, u32[]{:S(2)}) collective-permute-start(bf16[1536,4096]{1,0:T(8,128)(2,1)} %bitcast.177), channel_id=1, source_target_pairs={{0,8},{8,0},{16,24},{24,16},{1,9},{9,1},{17,25},{25,17},{2,10},{10... | collective-permute-start | bytes 37748744 | tf_op jit(solution)/shard_map/ppermute | solution.py:242
  425.4 359.9 %collective-permute-start.20 = (bf16[512,4096]{1,0:T(8,128)(2,1)}, bf16[512,4096]{1,0:T(8,128)(2,1)}, u32[]{:S(2)}, u32[]{:S(2)}) collective-permute-start(bf16[512,4096]{1,0:T(8,128)(2,1)} %collective-permute-done.19), channel_id=1, source_target_pairs={{0,8},{8,0},{16,24},{24,16},{1,9},{9,1},{17,25},{25,17},{2,10},{10... | collective-permute-start | bytes 12582920 | tf_op jit(solution)/shard_map/ppermute | solution.py:240
  448.1 23.8 %slice-start = ((s8[11272192]{0:T(1024)(128)(4,1)}), s8[4194304]{0:T(1024)(128)(4,1)S(1)}, s32[]{:S(2)}) async-start(s8[11272192]{0:T(1024)(128)(4,1)} %bitcast.209), calls=%async_computation.6 | async-start | bytes 8388608
  448.1 23.8 %slice-start.1 = ((s8[11272192]{0:T(1024)(128)(4,1)}), s8[4194304]{0:T(1024)(128)(4,1)S(1)}, s32[]{:S(2)}) async-start(s8[11272192]{0:T(1024)(128)(4,1)} %bitcast.209), calls=%async_computation.7 | async-start | bytes 8388608
  460.1 35.1 %slice-start.6 = ((s8[11272192]{0:T(1024)(128)(4,1)}), s8[4194304]{0:T(1024)(128)(4,1)S(1)}, s32[]{:S(2)}) async-start(s8[11272192]{0:T(1024)(128)(4,1)} %bitcast.213), calls=%async_computation.12 | async-start | bytes 8388608
  472.0 23.2 %slice-start.7 = ((s8[11272192]{0:T(1024)(128)(4,1)}), s8[4194304]{0:T(1024)(128)(4,1)S(1)}, s32[]{:S(2)}) async-start(s8[11272192]{0:T(1024)(128)(4,1)} %bitcast.213), calls=%async_computation.13 | async-start | bytes 8388608
  472.0 23.2 %slice-start.8 = ((s8[11272192]{0:T(1024)(128)(4,1)}), s8[2883584]{0:T(1024)(128)(4,1)S(1)}, s32[]{:S(2)}) async-start(s8[11272192]{0:T(1024)(128)(4,1)} %bitcast.213), calls=%async_computation.14 | async-start | bytes 5767168
  517.6 145.5 %all-to-all-start.4 = ((bf16[8,192,4096]{2,1,0:T(8,128)(2,1)}), bf16[8,192,4096]{2,1,0:T(8,128)(2,1)}, u32[]{:S(2)}, u32[]{:S(2)}) async-start(bf16[8,192,4096]{2,1,0:T(8,128)(2,1)} %bitcast.175), calls=%async_computation.4 | async-start | bytes 25165824 | tf_op jit(solution)/shard_map/all_to_all | solution.py:201
  560.4 239.3 %collective-permute-start.1 = (bf16[192,4096]{1,0:T(8,128)(2,1)}, bf16[192,4096]{1,0:T(8,128)(2,1)}, u32[]{:S(2)}, u32[]{:S(2)}) collective-permute-start(bf16[192,4096]{1,0:T(8,128)(2,1)} %get-tuple-element.93), channel_id=1, source_target_pairs={{0,1},{1,0},{2,3},{3,2},{4,5},{5,4},{6,7},{7,6},{8,9},{9,8},{10,11... | collective-permute-start | bytes 4718600 | tf_op jit(solution)/shard_map/ppermute | solution.py:231
  560.8 241.6 %collective-permute-start.2 = (bf16[192,4096]{1,0:T(8,128)(2,1)}, bf16[192,4096]{1,0:T(8,128)(2,1)}, u32[]{:S(2)}, u32[]{:S(2)}) collective-permute-start(bf16[192,4096]{1,0:T(8,128)(2,1)} %get-tuple-element.92), channel_id=1, source_target_pairs={{0,2},{1,3},{2,0},{3,1},{4,6},{5,7},{6,4},{7,5},{8,10},{9,11},{10,... | collective-permute-start | bytes 4718600 | tf_op jit(solution)/shard_map/ppermute | solution.py:231
  562.5 244.3 %collective-permute-start.3 = (bf16[192,4096]{1,0:T(8,128)(2,1)}, bf16[192,4096]{1,0:T(8,128)(2,1)}, u32[]{:S(2)}, u32[]{:S(2)}) collective-permute-start(bf16[192,4096]{1,0:T(8,128)(2,1)} %get-tuple-element.91), channel_id=1, source_target_pairs={{0,3},{1,2},{2,1},{3,0},{4,7},{5,6},{6,5},{7,4},{8,11},{9,10},{10,... | collective-permute-start | bytes 4718600 | tf_op jit(solution)/shard_map/ppermute | solution.py:231
  663.2 306.1 %all-to-all-start.3 = ((bf16[8,192,4096]{2,1,0:T(8,128)(2,1)}), bf16[8,192,4096]{2,1,0:T(8,128)(2,1)}, u32[]{:S(2)}, u32[]{:S(2)}) async-start(bf16[8,192,4096]{2,1,0:T(8,128)(2,1)} %bitcast.170), calls=%async_computation.3 | async-start | bytes 25165824 | tf_op jit(solution)/shard_map/all_to_all | solution.py:201
  695.0 90.2 %copy-start.9 = (bf16[192,4096]{1,0:T(8,128)(2,1)S(1)}, bf16[192,4096]{1,0:T(8,128)(2,1)}, u32[]{:S(2)}) copy-start(bf16[192,4096]{1,0:T(8,128)(2,1)} %get-tuple-element.90) | copy-start | bytes 4718596
  695.0 92.6 %copy-start.48 = (s32[1,512]{1,0:T(1,128)S(1)}, s32[1,512]{1,0:T(1,128)}, u32[]{:S(2)}) copy-start(s32[1,512]{1,0:T(1,128)} %copy-done.47) | copy-start | bytes 6148
  695.0 92.6 %copy-start.50 = (s32[1,512]{1,0:T(1,128)S(1)}, s32[1,512]{1,0:T(1,128)}, u32[]{:S(2)}) copy-start(s32[1,512]{1,0:T(1,128)} %copy-done.49) | copy-start | bytes 6148
  695.0 92.6 %copy-start.52 = (f32[1536]{0:T(1024)S(1)}, f32[1536]{0:T(1024)}, u32[]{:S(2)}) copy-start(f32[1536]{0:T(1024)} %add_reduce_fusion.1) | copy-start | bytes 18436
  785.3 21.5 %copy-start.6 = (bf16[192,4096]{1,0:T(8,128)(2,1)S(1)}, bf16[192,4096]{1,0:T(8,128)(2,1)}, u32[]{:S(2)}) copy-start(bf16[192,4096]{1,0:T(8,128)(2,1)} %get-tuple-element.87) | copy-start | bytes 4718596
  785.3 46.4 %collective-permute-start.4 = (bf16[192,4096]{1,0:T(8,128)(2,1)S(1)}, bf16[192,4096]{1,0:T(8,128)(2,1)S(1)}, u32[]{:S(2)}, u32[]{:S(2)}) collective-permute-start(bf16[192,4096]{1,0:T(8,128)(2,1)S(1)} %copy-done.9), channel_id=1, source_target_pairs={{0,4},{1,5},{2,6},{3,7},{4,0},{5,1},{6,2},{7,3},{8,12},{9,13},{10,... | collective-permute-start | bytes 4718600 | tf_op jit(solution)/shard_map/ppermute | solution.py:231
  799.6 165.7 %collective-permute-start.5 = (bf16[192,4096]{1,0:T(8,128)(2,1)S(1)}, bf16[192,4096]{1,0:T(8,128)(2,1)S(1)}, u32[]{:S(2)}, u32[]{:S(2)}) collective-permute-start(bf16[192,4096]{1,0:T(8,128)(2,1)S(1)} %copy-done.8), channel_id=1, source_target_pairs={{0,5},{1,4},{2,7},{3,6},{4,1},{5,0},{6,3},{7,2},{8,13},{9,12},{10,... | collective-permute-start | bytes 4718600 | tf_op jit(solution)/shard_map/ppermute | solution.py:231
  802.4 164.3 %collective-permute-start.6 = (bf16[192,4096]{1,0:T(8,128)(2,1)S(1)}, bf16[192,4096]{1,0:T(8,128)(2,1)S(1)}, u32[]{:S(2)}, u32[]{:S(2)}) collective-permute-start(bf16[192,4096]{1,0:T(8,128)(2,1)S(1)} %copy-done.7), channel_id=1, source_target_pairs={{0,6},{1,7},{2,4},{3,5},{4,2},{5,3},{6,0},{7,1},{8,14},{9,15},{10,... | collective-permute-start | bytes 4718600 | tf_op jit(solution)/shard_map/ppermute | solution.py:231
  806.8 161.2 %collective-permute-start.7 = (bf16[192,4096]{1,0:T(8,128)(2,1)S(1)}, bf16[192,4096]{1,0:T(8,128)(2,1)S(1)}, u32[]{:S(2)}, u32[]{:S(2)}) collective-permute-start(bf16[192,4096]{1,0:T(8,128)(2,1)S(1)} %copy-done.6), channel_id=1, source_target_pairs={{0,7},{1,6},{2,5},{3,4},{4,3},{5,2},{6,1},{7,0},{8,15},{9,14},{10,... | collective-permute-start | bytes 4718600 | tf_op jit(solution)/shard_map/ppermute | solution.py:231
  831.7 521.9 %collective-permute-start = (bf16[1536,4096]{1,0:T(8,128)(2,1)}, bf16[1536,4096]{1,0:T(8,128)(2,1)}, u32[]{:S(2)}, u32[]{:S(2)}) collective-permute-start(bf16[1536,4096]{1,0:T(8,128)(2,1)} %bitcast.1.refs_3_), channel_id=1, source_target_pairs={{0,8},{8,0},{16,24},{24,16},{1,9},{9,1},{17,25},{25,17},{2,10},{10... | collective-permute-start | bytes 37748744 | tf_op jit(solution)/shard_map/ppermute | solution.py:241
  969.3 31.1 %slice-start.9 = ((s8[11272192]{0:T(1024)(128)(4,1)}), s8[2883584]{0:T(1024)(128)(4,1)S(1)}, s32[]{:S(2)}) async-start(s8[11272192]{0:T(1024)(128)(4,1)} %bitcast.215), calls=%async_computation.15 | async-start | bytes 5767168
  969.3 144.6 %all-to-all-start.1 = ((bf16[8,192,4096]{2,1,0:T(8,128)(2,1)}), bf16[8,192,4096]{2,1,0:T(8,128)(2,1)}, u32[]{:S(2)}, u32[]{:S(2)}) async-start(bf16[8,192,4096]{2,1,0:T(8,128)(2,1)} %bitcast.172), calls=%async_computation.1 | async-start | bytes 25165824 | tf_op jit(solution)/shard_map/all_to_all | solution.py:201
  974.9 25.4 %slice-start.10 = ((s8[11272192]{0:T(1024)(128)(4,1)}), s8[4194304]{0:T(1024)(128)(4,1)S(1)}, s32[]{:S(2)}) async-start(s8[11272192]{0:T(1024)(128)(4,1)} %bitcast.215), calls=%async_computation.16 | async-start | bytes 8388608
  974.9 25.4 %slice-start.11 = ((s8[11272192]{0:T(1024)(128)(4,1)}), s8[4194304]{0:T(1024)(128)(4,1)S(1)}, s32[]{:S(2)}) async-start(s8[11272192]{0:T(1024)(128)(4,1)} %bitcast.215), calls=%async_computation.17 | async-start | bytes 8388608
  974.9 47.5 %slice-start.3 = ((s8[11272192]{0:T(1024)(128)(4,1)}), s8[4194304]{0:T(1024)(128)(4,1)S(1)}, s32[]{:S(2)}) async-start(s8[11272192]{0:T(1024)(128)(4,1)} %bitcast.211), calls=%async_computation.9 | async-start | bytes 8388608
  975.0 47.5 %slice-start.4 = ((s8[11272192]{0:T(1024)(128)(4,1)}), s8[4194304]{0:T(1024)(128)(4,1)S(1)}, s32[]{:S(2)}) async-start(s8[11272192]{0:T(1024)(128)(4,1)} %bitcast.211), calls=%async_computation.10 | async-start | bytes 8388608
  1000.4 22.1 %slice-start.5 = ((s8[11272192]{0:T(1024)(128)(4,1)}), s8[2883584]{0:T(1024)(128)(4,1)S(1)}, s32[]{:S(2)}) async-start(s8[11272192]{0:T(1024)(128)(4,1)} %bitcast.211), calls=%async_computation.11 | async-start | bytes 5767168
  1113.9 144.3 %all-to-all-start.2 = ((bf16[8,192,4096]{2,1,0:T(8,128)(2,1)}), bf16[8,192,4096]{2,1,0:T(8,128)(2,1)}, u32[]{:S(2)}, u32[]{:S(2)}) async-start(bf16[8,192,4096]{2,1,0:T(8,128)(2,1)} %bitcast.171), calls=%async_computation.2 | async-start | bytes 25165824 | tf_op jit(solution)/shard_map/all_to_all | solution.py:201
  1174.0 65.7 %copy-start.44 = (s32[512]{0:T(512)S(1)}, s32[512]{0:T(512)}, u32[]{:S(2)}) copy-start(s32[512]{0:T(512)} %copy-done.43) | copy-start | bytes 6148
  1174.0 65.7 %copy-start.46 = (s32[512]{0:T(512)S(1)}, s32[512]{0:T(512)}, u32[]{:S(2)}) copy-start(s32[512]{0:T(512)} %copy-done.45) | copy-start | bytes 6148
  1353.6 25.3 %copy-start.23 = (s32[512]{0:T(512)S(1)}, s32[512]{0:T(512)}, u32[]{:S(2)}) copy-start(s32[512]{0:T(512)} %param.16) | copy-start | bytes 6148
  1353.6 25.3 %copy-start.40 = (s32[512]{0:T(512)S(1)}, s32[512]{0:T(512)}, u32[]{:S(2)}) copy-start(s32[512]{0:T(512)} %param.19) | copy-start | bytes 6148
  1353.6 25.3 %copy-start.17 = (s32[512]{0:T(512)S(1)}, s32[512]{0:T(512)}, u32[]{:S(2)}) copy-start(s32[512]{0:T(512)} %param.15) | copy-start | bytes 6148
  1353.6 25.3 %copy-start.42 = (s32[512]{0:T(512)S(1)}, s32[512]{0:T(512)}, u32[]{:S(2)}) copy-start(s32[512]{0:T(512)} %param.18) | copy-start | bytes 6148
  1391.3 18.1 %copy-start.5 = (bf16[512,4096]{1,0:T(8,128)(2,1)S(1)}, bf16[512,4096]{1,0:T(8,128)(2,1)}, u32[]{:S(2)}) copy-start(bf16[512,4096]{1,0:T(8,128)(2,1)} %copy-done.3) | copy-start | bytes 12582916
  1391.3 18.1 %copy-start.11 = (f32[512,8]{0,1:T(8,128)S(1)}, f32[512,8]{0,1:T(8,128)}, u32[]{:S(2)}) copy-start(f32[512,8]{0,1:T(8,128)} %copy-done.10) | copy-start | bytes 49156
  1391.4 18.1 %copy-start.15 = (pred[512,8]{0,1:T(8,128)(4,1)S(1)}, pred[512,8]{0,1:T(8,128)(4,1)}, u32[]{:S(2)}) copy-start(pred[512,8]{0,1:T(8,128)(4,1)} %copy-done.14) | copy-start | bytes 12292
  1391.4 18.1 %copy-start.19 = (f32[512]{0:T(512)S(1)}, f32[512]{0:T(512)}, u32[]{:S(2)}) copy-start(f32[512]{0:T(512)} %copy-done.18) | copy-start | bytes 6148
  1391.4 18.1 %copy-start.21 = (f32[512]{0:T(512)S(1)}, f32[512]{0:T(512)}, u32[]{:S(2)}) copy-start(f32[512]{0:T(512)} %copy-done.20) | copy-start | bytes 6148
  1391.4 18.1 %copy-start.27 = (f32[512]{0:T(512)S(1)}, f32[512]{0:T(512)}, u32[]{:S(2)}) copy-start(f32[512]{0:T(512)} %copy-done.26) | copy-start | bytes 6148
  1391.4 18.7 %copy-start.13 = (f32[4096]{0:T(1024)S(1)}, f32[4096]{0:T(1024)}, u32[]{:S(2)}) copy-start(f32[4096]{0:T(1024)} %copy-done.12) | copy-start | bytes 49156
  1391.4 18.7 %copy-start.25 = (f32[512]{0:T(512)S(1)}, f32[512]{0:T(512)}, u32[]{:S(2)}) copy-start(f32[512]{0:T(512)} %copy-done.24) | copy-start | bytes 6148
  1391.4 18.7 %copy-start.35 = (f32[512]{0:T(512)S(1)}, f32[512]{0:T(512)}, u32[]{:S(2)}) copy-start(f32[512]{0:T(512)} %copy-done.34) | copy-start | bytes 6148
  (29 other events, 190.0 us)
